TPU v7x, 32 devices: a whole 2x2x4 slice. The times are simulated.
32 devices in a mesh: rows: 32 (over z, y, x, core).
Axes of the slice: x: 2, y: 2, z: 4, core: 2. Of those that a mesh axis runs over, the one named last changes fastest.
Arguments:
- left: bfloat16 [131072, 512], P('rows'), may hold values from -6 to 6
- right: bfloat16 [131072, 512], P('rows'), may hold values from -6 to 6
- tiles: bfloat16 [2, 64, 128, 128], replicated, may hold values from -0.1875 to 0.1875
- source_blocks: int32 [2, 1024, 16], P(None, 'rows'), may hold values from 0 to 95, as said below
- tile_index: int32 [2, 1024, 16], P(None, 'rows'), may hold values from -1 to 63
- send_blocks: int32 [1024, 2], P('rows'), may hold values from -1 to 31, as said below
Outputs:
- moments: float32 [2, 512, 512], P(None, 'rows')
Inputs may be any that keep to these rules, and one draw needn't show every extreme that they name: `source_blocks`: every slot with v >= 32 names a slot of send_blocks that is not -1. Empty slots (tile -1) name an own block. Each provided block is named by some slot of the receiving device. Some device receives 2 blocks from every device, and some device has all of its slots filled. `send_blocks`: slot 0 is never -1; the two blocks that one device provides to another are different.
All inputs are finite; a program needn't handle non-finite values.
Results may differ from a plain program's by a relative error of at most 0.0029.
Values may be sent and summed in bfloat16 or wider, within the bound.
No kernel may reach another device: no remote copies, remote signals or barrier semaphores. Data moves between devices by JAX's collectives and lax.ppermute only.
A program may use at most 192 MiB of HBM per device.

v0:
```python
import functools
import math

import jax
import jax.numpy as jnp
from jax import lax
from jax.experimental import pallas as pl
from jax.experimental.pallas import tpu as pltpu
from jax.sharding import PartitionSpec as P


F32 = jnp.float32
BF16 = jnp.bfloat16
SHIFT = 1024
ROOM = 8 * 2**20
EARLY = 3
AHEAD = 6
SMEM = pltpu.SMEM
VMEM = pltpu.VMEM
HBM = pltpu.HBM


def exchange_order(devices):
    half = devices // 2
    far, near = list(range(half, devices)), list(range(1, half))
    order, far = far[:EARLY], far[EARLY:]
    while far or near:
        order += near[:1] + far[:1]
        near, far = near[1:], far[1:]
    return order


def exchange_groups(count):
    first, second = (count + 1) // 2, count - max(1, count // 5)
    return [(0, first), (first, second), (second, count)]


def in_hbm(value):
    return pltpu.with_memory_space_constraint(value, HBM)


def in_vmem(value):
    return pltpu.with_memory_space_constraint(value, VMEM)


def whole(shape, space=VMEM):
    return pl.BlockSpec(shape, lambda *_: (0,) * len(shape), memory_space=space)


def pack_kernel(masks, after, rank_ref, send_ref, blocks_ref, *rest):
    rest = rest[after:]
    outs, (held_ref, in_sems, out_sems) = rest[: len(masks)], rest[len(masks):]
    cap = send_ref.shape[0]
    rank = rank_ref[0]
    inward, outward = [], []
    for n, mask in enumerate(masks):
        for c in range(cap):
            i = n * cap + c
            block = jnp.maximum(send_ref[c, rank ^ mask], 0)
            copy = pltpu.make_async_copy(blocks_ref.at[block], held_ref.at[i], in_sems.at[i])
            copy.start()
            inward.append(copy)
            outward.append(pltpu.make_async_copy(held_ref.at[i], outs[n].at[c], out_sems.at[i]))
    for one, two in zip(inward, outward):
        one.wait()
        two.start()
    for copy in outward:
        copy.wait()


def pack(rank, send, blocks, masks, after=()):
    cap = send.shape[0]
    count = len(masks) * cap
    return pl.pallas_call(
        functools.partial(pack_kernel, masks, len(after)),
        out_shape=[jax.ShapeDtypeStruct((cap,) + blocks.shape[1:], BF16)] * len(masks),
        in_specs=[whole((1,), SMEM), whole(send.shape, SMEM)]
        + [pl.BlockSpec(memory_space=HBM)] * (1 + len(after)),
        out_specs=[pl.BlockSpec(memory_space=HBM)] * len(masks),
        scratch_shapes=[
            VMEM((count,) + blocks.shape[1:], BF16),
            pltpu.SemaphoreType.DMA((count,)),
            pltpu.SemaphoreType.DMA((count,)),
        ],
        name="pack",
    )(rank, send, blocks, *after)


def slot_lists(rank, send, source, tile, local, order, starts, spare):
    cap = send.shape[0]
    slots = source.shape[1]
    mine = lax.dynamic_index_in_dim(send, rank[0], 1, keepdims=False)
    away = source >= local
    r = jnp.maximum(source - local, 0)
    c = r % cap
    mask = (r // cap) ^ rank[0]
    spot = jnp.where(
        mask[..., None] == jnp.array(order, jnp.int32), jnp.arange(len(order), dtype=jnp.int32), 0
    ).sum(-1)
    own = source
    for n in range(cap):
        own = jnp.where(away & (c == n), jnp.maximum(mine[n], 0), own)
    phase = jnp.zeros_like(source)
    first = jnp.zeros_like(source)
    far = away & (mask != 0)
    for n, start in enumerate(starts):
        phase = jnp.where(far & (spot >= start), n + 1, phase)
        first = jnp.where(far & (spot >= start), start, first)
    value = tile * SHIFT + jnp.where(far, (spot - first) * cap + c, own)
    phases = jnp.arange(len(starts) + 1, dtype=jnp.int32)[:, None, None]
    hit = (tile >= 0)[None] & (phase[None] == phases)
    k = jnp.arange(slots, dtype=jnp.int32)
    before = (hit[:, :, None, :] & (k[None, :] < k[:, None])).astype(jnp.int32).sum(-1)
    there = hit[:, :, None, :] & (before[:, :, None, :] == k[:, None])
    empty = spare * SHIFT
    lists = jnp.where(there, value[None, :, None, :] - empty, 0).sum(-1) + empty
    return lists.reshape(len(starts) + 1, -1), hit.astype(jnp.int32).sum(-1)


def pair(entry, j, tiles_ref, pool_ref):
    e0, e1 = entry(2 * j), entry(2 * j + 1)
    return jnp.dot(
        jnp.concatenate([tiles_ref[e0 // SHIFT], tiles_ref[e1 // SHIFT]], axis=1),
        jnp.concatenate([pool_ref[e0 % SHIFT], pool_ref[e1 % SHIFT]], axis=0),
        preferred_element_type=F32,
    )


def add_rest(acc_ref, done, count, entry, tiles_ref, pool_ref):
    def one(j, carry):
        acc_ref[...] += pair(entry, j, tiles_ref, pool_ref)
        return carry

    lax.fori_loop(done, (count + 1) // 2, one, 0)


def pool_loads(arrivals, pool_ref, sems):
    cap = arrivals[0].shape[0]
    return [
        pltpu.make_async_copy(ref, pool_ref.at[pl.ds(n * cap, cap)], sems.at[n])
        for n, ref in enumerate(arrivals)
    ]


def in_chunks(from_ref, to_ref, sems):
    size = from_ref.shape[0] // sems.shape[0]
    return lambda i: pltpu.make_async_copy(
        from_ref.at[pl.ds(i * size, size)], to_ref.at[pl.ds(i * size, size)], sems.at[i]
    )


def hops_kernel(phase, slots, fixed, count, lists_ref, counts_ref, tiles_ref, *rest):
    if phase == 0:
        pool_ref, out_ref, held_ref, out_sems = rest
    else:
        in_ref, arrivals = rest[0], rest[1:1 + count]
        out_ref, held_ref, out_sems, pool_ref, in_sems, sems = rest[1 + count:]
    chunks = out_sems.shape[0]
    steps = held_ref.shape[0]
    bunch = steps // chunks
    outward = in_chunks(held_ref, out_ref, out_sems)
    if phase:
        inward = in_chunks(in_ref, held_ref, in_sems)
        loads = pool_loads(arrivals, pool_ref, sems)
        for copy in loads:
            copy.start()
        ahead = min(AHEAD, chunks)
        for i in range(ahead):
            inward(i).start()
        for copy in loads:
            copy.wait()

    def some(step, carry):
        tiles = tiles_ref.at[2 * step // chunks]
        if phase:
            @pl.when(step + ahead < chunks)
            def _():
                inward(step + ahead).start()

            inward(step).wait()
        for g in range(bunch):
            block = step * bunch + g
            entry = lambda j, block=block: lists_ref[phase, block * slots + j]
            for j in range(fixed):
                value = pair(entry, j, tiles, pool_ref)
                if j or phase:
                    held_ref[block] += value
                else:
                    held_ref[block] = value
        for g in range(bunch):
            block = step * bunch + g
            entry = lambda j, block=block: lists_ref[phase, block * slots + j]
            add_rest(held_ref.at[block], fixed, counts_ref[phase, block], entry, tiles, pool_ref)
        outward(step).start()
        return carry

    lax.fori_loop(0, chunks, some, 0)
    for i in range(chunks):
        outward(i).wait()


def hops(phase, lists, counts, tiles, pool, current, fixed, bunch=4):
    steps = counts.shape[1]
    slots = lists.shape[1] // steps
    chunks = steps // math.gcd(bunch, steps // 2)
    rows, vectors = (pool if phase == 0 else pool[0]).shape[1:]
    dma = pltpu.SemaphoreType.DMA
    in_specs = [pl.BlockSpec(memory_space=SMEM)] * 2 + [pl.BlockSpec(memory_space=VMEM)]
    scratch = [VMEM((steps, rows, vectors), F32), dma((chunks,))]
    if phase == 0:
        operands, aliases, count, held = [pool], {}, 0, [pool]
        in_specs += [pl.BlockSpec(memory_space=VMEM)]
    else:
        count, held = len(pool), pool
        operands, aliases = [in_hbm(current), *map(in_hbm, pool)], {3: 0}
        in_specs += [pl.BlockSpec(memory_space=HBM)] * (1 + count)
        scratch += [VMEM((count * pool[0].shape[0], rows, vectors), BF16), dma((chunks,)), dma((count,))]
    room = ROOM + 4 * steps * rows * vectors + sum(2 * a.size for a in held)
    return pl.pallas_call(
        functools.partial(hops_kernel, phase, slots, fixed, count),
        out_shape=HBM((steps, rows, vectors), F32),
        in_specs=in_specs,
        out_specs=pl.BlockSpec(memory_space=HBM),
        scratch_shapes=scratch,
        input_output_aliases=aliases,
        compiler_params=pltpu.CompilerParams(vmem_limit_bytes=room),
        cost_estimate=pl.CostEstimate(flops=8 * 10**9, bytes_accessed=40 * 2**20, transcendentals=0),
    )(lists, counts, tiles, *operands)


def gram_kernel(
    phase, count, slots, fixed, rank_ref, lists_ref, counts_ref, tiles_ref, in_ref, left_ref, *rest
):
    arrivals, rest = rest[:count], rest[count:]
    outs, (pool_ref, held_ref, current_ref, sum_ref, in_sems, sems) = rest[:-6], rest[-6:]
    steps, rows, vectors = held_ref.shape
    per = steps // 2
    chunks = in_sems.shape[0] // 2
    bunch = per // chunks
    inward = in_chunks(in_ref, held_ref, in_sems)
    loads = pool_loads(arrivals, pool_ref, sems)
    for copy in loads:
        copy.start()
    ahead = min(AHEAD // 2, chunks)
    for i in range(ahead):
        for d in range(2):
            inward(d * chunks + i).start()
    for copy in loads:
        copy.wait()

    def some(step, carry):
        spots = [(d, g, d * per + step * bunch + g) for d in range(2) for g in range(bunch)]

        @pl.when(step + ahead < chunks)
        def _():
            for d in range(2):
                inward(d * chunks + step + ahead).start()

        for d in range(2):
            inward(d * chunks + step).wait()
        for d, g, block in spots:
            entry = lambda j, block=block: lists_ref[phase, block * slots + j]
            for j in range(fixed):
                held_ref[block] += pair(entry, j, tiles_ref.at[d], pool_ref)
        for d, g, block in spots:
            entry = lambda j, block=block: lists_ref[phase, block * slots + j]
            add_rest(
                held_ref.at[block], fixed, counts_ref[phase, block], entry, tiles_ref.at[d], pool_ref
            )
        for d, g, block in spots:
            current_ref[pl.ds(g * rows, rows), pl.ds(d * vectors, vectors)] = held_ref[block].astype(BF16)
        part = jnp.dot(left_ref[step], current_ref[...], preferred_element_type=F32)

        @pl.when(step == 0)
        def _():
            sum_ref[...] = part

        @pl.when(step > 0)
        def _():
            sum_ref[...] += part

        return carry

    lax.fori_loop(0, chunks, some, 0)
    if len(outs) == 1:
        outs[0][...] = sum_ref[...]
        return
    send_ref, keep_ref = outs
    core = rank_ref[0] % 2
    outer, inner, own = send_ref.shape[:3]
    for n in range(outer * inner):
        keep_ref[n // inner, n % inner] = sum_ref[pl.ds(pl.multiple_of((2 * n + core) * own, own), own), :]
        send_ref[n // inner, n % inner] = sum_ref[pl.ds(pl.multiple_of((2 * n + 1 - core) * own, own), own), :].astype(send_ref.dtype)


def gram(phase, rank, lists, counts, tiles, current, left_t, arrivals, devices, sent, fixed):
    steps, rows, vectors = current.shape
    slots = lists.shape[1] // steps
    chunks = left_t.shape[0]
    cap = arrivals[0].shape[0]
    columns = left_t.shape[1]
    own = columns // devices
    block = pl.BlockSpec(memory_space=VMEM)
    dma = pltpu.SemaphoreType.DMA
    if own % 8:
        halves = [jax.ShapeDtypeStruct((columns, 2 * vectors), F32)]
    else:
        half = (devices // 8, 4, own, 2 * vectors)
        halves = [VMEM(half, sent), VMEM(half, F32)]
    room = 2 * ROOM + 4 * current.size + sum(2 * a.size for a in arrivals)
    return pl.pallas_call(
        functools.partial(gram_kernel, phase, len(arrivals), slots, fixed),
        out_shape=halves,
        in_specs=[pl.BlockSpec(memory_space=SMEM)] * 3
        + [block, pl.BlockSpec(memory_space=HBM), block]
        + [pl.BlockSpec(memory_space=HBM)] * len(arrivals),
        out_specs=[block] * len(halves),
        scratch_shapes=[
            VMEM((len(arrivals) * cap, rows, vectors), BF16),
            VMEM((steps, rows, vectors), F32),
            VMEM((left_t.shape[2], 2 * vectors), BF16),
            VMEM((columns, 2 * vectors), F32),
            dma((2 * chunks,)),
            dma((len(arrivals),)),
        ],
        compiler_params=pltpu.CompilerParams(vmem_limit_bytes=room),
        cost_estimate=pl.CostEstimate(flops=6 * 10**9, bytes_accessed=24 * 2**20, transcendentals=0),
        name="gram",
    )(rank, lists, counts, tiles, in_hbm(current), in_vmem(left_t), *map(in_hbm, arrivals))


def split_kernel(width, shift, count, final, scale, rank_ref, keep_ref, *rest):
    arrived, outs = rest[:count], rest[count:]
    mine = (rank_ref[0] >> shift) % width
    if final:
        vectors = outs[0].shape[-1]
        total = keep_ref[...]
        for ref in arrived:
            total = total + ref[...].astype(F32)
        total = total * scale
        for d in range(2):
            outs[0][d] = total[:, d * vectors:(d + 1) * vectors]
        return
    for mask in range(width):
        where = mine ^ mask
        if len(keep_ref.shape) == 4:
            part = keep_ref[:, where]
            for ref in arrived:
                part = part + ref[:, where].astype(F32)
        else:
            part = keep_ref[where]
            for ref in arrived:
                part = part + ref[where].astype(F32)
        outs[mask][...] = part.astype(outs[mask].dtype)


def split(rank, keep, arrived, width, shift, sent):
    part = keep.shape[:-3] + keep.shape[-2:]
    return pl.pallas_call(
        functools.partial(split_kernel, width, shift, len(arrived), False, None),
        out_shape=[VMEM(part, sent if n else F32) for n in range(width)],
        in_specs=[pl.BlockSpec(memory_space=SMEM)] + [pl.BlockSpec(memory_space=VMEM)] * (1 + len(arrived)),
        out_specs=[pl.BlockSpec(memory_space=VMEM)] * width,
        compiler_params=pltpu.CompilerParams(vmem_limit_bytes=ROOM),
    )(rank, *map(in_vmem, (keep, *arrived)))


def finish(rank, keep, arrived, scale):
    own, both = keep.shape
    return pl.pallas_call(
        functools.partial(split_kernel, 1, 0, len(arrived), True, scale),
        out_shape=jax.ShapeDtypeStruct((2, own, both // 2), F32),
        in_specs=[pl.BlockSpec(memory_space=SMEM)] + [pl.BlockSpec(memory_space=VMEM)] * (1 + len(arrived)),
        out_specs=pl.BlockSpec(memory_space=VMEM),
        compiler_params=pltpu.CompilerParams(vmem_limit_bytes=ROOM),
        name="finish",
    )(rank, *map(in_vmem, (keep, *arrived)))


def swap(value, mask, devices):
    return lax.ppermute(value, "rows", [(i, i ^ mask) for i in range(devices)])


def body(left, right, tiles, source_blocks, tile_index, send_blocks):
    block_rows = tiles.shape[-1]
    vectors = right.shape[1]
    local = right.shape[0] // block_rows
    devices = lax.axis_size("rows")
    slots = source_blocks.shape[-1]
    scale = 1.0 / math.sqrt(local * block_rows * devices)
    rank = lax.axis_index("rows").astype(jnp.int32).reshape(1)
    blocks = right.reshape(local, block_rows, vectors)
    order = exchange_order(devices)
    groups = exchange_groups(len(order))
    send = send_blocks.T

    early = min(EARLY, len(order))
    packed = pack(rank, send, blocks, order[:early])
    packed += pack(rank, send, blocks, order[early:], packed[:1])
    arrived = []
    for n, mask in enumerate(order):
        arrived.append(swap(packed[n], mask, devices))

    lists, counts = slot_lists(
        rank, send, source_blocks.reshape(2 * local, slots), tile_index.reshape(2 * local, slots),
        local, order, [start for start, _ in groups], tiles.shape[1],
    )
    tiles = jnp.concatenate([tiles, jnp.zeros((2, 1) + tiles.shape[2:], tiles.dtype)], axis=1)
    bunch = math.gcd(local, 4) * block_rows
    left_t = left.reshape(-1, bunch, vectors).transpose(0, 2, 1)
    tiles = in_vmem(tiles)
    current = hops(0, lists, counts, tiles, blocks, None, 4)
    for n, (start, stop) in enumerate(groups[:-1]):
        current = hops(n + 1, lists, counts, tiles, arrived[start:stop], current, 2)
    start, stop = groups[-1]
    sums = gram(
        len(groups), rank, lists, counts, tiles, current, left_t, arrived[start:stop], devices, F32, 1
    )
    if len(sums) == 1:
        mine = lax.psum_scatter(sums[0] * scale, "rows", scatter_dimension=0, tiled=True)
        return mine.reshape(mine.shape[0], 2, vectors).transpose(1, 0, 2)
    send, keep = sums
    outer = devices // 8
    got = swap(send, 1, devices)
    parts = split(rank, keep, [got], 4, 1, BF16)
    got = [swap(parts[n], n << 1, devices) for n in range(1, 4)]
    parts = split(rank, parts[0], got, outer, 3, F32)
    got = [swap(parts[n], n << 3, devices) for n in range(1, outer)]
    return finish(rank, parts[0], got, scale)


def solution(mesh):
    placed = (
        P("rows", None),
        P("rows", None),
        P(),
        P(None, "rows", None),
        P(None, "rows", None),
        P("rows", None),
    )

    return jax.shard_map(body, mesh=mesh, in_specs=placed, out_specs=P(None, "rows", None), check_vma=False)
```

profile of v0, /device:TPU:0, one launch (start us, length us, event | category | flops | bytes accessed | tf_op | source)
XLA Modules:
  0.0 263.7 jit_solution(10895934583502139911)
XLA Ops:
  0.0 2.8 %pack.2 = (bf16[2,128,512]{2,1,0:T(8,128)(2,1)}, bf16[2,128,512]{2,1,0:T(8,128)(2,1)}, bf16[2,128,512]{2,1,0:T(8,128)(2,1)}) custom-call(s32[1]{0:T(128)} %bitcast.rank_ref, s32[2,32]{1,0:T(2,128)} %bitcast.20, bf16[32,128,512]{2,1,0:T(8,128)(2,1)} %bitcast.15), custom_call_target="tpu_custom_call" | custom-call | tf_op jit(solution)/shard_map/pack/pallas_call | solution.py:74
  2.8 8.4 %pack.3 = (bf16[2,128,512]{2,1,0:T(8,128)(2,1)}, bf16[2,128,512]{2,1,0:T(8,128)(2,1)}, bf16[2,128,512]{2,1,0:T(8,128)(2,1)}, bf16[2,128,512]{2,1,0:T(8,128)(2,1)...) custom-call(s32[1]{0:T(128)} %bitcast.rank_ref, ...), custom_call_target="tpu_custom_call" | custom-call | tf_op jit(solution)/shard_map/pack/pallas_call | solution.py:74
  11.2 5.6 %collective-permute-start.10 = (bf16[2,128,512]{2,1,0:T(8,128)(2,1)}, bf16[2,128,512]{2,1,0:T(8,128)(2,1)S(1)}, u32[]{:S(2)}, u32[]{:S(2)}) collective-permute-start(bf16[2,128,512]{2,1,0:T(8,128)(2,1)} %get-tuple-element.56), channel_id=1, source_target_pairs={{0,22},{1,23},{2,20},{3,21},{4,18},{5,19},{6,16},{7,17},{8,30},{9,... | collective-permute-start | bytes 786440 | tf_op jit(solution)/shard_map/ppermute | solution.py:381
  16.8 1.6 collective-permute-start.12
  18.4 1.7 collective-permute-start.13
  20.1 3.6 %collective-permute-start.14 = (bf16[2,128,512]{2,1,0:T(8,128)(2,1)}, bf16[2,128,512]{2,1,0:T(8,128)(2,1)S(1)}, u32[]{:S(2)}, u32[]{:S(2)}) collective-permute-start(bf16[2,128,512]{2,1,0:T(8,128)(2,1)} %get-tuple-element.60), channel_id=1, source_target_pairs={{0,24},{1,25},{2,26},{3,27},{4,28},{5,29},{6,30},{7,31},{8,16},{9,... | collective-permute-start | bytes 786440 | tf_op jit(solution)/shard_map/ppermute | solution.py:381
  24.1 16.9 %collective-permute-done.10.rest_11_ = bf16[2,128,512]{2,1,0:T(8,128)(2,1)S(1)} collective-permute-done((bf16[2,128,512]{2,1,0:T(8,128)(2,1)}, bf16[2,128,512]{2,1,0:T(8,128)(2,1)S(1)}, u32[]{:S(2)}, u32[]{:S(2)}) %collective-permute-start.10) | collective-permute-done | bytes 262176 | tf_op jit(solution)/shard_map/ppermute | solution.py:381
  41.4 0.5 fusion.5
  43.4 2.6 collective-permute-start.3
  46.3 0.4 collective-permute-start.5
  46.6 13.2 %collective-permute-start.6 = (bf16[2,128,512]{2,1,0:T(8,128)(2,1)}, bf16[2,128,512]{2,1,0:T(8,128)(2,1)S(1)}, u32[]{:S(2)}, u32[]{:S(2)}) collective-permute-start(bf16[2,128,512]{2,1,0:T(8,128)(2,1)} %get-tuple-element.52), channel_id=1, source_target_pairs={{0,20},{1,21},{2,22},{3,23},{4,16},{5,17},{6,18},{7,19},{8,28},{9,... | collective-permute-start | bytes 786440 | tf_op jit(solution)/shard_map/ppermute | solution.py:381
  60.1 0.6 collective-permute-start
  60.8 12.9 %collective-permute-done.4.rest_5_ = bf16[2,128,512]{2,1,0:T(8,128)(2,1)S(1)} collective-permute-done((bf16[2,128,512]{2,1,0:T(8,128)(2,1)}, bf16[2,128,512]{2,1,0:T(8,128)(2,1)S(1)}, u32[]{:S(2)}, u32[]{:S(2)}) %collective-permute-start.4) | collective-permute-done | bytes 262176 | tf_op jit(solution)/shard_map/ppermute | solution.py:381
  73.7 1.0 collective-permute-start.9
  74.8 11.0 %collective-permute-done.6.rest_7_ = bf16[2,128,512]{2,1,0:T(8,128)(2,1)S(1)} collective-permute-done((bf16[2,128,512]{2,1,0:T(8,128)(2,1)}, bf16[2,128,512]{2,1,0:T(8,128)(2,1)S(1)}, u32[]{:S(2)}, u32[]{:S(2)}) %collective-permute-start.6) | collective-permute-done | bytes 262176 | tf_op jit(solution)/shard_map/ppermute | solution.py:381
  86.3 3.2 %concatenate.3.tiles_ref = bf16[2,65,128,128]{3,2,1,0:T(8,128)(2,1)S(1)} pad(bf16[2,64,128,128]{3,2,1,0:T(8,128)(2,1)} %param.9, bf16[]{:T(256)} %constant.71.clone.1), padding=0_0x0_1x0_0x0_0 | pad | bytes 8454146 | tf_op jit(solution)/shard_map/concatenate | solution.py:408
  89.6 17.6 %collective-permute-done.8.rest_9_ = bf16[2,128,512]{2,1,0:T(8,128)(2,1)} collective-permute-done((bf16[2,128,512]{2,1,0:T(8,128)(2,1)}, bf16[2,128,512]{2,1,0:T(8,128)(2,1)}, u32[]{:S(2)}, u32[]{:S(2)}) %collective-permute-start.8) | collective-permute-done | bytes 262176 | tf_op jit(solution)/shard_map/ppermute | solution.py:381
  107.2 3.8 %collective-permute-start.16 = (bf16[2,128,512]{2,1,0:T(8,128)(2,1)}, bf16[2,128,512]{2,1,0:T(8,128)(2,1)S(1)}, u32[]{:S(2)}, u32[]{:S(2)}) collective-permute-start(bf16[2,128,512]{2,1,0:T(8,128)(2,1)} %get-tuple-element.62), channel_id=1, source_target_pairs={{0,25},{1,24},{2,27},{3,26},{4,29},{5,28},{6,31},{7,30},{8,17},{9,... | collective-permute-start | bytes 786440 | tf_op jit(solution)/shard_map/ppermute | solution.py:381
  111.0 1.0 collective-permute-start.18
  112.0 0.4 collective-permute-done.1.rest_2_
  112.4 0.7 collective-permute-start.19
  113.1 17.4 %collective-permute-done.2.rest_3_ = bf16[2,128,512]{2,1,0:T(8,128)(2,1)} collective-permute-done((bf16[2,128,512]{2,1,0:T(8,128)(2,1)}, bf16[2,128,512]{2,1,0:T(8,128)(2,1)}, u32[]{:S(2)}, u32[]{:S(2)}) %collective-permute-start.2) | collective-permute-done | bytes 262176 | tf_op jit(solution)/shard_map/ppermute | solution.py:381
  130.5 14.7 %shard_map.73.rest_0_ = f32[64,128,512]{2,1,0:T(8,128)} custom-call(s32[4,1024]{1,0:T(4,128)S(1)} %add.78.lists_ref, s32[4,64]{1,0:T(4,128)S(1)} %get-tuple-element.87.counts_ref, bf16[2,65,128,128]{3,2,1,0:T(8,128)(2,1)S(1)} %concatenate.3.tiles_ref, bf16[32,128,512]{2,1,0:T(8,128)(2,1)S(1)} %bitcast.17), custom_call_target="tpu_custom_call" | custom-call | flops 8000000000 | bytes 41943040 | tf_op jit(solution)/shard_map/pallas_call | solution.py:219
  145.3 6.6 %copy.22 = bf16[8,512,512]{1,2,0:T(8,128)(2,1)} copy(bf16[8,512,512]{2,1,0:T(8,128)(2,1)} %bitcast.19) | data formatting | bytes 8388608 | tf_op jit(solution)/shard_map/reshape | solution.py:410
  151.9 8.5 %collective-permute-start.22 = (bf16[2,128,512]{2,1,0:T(8,128)(2,1)S(1)}, bf16[2,128,512]{2,1,0:T(8,128)(2,1)S(1)}, u32[]{:S(2)}, u32[]{:S(2)}) collective-permute-start(bf16[2,128,512]{2,1,0:T(8,128)(2,1)S(1)} %copy-done.43), channel_id=1, source_target_pairs={{0,28},{1,29},{2,30},{3,31},{4,24},{5,25},{6,26},{7,27},{8,20},{9,... | collective-permute-start | bytes 786440 | tf_op jit(solution)/shard_map/ppermute | solution.py:381
  160.9 2.2 copy-done.1
  163.1 16.2 %shard_map.74.rest_0_ = f32[64,128,512]{2,1,0:T(8,128)} custom-call(s32[4,1024]{1,0:T(4,128)S(1)} %add.78.lists_ref, s32[4,64]{1,0:T(4,128)S(1)} %get-tuple-element.87.counts_ref, bf16[2,65,128,128]{3,2,1,0:T(8,128)(2,1)S(1)} %copy-done.1, f32[64,128,512]{2,1,0:T(8,128)} %shard_map.73.rest_0_, ...), custom_call_target="tpu_custom_call", output_to_operand_aliasing={{}: (3, {})} | custom-call | flops 8000000000 | bytes 41943040 | tf_op jit(solution)/shard_map/pallas_call | solution.py:219
  179.4 6.7 %collective-permute-start.26 = (bf16[2,128,512]{2,1,0:T(8,128)(2,1)S(1)}, bf16[2,128,512]{2,1,0:T(8,128)(2,1)S(1)}, u32[]{:S(2)}, u32[]{:S(2)}) collective-permute-start(bf16[2,128,512]{2,1,0:T(8,128)(2,1)S(1)} %copy-done.39), channel_id=1, source_target_pairs={{0,30},{1,31},{2,28},{3,29},{4,26},{5,27},{6,24},{7,25},{8,22},{9,... | collective-permute-start | bytes 786440 | tf_op jit(solution)/shard_map/ppermute | solution.py:381
  186.1 2.5 collective-permute-start.27
  188.6 2.3 collective-permute-start.28
  191.0 9.3 %collective-permute-start.29 = (bf16[2,128,512]{2,1,0:T(8,128)(2,1)S(1)}, bf16[2,128,512]{2,1,0:T(8,128)(2,1)S(1)}, u32[]{:S(2)}, u32[]{:S(2)}) collective-permute-start(bf16[2,128,512]{2,1,0:T(8,128)(2,1)S(1)} %copy-done.36), channel_id=1, source_target_pairs={{0,14},{1,15},{2,12},{3,13},{4,10},{5,11},{6,8},{7,9},{8,6},{9,7},... | collective-permute-start | bytes 786440 | tf_op jit(solution)/shard_map/ppermute | solution.py:381
  200.4 16.1 %shard_map.75.in_ref = f32[64,128,512]{2,1,0:T(8,128)} custom-call(s32[4,1024]{1,0:T(4,128)S(1)} %add.78.lists_ref, s32[4,64]{1,0:T(4,128)S(1)} %get-tuple-element.87.counts_ref, bf16[2,65,128,128]{3,2,1,0:T(8,128)(2,1)S(1)} %copy-done.1, f32[64,128,512]{2,1,0:T(8,128)} %shard_map.74.rest_0_, ...), custom_call_target="tpu_custom_call", output_to_operand_aliasing={{}: (3, {})} | custom-call | flops 8000000000 | bytes 41943040 | tf_op jit(solution)/shard_map/pallas_call | solution.py:219
  216.6 3.0 %collective-permute-done.30.rest_5_ = bf16[2,128,512]{2,1,0:T(8,128)(2,1)S(1)} collective-permute-done((bf16[2,128,512]{2,1,0:T(8,128)(2,1)S(1)}, bf16[2,128,512]{2,1,0:T(8,128)(2,1)S(1)}, u32[]{:S(2)}, u32[]{:S(2)}) %collective-permute-start.30) | collective-permute-done | bytes 262176 | tf_op jit(solution)/shard_map/ppermute | solution.py:381
  219.6 0.7 copy-done.30
  220.3 17.3 %gram.1 = (f32[4,4,16,1024]{3,2,1,0:T(8,128)S(1)}, f32[4,4,16,1024]{3,2,1,0:T(8,128)S(1)}) custom-call(s32[1]{0:T(128)} %bitcast.rank_ref, s32[4,1024]{1,0:T(4,128)S(1)} %add.78.lists_ref, s32[4,64]{1,0:T(4,128)S(1)} %get-tuple-element.87.counts_ref, bf16[2,65,128,128]{3,2,1,0:T(8,128)(2,1)S(1)} %bitcast.14, f32[64,128,512]{2,1,0:T(8,128)} %shard_map.75.in_ref, ...), custom_call_target="tpu_custom_call" | custom-call | flops 6000000000 | bytes 25165824 | tf_op jit(solution)/shard_map/gram/pallas_call | solution.py:311
  237.7 2.6 %collective-permute-done.31.rest_0_ = f32[4,4,16,1024]{3,2,1,0:T(8,128)S(1)} collective-permute-done((f32[4,4,16,1024]{3,2,1,0:T(8,128)S(1)}, f32[4,4,16,1024]{3,2,1,0:T(8,128)S(1)}, u32[]{:S(2)}, u32[]{:S(2)}) %collective-permute-start.31) | collective-permute-done | bytes 1048608 | tf_op jit(solution)/shard_map/ppermute | solution.py:381
  240.5 1.3 collective-permute-start.32
  241.8 1.2 collective-permute-start.33
  242.9 1.4 collective-permute-start.34
  244.3 2.2 collective-permute-done.32.rest_0_
  246.6 2.5 collective-permute-done.33.rest_1_
  249.1 1.8 collective-permute-done.34.rest_2_
  250.9 1.3 collective-permute-start.35
  252.2 4.7 %collective-permute-start.36 = (f32[16,1024]{1,0:T(8,128)S(1)}, f32[16,1024]{1,0:T(8,128)S(1)}, u32[]{:S(2)}, u32[]{:S(2)}) collective-permute-start(f32[16,1024]{1,0:T(8,128)S(1)} %get-tuple-element.85), channel_id=1, source_target_pairs={{0,16},{1,17},{2,18},{3,19},{4,20},{5,21},{6,22},{7,23},{8,24},{9,... | collective-permute-start | bytes 196616 | tf_op jit(solution)/shard_map/ppermute | solution.py:381
  256.9 1.4 collective-permute-start.37
  258.3 0.9 collective-permute-done.36.rest_1_
  259.2 3.8 %collective-permute-done.37.rest_2_ = f32[16,1024]{1,0:T(8,128)S(1)} collective-permute-done((f32[16,1024]{1,0:T(8,128)S(1)}, f32[16,1024]{1,0:T(8,128)S(1)}, u32[]{:S(2)}, u32[]{:S(2)}) %collective-permute-start.37) | collective-permute-done | bytes 65568 | tf_op jit(solution)/shard_map/ppermute | solution.py:381
  263.0 0.6 finish.1
  (152 shorter events, 2.8 us)
Async XLA Ops:
  11.2 29.8 %collective-permute-start.10 = (bf16[2,128,512]{2,1,0:T(8,128)(2,1)}, bf16[2,128,512]{2,1,0:T(8,128)(2,1)S(1)}, u32[]{:S(2)}, u32[]{:S(2)}) collective-permute-start(bf16[2,128,512]{2,1,0:T(8,128)(2,1)} %get-tuple-element.56), channel_id=1, source_target_pairs={{0,22},{1,23},{2,20},{3,21},{4,18},{5,19},{6,16},{7,17},{8,30},{9,... | collective-permute-start | bytes 786440 | tf_op jit(solution)/shard_map/ppermute | solution.py:381
  16.8 26.5 %collective-permute-start.11 = (bf16[2,128,512]{2,1,0:T(8,128)(2,1)}, bf16[2,128,512]{2,1,0:T(8,128)(2,1)S(1)}, u32[]{:S(2)}, u32[]{:S(2)}) collective-permute-start(bf16[2,128,512]{2,1,0:T(8,128)(2,1)} %get-tuple-element.57), channel_id=1, source_target_pairs={{0,5},{1,4},{2,7},{3,6},{4,1},{5,0},{6,3},{7,2},{8,13},{9,12},{10,... | collective-permute-start | bytes 786440 | tf_op jit(solution)/shard_map/ppermute | solution.py:381
  16.8 29.4 %collective-permute-start.12 = (bf16[2,128,512]{2,1,0:T(8,128)(2,1)}, bf16[2,128,512]{2,1,0:T(8,128)(2,1)S(1)}, u32[]{:S(2)}, u32[]{:S(2)}) collective-permute-start(bf16[2,128,512]{2,1,0:T(8,128)(2,1)} %get-tuple-element.58), channel_id=1, source_target_pairs={{0,23},{1,22},{2,21},{3,20},{4,19},{5,18},{6,17},{7,16},{8,31},{9,... | collective-permute-start | bytes 786440 | tf_op jit(solution)/shard_map/ppermute | solution.py:381
  18.4 27.8 %collective-permute-start.13 = (bf16[2,128,512]{2,1,0:T(8,128)(2,1)}, bf16[2,128,512]{2,1,0:T(8,128)(2,1)S(1)}, u32[]{:S(2)}, u32[]{:S(2)}) collective-permute-start(bf16[2,128,512]{2,1,0:T(8,128)(2,1)} %get-tuple-element.59), channel_id=1, source_target_pairs={{0,6},{1,7},{2,4},{3,5},{4,2},{5,3},{6,0},{7,1},{8,14},{9,15},{10,... | collective-permute-start | bytes 786440 | tf_op jit(solution)/shard_map/ppermute | solution.py:381
  20.1 26.5 %collective-permute-start.14 = (bf16[2,128,512]{2,1,0:T(8,128)(2,1)}, bf16[2,128,512]{2,1,0:T(8,128)(2,1)S(1)}, u32[]{:S(2)}, u32[]{:S(2)}) collective-permute-start(bf16[2,128,512]{2,1,0:T(8,128)(2,1)} %get-tuple-element.60), channel_id=1, source_target_pairs={{0,24},{1,25},{2,26},{3,27},{4,28},{5,29},{6,30},{7,31},{8,16},{9,... | collective-permute-start | bytes 786440 | tf_op jit(solution)/shard_map/ppermute | solution.py:381
  41.0 48.5 %copy-start.4 = (bf16[2,128,512]{2,1,0:T(8,128)(2,1)}, bf16[2,128,512]{2,1,0:T(8,128)(2,1)S(1)}, u32[]{:S(2)}) copy-start(bf16[2,128,512]{2,1,0:T(8,128)(2,1)S(1)} %collective-permute-done.10.rest_11_) | copy-start | bytes 786436
  41.0 18.8 %collective-permute-start.15 = (bf16[2,128,512]{2,1,0:T(8,128)(2,1)}, bf16[2,128,512]{2,1,0:T(8,128)(2,1)S(1)}, u32[]{:S(2)}, u32[]{:S(2)}) collective-permute-start(bf16[2,128,512]{2,1,0:T(8,128)(2,1)} %get-tuple-element.61), channel_id=1, source_target_pairs={{0,7},{1,6},{2,5},{3,4},{4,3},{5,2},{6,1},{7,0},{8,15},{9,14},{10,... | collective-permute-start | bytes 786440 | tf_op jit(solution)/shard_map/ppermute | solution.py:381
  43.4 46.2 %copy-start.5 = (bf16[2,128,512]{2,1,0:T(8,128)(2,1)}, bf16[2,128,512]{2,1,0:T(8,128)(2,1)S(1)}, u32[]{:S(2)}) copy-start(bf16[2,128,512]{2,1,0:T(8,128)(2,1)S(1)} %collective-permute-done.11.rest_12_) | copy-start | bytes 786436
  43.4 16.8 %collective-permute-start.3 = (bf16[2,128,512]{2,1,0:T(8,128)(2,1)}, bf16[2,128,512]{2,1,0:T(8,128)(2,1)S(1)}, u32[]{:S(2)}, u32[]{:S(2)}) collective-permute-start(bf16[2,128,512]{2,1,0:T(8,128)(2,1)} %get-tuple-element.49), channel_id=1, source_target_pairs={{0,1},{1,0},{2,3},{3,2},{4,5},{5,4},{6,7},{7,6},{8,9},{9,8},{10,11... | collective-permute-start | bytes 786440 | tf_op jit(solution)/shard_map/ppermute | solution.py:381
  46.2 43.3 %copy-start.6 = (bf16[2,128,512]{2,1,0:T(8,128)(2,1)}, bf16[2,128,512]{2,1,0:T(8,128)(2,1)S(1)}, u32[]{:S(2)}) copy-start(bf16[2,128,512]{2,1,0:T(8,128)(2,1)S(1)} %collective-permute-done.12.rest_13_) | copy-start | bytes 786436
  46.2 27.5 %collective-permute-start.4 = (bf16[2,128,512]{2,1,0:T(8,128)(2,1)}, bf16[2,128,512]{2,1,0:T(8,128)(2,1)S(1)}, u32[]{:S(2)}, u32[]{:S(2)}) collective-permute-start(bf16[2,128,512]{2,1,0:T(8,128)(2,1)} %get-tuple-element.50), channel_id=1, source_target_pairs={{0,19},{1,18},{2,17},{3,16},{4,23},{5,22},{6,21},{7,20},{8,27},{9,... | collective-permute-start | bytes 786440 | tf_op jit(solution)/shard_map/ppermute | solution.py:381
  46.3 43.3 %copy-start.7 = (bf16[2,128,512]{2,1,0:T(8,128)(2,1)}, bf16[2,128,512]{2,1,0:T(8,128)(2,1)S(1)}, u32[]{:S(2)}) copy-start(bf16[2,128,512]{2,1,0:T(8,128)(2,1)S(1)} %collective-permute-done.13.rest_14_) | copy-start | bytes 786436
  46.3 27.5 %collective-permute-start.5 = (bf16[2,128,512]{2,1,0:T(8,128)(2,1)}, bf16[2,128,512]{2,1,0:T(8,128)(2,1)S(1)}, u32[]{:S(2)}, u32[]{:S(2)}) collective-permute-start(bf16[2,128,512]{2,1,0:T(8,128)(2,1)} %get-tuple-element.51), channel_id=1, source_target_pairs={{0,2},{1,3},{2,0},{3,1},{4,6},{5,7},{6,4},{7,5},{8,10},{9,11},{10,... | collective-permute-start | bytes 786440 | tf_op jit(solution)/shard_map/ppermute | solution.py:381
  46.6 42.9 %copy-start.8 = (bf16[2,128,512]{2,1,0:T(8,128)(2,1)}, bf16[2,128,512]{2,1,0:T(8,128)(2,1)S(1)}, u32[]{:S(2)}) copy-start(bf16[2,128,512]{2,1,0:T(8,128)(2,1)S(1)} %collective-permute-done.14.rest_15_) | copy-start | bytes 786436
  46.6 39.1 %collective-permute-start.6 = (bf16[2,128,512]{2,1,0:T(8,128)(2,1)}, bf16[2,128,512]{2,1,0:T(8,128)(2,1)S(1)}, u32[]{:S(2)}, u32[]{:S(2)}) collective-permute-start(bf16[2,128,512]{2,1,0:T(8,128)(2,1)} %get-tuple-element.52), channel_id=1, source_target_pairs={{0,20},{1,21},{2,22},{3,23},{4,16},{5,17},{6,18},{7,19},{8,28},{9,... | collective-permute-start | bytes 786440 | tf_op jit(solution)/shard_map/ppermute | solution.py:381
  59.9 29.7 %copy-start.9 = (bf16[2,128,512]{2,1,0:T(8,128)(2,1)}, bf16[2,128,512]{2,1,0:T(8,128)(2,1)S(1)}, u32[]{:S(2)}) copy-start(bf16[2,128,512]{2,1,0:T(8,128)(2,1)S(1)} %collective-permute-done.15.rest_16_) | copy-start | bytes 786436
  59.9 25.9 %collective-permute-start.7 = (bf16[2,128,512]{2,1,0:T(8,128)(2,1)}, bf16[2,128,512]{2,1,0:T(8,128)(2,1)S(1)}, u32[]{:S(2)}, u32[]{:S(2)}) collective-permute-start(bf16[2,128,512]{2,1,0:T(8,128)(2,1)} %get-tuple-element.53), channel_id=1, source_target_pairs={{0,3},{1,2},{2,1},{3,0},{4,7},{5,6},{6,5},{7,4},{8,11},{9,10},{10,... | collective-permute-start | bytes 786440 | tf_op jit(solution)/shard_map/ppermute | solution.py:381
  60.1 50.8 %collective-permute-start = (bf16[2,128,512]{2,1,0:T(8,128)(2,1)}, bf16[2,128,512]{2,1,0:T(8,128)(2,1)S(1)}, u32[]{:S(2)}, u32[]{:S(2)}) collective-permute-start(bf16[2,128,512]{2,1,0:T(8,128)(2,1)} %get-tuple-element.46.rest_0_), channel_id=1, source_target_pairs={{0,16},{1,17},{2,18},{3,19},{4,20},{5,21},{6,22},{7,23},{8,24},{9,... | collective-permute-start | bytes 786440 | tf_op jit(solution)/shard_map/ppermute | solution.py:381
  73.7 33.5 %collective-permute-start.8 = (bf16[2,128,512]{2,1,0:T(8,128)(2,1)}, bf16[2,128,512]{2,1,0:T(8,128)(2,1)}, u32[]{:S(2)}, u32[]{:S(2)}) collective-permute-start(bf16[2,128,512]{2,1,0:T(8,128)(2,1)} %get-tuple-element.54), channel_id=1, source_target_pairs={{0,21},{1,20},{2,23},{3,22},{4,17},{5,16},{6,19},{7,18},{8,29},{9,... | collective-permute-start | bytes 786440 | tf_op jit(solution)/shard_map/ppermute | solution.py:381
  73.7 37.2 %collective-permute-start.9 = (bf16[2,128,512]{2,1,0:T(8,128)(2,1)}, bf16[2,128,512]{2,1,0:T(8,128)(2,1)}, u32[]{:S(2)}, u32[]{:S(2)}) collective-permute-start(bf16[2,128,512]{2,1,0:T(8,128)(2,1)} %get-tuple-element.55), channel_id=1, source_target_pairs={{0,4},{1,5},{2,6},{3,7},{4,0},{5,1},{6,2},{7,3},{8,12},{9,13},{10,... | collective-permute-start | bytes 786440 | tf_op jit(solution)/shard_map/ppermute | solution.py:381
  85.8 26.6 %collective-permute-start.1 = (bf16[2,128,512]{2,1,0:T(8,128)(2,1)}, bf16[2,128,512]{2,1,0:T(8,128)(2,1)}, u32[]{:S(2)}, u32[]{:S(2)}) collective-permute-start(bf16[2,128,512]{2,1,0:T(8,128)(2,1)} %get-tuple-element.47), channel_id=1, source_target_pairs={{0,17},{1,16},{2,19},{3,18},{4,21},{5,20},{6,23},{7,22},{8,25},{9,... | collective-permute-start | bytes 786440 | tf_op jit(solution)/shard_map/ppermute | solution.py:381
  85.8 44.7 %collective-permute-start.2 = (bf16[2,128,512]{2,1,0:T(8,128)(2,1)}, bf16[2,128,512]{2,1,0:T(8,128)(2,1)}, u32[]{:S(2)}, u32[]{:S(2)}) collective-permute-start(bf16[2,128,512]{2,1,0:T(8,128)(2,1)} %get-tuple-element.48), channel_id=1, source_target_pairs={{0,18},{1,19},{2,16},{3,17},{4,22},{5,23},{6,20},{7,21},{8,26},{9,... | collective-permute-start | bytes 786440 | tf_op jit(solution)/shard_map/ppermute | solution.py:381
  86.3 44.2 %copy-start.2 = (bf16[4096,512]{1,0:T(8,128)(2,1)S(1)}, bf16[4096,512]{1,0:T(8,128)(2,1)}, u32[]{:S(2)}) copy-start(bf16[4096,512]{1,0:T(8,128)(2,1)} %param.8) | copy-start | bytes 12582916
  89.6 55.6 %copy-start = (bf16[2,65,128,128]{3,2,1,0:T(8,128)(2,1)}, bf16[2,65,128,128]{3,2,1,0:T(8,128)(2,1)S(1)}, u32[]{:S(2)}) copy-start(bf16[2,65,128,128]{3,2,1,0:T(8,128)(2,1)S(1)} %concatenate.3.tiles_ref) | copy-start | bytes 12779524
  107.2 44.7 %collective-permute-start.16 = (bf16[2,128,512]{2,1,0:T(8,128)(2,1)}, bf16[2,128,512]{2,1,0:T(8,128)(2,1)S(1)}, u32[]{:S(2)}, u32[]{:S(2)}) collective-permute-start(bf16[2,128,512]{2,1,0:T(8,128)(2,1)} %get-tuple-element.62), channel_id=1, source_target_pairs={{0,25},{1,24},{2,27},{3,26},{4,29},{5,28},{6,31},{7,30},{8,17},{9,... | collective-permute-start | bytes 786440 | tf_op jit(solution)/shard_map/ppermute | solution.py:381
  111.0 40.9 %collective-permute-start.17 = (bf16[2,128,512]{2,1,0:T(8,128)(2,1)}, bf16[2,128,512]{2,1,0:T(8,128)(2,1)S(1)}, u32[]{:S(2)}, u32[]{:S(2)}) collective-permute-start(bf16[2,128,512]{2,1,0:T(8,128)(2,1)} %get-tuple-element.63), channel_id=1, source_target_pairs={{0,8},{1,9},{2,10},{3,11},{4,12},{5,13},{6,14},{7,15},{8,0},{9,1},... | collective-permute-start | bytes 786440 | tf_op jit(solution)/shard_map/ppermute | solution.py:381
  111.0 34.2 %copy-start.15 = (bf16[2,128,512]{2,1,0:T(8,128)(2,1)}, bf16[2,128,512]{2,1,0:T(8,128)(2,1)S(1)}, u32[]{:S(2)}) copy-start(bf16[2,128,512]{2,1,0:T(8,128)(2,1)S(1)} %collective-permute-done.rest_1_) | copy-start | bytes 786436
  111.0 49.4 %collective-permute-start.18 = (bf16[2,128,512]{2,1,0:T(8,128)(2,1)}, bf16[2,128,512]{2,1,0:T(8,128)(2,1)S(1)}, u32[]{:S(2)}, u32[]{:S(2)}) collective-permute-start(bf16[2,128,512]{2,1,0:T(8,128)(2,1)} %get-tuple-element.64), channel_id=1, source_target_pairs={{0,26},{1,27},{2,24},{3,25},{4,30},{5,31},{6,28},{7,29},{8,18},{9,... | collective-permute-start | bytes 786440 | tf_op jit(solution)/shard_map/ppermute | solution.py:381
  112.4 48.1 %collective-permute-start.19 = (bf16[2,128,512]{2,1,0:T(8,128)(2,1)}, bf16[2,128,512]{2,1,0:T(8,128)(2,1)S(1)}, u32[]{:S(2)}, u32[]{:S(2)}) collective-permute-start(bf16[2,128,512]{2,1,0:T(8,128)(2,1)} %get-tuple-element.65), channel_id=1, source_target_pairs={{0,9},{1,8},{2,11},{3,10},{4,13},{5,12},{6,15},{7,14},{8,1},{9,0},... | collective-permute-start | bytes 786440 | tf_op jit(solution)/shard_map/ppermute | solution.py:381
  130.5 30.3 %collective-permute-start.20 = (bf16[2,128,512]{2,1,0:T(8,128)(2,1)}, bf16[2,128,512]{2,1,0:T(8,128)(2,1)S(1)}, u32[]{:S(2)}, u32[]{:S(2)}) collective-permute-start(bf16[2,128,512]{2,1,0:T(8,128)(2,1)} %get-tuple-element.66), channel_id=1, source_target_pairs={{0,27},{1,26},{2,25},{3,24},{4,31},{5,30},{6,29},{7,28},{8,19},{9,... | collective-permute-start | bytes 786440 | tf_op jit(solution)/shard_map/ppermute | solution.py:381
  151.9 27.5 %collective-permute-start.21 = (bf16[2,128,512]{2,1,0:T(8,128)(2,1)}, bf16[2,128,512]{2,1,0:T(8,128)(2,1)S(1)}, u32[]{:S(2)}, u32[]{:S(2)}) collective-permute-start(bf16[2,128,512]{2,1,0:T(8,128)(2,1)} %get-tuple-element.67), channel_id=1, source_target_pairs={{0,10},{1,11},{2,8},{3,9},{4,14},{5,15},{6,12},{7,13},{8,2},{9,3},... | collective-permute-start | bytes 786440 | tf_op jit(solution)/shard_map/ppermute | solution.py:381
  151.9 34.2 %collective-permute-start.22 = (bf16[2,128,512]{2,1,0:T(8,128)(2,1)S(1)}, bf16[2,128,512]{2,1,0:T(8,128)(2,1)S(1)}, u32[]{:S(2)}, u32[]{:S(2)}) collective-permute-start(bf16[2,128,512]{2,1,0:T(8,128)(2,1)S(1)} %copy-done.43), channel_id=1, source_target_pairs={{0,28},{1,29},{2,30},{3,31},{4,24},{5,25},{6,26},{7,27},{8,20},{9,... | collective-permute-start | bytes 786440 | tf_op jit(solution)/shard_map/ppermute | solution.py:381
  160.4 28.2 %collective-permute-start.23 = (bf16[2,128,512]{2,1,0:T(8,128)(2,1)S(1)}, bf16[2,128,512]{2,1,0:T(8,128)(2,1)S(1)}, u32[]{:S(2)}, u32[]{:S(2)}) collective-permute-start(bf16[2,128,512]{2,1,0:T(8,128)(2,1)S(1)} %copy-done.42), channel_id=1, source_target_pairs={{0,11},{1,10},{2,9},{3,8},{4,15},{5,14},{6,13},{7,12},{8,3},{9,2},... | collective-permute-start | bytes 786440 | tf_op jit(solution)/shard_map/ppermute | solution.py:381
  160.5 30.5 %collective-permute-start.24 = (bf16[2,128,512]{2,1,0:T(8,128)(2,1)S(1)}, bf16[2,128,512]{2,1,0:T(8,128)(2,1)S(1)}, u32[]{:S(2)}, u32[]{:S(2)}) collective-permute-start(bf16[2,128,512]{2,1,0:T(8,128)(2,1)S(1)} %copy-done.41), channel_id=1, source_target_pairs={{0,29},{1,28},{2,31},{3,30},{4,25},{5,24},{6,27},{7,26},{8,21},{9,... | collective-permute-start | bytes 786440 | tf_op jit(solution)/shard_map/ppermute | solution.py:381
  160.8 39.5 %collective-permute-start.25 = (bf16[2,128,512]{2,1,0:T(8,128)(2,1)S(1)}, bf16[2,128,512]{2,1,0:T(8,128)(2,1)S(1)}, u32[]{:S(2)}, u32[]{:S(2)}) collective-permute-start(bf16[2,128,512]{2,1,0:T(8,128)(2,1)S(1)} %copy-done.40), channel_id=1, source_target_pairs={{0,12},{1,13},{2,14},{3,15},{4,8},{5,9},{6,10},{7,11},{8,4},{9,5},... | collective-permute-start | bytes 786440 | tf_op jit(solution)/shard_map/ppermute | solution.py:381
  163.1 37.2 %copy-start.35 = (bf16[2,128,512]{2,1,0:T(8,128)(2,1)S(1)}, bf16[2,128,512]{2,1,0:T(8,128)(2,1)}, u32[]{:S(2)}) copy-start(bf16[2,128,512]{2,1,0:T(8,128)(2,1)} %get-tuple-element.76) | copy-start | bytes 786436
  179.4 37.1 %collective-permute-start.26 = (bf16[2,128,512]{2,1,0:T(8,128)(2,1)S(1)}, bf16[2,128,512]{2,1,0:T(8,128)(2,1)S(1)}, u32[]{:S(2)}, u32[]{:S(2)}) collective-permute-start(bf16[2,128,512]{2,1,0:T(8,128)(2,1)S(1)} %copy-done.39), channel_id=1, source_target_pairs={{0,30},{1,31},{2,28},{3,29},{4,26},{5,27},{6,24},{7,25},{8,22},{9,... | collective-permute-start | bytes 786440 | tf_op jit(solution)/shard_map/ppermute | solution.py:381
  186.1 30.5 %collective-permute-start.27 = (bf16[2,128,512]{2,1,0:T(8,128)(2,1)S(1)}, bf16[2,128,512]{2,1,0:T(8,128)(2,1)S(1)}, u32[]{:S(2)}, u32[]{:S(2)}) collective-permute-start(bf16[2,128,512]{2,1,0:T(8,128)(2,1)S(1)} %copy-done.38), channel_id=1, source_target_pairs={{0,13},{1,12},{2,15},{3,14},{4,9},{5,8},{6,11},{7,10},{8,5},{9,4},... | collective-permute-start | bytes 786440 | tf_op jit(solution)/shard_map/ppermute | solution.py:381
  188.6 28.0 %collective-permute-start.28 = (bf16[2,128,512]{2,1,0:T(8,128)(2,1)S(1)}, bf16[2,128,512]{2,1,0:T(8,128)(2,1)S(1)}, u32[]{:S(2)}, u32[]{:S(2)}) collective-permute-start(bf16[2,128,512]{2,1,0:T(8,128)(2,1)S(1)} %copy-done.37), channel_id=1, source_target_pairs={{0,31},{1,30},{2,29},{3,28},{4,27},{5,26},{6,25},{7,24},{8,23},{9,... | collective-permute-start | bytes 786440 | tf_op jit(solution)/shard_map/ppermute | solution.py:381
  191.0 25.6 %collective-permute-start.29 = (bf16[2,128,512]{2,1,0:T(8,128)(2,1)S(1)}, bf16[2,128,512]{2,1,0:T(8,128)(2,1)S(1)}, u32[]{:S(2)}, u32[]{:S(2)}) collective-permute-start(bf16[2,128,512]{2,1,0:T(8,128)(2,1)S(1)} %copy-done.36), channel_id=1, source_target_pairs={{0,14},{1,15},{2,12},{3,13},{4,10},{5,11},{6,8},{7,9},{8,6},{9,7},... | collective-permute-start | bytes 786440 | tf_op jit(solution)/shard_map/ppermute | solution.py:381
  200.3 19.3 %collective-permute-start.30 = (bf16[2,128,512]{2,1,0:T(8,128)(2,1)S(1)}, bf16[2,128,512]{2,1,0:T(8,128)(2,1)S(1)}, u32[]{:S(2)}, u32[]{:S(2)}) collective-permute-start(bf16[2,128,512]{2,1,0:T(8,128)(2,1)S(1)} %copy-done.35), channel_id=1, source_target_pairs={{0,15},{1,14},{2,13},{3,12},{4,11},{5,10},{6,9},{7,8},{8,7},{9,6},... | collective-permute-start | bytes 786440 | tf_op jit(solution)/shard_map/ppermute | solution.py:381
  237.6 2.7 %collective-permute-start.31 = (f32[4,4,16,1024]{3,2,1,0:T(8,128)S(1)}, f32[4,4,16,1024]{3,2,1,0:T(8,128)S(1)}, u32[]{:S(2)}, u32[]{:S(2)}) collective-permute-start(f32[4,4,16,1024]{3,2,1,0:T(8,128)S(1)} %get-tuple-element.78), channel_id=1, source_target_pairs={{0,1},{1,0},{2,3},{3,2},{4,5},{5,4},{6,7},{7,6},{8,9},{9,8},{10,11... | collective-permute-start | bytes 3145736 | tf_op jit(solution)/shard_map/ppermute | solution.py:381
  240.5 6.1 %collective-permute-start.32 = (bf16[4,16,1024]{2,1,0:T(8,128)(2,1)S(1)}, bf16[4,16,1024]{2,1,0:T(8,128)(2,1)S(1)}, u32[]{:S(2)}, u32[]{:S(2)}) collective-permute-start(bf16[4,16,1024]{2,1,0:T(8,128)(2,1)S(1)} %get-tuple-element.80), channel_id=1, source_target_pairs={{0,2},{1,3},{2,0},{3,1},{4,6},{5,7},{6,4},{7,5},{8,10},{9,11},{10,... | collective-permute-start | bytes 393224 | tf_op jit(solution)/shard_map/ppermute | solution.py:381
  241.8 7.3 %collective-permute-start.33 = (bf16[4,16,1024]{2,1,0:T(8,128)(2,1)S(1)}, bf16[4,16,1024]{2,1,0:T(8,128)(2,1)S(1)}, u32[]{:S(2)}, u32[]{:S(2)}) collective-permute-start(bf16[4,16,1024]{2,1,0:T(8,128)(2,1)S(1)} %get-tuple-element.81), channel_id=1, source_target_pairs={{0,4},{1,5},{2,6},{3,7},{4,0},{5,1},{6,2},{7,3},{8,12},{9,13},{10,... | collective-permute-start | bytes 393224 | tf_op jit(solution)/shard_map/ppermute | solution.py:381
  242.9 7.9 %collective-permute-start.34 = (bf16[4,16,1024]{2,1,0:T(8,128)(2,1)S(1)}, bf16[4,16,1024]{2,1,0:T(8,128)(2,1)S(1)}, u32[]{:S(2)}, u32[]{:S(2)}) collective-permute-start(bf16[4,16,1024]{2,1,0:T(8,128)(2,1)S(1)} %get-tuple-element.82), channel_id=1, source_target_pairs={{0,6},{1,7},{2,4},{3,5},{4,2},{5,3},{6,0},{7,1},{8,14},{9,15},{10,... | collective-permute-start | bytes 393224 | tf_op jit(solution)/shard_map/ppermute | solution.py:381
  250.9 7.4 %collective-permute-start.35 = (f32[16,1024]{1,0:T(8,128)S(1)}, f32[16,1024]{1,0:T(8,128)S(1)}, u32[]{:S(2)}, u32[]{:S(2)}) collective-permute-start(f32[16,1024]{1,0:T(8,128)S(1)} %get-tuple-element.84), channel_id=1, source_target_pairs={{0,8},{1,9},{2,10},{3,11},{4,12},{5,13},{6,14},{7,15},{8,0},{9,1},... | collective-permute-start | bytes 196616 | tf_op jit(solution)/shard_map/ppermute | solution.py:381
  252.2 7.0 %collective-permute-start.36 = (f32[16,1024]{1,0:T(8,128)S(1)}, f32[16,1024]{1,0:T(8,128)S(1)}, u32[]{:S(2)}, u32[]{:S(2)}) collective-permute-start(f32[16,1024]{1,0:T(8,128)S(1)} %get-tuple-element.85), channel_id=1, source_target_pairs={{0,16},{1,17},{2,18},{3,19},{4,20},{5,21},{6,22},{7,23},{8,24},{9,... | collective-permute-start | bytes 196616 | tf_op jit(solution)/shard_map/ppermute | solution.py:381
  256.9 6.1 %collective-permute-start.37 = (f32[16,1024]{1,0:T(8,128)S(1)}, f32[16,1024]{1,0:T(8,128)S(1)}, u32[]{:S(2)}, u32[]{:S(2)}) collective-permute-start(f32[16,1024]{1,0:T(8,128)S(1)} %get-tuple-element.86), channel_id=1, source_target_pairs={{0,24},{1,25},{2,26},{3,27},{4,28},{5,29},{6,30},{7,31},{8,16},{9,... | collective-permute-start | bytes 196616 | tf_op jit(solution)/shard_map/ppermute | solution.py:381
  (36 other events, 569.1 us)
where the time goes:
time: 264 us
  waiting for transfers between devices  93.5 us (35%)
  starting transfers between devices  77.4 us (29%)
  Pallas kernels  76.3 us (29%)
  local copies, waits for them, and re-layouts  14 us (5%)
    ppermute x38, waiting for transfers between devices, swap(): return lax.ppermute(value, 'rows', [(i, i ^ mask) for i in range(devices)])  93.5 us
    ppermute x38, starting transfers between devices, swap(): return lax.ppermute(value, 'rows', [(i, i ^ mask) for i in range(devices)])  77.4 us
    pallas_call x3, Pallas kernels, hops(): pl.pallas_call(functools.partial(hops_kernel, phase, slots, fixed, count)...  47 us
    pallas_call x1, Pallas kernels, gram(): pl.pallas_call(functools.partial(gram_kernel, phase, len(arrivals), slots...  17.3 us
    pallas_call x2, Pallas kernels, pack(): pl.pallas_call(functools.partial(pack_kernel, masks, len(after)), out_sha...  11.2 us
    reshape x1, local copies, waits for them, and re-layouts, body(): left_t = left.reshape(-1, bunch, vectors).transpose(0, 2, 1)  6.61 us
  transfers between devices with their start and end apart: 38, of which 14 were waited for; matrix products, arithmetic and copies ran while one was open for 4% of the time, Pallas kernels for 18%

commit v1 on v0

--- a/solution.py
+++ b/solution.py
@@ -30,9 +30,12 @@
     return order
 
 
-def exchange_groups(count):
-    first, second = (count + 1) // 2, count - max(1, count // 5)
-    return [(0, first), (first, second), (second, count)]
+def exchange_groups(devices):
+    half = devices // 2
+    far, near = list(range(half, devices)), list(range(1, half))
+    last = half - max(1, half // 8)
+    first = half * 5 // 8
+    return [near + far[:first], far[first:last], far[last:]]
 
 
 def in_hbm(value):
@@ -241,10 +244,11 @@
     loads = pool_loads(arrivals, pool_ref, sems)
     for copy in loads:
         copy.start()
-    ahead = min(AHEAD // 2, chunks)
+    ahead = min(2, chunks)
     for i in range(ahead):
         for d in range(2):
             inward(d * chunks + i).start()
+    sum_ref[...] = jnp.zeros_like(sum_ref)
     for copy in loads:
         copy.wait()
 
@@ -269,16 +273,7 @@
             )
         for d, g, block in spots:
             current_ref[pl.ds(g * rows, rows), pl.ds(d * vectors, vectors)] = held_ref[block].astype(BF16)
-        part = jnp.dot(left_ref[step], current_ref[...], preferred_element_type=F32)
-
-        @pl.when(step == 0)
-        def _():
-            sum_ref[...] = part
-
-        @pl.when(step > 0)
-        def _():
-            sum_ref[...] += part
-
+        sum_ref[...] += jnp.dot(left_ref[step], current_ref[...], preferred_element_type=F32)
         return carry
 
     lax.fori_loop(0, chunks, some, 0)
@@ -391,30 +386,33 @@
     rank = lax.axis_index("rows").astype(jnp.int32).reshape(1)
     blocks = right.reshape(local, block_rows, vectors)
     order = exchange_order(devices)
-    groups = exchange_groups(len(order))
+    groups = exchange_groups(devices)
     send = send_blocks.T
 
     early = min(EARLY, len(order))
     packed = pack(rank, send, blocks, order[:early])
     packed += pack(rank, send, blocks, order[early:], packed[:1])
-    arrived = []
+    arrived = {}
     for n, mask in enumerate(order):
-        arrived.append(swap(packed[n], mask, devices))
-
+        arrived[mask] = swap(packed[n], mask, devices)
+
+    starts = [sum(map(len, groups[:n])) for n in range(len(groups))]
     lists, counts = slot_lists(
         rank, send, source_blocks.reshape(2 * local, slots), tile_index.reshape(2 * local, slots),
-        local, order, [start for start, _ in groups], tiles.shape[1],
+        local, sum(groups, []), starts, tiles.shape[1],
     )
     tiles = jnp.concatenate([tiles, jnp.zeros((2, 1) + tiles.shape[2:], tiles.dtype)], axis=1)
-    bunch = math.gcd(local, 4) * block_rows
+    bunch = math.gcd(local, 8) * block_rows
     left_t = left.reshape(-1, bunch, vectors).transpose(0, 2, 1)
     tiles = in_vmem(tiles)
     current = hops(0, lists, counts, tiles, blocks, None, 4)
-    for n, (start, stop) in enumerate(groups[:-1]):
-        current = hops(n + 1, lists, counts, tiles, arrived[start:stop], current, 2)
-    start, stop = groups[-1]
+    for n, group in enumerate(groups[:-1]):
+        current = hops(
+            n + 1, lists, counts, tiles, [arrived[mask] for mask in group], current, 2 if n else 4
+        )
     sums = gram(
-        len(groups), rank, lists, counts, tiles, current, left_t, arrived[start:stop], devices, F32, 1
+        len(groups), rank, lists, counts, tiles, current, left_t,
+        [arrived[mask] for mask in groups[-1]], devices, F32, 1,
     )
     if len(sums) == 1:
         mine = lax.psum_scatter(sums[0] * scale, "rows", scatter_dimension=0, tiled=True)

time: 264 us -> 270 us (1.023)
  starting transfers between devices: 77.4 us -> 99.3 us
  waiting for transfers between devices: 93.5 us -> 78.1 us
    ppermute x38, starting transfers between devices: 77.4 us -> 99.3 us  [swap(): return lax.ppermute(value, 'rows', [(i, i ^ mask) for i in range(devices)])]
    ppermute x38, waiting for transfers between devices: 93.5 us -> 78.1 us  [swap(): return lax.ppermute(value, 'rows', [(i, i ^ mask) for i in range(devices)])]
    pallas_call x1, Pallas kernels: 17.3 us -> 13.2 us  [gram(): pl.pallas_call(functools.partial(gram_kernel, phase, len(arrivals), slots...]
  transfers between devices with their start and end apart: 38 -> 38, of which waited for: 14 -> 13; matrix products, arithmetic and copies ran while one was open for 4% -> 4% of each run, Pallas kernels for 18% -> 18%
where the time goes in v1:
time: 270 us; the launch traced here: 269 us
  starting transfers between devices  99.3 us (37%)
  waiting for transfers between devices  78.1 us (29%)
  Pallas kernels  74 us (27%)
  local copies, waits for them, and re-layouts  15.4 us (6%)
    ppermute x38, starting transfers between devices, swap(): return lax.ppermute(value, 'rows', [(i, i ^ mask) for i in range(devices)])  99.3 us
    ppermute x38, waiting for transfers between devices, swap(): return lax.ppermute(value, 'rows', [(i, i ^ mask) for i in range(devices)])  78.1 us
    pallas_call x3, Pallas kernels, hops(): pl.pallas_call(functools.partial(hops_kernel, phase, slots, fixed, count)...  48.8 us
    pallas_call x1, Pallas kernels, gram(): pl.pallas_call(functools.partial(gram_kernel, phase, len(arrivals), slots...  13.2 us
    pallas_call x2, Pallas kernels, pack(): pl.pallas_call(functools.partial(pack_kernel, masks, len(after)), out_sha...  11.2 us
    reshape x1, local copies, waits for them, and re-layouts, body(): left_t = left.reshape(-1, bunch, vectors).transpose(0, 2, 1)  6.49 us
  transfers between devices with their start and end apart: 38, of which 13 were waited for; matrix products, arithmetic and copies ran while one was open for 4% of the time, Pallas kernels for 18%

profile of v1, /device:TPU:0, one launch (start us, length us, event | category | flops | bytes accessed | tf_op | source)
XLA Modules:
  0.0 269.2 jit_solution(5270973365730757126)
XLA Ops:
  0.0 2.8 %pack.2 = (bf16[2,128,512]{2,1,0:T(8,128)(2,1)}, bf16[2,128,512]{2,1,0:T(8,128)(2,1)}, bf16[2,128,512]{2,1,0:T(8,128)(2,1)}) custom-call(s32[1]{0:T(128)} %bitcast.rank_ref, s32[2,32]{1,0:T(2,128)} %bitcast.20, bf16[32,128,512]{2,1,0:T(8,128)(2,1)} %bitcast.16), custom_call_target="tpu_custom_call" | custom-call | tf_op jit(solution)/shard_map/pack/pallas_call | solution.py:77
  2.8 8.4 %pack.3 = (bf16[2,128,512]{2,1,0:T(8,128)(2,1)}, bf16[2,128,512]{2,1,0:T(8,128)(2,1)}, bf16[2,128,512]{2,1,0:T(8,128)(2,1)}, bf16[2,128,512]{2,1,0:T(8,128)(2,1)...) custom-call(s32[1]{0:T(128)} %bitcast.rank_ref, ...), custom_call_target="tpu_custom_call" | custom-call | tf_op jit(solution)/shard_map/pack/pallas_call | solution.py:77
  11.5 2.9 %collective-permute-start.1 = (bf16[2,128,512]{2,1,0:T(8,128)(2,1)}, bf16[2,128,512]{2,1,0:T(8,128)(2,1)S(1)}, u32[]{:S(2)}, u32[]{:S(2)}) collective-permute-start(bf16[2,128,512]{2,1,0:T(8,128)(2,1)} %get-tuple-element.48), channel_id=1, source_target_pairs={{0,2},{1,3},{2,0},{3,1},{4,6},{5,7},{6,4},{7,5},{8,10},{9,11},{10,... | collective-permute-start | bytes 786440 | tf_op jit(solution)/shard_map/ppermute | solution.py:376
  14.3 1.1 collective-permute-start.10
  15.4 1.6 collective-permute-start.11
  17.0 1.2 collective-permute-start.12
  18.6 2.1 collective-permute-start.13
  20.7 6.4 %collective-permute-done.1.rest_2_ = bf16[2,128,512]{2,1,0:T(8,128)(2,1)S(1)} collective-permute-done((bf16[2,128,512]{2,1,0:T(8,128)(2,1)}, bf16[2,128,512]{2,1,0:T(8,128)(2,1)S(1)}, u32[]{:S(2)}, u32[]{:S(2)}) %collective-permute-start.1) | collective-permute-done | bytes 262176 | tf_op jit(solution)/shard_map/ppermute | solution.py:376
  27.1 3.0 %collective-permute-start.14 = (bf16[2,128,512]{2,1,0:T(8,128)(2,1)}, bf16[2,128,512]{2,1,0:T(8,128)(2,1)S(1)}, u32[]{:S(2)}, u32[]{:S(2)}) collective-permute-start(bf16[2,128,512]{2,1,0:T(8,128)(2,1)} %get-tuple-element.61), channel_id=1, source_target_pairs={{0,15},{1,14},{2,13},{3,12},{4,11},{5,10},{6,9},{7,8},{8,7},{9,6},... | collective-permute-start | bytes 786440 | tf_op jit(solution)/shard_map/ppermute | solution.py:376
  30.1 2.8 %collective-permute-start.18 = (bf16[2,128,512]{2,1,0:T(8,128)(2,1)}, bf16[2,128,512]{2,1,0:T(8,128)(2,1)S(1)}, u32[]{:S(2)}, u32[]{:S(2)}) collective-permute-start(bf16[2,128,512]{2,1,0:T(8,128)(2,1)} %get-tuple-element.64), channel_id=1, source_target_pairs={{0,19},{1,18},{2,17},{3,16},{4,23},{5,22},{6,21},{7,20},{8,27},{9,... | collective-permute-start | bytes 786440 | tf_op jit(solution)/shard_map/ppermute | solution.py:376
  33.1 1.4 collective-permute-done.12.rest_13_
  34.6 13.0 %collective-permute-start.2 = (bf16[2,128,512]{2,1,0:T(8,128)(2,1)}, bf16[2,128,512]{2,1,0:T(8,128)(2,1)S(1)}, u32[]{:S(2)}, u32[]{:S(2)}) collective-permute-start(bf16[2,128,512]{2,1,0:T(8,128)(2,1)} %get-tuple-element.49), channel_id=1, source_target_pairs={{0,3},{1,2},{2,1},{3,0},{4,7},{5,6},{6,5},{7,4},{8,11},{9,10},{10,... | collective-permute-start | bytes 786440 | tf_op jit(solution)/shard_map/ppermute | solution.py:376
  49.7 3.5 %collective-permute-done.13.rest_14_ = bf16[2,128,512]{2,1,0:T(8,128)(2,1)S(1)} collective-permute-done((bf16[2,128,512]{2,1,0:T(8,128)(2,1)}, bf16[2,128,512]{2,1,0:T(8,128)(2,1)S(1)}, u32[]{:S(2)}, u32[]{:S(2)}) %collective-permute-start.13) | collective-permute-done | bytes 262176 | tf_op jit(solution)/shard_map/ppermute | solution.py:376
  53.3 4.9 %collective-permute-done.14.rest_15_ = bf16[2,128,512]{2,1,0:T(8,128)(2,1)S(1)} collective-permute-done((bf16[2,128,512]{2,1,0:T(8,128)(2,1)}, bf16[2,128,512]{2,1,0:T(8,128)(2,1)S(1)}, u32[]{:S(2)}, u32[]{:S(2)}) %collective-permute-start.14) | collective-permute-done | bytes 262176 | tf_op jit(solution)/shard_map/ppermute | solution.py:376
  58.2 2.2 collective-permute-start.21
  60.5 2.3 collective-permute-start.22
  62.7 3.7 %collective-permute-start.23 = (bf16[2,128,512]{2,1,0:T(8,128)(2,1)}, bf16[2,128,512]{2,1,0:T(8,128)(2,1)S(1)}, u32[]{:S(2)}, u32[]{:S(2)}) collective-permute-start(bf16[2,128,512]{2,1,0:T(8,128)(2,1)} %get-tuple-element.69), channel_id=1, source_target_pairs={{0,24},{1,25},{2,26},{3,27},{4,28},{5,29},{6,30},{7,31},{8,16},{9,... | collective-permute-start | bytes 786440 | tf_op jit(solution)/shard_map/ppermute | solution.py:376
  67.0 26.9 %collective-permute-done.20.rest_21_ = bf16[2,128,512]{2,1,0:T(8,128)(2,1)S(1)} collective-permute-done((bf16[2,128,512]{2,1,0:T(8,128)(2,1)}, bf16[2,128,512]{2,1,0:T(8,128)(2,1)S(1)}, u32[]{:S(2)}, u32[]{:S(2)}) %collective-permute-start.20) | collective-permute-done | bytes 262176 | tf_op jit(solution)/shard_map/ppermute | solution.py:376
  93.9 6.2 %collective-permute-done.21.rest_22_ = bf16[2,128,512]{2,1,0:T(8,128)(2,1)S(1)} collective-permute-done((bf16[2,128,512]{2,1,0:T(8,128)(2,1)}, bf16[2,128,512]{2,1,0:T(8,128)(2,1)S(1)}, u32[]{:S(2)}, u32[]{:S(2)}) %collective-permute-start.21) | collective-permute-done | bytes 262176 | tf_op jit(solution)/shard_map/ppermute | solution.py:376
  100.1 5.7 %collective-permute-done.22.rest_23_ = bf16[2,128,512]{2,1,0:T(8,128)(2,1)S(1)} collective-permute-done((bf16[2,128,512]{2,1,0:T(8,128)(2,1)}, bf16[2,128,512]{2,1,0:T(8,128)(2,1)S(1)}, u32[]{:S(2)}, u32[]{:S(2)}) %collective-permute-start.22) | collective-permute-done | bytes 262176 | tf_op jit(solution)/shard_map/ppermute | solution.py:376
  106.1 1.9 collective-permute-start.6
  108.0 7.4 %collective-permute-start.7 = (bf16[2,128,512]{2,1,0:T(8,128)(2,1)}, bf16[2,128,512]{2,1,0:T(8,128)(2,1)}, u32[]{:S(2)}, u32[]{:S(2)}) collective-permute-start(bf16[2,128,512]{2,1,0:T(8,128)(2,1)} %get-tuple-element.54), channel_id=1, source_target_pairs={{0,8},{1,9},{2,10},{3,11},{4,12},{5,13},{6,14},{7,15},{8,0},{9,1},... | collective-permute-start | bytes 786440 | tf_op jit(solution)/shard_map/ppermute | solution.py:376
  115.9 3.2 %concatenate.3.tiles_ref = bf16[2,65,128,128]{3,2,1,0:T(8,128)(2,1)S(1)} pad(bf16[2,64,128,128]{3,2,1,0:T(8,128)(2,1)} %param.9, bf16[]{:T(256)} %constant.71.clone.1), padding=0_0x0_1x0_0x0_0 | pad | bytes 8454146 | tf_op jit(solution)/shard_map/concatenate | solution.py:404
  119.3 3.5 %collective-permute-done.3.rest_4_ = bf16[2,128,512]{2,1,0:T(8,128)(2,1)} collective-permute-done((bf16[2,128,512]{2,1,0:T(8,128)(2,1)}, bf16[2,128,512]{2,1,0:T(8,128)(2,1)}, u32[]{:S(2)}, u32[]{:S(2)}) %collective-permute-start.3) | collective-permute-done | bytes 262176 | tf_op jit(solution)/shard_map/ppermute | solution.py:376
  122.8 5.4 %collective-permute-done.4.rest_5_ = bf16[2,128,512]{2,1,0:T(8,128)(2,1)} collective-permute-done((bf16[2,128,512]{2,1,0:T(8,128)(2,1)}, bf16[2,128,512]{2,1,0:T(8,128)(2,1)}, u32[]{:S(2)}, u32[]{:S(2)}) %collective-permute-start.4) | collective-permute-done | bytes 262176 | tf_op jit(solution)/shard_map/ppermute | solution.py:376
  128.2 2.0 collective-permute-start.9
  130.2 3.3 %collective-permute-start.17 = (bf16[2,128,512]{2,1,0:T(8,128)(2,1)}, bf16[2,128,512]{2,1,0:T(8,128)(2,1)S(1)}, u32[]{:S(2)}, u32[]{:S(2)}) collective-permute-start(bf16[2,128,512]{2,1,0:T(8,128)(2,1)} %get-tuple-element.63), channel_id=1, source_target_pairs={{0,18},{1,19},{2,16},{3,17},{4,22},{5,23},{6,20},{7,21},{8,26},{9,... | collective-permute-start | bytes 786440 | tf_op jit(solution)/shard_map/ppermute | solution.py:376
  133.5 14.9 %shard_map.73.rest_0_ = f32[64,128,512]{2,1,0:T(8,128)} custom-call(s32[4,1024]{1,0:T(4,128)S(1)} %add.78.lists_ref, s32[4,64]{1,0:T(4,128)S(1)} %get-tuple-element.87.counts_ref, bf16[2,65,128,128]{3,2,1,0:T(8,128)(2,1)S(1)} %concatenate.3.tiles_ref, bf16[32,128,512]{2,1,0:T(8,128)(2,1)S(1)} %bitcast.18), custom_call_target="tpu_custom_call" | custom-call | flops 8000000000 | bytes 41943040 | tf_op jit(solution)/shard_map/pallas_call | solution.py:222
  148.5 6.5 %copy.22 = bf16[4,1024,512]{1,2,0:T(8,128)(2,1)} copy(bf16[4,1024,512]{2,1,0:T(8,128)(2,1)} %bitcast.19) | data formatting | bytes 8388608 | tf_op jit(solution)/shard_map/reshape | solution.py:406
  155.0 2.1 collective-permute-start.25
  157.1 1.7 collective-permute-start.26
  158.8 1.1 collective-permute-start.27
  159.9 4.2 %collective-permute-start.28 = (bf16[2,128,512]{2,1,0:T(8,128)(2,1)S(1)}, bf16[2,128,512]{2,1,0:T(8,128)(2,1)S(1)}, u32[]{:S(2)}, u32[]{:S(2)}) collective-permute-start(bf16[2,128,512]{2,1,0:T(8,128)(2,1)S(1)} %copy-done.37), channel_id=1, source_target_pairs={{0,29},{1,28},{2,31},{3,30},{4,25},{5,24},{6,27},{7,26},{8,21},{9,... | collective-permute-start | bytes 786440 | tf_op jit(solution)/shard_map/ppermute | solution.py:376
  164.1 20.4 %collective-permute-start.29 = (bf16[2,128,512]{2,1,0:T(8,128)(2,1)S(1)}, bf16[2,128,512]{2,1,0:T(8,128)(2,1)S(1)}, u32[]{:S(2)}, u32[]{:S(2)}) collective-permute-start(bf16[2,128,512]{2,1,0:T(8,128)(2,1)S(1)} %copy-done.36), channel_id=1, source_target_pairs={{0,30},{1,31},{2,28},{3,29},{4,26},{5,27},{6,24},{7,25},{8,22},{9,... | collective-permute-start | bytes 786440 | tf_op jit(solution)/shard_map/ppermute | solution.py:376
  184.5 2.2 copy-done.1
  186.7 19.5 %shard_map.74.rest_0_ = f32[64,128,512]{2,1,0:T(8,128)} custom-call(s32[4,1024]{1,0:T(4,128)S(1)} %add.78.lists_ref, s32[4,64]{1,0:T(4,128)S(1)} %get-tuple-element.87.counts_ref, bf16[2,65,128,128]{3,2,1,0:T(8,128)(2,1)S(1)} %copy-done.1, f32[64,128,512]{2,1,0:T(8,128)} %shard_map.73.rest_0_, ...), custom_call_target="tpu_custom_call", output_to_operand_aliasing={{}: (3, {})} | custom-call | flops 8000000000 | bytes 41943040 | tf_op jit(solution)/shard_map/pallas_call | solution.py:222
  207.2 0.7 copy-done.8
  207.9 14.4 %shard_map.75.in_ref = f32[64,128,512]{2,1,0:T(8,128)} custom-call(s32[4,1024]{1,0:T(4,128)S(1)} %add.78.lists_ref, s32[4,64]{1,0:T(4,128)S(1)} %get-tuple-element.87.counts_ref, bf16[2,65,128,128]{3,2,1,0:T(8,128)(2,1)S(1)} %copy-done.1, f32[64,128,512]{2,1,0:T(8,128)} %shard_map.74.rest_0_, ...), custom_call_target="tpu_custom_call", output_to_operand_aliasing={{}: (3, {})} | custom-call | flops 8000000000 | bytes 41943040 | tf_op jit(solution)/shard_map/pallas_call | solution.py:222
  222.4 0.7 copy-done.6
  223.1 13.2 %gram.1 = (f32[4,4,16,1024]{3,2,1,0:T(8,128)S(1)}, f32[4,4,16,1024]{3,2,1,0:T(8,128)S(1)}) custom-call(s32[1]{0:T(128)} %bitcast.rank_ref, s32[4,1024]{1,0:T(4,128)S(1)} %add.78.lists_ref, s32[4,64]{1,0:T(4,128)S(1)} %get-tuple-element.87.counts_ref, bf16[2,65,128,128]{3,2,1,0:T(8,128)(2,1)S(1)} %bitcast.14, f32[64,128,512]{2,1,0:T(8,128)} %shard_map.75.in_ref, ...), custom_call_target="tpu_custom_call" | custom-call | flops 6000000000 | bytes 25165824 | tf_op jit(solution)/shard_map/gram/pallas_call | solution.py:306
  236.4 2.6 collective-permute-done.31.rest_0_
  239.1 7.7 %collective-permute-start.32 = (bf16[4,16,1024]{2,1,0:T(8,128)(2,1)S(1)}, bf16[4,16,1024]{2,1,0:T(8,128)(2,1)S(1)}, u32[]{:S(2)}, u32[]{:S(2)}) collective-permute-start(bf16[4,16,1024]{2,1,0:T(8,128)(2,1)S(1)} %get-tuple-element.80), channel_id=1, source_target_pairs={{0,2},{1,3},{2,0},{3,1},{4,6},{5,7},{6,4},{7,5},{8,10},{9,11},{10,... | collective-permute-start | bytes 393224 | tf_op jit(solution)/shard_map/ppermute | solution.py:376
  246.8 1.5 collective-permute-start.34
  248.3 2.4 collective-permute-done.32.rest_0_
  250.8 4.1 %collective-permute-done.33.rest_1_ = bf16[4,16,1024]{2,1,0:T(8,128)(2,1)S(1)} collective-permute-done((bf16[4,16,1024]{2,1,0:T(8,128)(2,1)S(1)}, bf16[4,16,1024]{2,1,0:T(8,128)(2,1)S(1)}, u32[]{:S(2)}, u32[]{:S(2)}) %collective-permute-start.33) | collective-permute-done | bytes 131104 | tf_op jit(solution)/shard_map/ppermute | solution.py:376
  254.9 6.3 %collective-permute-start.35 = (f32[16,1024]{1,0:T(8,128)S(1)}, f32[16,1024]{1,0:T(8,128)S(1)}, u32[]{:S(2)}, u32[]{:S(2)}) collective-permute-start(f32[16,1024]{1,0:T(8,128)S(1)} %get-tuple-element.84), channel_id=1, source_target_pairs={{0,8},{1,9},{2,10},{3,11},{4,12},{5,13},{6,14},{7,15},{8,0},{9,1},... | collective-permute-start | bytes 196616 | tf_op jit(solution)/shard_map/ppermute | solution.py:376
  261.2 2.4 collective-permute-start.37
  263.6 4.9 %collective-permute-done.36.rest_1_ = f32[16,1024]{1,0:T(8,128)S(1)} collective-permute-done((f32[16,1024]{1,0:T(8,128)S(1)}, f32[16,1024]{1,0:T(8,128)S(1)}, u32[]{:S(2)}, u32[]{:S(2)}) %collective-permute-start.36) | collective-permute-done | bytes 65568 | tf_op jit(solution)/shard_map/ppermute | solution.py:376
  (146 shorter events, 4.9 us)
Async XLA Ops:
  11.2 7.3 %collective-permute-start = (bf16[2,128,512]{2,1,0:T(8,128)(2,1)}, bf16[2,128,512]{2,1,0:T(8,128)(2,1)S(1)}, u32[]{:S(2)}, u32[]{:S(2)}) collective-permute-start(bf16[2,128,512]{2,1,0:T(8,128)(2,1)} %get-tuple-element.47), channel_id=1, source_target_pairs={{0,1},{1,0},{2,3},{3,2},{4,5},{5,4},{6,7},{7,6},{8,9},{9,8},{10,11... | collective-permute-start | bytes 786440 | tf_op jit(solution)/shard_map/ppermute | solution.py:376
  11.5 15.6 %collective-permute-start.1 = (bf16[2,128,512]{2,1,0:T(8,128)(2,1)}, bf16[2,128,512]{2,1,0:T(8,128)(2,1)S(1)}, u32[]{:S(2)}, u32[]{:S(2)}) collective-permute-start(bf16[2,128,512]{2,1,0:T(8,128)(2,1)} %get-tuple-element.48), channel_id=1, source_target_pairs={{0,2},{1,3},{2,0},{3,1},{4,6},{5,7},{6,4},{7,5},{8,10},{9,11},{10,... | collective-permute-start | bytes 786440 | tf_op jit(solution)/shard_map/ppermute | solution.py:376
  14.3 15.7 %collective-permute-start.10 = (bf16[2,128,512]{2,1,0:T(8,128)(2,1)}, bf16[2,128,512]{2,1,0:T(8,128)(2,1)S(1)}, u32[]{:S(2)}, u32[]{:S(2)}) collective-permute-start(bf16[2,128,512]{2,1,0:T(8,128)(2,1)} %get-tuple-element.57), channel_id=1, source_target_pairs={{0,11},{1,10},{2,9},{3,8},{4,15},{5,14},{6,13},{7,12},{8,3},{9,2},... | collective-permute-start | bytes 786440 | tf_op jit(solution)/shard_map/ppermute | solution.py:376
  15.4 17.5 %collective-permute-start.11 = (bf16[2,128,512]{2,1,0:T(8,128)(2,1)}, bf16[2,128,512]{2,1,0:T(8,128)(2,1)S(1)}, u32[]{:S(2)}, u32[]{:S(2)}) collective-permute-start(bf16[2,128,512]{2,1,0:T(8,128)(2,1)} %get-tuple-element.58), channel_id=1, source_target_pairs={{0,12},{1,13},{2,14},{3,15},{4,8},{5,9},{6,10},{7,11},{8,4},{9,5},... | collective-permute-start | bytes 786440 | tf_op jit(solution)/shard_map/ppermute | solution.py:376
  17.0 17.6 %collective-permute-start.12 = (bf16[2,128,512]{2,1,0:T(8,128)(2,1)}, bf16[2,128,512]{2,1,0:T(8,128)(2,1)S(1)}, u32[]{:S(2)}, u32[]{:S(2)}) collective-permute-start(bf16[2,128,512]{2,1,0:T(8,128)(2,1)} %get-tuple-element.59), channel_id=1, source_target_pairs={{0,13},{1,12},{2,15},{3,14},{4,9},{5,8},{6,11},{7,10},{8,5},{9,4},... | collective-permute-start | bytes 786440 | tf_op jit(solution)/shard_map/ppermute | solution.py:376
  18.6 100.6 %copy-start.11 = (bf16[2,128,512]{2,1,0:T(8,128)(2,1)}, bf16[2,128,512]{2,1,0:T(8,128)(2,1)S(1)}, u32[]{:S(2)}) copy-start(bf16[2,128,512]{2,1,0:T(8,128)(2,1)S(1)} %collective-permute-done.rest_1_) | copy-start | bytes 786436
  18.6 34.7 %collective-permute-start.13 = (bf16[2,128,512]{2,1,0:T(8,128)(2,1)}, bf16[2,128,512]{2,1,0:T(8,128)(2,1)S(1)}, u32[]{:S(2)}, u32[]{:S(2)}) collective-permute-start(bf16[2,128,512]{2,1,0:T(8,128)(2,1)} %get-tuple-element.60), channel_id=1, source_target_pairs={{0,14},{1,15},{2,12},{3,13},{4,10},{5,11},{6,8},{7,9},{8,6},{9,7},... | collective-permute-start | bytes 786440 | tf_op jit(solution)/shard_map/ppermute | solution.py:376
  27.1 92.1 %copy-start.12 = (bf16[2,128,512]{2,1,0:T(8,128)(2,1)}, bf16[2,128,512]{2,1,0:T(8,128)(2,1)S(1)}, u32[]{:S(2)}) copy-start(bf16[2,128,512]{2,1,0:T(8,128)(2,1)S(1)} %collective-permute-done.1.rest_2_) | copy-start | bytes 786436
  27.1 31.2 %collective-permute-start.14 = (bf16[2,128,512]{2,1,0:T(8,128)(2,1)}, bf16[2,128,512]{2,1,0:T(8,128)(2,1)S(1)}, u32[]{:S(2)}, u32[]{:S(2)}) collective-permute-start(bf16[2,128,512]{2,1,0:T(8,128)(2,1)} %get-tuple-element.61), channel_id=1, source_target_pairs={{0,15},{1,14},{2,13},{3,12},{4,11},{5,10},{6,9},{7,8},{8,7},{9,6},... | collective-permute-start | bytes 786440 | tf_op jit(solution)/shard_map/ppermute | solution.py:376
  30.1 89.1 %copy-start.13 = (bf16[2,128,512]{2,1,0:T(8,128)(2,1)}, bf16[2,128,512]{2,1,0:T(8,128)(2,1)S(1)}, u32[]{:S(2)}) copy-start(bf16[2,128,512]{2,1,0:T(8,128)(2,1)S(1)} %collective-permute-done.10.rest_11_) | copy-start | bytes 786436
  30.1 30.4 %collective-permute-start.18 = (bf16[2,128,512]{2,1,0:T(8,128)(2,1)}, bf16[2,128,512]{2,1,0:T(8,128)(2,1)S(1)}, u32[]{:S(2)}, u32[]{:S(2)}) collective-permute-start(bf16[2,128,512]{2,1,0:T(8,128)(2,1)} %get-tuple-element.64), channel_id=1, source_target_pairs={{0,19},{1,18},{2,17},{3,16},{4,23},{5,22},{6,21},{7,20},{8,27},{9,... | collective-permute-start | bytes 786440 | tf_op jit(solution)/shard_map/ppermute | solution.py:376
  32.9 86.2 %copy-start.14 = (bf16[2,128,512]{2,1,0:T(8,128)(2,1)}, bf16[2,128,512]{2,1,0:T(8,128)(2,1)S(1)}, u32[]{:S(2)}) copy-start(bf16[2,128,512]{2,1,0:T(8,128)(2,1)S(1)} %collective-permute-done.11.rest_12_) | copy-start | bytes 786436
  32.9 29.8 %collective-permute-start.19 = (bf16[2,128,512]{2,1,0:T(8,128)(2,1)}, bf16[2,128,512]{2,1,0:T(8,128)(2,1)S(1)}, u32[]{:S(2)}, u32[]{:S(2)}) collective-permute-start(bf16[2,128,512]{2,1,0:T(8,128)(2,1)} %get-tuple-element.65), channel_id=1, source_target_pairs={{0,20},{1,21},{2,22},{3,23},{4,16},{5,17},{6,18},{7,19},{8,28},{9,... | collective-permute-start | bytes 786440 | tf_op jit(solution)/shard_map/ppermute | solution.py:376
  34.6 84.6 %copy-start.15 = (bf16[2,128,512]{2,1,0:T(8,128)(2,1)}, bf16[2,128,512]{2,1,0:T(8,128)(2,1)S(1)}, u32[]{:S(2)}) copy-start(bf16[2,128,512]{2,1,0:T(8,128)(2,1)S(1)} %collective-permute-done.12.rest_13_) | copy-start | bytes 786436
  34.6 31.9 %collective-permute-start.2 = (bf16[2,128,512]{2,1,0:T(8,128)(2,1)}, bf16[2,128,512]{2,1,0:T(8,128)(2,1)S(1)}, u32[]{:S(2)}, u32[]{:S(2)}) collective-permute-start(bf16[2,128,512]{2,1,0:T(8,128)(2,1)} %get-tuple-element.49), channel_id=1, source_target_pairs={{0,3},{1,2},{2,1},{3,0},{4,7},{5,6},{6,5},{7,4},{8,11},{9,10},{10,... | collective-permute-start | bytes 786440 | tf_op jit(solution)/shard_map/ppermute | solution.py:376
  53.2 65.9 %copy-start.16 = (bf16[2,128,512]{2,1,0:T(8,128)(2,1)}, bf16[2,128,512]{2,1,0:T(8,128)(2,1)S(1)}, u32[]{:S(2)}) copy-start(bf16[2,128,512]{2,1,0:T(8,128)(2,1)S(1)} %collective-permute-done.13.rest_14_) | copy-start | bytes 786436
  53.2 40.6 %collective-permute-start.20 = (bf16[2,128,512]{2,1,0:T(8,128)(2,1)}, bf16[2,128,512]{2,1,0:T(8,128)(2,1)S(1)}, u32[]{:S(2)}, u32[]{:S(2)}) collective-permute-start(bf16[2,128,512]{2,1,0:T(8,128)(2,1)} %get-tuple-element.66), channel_id=1, source_target_pairs={{0,21},{1,20},{2,23},{3,22},{4,17},{5,16},{6,19},{7,18},{8,29},{9,... | collective-permute-start | bytes 786440 | tf_op jit(solution)/shard_map/ppermute | solution.py:376
  58.2 61.0 %copy-start.17 = (bf16[2,128,512]{2,1,0:T(8,128)(2,1)}, bf16[2,128,512]{2,1,0:T(8,128)(2,1)S(1)}, u32[]{:S(2)}) copy-start(bf16[2,128,512]{2,1,0:T(8,128)(2,1)S(1)} %collective-permute-done.14.rest_15_) | copy-start | bytes 786436
  58.2 41.9 %collective-permute-start.21 = (bf16[2,128,512]{2,1,0:T(8,128)(2,1)}, bf16[2,128,512]{2,1,0:T(8,128)(2,1)S(1)}, u32[]{:S(2)}, u32[]{:S(2)}) collective-permute-start(bf16[2,128,512]{2,1,0:T(8,128)(2,1)} %get-tuple-element.67), channel_id=1, source_target_pairs={{0,22},{1,23},{2,20},{3,21},{4,18},{5,19},{6,16},{7,17},{8,30},{9,... | collective-permute-start | bytes 786440 | tf_op jit(solution)/shard_map/ppermute | solution.py:376
  60.5 58.7 %copy-start.18 = (bf16[2,128,512]{2,1,0:T(8,128)(2,1)}, bf16[2,128,512]{2,1,0:T(8,128)(2,1)S(1)}, u32[]{:S(2)}) copy-start(bf16[2,128,512]{2,1,0:T(8,128)(2,1)S(1)} %collective-permute-done.18.rest_19_) | copy-start | bytes 786436
  60.5 45.4 %collective-permute-start.22 = (bf16[2,128,512]{2,1,0:T(8,128)(2,1)}, bf16[2,128,512]{2,1,0:T(8,128)(2,1)S(1)}, u32[]{:S(2)}, u32[]{:S(2)}) collective-permute-start(bf16[2,128,512]{2,1,0:T(8,128)(2,1)} %get-tuple-element.68), channel_id=1, source_target_pairs={{0,23},{1,22},{2,21},{3,20},{4,19},{5,18},{6,17},{7,16},{8,31},{9,... | collective-permute-start | bytes 786440 | tf_op jit(solution)/shard_map/ppermute | solution.py:376
  62.7 56.5 %copy-start.19 = (bf16[2,128,512]{2,1,0:T(8,128)(2,1)}, bf16[2,128,512]{2,1,0:T(8,128)(2,1)S(1)}, u32[]{:S(2)}) copy-start(bf16[2,128,512]{2,1,0:T(8,128)(2,1)S(1)} %collective-permute-done.19.rest_20_) | copy-start | bytes 786436
  62.7 43.4 %collective-permute-start.23 = (bf16[2,128,512]{2,1,0:T(8,128)(2,1)}, bf16[2,128,512]{2,1,0:T(8,128)(2,1)S(1)}, u32[]{:S(2)}, u32[]{:S(2)}) collective-permute-start(bf16[2,128,512]{2,1,0:T(8,128)(2,1)} %get-tuple-element.69), channel_id=1, source_target_pairs={{0,24},{1,25},{2,26},{3,27},{4,28},{5,29},{6,30},{7,31},{8,16},{9,... | collective-permute-start | bytes 786440 | tf_op jit(solution)/shard_map/ppermute | solution.py:376
  66.4 52.8 %copy-start.20 = (bf16[2,128,512]{2,1,0:T(8,128)(2,1)}, bf16[2,128,512]{2,1,0:T(8,128)(2,1)S(1)}, u32[]{:S(2)}) copy-start(bf16[2,128,512]{2,1,0:T(8,128)(2,1)S(1)} %collective-permute-done.2.rest_3_) | copy-start | bytes 786436
  66.4 41.6 %collective-permute-start.24 = (bf16[2,128,512]{2,1,0:T(8,128)(2,1)}, bf16[2,128,512]{2,1,0:T(8,128)(2,1)S(1)}, u32[]{:S(2)}, u32[]{:S(2)}) collective-permute-start(bf16[2,128,512]{2,1,0:T(8,128)(2,1)} %get-tuple-element.70), channel_id=1, source_target_pairs={{0,25},{1,24},{2,27},{3,26},{4,29},{5,28},{6,31},{7,30},{8,17},{9,... | collective-permute-start | bytes 786440 | tf_op jit(solution)/shard_map/ppermute | solution.py:376
  93.9 28.9 %collective-permute-start.3 = (bf16[2,128,512]{2,1,0:T(8,128)(2,1)}, bf16[2,128,512]{2,1,0:T(8,128)(2,1)}, u32[]{:S(2)}, u32[]{:S(2)}) collective-permute-start(bf16[2,128,512]{2,1,0:T(8,128)(2,1)} %get-tuple-element.50), channel_id=1, source_target_pairs={{0,4},{1,5},{2,6},{3,7},{4,0},{5,1},{6,2},{7,3},{8,12},{9,13},{10,... | collective-permute-start | bytes 786440 | tf_op jit(solution)/shard_map/ppermute | solution.py:376
  100.1 28.1 %collective-permute-start.4 = (bf16[2,128,512]{2,1,0:T(8,128)(2,1)}, bf16[2,128,512]{2,1,0:T(8,128)(2,1)}, u32[]{:S(2)}, u32[]{:S(2)}) collective-permute-start(bf16[2,128,512]{2,1,0:T(8,128)(2,1)} %get-tuple-element.51), channel_id=1, source_target_pairs={{0,5},{1,4},{2,7},{3,6},{4,1},{5,0},{6,3},{7,2},{8,13},{9,12},{10,... | collective-permute-start | bytes 786440 | tf_op jit(solution)/shard_map/ppermute | solution.py:376
  105.8 22.4 %collective-permute-start.5 = (bf16[2,128,512]{2,1,0:T(8,128)(2,1)}, bf16[2,128,512]{2,1,0:T(8,128)(2,1)}, u32[]{:S(2)}, u32[]{:S(2)}) collective-permute-start(bf16[2,128,512]{2,1,0:T(8,128)(2,1)} %get-tuple-element.52), channel_id=1, source_target_pairs={{0,6},{1,7},{2,4},{3,5},{4,2},{5,3},{6,0},{7,1},{8,14},{9,15},{10,... | collective-permute-start | bytes 786440 | tf_op jit(solution)/shard_map/ppermute | solution.py:376
  106.1 24.0 %collective-permute-start.6 = (bf16[2,128,512]{2,1,0:T(8,128)(2,1)}, bf16[2,128,512]{2,1,0:T(8,128)(2,1)}, u32[]{:S(2)}, u32[]{:S(2)}) collective-permute-start(bf16[2,128,512]{2,1,0:T(8,128)(2,1)} %get-tuple-element.53), channel_id=1, source_target_pairs={{0,7},{1,6},{2,5},{3,4},{4,3},{5,2},{6,1},{7,0},{8,15},{9,14},{10,... | collective-permute-start | bytes 786440 | tf_op jit(solution)/shard_map/ppermute | solution.py:376
  108.0 22.2 %collective-permute-start.7 = (bf16[2,128,512]{2,1,0:T(8,128)(2,1)}, bf16[2,128,512]{2,1,0:T(8,128)(2,1)}, u32[]{:S(2)}, u32[]{:S(2)}) collective-permute-start(bf16[2,128,512]{2,1,0:T(8,128)(2,1)} %get-tuple-element.54), channel_id=1, source_target_pairs={{0,8},{1,9},{2,10},{3,11},{4,12},{5,13},{6,14},{7,15},{8,0},{9,1},... | collective-permute-start | bytes 786440 | tf_op jit(solution)/shard_map/ppermute | solution.py:376
  122.8 36.1 %collective-permute-start.15 = (bf16[2,128,512]{2,1,0:T(8,128)(2,1)S(1)}, bf16[2,128,512]{2,1,0:T(8,128)(2,1)S(1)}, u32[]{:S(2)}, u32[]{:S(2)}) collective-permute-start(bf16[2,128,512]{2,1,0:T(8,128)(2,1)S(1)} %copy-done.10), channel_id=1, source_target_pairs={{0,16},{1,17},{2,18},{3,19},{4,20},{5,21},{6,22},{7,23},{8,24},{9,... | collective-permute-start | bytes 786440 | tf_op jit(solution)/shard_map/ppermute | solution.py:376
  128.2 26.7 %collective-permute-start.8 = (bf16[2,128,512]{2,1,0:T(8,128)(2,1)}, bf16[2,128,512]{2,1,0:T(8,128)(2,1)S(1)}, u32[]{:S(2)}, u32[]{:S(2)}) collective-permute-start(bf16[2,128,512]{2,1,0:T(8,128)(2,1)} %get-tuple-element.55), channel_id=1, source_target_pairs={{0,9},{1,8},{2,11},{3,10},{4,13},{5,12},{6,15},{7,14},{8,1},{9,0},... | collective-permute-start | bytes 786440 | tf_op jit(solution)/shard_map/ppermute | solution.py:376
  128.2 28.9 %collective-permute-start.9 = (bf16[2,128,512]{2,1,0:T(8,128)(2,1)}, bf16[2,128,512]{2,1,0:T(8,128)(2,1)S(1)}, u32[]{:S(2)}, u32[]{:S(2)}) collective-permute-start(bf16[2,128,512]{2,1,0:T(8,128)(2,1)} %get-tuple-element.56), channel_id=1, source_target_pairs={{0,10},{1,11},{2,8},{3,9},{4,14},{5,15},{6,12},{7,13},{8,2},{9,3},... | collective-permute-start | bytes 786440 | tf_op jit(solution)/shard_map/ppermute | solution.py:376
  130.2 29.7 %collective-permute-start.16 = (bf16[2,128,512]{2,1,0:T(8,128)(2,1)}, bf16[2,128,512]{2,1,0:T(8,128)(2,1)S(1)}, u32[]{:S(2)}, u32[]{:S(2)}) collective-permute-start(bf16[2,128,512]{2,1,0:T(8,128)(2,1)} %get-tuple-element.62), channel_id=1, source_target_pairs={{0,17},{1,16},{2,19},{3,18},{4,21},{5,20},{6,23},{7,22},{8,25},{9,... | collective-permute-start | bytes 786440 | tf_op jit(solution)/shard_map/ppermute | solution.py:376
  130.2 33.9 %collective-permute-start.17 = (bf16[2,128,512]{2,1,0:T(8,128)(2,1)}, bf16[2,128,512]{2,1,0:T(8,128)(2,1)S(1)}, u32[]{:S(2)}, u32[]{:S(2)}) collective-permute-start(bf16[2,128,512]{2,1,0:T(8,128)(2,1)} %get-tuple-element.63), channel_id=1, source_target_pairs={{0,18},{1,19},{2,16},{3,17},{4,22},{5,23},{6,20},{7,21},{8,26},{9,... | collective-permute-start | bytes 786440 | tf_op jit(solution)/shard_map/ppermute | solution.py:376
  155.0 51.3 %collective-permute-start.25 = (bf16[2,128,512]{2,1,0:T(8,128)(2,1)S(1)}, bf16[2,128,512]{2,1,0:T(8,128)(2,1)S(1)}, u32[]{:S(2)}, u32[]{:S(2)}) collective-permute-start(bf16[2,128,512]{2,1,0:T(8,128)(2,1)S(1)} %copy-done.40), channel_id=1, source_target_pairs={{0,26},{1,27},{2,24},{3,25},{4,30},{5,31},{6,28},{7,29},{8,18},{9,... | collective-permute-start | bytes 786440 | tf_op jit(solution)/shard_map/ppermute | solution.py:376
  157.1 49.3 %collective-permute-start.26 = (bf16[2,128,512]{2,1,0:T(8,128)(2,1)S(1)}, bf16[2,128,512]{2,1,0:T(8,128)(2,1)S(1)}, u32[]{:S(2)}, u32[]{:S(2)}) collective-permute-start(bf16[2,128,512]{2,1,0:T(8,128)(2,1)S(1)} %copy-done.39), channel_id=1, source_target_pairs={{0,27},{1,26},{2,25},{3,24},{4,31},{5,30},{6,29},{7,28},{8,19},{9,... | collective-permute-start | bytes 786440 | tf_op jit(solution)/shard_map/ppermute | solution.py:376
  158.8 47.5 %collective-permute-start.27 = (bf16[2,128,512]{2,1,0:T(8,128)(2,1)S(1)}, bf16[2,128,512]{2,1,0:T(8,128)(2,1)S(1)}, u32[]{:S(2)}, u32[]{:S(2)}) collective-permute-start(bf16[2,128,512]{2,1,0:T(8,128)(2,1)S(1)} %copy-done.38), channel_id=1, source_target_pairs={{0,28},{1,29},{2,30},{3,31},{4,24},{5,25},{6,26},{7,27},{8,20},{9,... | collective-permute-start | bytes 786440 | tf_op jit(solution)/shard_map/ppermute | solution.py:376
  159.9 46.5 %collective-permute-start.28 = (bf16[2,128,512]{2,1,0:T(8,128)(2,1)S(1)}, bf16[2,128,512]{2,1,0:T(8,128)(2,1)S(1)}, u32[]{:S(2)}, u32[]{:S(2)}) collective-permute-start(bf16[2,128,512]{2,1,0:T(8,128)(2,1)S(1)} %copy-done.37), channel_id=1, source_target_pairs={{0,29},{1,28},{2,31},{3,30},{4,25},{5,24},{6,27},{7,26},{8,21},{9,... | collective-permute-start | bytes 786440 | tf_op jit(solution)/shard_map/ppermute | solution.py:376
  164.1 58.2 %collective-permute-start.29 = (bf16[2,128,512]{2,1,0:T(8,128)(2,1)S(1)}, bf16[2,128,512]{2,1,0:T(8,128)(2,1)S(1)}, u32[]{:S(2)}, u32[]{:S(2)}) collective-permute-start(bf16[2,128,512]{2,1,0:T(8,128)(2,1)S(1)} %copy-done.36), channel_id=1, source_target_pairs={{0,30},{1,31},{2,28},{3,29},{4,26},{5,27},{6,24},{7,25},{8,22},{9,... | collective-permute-start | bytes 786440 | tf_op jit(solution)/shard_map/ppermute | solution.py:376
  206.3 16.0 %collective-permute-start.30 = (bf16[2,128,512]{2,1,0:T(8,128)(2,1)S(1)}, bf16[2,128,512]{2,1,0:T(8,128)(2,1)S(1)}, u32[]{:S(2)}, u32[]{:S(2)}) collective-permute-start(bf16[2,128,512]{2,1,0:T(8,128)(2,1)S(1)} %copy-done.35), channel_id=1, source_target_pairs={{0,31},{1,30},{2,29},{3,28},{4,27},{5,26},{6,25},{7,24},{8,23},{9,... | collective-permute-start | bytes 786440 | tf_op jit(solution)/shard_map/ppermute | solution.py:376
  236.3 2.7 %collective-permute-start.31 = (f32[4,4,16,1024]{3,2,1,0:T(8,128)S(1)}, f32[4,4,16,1024]{3,2,1,0:T(8,128)S(1)}, u32[]{:S(2)}, u32[]{:S(2)}) collective-permute-start(f32[4,4,16,1024]{3,2,1,0:T(8,128)S(1)} %get-tuple-element.78), channel_id=1, source_target_pairs={{0,1},{1,0},{2,3},{3,2},{4,5},{5,4},{6,7},{7,6},{8,9},{9,8},{10,11... | collective-permute-start | bytes 3145736 | tf_op jit(solution)/shard_map/ppermute | solution.py:376
  239.1 11.6 %collective-permute-start.32 = (bf16[4,16,1024]{2,1,0:T(8,128)(2,1)S(1)}, bf16[4,16,1024]{2,1,0:T(8,128)(2,1)S(1)}, u32[]{:S(2)}, u32[]{:S(2)}) collective-permute-start(bf16[4,16,1024]{2,1,0:T(8,128)(2,1)S(1)} %get-tuple-element.80), channel_id=1, source_target_pairs={{0,2},{1,3},{2,0},{3,1},{4,6},{5,7},{6,4},{7,5},{8,10},{9,11},{10,... | collective-permute-start | bytes 393224 | tf_op jit(solution)/shard_map/ppermute | solution.py:376
  246.8 8.1 %collective-permute-start.33 = (bf16[4,16,1024]{2,1,0:T(8,128)(2,1)S(1)}, bf16[4,16,1024]{2,1,0:T(8,128)(2,1)S(1)}, u32[]{:S(2)}, u32[]{:S(2)}) collective-permute-start(bf16[4,16,1024]{2,1,0:T(8,128)(2,1)S(1)} %get-tuple-element.81), channel_id=1, source_target_pairs={{0,4},{1,5},{2,6},{3,7},{4,0},{5,1},{6,2},{7,3},{8,12},{9,13},{10,... | collective-permute-start | bytes 393224 | tf_op jit(solution)/shard_map/ppermute | solution.py:376
  246.8 8.1 %collective-permute-start.34 = (bf16[4,16,1024]{2,1,0:T(8,128)(2,1)S(1)}, bf16[4,16,1024]{2,1,0:T(8,128)(2,1)S(1)}, u32[]{:S(2)}, u32[]{:S(2)}) collective-permute-start(bf16[4,16,1024]{2,1,0:T(8,128)(2,1)S(1)} %get-tuple-element.82), channel_id=1, source_target_pairs={{0,6},{1,7},{2,4},{3,5},{4,2},{5,3},{6,0},{7,1},{8,14},{9,15},{10,... | collective-permute-start | bytes 393224 | tf_op jit(solution)/shard_map/ppermute | solution.py:376
  254.9 8.7 %collective-permute-start.35 = (f32[16,1024]{1,0:T(8,128)S(1)}, f32[16,1024]{1,0:T(8,128)S(1)}, u32[]{:S(2)}, u32[]{:S(2)}) collective-permute-start(f32[16,1024]{1,0:T(8,128)S(1)} %get-tuple-element.84), channel_id=1, source_target_pairs={{0,8},{1,9},{2,10},{3,11},{4,12},{5,13},{6,14},{7,15},{8,0},{9,1},... | collective-permute-start | bytes 196616 | tf_op jit(solution)/shard_map/ppermute | solution.py:376
  261.2 7.4 %collective-permute-start.36 = (f32[16,1024]{1,0:T(8,128)S(1)}, f32[16,1024]{1,0:T(8,128)S(1)}, u32[]{:S(2)}, u32[]{:S(2)}) collective-permute-start(f32[16,1024]{1,0:T(8,128)S(1)} %get-tuple-element.85), channel_id=1, source_target_pairs={{0,16},{1,17},{2,18},{3,19},{4,20},{5,21},{6,22},{7,23},{8,24},{9,... | collective-permute-start | bytes 196616 | tf_op jit(solution)/shard_map/ppermute | solution.py:376
  261.2 7.4 %collective-permute-start.37 = (f32[16,1024]{1,0:T(8,128)S(1)}, f32[16,1024]{1,0:T(8,128)S(1)}, u32[]{:S(2)}, u32[]{:S(2)}) collective-permute-start(f32[16,1024]{1,0:T(8,128)S(1)} %get-tuple-element.86), channel_id=1, source_target_pairs={{0,24},{1,25},{2,26},{3,27},{4,28},{5,29},{6,30},{7,31},{8,16},{9,... | collective-permute-start | bytes 196616 | tf_op jit(solution)/shard_map/ppermute | solution.py:376
  (33 other events, 455.5 us)

commit v2 on v0

--- a/solution.py
+++ b/solution.py
@@ -13,8 +13,9 @@
 BF16 = jnp.bfloat16
 SHIFT = 1024
 ROOM = 8 * 2**20
+LATE = 13
+MOST = 40
 EARLY = 3
-AHEAD = 6
 SMEM = pltpu.SMEM
 VMEM = pltpu.VMEM
 HBM = pltpu.HBM
@@ -31,8 +32,10 @@
 
 
 def exchange_groups(count):
-    first, second = (count + 1) // 2, count - max(1, count // 5)
-    return [(0, first), (first, second), (second, count)]
+    early = count - min(LATE, count // 2)
+    parts = -(-early // MOST)
+    cuts = [early * n // parts for n in range(parts + 1)]
+    return list(zip(cuts, cuts[1:] + [count]))
 
 
 def in_hbm(value):
@@ -149,48 +152,26 @@
     )
 
 
-def hops_kernel(phase, slots, fixed, count, lists_ref, counts_ref, tiles_ref, *rest):
-    if phase == 0:
-        pool_ref, out_ref, held_ref, out_sems = rest
-    else:
-        in_ref, arrivals = rest[0], rest[1:1 + count]
-        out_ref, held_ref, out_sems, pool_ref, in_sems, sems = rest[1 + count:]
+def hops_kernel(slots, fixed, lists_ref, counts_ref, tiles_ref, pool_ref, out_ref, held_ref, out_sems):
     chunks = out_sems.shape[0]
-    steps = held_ref.shape[0]
-    bunch = steps // chunks
+    bunch = held_ref.shape[0] // chunks
     outward = in_chunks(held_ref, out_ref, out_sems)
-    if phase:
-        inward = in_chunks(in_ref, held_ref, in_sems)
-        loads = pool_loads(arrivals, pool_ref, sems)
-        for copy in loads:
-            copy.start()
-        ahead = min(AHEAD, chunks)
-        for i in range(ahead):
-            inward(i).start()
-        for copy in loads:
-            copy.wait()
 
     def some(step, carry):
         tiles = tiles_ref.at[2 * step // chunks]
-        if phase:
-            @pl.when(step + ahead < chunks)
-            def _():
-                inward(step + ahead).start()
-
-            inward(step).wait()
         for g in range(bunch):
             block = step * bunch + g
-            entry = lambda j, block=block: lists_ref[phase, block * slots + j]
+            entry = lambda j, block=block: lists_ref[0, block * slots + j]
             for j in range(fixed):
                 value = pair(entry, j, tiles, pool_ref)
-                if j or phase:
+                if j:
                     held_ref[block] += value
                 else:
                     held_ref[block] = value
         for g in range(bunch):
             block = step * bunch + g
-            entry = lambda j, block=block: lists_ref[phase, block * slots + j]
-            add_rest(held_ref.at[block], fixed, counts_ref[phase, block], entry, tiles, pool_ref)
+            entry = lambda j, block=block: lists_ref[0, block * slots + j]
+            add_rest(held_ref.at[block], fixed, counts_ref[0, block], entry, tiles, pool_ref)
         outward(step).start()
         return carry
 
@@ -199,67 +180,109 @@
         outward(i).wait()
 
 
-def hops(phase, lists, counts, tiles, pool, current, fixed, bunch=4):
+def hops(lists, counts, tiles, pool, fixed, bunch=4):
     steps = counts.shape[1]
     slots = lists.shape[1] // steps
     chunks = steps // math.gcd(bunch, steps // 2)
-    rows, vectors = (pool if phase == 0 else pool[0]).shape[1:]
-    dma = pltpu.SemaphoreType.DMA
-    in_specs = [pl.BlockSpec(memory_space=SMEM)] * 2 + [pl.BlockSpec(memory_space=VMEM)]
-    scratch = [VMEM((steps, rows, vectors), F32), dma((chunks,))]
-    if phase == 0:
-        operands, aliases, count, held = [pool], {}, 0, [pool]
-        in_specs += [pl.BlockSpec(memory_space=VMEM)]
-    else:
-        count, held = len(pool), pool
-        operands, aliases = [in_hbm(current), *map(in_hbm, pool)], {3: 0}
-        in_specs += [pl.BlockSpec(memory_space=HBM)] * (1 + count)
-        scratch += [VMEM((count * pool[0].shape[0], rows, vectors), BF16), dma((chunks,)), dma((count,))]
-    room = ROOM + 4 * steps * rows * vectors + sum(2 * a.size for a in held)
-    return pl.pallas_call(
-        functools.partial(hops_kernel, phase, slots, fixed, count),
+    rows, vectors = pool.shape[1:]
+    block = pl.BlockSpec(memory_space=VMEM)
+    return pl.pallas_call(
+        functools.partial(hops_kernel, slots, fixed),
         out_shape=HBM((steps, rows, vectors), F32),
-        in_specs=in_specs,
+        in_specs=[pl.BlockSpec(memory_space=SMEM)] * 2 + [block] * 2,
         out_specs=pl.BlockSpec(memory_space=HBM),
-        scratch_shapes=scratch,
-        input_output_aliases=aliases,
-        compiler_params=pltpu.CompilerParams(vmem_limit_bytes=room),
+        scratch_shapes=[VMEM((steps, rows, vectors), F32), pltpu.SemaphoreType.DMA((chunks,))],
+        compiler_params=pltpu.CompilerParams(
+            vmem_limit_bytes=ROOM + 4 * steps * rows * vectors + 2 * pool.size
+        ),
         cost_estimate=pl.CostEstimate(flops=8 * 10**9, bytes_accessed=40 * 2**20, transcendentals=0),
-    )(lists, counts, tiles, *operands)
+        name="hops",
+    )(lists, counts, tiles, pool)
+
+
+def adjoint_kernel(phase, slots, count, lists_ref, counts_ref, tiles_ref, left_ref, out_ref, sum_ref):
+    local, rows = left_ref.shape[:2]
+    for s in range(2 * count):
+        sum_ref[s] = jnp.zeros_like(sum_ref[s])
+
+    def one_block(block, carry):
+        d = block // local
+        tiles = tiles_ref.at[d]
+
+        def two(j, carry):
+            e0 = lists_ref[phase, block * slots + 2 * j]
+            e1 = lists_ref[phase, block * slots + 2 * j + 1]
+            value = lax.dot_general(
+                jnp.concatenate([tiles[e0 // SHIFT], tiles[e1 // SHIFT]], axis=1),
+                left_ref[block % local], (((0,), (0,)), ((), ())), preferred_element_type=F32,
+            )
+            sum_ref[d * count + e0 % SHIFT] += value[:rows]
+            sum_ref[d * count + e1 % SHIFT] += value[rows:]
+            return carry
+
+        return lax.fori_loop(0, (counts_ref[phase, block] + 1) // 2, two, carry)
+
+    lax.fori_loop(0, 2 * local, one_block, 0)
+    for d in range(2):
+        for s in range(count):
+            out_ref[d, :, s * rows:(s + 1) * rows] = sum_ref[d * count + s].astype(BF16).T
+
+
+def adjoint(phase, lists, counts, tiles, left, count):
+    slots = lists.shape[1] // counts.shape[1]
+    rows, vectors = left.shape[1:]
+    block = pl.BlockSpec(memory_space=VMEM)
+    size = 2 * count * rows * vectors
+    return pl.pallas_call(
+        functools.partial(adjoint_kernel, phase, slots, count),
+        out_shape=jax.ShapeDtypeStruct((2, vectors, count * rows), BF16),
+        in_specs=[pl.BlockSpec(memory_space=SMEM)] * 2 + [block] * 2,
+        out_specs=block,
+        scratch_shapes=[VMEM((2 * count, rows, vectors), F32)],
+        compiler_params=pltpu.CompilerParams(vmem_limit_bytes=ROOM + 6 * size + 2 * left.size),
+        cost_estimate=pl.CostEstimate(flops=8 * 10**9, bytes_accessed=16 * 2**20, transcendentals=0),
+        name="adjoint",
+    )(lists, counts, tiles, left)
 
 
 def gram_kernel(
-    phase, count, slots, fixed, rank_ref, lists_ref, counts_ref, tiles_ref, in_ref, left_ref, *rest
+    phase, count, slots, fixed, more, lists_ref, counts_ref, tiles_ref, in_ref, left_ref, *rest
 ):
-    arrivals, rest = rest[:count], rest[count:]
-    outs, (pool_ref, held_ref, current_ref, sum_ref, in_sems, sems) = rest[:-6], rest[-6:]
+    arrivals, (sum_ref, pool_ref, held_ref, high_ref, low_ref, in_sems, sems) = rest[:count], rest[count:]
     steps, rows, vectors = held_ref.shape
     per = steps // 2
     chunks = in_sems.shape[0] // 2
     bunch = per // chunks
-    inward = in_chunks(in_ref, held_ref, in_sems)
+    inward = None if more else in_chunks(in_ref, held_ref, in_sems)
     loads = pool_loads(arrivals, pool_ref, sems)
     for copy in loads:
         copy.start()
-    ahead = min(AHEAD // 2, chunks)
-    for i in range(ahead):
-        for d in range(2):
-            inward(d * chunks + i).start()
+    ahead = min(2, chunks)
+    if more:
+        sum_ref[...] = in_ref[...]
+    else:
+        for i in range(ahead):
+            for d in range(2):
+                inward(d * chunks + i).start()
+        sum_ref[...] = jnp.zeros_like(sum_ref)
     for copy in loads:
         copy.wait()
 
     def some(step, carry):
         spots = [(d, g, d * per + step * bunch + g) for d in range(2) for g in range(bunch)]
 
-        @pl.when(step + ahead < chunks)
-        def _():
+        if not more:
+            @pl.when(step + ahead < chunks)
+            def _():
+                for d in range(2):
+                    inward(d * chunks + step + ahead).start()
+
             for d in range(2):
-                inward(d * chunks + step + ahead).start()
-
-        for d in range(2):
-            inward(d * chunks + step).wait()
+                inward(d * chunks + step).wait()
         for d, g, block in spots:
             entry = lambda j, block=block: lists_ref[phase, block * slots + j]
+            if more:
+                held_ref[block] = jnp.zeros_like(held_ref[block])
             for j in range(fixed):
                 held_ref[block] += pair(entry, j, tiles_ref.at[d], pool_ref)
         for d, g, block in spots:
@@ -268,20 +291,62 @@
                 held_ref.at[block], fixed, counts_ref[phase, block], entry, tiles_ref.at[d], pool_ref
             )
         for d, g, block in spots:
-            current_ref[pl.ds(g * rows, rows), pl.ds(d * vectors, vectors)] = held_ref[block].astype(BF16)
-        part = jnp.dot(left_ref[step], current_ref[...], preferred_element_type=F32)
-
-        @pl.when(step == 0)
-        def _():
-            sum_ref[...] = part
-
-        @pl.when(step > 0)
-        def _():
-            sum_ref[...] += part
-
+            value = held_ref[block]
+            high = value.astype(BF16)
+            spot = (pl.ds(g * rows, rows), pl.ds(d * vectors, vectors))
+            high_ref[spot] = high
+            low_ref[spot] = (value - high.astype(F32)).astype(BF16)
+        sum_ref[...] += jnp.dot(left_ref[step], high_ref[...], preferred_element_type=F32)
+        sum_ref[...] += jnp.dot(left_ref[step], low_ref[...], preferred_element_type=F32)
         return carry
 
     lax.fori_loop(0, chunks, some, 0)
+
+
+def gram(phase, lists, counts, tiles, current, left_t, arrivals, fixed):
+    steps = counts.shape[1]
+    more = current.ndim == 2
+    rows, vectors = arrivals[0].shape[1:]
+    slots = lists.shape[1] // steps
+    chunks, columns, depth = left_t.shape
+    cap = arrivals[0].shape[0]
+    block = pl.BlockSpec(memory_space=VMEM)
+    dma = pltpu.SemaphoreType.DMA
+    room = 2 * ROOM + 4 * steps * rows * vectors + sum(2 * a.size for a in arrivals)
+    return pl.pallas_call(
+        functools.partial(gram_kernel, phase, len(arrivals), slots, fixed, more),
+        out_shape=jax.ShapeDtypeStruct((columns, 2 * vectors), F32),
+        in_specs=[pl.BlockSpec(memory_space=SMEM)] * 2
+        + [block, block if more else pl.BlockSpec(memory_space=HBM), block]
+        + [pl.BlockSpec(memory_space=HBM)] * len(arrivals),
+        out_specs=block,
+        scratch_shapes=[
+            VMEM((len(arrivals) * cap, rows, vectors), BF16),
+            VMEM((steps, rows, vectors), F32),
+            VMEM((depth, 2 * vectors), BF16),
+            VMEM((depth, 2 * vectors), BF16),
+            dma((2 * chunks,)),
+            dma((len(arrivals),)),
+        ],
+        compiler_params=pltpu.CompilerParams(vmem_limit_bytes=room),
+        cost_estimate=pl.CostEstimate(flops=12 * 10**9, bytes_accessed=24 * 2**20, transcendentals=0),
+        name="gram",
+    )(lists, counts, tiles, current if more else in_hbm(current), in_vmem(left_t), *map(in_hbm, arrivals))
+
+
+def late_kernel(count, rank_ref, in_ref, adjoint_ref, *rest):
+    arrivals, rest = rest[:count], rest[count:]
+    outs, (sum_ref, pool_ref, sems) = rest[:-3], rest[-3:]
+    blocks, rows, vectors = pool_ref.shape
+    loads = pool_loads(arrivals, pool_ref, sems)
+    for copy in loads:
+        copy.start()
+    for copy in loads:
+        copy.wait()
+    pool = pool_ref[...].reshape(blocks * rows, vectors)
+    for d in range(2):
+        side = (slice(None), slice(d * vectors, (d + 1) * vectors))
+        sum_ref[side] = in_ref[side] + jnp.dot(adjoint_ref[d], pool, preferred_element_type=F32)
     if len(outs) == 1:
         outs[0][...] = sum_ref[...]
         return
@@ -290,43 +355,38 @@
     outer, inner, own = send_ref.shape[:3]
     for n in range(outer * inner):
         keep_ref[n // inner, n % inner] = sum_ref[pl.ds(pl.multiple_of((2 * n + core) * own, own), own), :]
-        send_ref[n // inner, n % inner] = sum_ref[pl.ds(pl.multiple_of((2 * n + 1 - core) * own, own), own), :].astype(send_ref.dtype)
-
-
-def gram(phase, rank, lists, counts, tiles, current, left_t, arrivals, devices, sent, fixed):
-    steps, rows, vectors = current.shape
-    slots = lists.shape[1] // steps
-    chunks = left_t.shape[0]
-    cap = arrivals[0].shape[0]
-    columns = left_t.shape[1]
+        send_ref[n // inner, n % inner] = sum_ref[
+            pl.ds(pl.multiple_of((2 * n + 1 - core) * own, own), own), :
+        ].astype(send_ref.dtype)
+
+
+def late(rank, sums, adjoint, arrivals, devices, sent):
+    columns, both = sums.shape
     own = columns // devices
+    cap, rows, vectors = arrivals[0].shape
     block = pl.BlockSpec(memory_space=VMEM)
-    dma = pltpu.SemaphoreType.DMA
     if own % 8:
-        halves = [jax.ShapeDtypeStruct((columns, 2 * vectors), F32)]
+        halves = [jax.ShapeDtypeStruct(sums.shape, F32)]
     else:
-        half = (devices // 8, 4, own, 2 * vectors)
+        half = (devices // 8, 4, own, both)
         halves = [VMEM(half, sent), VMEM(half, F32)]
-    room = 2 * ROOM + 4 * current.size + sum(2 * a.size for a in arrivals)
-    return pl.pallas_call(
-        functools.partial(gram_kernel, phase, len(arrivals), slots, fixed),
+    return pl.pallas_call(
+        functools.partial(late_kernel, len(arrivals)),
         out_shape=halves,
-        in_specs=[pl.BlockSpec(memory_space=SMEM)] * 3
-        + [block, pl.BlockSpec(memory_space=HBM), block]
+        in_specs=[pl.BlockSpec(memory_space=SMEM), block, block]
         + [pl.BlockSpec(memory_space=HBM)] * len(arrivals),
         out_specs=[block] * len(halves),
         scratch_shapes=[
+            VMEM(sums.shape, F32),
             VMEM((len(arrivals) * cap, rows, vectors), BF16),
-            VMEM((steps, rows, vectors), F32),
-            VMEM((left_t.shape[2], 2 * vectors), BF16),
-            VMEM((columns, 2 * vectors), F32),
-            dma((2 * chunks,)),
-            dma((len(arrivals),)),
+            pltpu.SemaphoreType.DMA((len(arrivals),)),
         ],
-        compiler_params=pltpu.CompilerParams(vmem_limit_bytes=room),
-        cost_estimate=pl.CostEstimate(flops=6 * 10**9, bytes_accessed=24 * 2**20, transcendentals=0),
-        name="gram",
-    )(rank, lists, counts, tiles, in_hbm(current), in_vmem(left_t), *map(in_hbm, arrivals))
+        compiler_params=pltpu.CompilerParams(
+            vmem_limit_bytes=2 * ROOM + sum(2 * a.size for a in arrivals)
+        ),
+        cost_estimate=pl.CostEstimate(flops=4 * 10**9, bytes_accessed=12 * 2**20, transcendentals=0),
+        name="late",
+    )(rank, in_vmem(sums), in_vmem(adjoint), *map(in_hbm, arrivals))
 
 
 def split_kernel(width, shift, count, final, scale, rank_ref, keep_ref, *rest):
@@ -406,16 +466,17 @@
         local, order, [start for start, _ in groups], tiles.shape[1],
     )
     tiles = jnp.concatenate([tiles, jnp.zeros((2, 1) + tiles.shape[2:], tiles.dtype)], axis=1)
-    bunch = math.gcd(local, 4) * block_rows
+    bunch = math.gcd(local, 8) * block_rows
     left_t = left.reshape(-1, bunch, vectors).transpose(0, 2, 1)
     tiles = in_vmem(tiles)
-    current = hops(0, lists, counts, tiles, blocks, None, 4)
-    for n, (start, stop) in enumerate(groups[:-1]):
-        current = hops(n + 1, lists, counts, tiles, arrived[start:stop], current, 2)
+    sums = hops(lists, counts, tiles, blocks, 4)
     start, stop = groups[-1]
-    sums = gram(
-        len(groups), rank, lists, counts, tiles, current, left_t, arrived[start:stop], devices, F32, 1
+    met = adjoint(
+        len(groups), lists, counts, tiles, left.reshape(blocks.shape), (stop - start) * send.shape[0]
     )
+    for n, (first, last) in enumerate(groups[:-1]):
+        sums = gram(n + 1, lists, counts, tiles, sums, left_t, arrived[first:last], 3)
+    sums = late(rank, sums, met, arrived[start:stop], devices, F32)
     if len(sums) == 1:
         mine = lax.psum_scatter(sums[0] * scale, "rows", scatter_dimension=0, tiled=True)
         return mine.reshape(mine.shape[0], 2, vectors).transpose(1, 0, 2)

time: 264 us -> 280 us (1.061)
  starting transfers between devices: 77.4 us -> 101 us
  waiting for transfers between devices: 93.5 us -> 71.7 us
  Pallas kernels: 76.3 us -> 84.2 us
  local copies, waits for them, and re-layouts: 14 us -> 19.6 us
    ppermute x38, starting transfers between devices: 77.4 us -> 101 us  [swap(): return lax.ppermute(value, 'rows', [(i, i ^ mask) for i in range(devices)])]
    ppermute x38, waiting for transfers between devices: 93.5 us -> 71.7 us  [swap(): return lax.ppermute(value, 'rows', [(i, i ^ mask) for i in range(devices)])]
    unnamed x93 -> x105, local copies, waits for them, and re-layouts: 3.1 us -> 8.93 us
    pallas_call x1, Pallas kernels: 17.3 us -> 23 us  [gram(): pl.pallas_call(functools.partial(gram_kernel, phase, len(arrivals), slots...]
  transfers between devices with their start and end apart: 38 -> 38, of which waited for: 14 -> 10; matrix products, arithmetic and copies ran while one was open for 4% -> 4% of each run, Pallas kernels for 18% -> 23%
where the time goes in v2:
time: 280 us; the launch traced here: 279 us
  starting transfers between devices  101 us (36%)
  Pallas kernels  84.2 us (30%)
  waiting for transfers between devices  71.7 us (26%)
  local copies, waits for them, and re-layouts  19.6 us (7%)
    ppermute x38, starting transfers between devices, swap(): return lax.ppermute(value, 'rows', [(i, i ^ mask) for i in range(devices)])  101 us
    ppermute x38, waiting for transfers between devices, swap(): return lax.ppermute(value, 'rows', [(i, i ^ mask) for i in range(devices)])  71.7 us
    pallas_call x1, Pallas kernels, adjoint(): pl.pallas_call(functools.partial(adjoint_kernel, phase, slots, count), ou...  27.3 us
    pallas_call x1, Pallas kernels, gram(): pl.pallas_call(functools.partial(gram_kernel, phase, len(arrivals), slots...  23 us
    pallas_call x1, Pallas kernels, hops(): pl.pallas_call(functools.partial(hops_kernel, slots, fixed), out_shape=HB...  14.9 us
    pallas_call x2, Pallas kernels, pack(): pl.pallas_call(functools.partial(pack_kernel, masks, len(after)), out_sha...  12.4 us
    unnamed x105, local copies, waits for them, and re-layouts  8.93 us
    reshape x1, local copies, waits for them, and re-layouts, body(): left_t = left.reshape(-1, bunch, vectors).transpose(0, 2, 1)  6.46 us
  transfers between devices with their start and end apart: 38, of which 10 were waited for; matrix products, arithmetic and copies ran while one was open for 4% of the time, Pallas kernels for 23%

profile of v2, /device:TPU:0, one launch (start us, length us, event | category | flops | bytes accessed | tf_op | source)
XLA Modules:
  0.0 279.3 jit_solution(4791928823197739732)
XLA Ops:
  0.0 3.1 %pack.2 = (bf16[2,128,512]{2,1,0:T(8,128)(2,1)}, bf16[2,128,512]{2,1,0:T(8,128)(2,1)}, bf16[2,128,512]{2,1,0:T(8,128)(2,1)}) custom-call(s32[1]{0:T(128)} %bitcast.rank_ref, s32[2,32]{1,0:T(2,128)} %bitcast.20, bf16[32,128,512]{2,1,0:T(8,128)(2,1)} %bitcast.14), custom_call_target="tpu_custom_call" | custom-call | tf_op jit(solution)/shard_map/pack/pallas_call | solution.py:77
  3.1 9.3 %pack.3 = (bf16[2,128,512]{2,1,0:T(8,128)(2,1)}, bf16[2,128,512]{2,1,0:T(8,128)(2,1)}, bf16[2,128,512]{2,1,0:T(8,128)(2,1)}, bf16[2,128,512]{2,1,0:T(8,128)(2,1)...) custom-call(s32[1]{0:T(128)} %bitcast.rank_ref, ...), custom_call_target="tpu_custom_call" | custom-call | tf_op jit(solution)/shard_map/pack/pallas_call | solution.py:77
  12.4 5.0 %collective-permute-start.10 = (bf16[2,128,512]{2,1,0:T(8,128)(2,1)}, bf16[2,128,512]{2,1,0:T(8,128)(2,1)S(1)}, u32[]{:S(2)}, u32[]{:S(2)}) collective-permute-start(bf16[2,128,512]{2,1,0:T(8,128)(2,1)} %get-tuple-element.56), channel_id=1, source_target_pairs={{0,22},{1,23},{2,20},{3,21},{4,18},{5,19},{6,16},{7,17},{8,30},{9,... | collective-permute-start | bytes 786440 | tf_op jit(solution)/shard_map/ppermute | solution.py:441
  17.4 1.4 collective-permute-start.12
  18.9 2.0 collective-permute-start.13
  20.8 3.7 %collective-permute-start.14 = (bf16[2,128,512]{2,1,0:T(8,128)(2,1)}, bf16[2,128,512]{2,1,0:T(8,128)(2,1)S(1)}, u32[]{:S(2)}, u32[]{:S(2)}) collective-permute-start(bf16[2,128,512]{2,1,0:T(8,128)(2,1)} %get-tuple-element.60), channel_id=1, source_target_pairs={{0,24},{1,25},{2,26},{3,27},{4,28},{5,29},{6,30},{7,31},{8,16},{9,... | collective-permute-start | bytes 786440 | tf_op jit(solution)/shard_map/ppermute | solution.py:441
  24.9 16.8 %collective-permute-done.10.rest_10_ = bf16[2,128,512]{2,1,0:T(8,128)(2,1)S(1)} collective-permute-done((bf16[2,128,512]{2,1,0:T(8,128)(2,1)}, bf16[2,128,512]{2,1,0:T(8,128)(2,1)S(1)}, u32[]{:S(2)}, u32[]{:S(2)}) %collective-permute-start.10) | collective-permute-done | bytes 262176 | tf_op jit(solution)/shard_map/ppermute | solution.py:441
  41.7 1.4 collective-permute-start.15
  45.0 4.4 %collective-permute-start.16 = (bf16[2,128,512]{2,1,0:T(8,128)(2,1)}, bf16[2,128,512]{2,1,0:T(8,128)(2,1)S(1)}, u32[]{:S(2)}, u32[]{:S(2)}) collective-permute-start(bf16[2,128,512]{2,1,0:T(8,128)(2,1)} %get-tuple-element.62), channel_id=1, source_target_pairs={{0,25},{1,24},{2,27},{3,26},{4,29},{5,28},{6,31},{7,30},{8,17},{9,... | collective-permute-start | bytes 786440 | tf_op jit(solution)/shard_map/ppermute | solution.py:441
  49.6 10.2 %collective-permute-start.4 = (bf16[2,128,512]{2,1,0:T(8,128)(2,1)}, bf16[2,128,512]{2,1,0:T(8,128)(2,1)S(1)}, u32[]{:S(2)}, u32[]{:S(2)}) collective-permute-start(bf16[2,128,512]{2,1,0:T(8,128)(2,1)} %get-tuple-element.50), channel_id=1, source_target_pairs={{0,19},{1,18},{2,17},{3,16},{4,23},{5,22},{6,21},{7,20},{8,27},{9,... | collective-permute-start | bytes 786440 | tf_op jit(solution)/shard_map/ppermute | solution.py:441
  59.8 1.1 collective-permute-start.5
  61.2 9.8 %collective-permute-start = (bf16[2,128,512]{2,1,0:T(8,128)(2,1)S(1)}, bf16[2,128,512]{2,1,0:T(8,128)(2,1)S(1)}, u32[]{:S(2)}, u32[]{:S(2)}) collective-permute-start(bf16[2,128,512]{2,1,0:T(8,128)(2,1)S(1)} %copy-done.7), channel_id=1, source_target_pairs={{0,16},{1,17},{2,18},{3,19},{4,20},{5,21},{6,22},{7,23},{8,24},{9,... | collective-permute-start | bytes 786440 | tf_op jit(solution)/shard_map/ppermute | solution.py:441
  72.2 13.0 %collective-permute-done.4.rest_4_ = bf16[2,128,512]{2,1,0:T(8,128)(2,1)S(1)} collective-permute-done((bf16[2,128,512]{2,1,0:T(8,128)(2,1)}, bf16[2,128,512]{2,1,0:T(8,128)(2,1)S(1)}, u32[]{:S(2)}, u32[]{:S(2)}) %collective-permute-start.4) | collective-permute-done | bytes 262176 | tf_op jit(solution)/shard_map/ppermute | solution.py:441
  85.2 2.0 collective-permute-start.9
  87.7 3.2 %concatenate.3.tiles_ref = bf16[2,65,128,128]{3,2,1,0:T(8,128)(2,1)S(1)} pad(bf16[2,64,128,128]{3,2,1,0:T(8,128)(2,1)} %param.9, bf16[]{:T(256)} %constant.66.clone.1), padding=0_0x0_1x0_0x0_0 | pad | bytes 8454146 | tf_op jit(solution)/shard_map/concatenate | solution.py:468
  91.0 12.6 %collective-permute-done.6.rest_6_ = bf16[2,128,512]{2,1,0:T(8,128)(2,1)S(1)} collective-permute-done((bf16[2,128,512]{2,1,0:T(8,128)(2,1)}, bf16[2,128,512]{2,1,0:T(8,128)(2,1)S(1)}, u32[]{:S(2)}, u32[]{:S(2)}) %collective-permute-start.6) | collective-permute-done | bytes 262176 | tf_op jit(solution)/shard_map/ppermute | solution.py:441
  103.6 2.5 collective-permute-start.2
  106.1 12.8 %collective-permute-done.8.rest_8_ = bf16[2,128,512]{2,1,0:T(8,128)(2,1)} collective-permute-done((bf16[2,128,512]{2,1,0:T(8,128)(2,1)}, bf16[2,128,512]{2,1,0:T(8,128)(2,1)}, u32[]{:S(2)}, u32[]{:S(2)}) %collective-permute-start.8) | collective-permute-done | bytes 262176 | tf_op jit(solution)/shard_map/ppermute | solution.py:441
  119.0 4.5 %collective-permute-start.18 = (bf16[2,128,512]{2,1,0:T(8,128)(2,1)S(1)}, bf16[2,128,512]{2,1,0:T(8,128)(2,1)S(1)}, u32[]{:S(2)}, u32[]{:S(2)}) collective-permute-start(bf16[2,128,512]{2,1,0:T(8,128)(2,1)S(1)} %copy-done.32), channel_id=1, source_target_pairs={{0,26},{1,27},{2,24},{3,25},{4,30},{5,31},{6,28},{7,29},{8,18},{9,... | collective-permute-start | bytes 786440 | tf_op jit(solution)/shard_map/ppermute | solution.py:441
  123.5 1.4 collective-permute-start.20
  124.9 14.9 %hops.1.in_ref = f32[64,128,512]{2,1,0:T(8,128)} custom-call(s32[3,1024]{1,0:T(4,128)S(1)} %add.78.lists_ref, s32[3,64]{1,0:T(4,128)S(1)} %get-tuple-element.87.counts_ref, bf16[2,65,128,128]{3,2,1,0:T(8,128)(2,1)S(1)} %concatenate.3.tiles_ref, bf16[32,128,512]{2,1,0:T(8,128)(2,1)S(1)} %bitcast.16), custom_call_target="tpu_custom_call" | custom-call | flops 8000000000 | bytes 41943040 | tf_op jit(solution)/shard_map/hops/pallas_call | solution.py:189
  139.9 0.9 collective-permute-start.21
  140.8 2.3 collective-permute-done.2.rest_2_
  143.1 8.7 %collective-permute-start.22 = (bf16[2,128,512]{2,1,0:T(8,128)(2,1)S(1)}, bf16[2,128,512]{2,1,0:T(8,128)(2,1)S(1)}, u32[]{:S(2)}, u32[]{:S(2)}) collective-permute-start(bf16[2,128,512]{2,1,0:T(8,128)(2,1)S(1)} %copy-done.25), channel_id=1, source_target_pairs={{0,28},{1,29},{2,30},{3,31},{4,24},{5,25},{6,26},{7,27},{8,20},{9,... | collective-permute-start | bytes 786440 | tf_op jit(solution)/shard_map/ppermute | solution.py:441
  151.8 0.9 collective-permute-start.23
  152.6 3.1 %collective-permute-start.24 = (bf16[2,128,512]{2,1,0:T(8,128)(2,1)S(1)}, bf16[2,128,512]{2,1,0:T(8,128)(2,1)}, u32[]{:S(2)}, u32[]{:S(2)}) collective-permute-start(bf16[2,128,512]{2,1,0:T(8,128)(2,1)S(1)} %copy-done.21), channel_id=1, source_target_pairs={{0,29},{1,28},{2,31},{3,30},{4,25},{5,24},{6,27},{7,26},{8,21},{9,... | collective-permute-start | bytes 786440 | tf_op jit(solution)/shard_map/ppermute | solution.py:441
  155.8 9.4 %collective-permute-start.25 = (bf16[2,128,512]{2,1,0:T(8,128)(2,1)S(1)}, bf16[2,128,512]{2,1,0:T(8,128)(2,1)}, u32[]{:S(2)}, u32[]{:S(2)}) collective-permute-start(bf16[2,128,512]{2,1,0:T(8,128)(2,1)S(1)} %copy-done.17), channel_id=1, source_target_pairs={{0,12},{1,13},{2,14},{3,15},{4,8},{5,9},{6,10},{7,11},{8,4},{9,5},... | collective-permute-start | bytes 786440 | tf_op jit(solution)/shard_map/ppermute | solution.py:441
  165.2 27.3 %adjoint.1.adjoint_ref = bf16[2,512,3328]{2,1,0:T(8,128)(2,1)S(1)} custom-call(s32[3,1024]{1,0:T(4,128)S(1)} %add.78.lists_ref, s32[3,64]{1,0:T(4,128)S(1)} %get-tuple-element.87.counts_ref, bf16[2,65,128,128]{3,2,1,0:T(8,128)(2,1)S(1)} %concatenate.3.tiles_ref, bf16[32,128,512]{2,1,0:T(8,128)(2,1)S(1)} %bitcast.18), custom_call_target="tpu_custom_call" | custom-call | flops 8000000000 | bytes 16777216 | tf_op jit(solution)/shard_map/adjoint/pallas_call | solution.py:236
  192.5 2.7 copy-done.5
  195.3 6.5 %copy.20 = bf16[4,1024,512]{1,2,0:T(8,128)(2,1)} copy(bf16[4,1024,512]{2,1,0:T(8,128)(2,1)} %bitcast.17) | data formatting | bytes 8388608 | tf_op jit(solution)/shard_map/reshape | solution.py:470
  201.8 6.5 %collective-permute-start.27 = (bf16[2,128,512]{2,1,0:T(8,128)(2,1)S(1)}, bf16[2,128,512]{2,1,0:T(8,128)(2,1)S(1)}, u32[]{:S(2)}, u32[]{:S(2)}) collective-permute-start(bf16[2,128,512]{2,1,0:T(8,128)(2,1)S(1)} %copy-done.15), channel_id=1, source_target_pairs={{0,13},{1,12},{2,15},{3,14},{4,9},{5,8},{6,11},{7,10},{8,5},{9,4},... | collective-permute-start | bytes 786440 | tf_op jit(solution)/shard_map/ppermute | solution.py:441
  208.3 2.8 %collective-permute-start.28 = (bf16[2,128,512]{2,1,0:T(8,128)(2,1)S(1)}, bf16[2,128,512]{2,1,0:T(8,128)(2,1)S(1)}, u32[]{:S(2)}, u32[]{:S(2)}) collective-permute-start(bf16[2,128,512]{2,1,0:T(8,128)(2,1)S(1)} %copy-done.14), channel_id=1, source_target_pairs={{0,31},{1,30},{2,29},{3,28},{4,27},{5,26},{6,25},{7,24},{8,23},{9,... | collective-permute-start | bytes 786440 | tf_op jit(solution)/shard_map/ppermute | solution.py:441
  211.2 2.3 collective-permute-start.29
  213.9 2.2 copy-done.2
  216.1 2.2 copy-done.4
  218.3 23.0 %gram.1.in_ref = f32[512,1024]{1,0:T(8,128)S(1)} custom-call(s32[3,1024]{1,0:T(4,128)S(1)} %add.78.lists_ref, s32[3,64]{1,0:T(4,128)S(1)} %get-tuple-element.87.counts_ref, bf16[2,65,128,128]{3,2,1,0:T(8,128)(2,1)S(1)} %copy-done.2, f32[64,128,512]{2,1,0:T(8,128)} %hops.1.in_ref, bf16[4,512,1024]{2,1,0:T(8,128)(2,1)S(1)} %bitcast.19, ...), custom_call_target="tpu_custom_call" | custom-call | flops 12000000000 | bytes 25165824 | tf_op jit(solution)/shard_map/gram/pallas_call | solution.py:316
  243.0 5.9 %late.1 = (f32[4,4,16,1024]{3,2,1,0:T(8,128)S(1)}, f32[4,4,16,1024]{3,2,1,0:T(8,128)S(1)}) custom-call(s32[1]{0:T(128)} %bitcast.rank_ref, f32[512,1024]{1,0:T(8,128)S(1)} %gram.1.in_ref, bf16[2,512,3328]{2,1,0:T(8,128)(2,1)S(1)} %copy-done.6, bf16[2,128,512]{2,1,0:T(8,128)(2,1)} %copy-done.40, bf16[2,128,512]{2,1,0:T(8,128)(2,1)} %copy-done.41, ...), custom_call_target="tpu_custom_call" | custom-call | flops 4000000000 | bytes 12582912 | tf_op jit(solution)/shard_map/late/pallas_call | solution.py:373
  248.9 1.1 collective-permute-start.31
  250.0 2.3 collective-permute-done.31.rest_0_
  252.4 3.6 %collective-permute-start.32 = (bf16[4,16,1024]{2,1,0:T(8,128)(2,1)S(1)}, bf16[4,16,1024]{2,1,0:T(8,128)(2,1)S(1)}, u32[]{:S(2)}, u32[]{:S(2)}) collective-permute-start(bf16[4,16,1024]{2,1,0:T(8,128)(2,1)S(1)} %get-tuple-element.80), channel_id=1, source_target_pairs={{0,2},{1,3},{2,0},{3,1},{4,6},{5,7},{6,4},{7,5},{8,10},{9,11},{10,... | collective-permute-start | bytes 393224 | tf_op jit(solution)/shard_map/ppermute | solution.py:441
  255.9 4.2 %collective-permute-start.33 = (bf16[4,16,1024]{2,1,0:T(8,128)(2,1)S(1)}, bf16[4,16,1024]{2,1,0:T(8,128)(2,1)S(1)}, u32[]{:S(2)}, u32[]{:S(2)}) collective-permute-start(bf16[4,16,1024]{2,1,0:T(8,128)(2,1)S(1)} %get-tuple-element.81), channel_id=1, source_target_pairs={{0,4},{1,5},{2,6},{3,7},{4,0},{5,1},{6,2},{7,3},{8,12},{9,13},{10,... | collective-permute-start | bytes 393224 | tf_op jit(solution)/shard_map/ppermute | solution.py:441
  260.1 1.4 collective-permute-start.34
  261.5 4.7 %collective-permute-done.33.rest_1_ = bf16[4,16,1024]{2,1,0:T(8,128)(2,1)S(1)} collective-permute-done((bf16[4,16,1024]{2,1,0:T(8,128)(2,1)S(1)}, bf16[4,16,1024]{2,1,0:T(8,128)(2,1)S(1)}, u32[]{:S(2)}, u32[]{:S(2)}) %collective-permute-start.33) | collective-permute-done | bytes 131104 | tf_op jit(solution)/shard_map/ppermute | solution.py:441
  266.2 1.8 collective-permute-done.34.rest_2_
  268.6 3.8 %collective-permute-start.36 = (f32[16,1024]{1,0:T(8,128)S(1)}, f32[16,1024]{1,0:T(8,128)S(1)}, u32[]{:S(2)}, u32[]{:S(2)}) collective-permute-start(f32[16,1024]{1,0:T(8,128)S(1)} %get-tuple-element.85), channel_id=1, source_target_pairs={{0,16},{1,17},{2,18},{3,19},{4,20},{5,21},{6,22},{7,23},{8,24},{9,... | collective-permute-start | bytes 196616 | tf_op jit(solution)/shard_map/ppermute | solution.py:441
  272.5 0.9 collective-permute-start.37
  273.3 4.0 %collective-permute-done.36.rest_1_ = f32[16,1024]{1,0:T(8,128)S(1)} collective-permute-done((f32[16,1024]{1,0:T(8,128)S(1)}, f32[16,1024]{1,0:T(8,128)S(1)}, u32[]{:S(2)}, u32[]{:S(2)}) %collective-permute-start.36) | collective-permute-done | bytes 65568 | tf_op jit(solution)/shard_map/ppermute | solution.py:441
  277.3 1.3 collective-permute-done.37.rest_2_
  (163 shorter events, 6.4 us)
Async XLA Ops:
  3.1 58.1 %copy-start.7 = (bf16[2,128,512]{2,1,0:T(8,128)(2,1)S(1)}, bf16[2,128,512]{2,1,0:T(8,128)(2,1)}, u32[]{:S(2)}) copy-start(bf16[2,128,512]{2,1,0:T(8,128)(2,1)} %get-tuple-element.46.rest_0_) | copy-start | bytes 786436
  12.4 29.2 %collective-permute-start.10 = (bf16[2,128,512]{2,1,0:T(8,128)(2,1)}, bf16[2,128,512]{2,1,0:T(8,128)(2,1)S(1)}, u32[]{:S(2)}, u32[]{:S(2)}) collective-permute-start(bf16[2,128,512]{2,1,0:T(8,128)(2,1)} %get-tuple-element.56), channel_id=1, source_target_pairs={{0,22},{1,23},{2,20},{3,21},{4,18},{5,19},{6,16},{7,17},{8,30},{9,... | collective-permute-start | bytes 786440 | tf_op jit(solution)/shard_map/ppermute | solution.py:441
  17.4 27.6 %collective-permute-start.11 = (bf16[2,128,512]{2,1,0:T(8,128)(2,1)}, bf16[2,128,512]{2,1,0:T(8,128)(2,1)S(1)}, u32[]{:S(2)}, u32[]{:S(2)}) collective-permute-start(bf16[2,128,512]{2,1,0:T(8,128)(2,1)} %get-tuple-element.57), channel_id=1, source_target_pairs={{0,5},{1,4},{2,7},{3,6},{4,1},{5,0},{6,3},{7,2},{8,13},{9,12},{10,... | collective-permute-start | bytes 786440 | tf_op jit(solution)/shard_map/ppermute | solution.py:441
  17.4 32.0 %collective-permute-start.12 = (bf16[2,128,512]{2,1,0:T(8,128)(2,1)}, bf16[2,128,512]{2,1,0:T(8,128)(2,1)S(1)}, u32[]{:S(2)}, u32[]{:S(2)}) collective-permute-start(bf16[2,128,512]{2,1,0:T(8,128)(2,1)} %get-tuple-element.58), channel_id=1, source_target_pairs={{0,23},{1,22},{2,21},{3,20},{4,19},{5,18},{6,17},{7,16},{8,31},{9,... | collective-permute-start | bytes 786440 | tf_op jit(solution)/shard_map/ppermute | solution.py:441
  18.9 30.6 %collective-permute-start.13 = (bf16[2,128,512]{2,1,0:T(8,128)(2,1)}, bf16[2,128,512]{2,1,0:T(8,128)(2,1)S(1)}, u32[]{:S(2)}, u32[]{:S(2)}) collective-permute-start(bf16[2,128,512]{2,1,0:T(8,128)(2,1)} %get-tuple-element.59), channel_id=1, source_target_pairs={{0,6},{1,7},{2,4},{3,5},{4,2},{5,3},{6,0},{7,1},{8,14},{9,15},{10,... | collective-permute-start | bytes 786440 | tf_op jit(solution)/shard_map/ppermute | solution.py:441
  20.8 28.7 %collective-permute-start.14 = (bf16[2,128,512]{2,1,0:T(8,128)(2,1)}, bf16[2,128,512]{2,1,0:T(8,128)(2,1)S(1)}, u32[]{:S(2)}, u32[]{:S(2)}) collective-permute-start(bf16[2,128,512]{2,1,0:T(8,128)(2,1)} %get-tuple-element.60), channel_id=1, source_target_pairs={{0,24},{1,25},{2,26},{3,27},{4,28},{5,29},{6,30},{7,31},{8,16},{9,... | collective-permute-start | bytes 786440 | tf_op jit(solution)/shard_map/ppermute | solution.py:441
  41.7 49.3 %copy-start.18 = (bf16[2,128,512]{2,1,0:T(8,128)(2,1)}, bf16[2,128,512]{2,1,0:T(8,128)(2,1)S(1)}, u32[]{:S(2)}) copy-start(bf16[2,128,512]{2,1,0:T(8,128)(2,1)S(1)} %collective-permute-done.10.rest_10_) | copy-start | bytes 786436
  41.7 18.2 %collective-permute-start.15 = (bf16[2,128,512]{2,1,0:T(8,128)(2,1)}, bf16[2,128,512]{2,1,0:T(8,128)(2,1)S(1)}, u32[]{:S(2)}, u32[]{:S(2)}) collective-permute-start(bf16[2,128,512]{2,1,0:T(8,128)(2,1)} %get-tuple-element.61), channel_id=1, source_target_pairs={{0,7},{1,6},{2,5},{3,4},{4,3},{5,2},{6,1},{7,0},{8,15},{9,14},{10,... | collective-permute-start | bytes 786440 | tf_op jit(solution)/shard_map/ppermute | solution.py:441
  45.0 45.9 %copy-start.19 = (bf16[2,128,512]{2,1,0:T(8,128)(2,1)}, bf16[2,128,512]{2,1,0:T(8,128)(2,1)S(1)}, u32[]{:S(2)}) copy-start(bf16[2,128,512]{2,1,0:T(8,128)(2,1)S(1)} %collective-permute-done.11.rest_11_) | copy-start | bytes 786436
  45.0 16.1 %collective-permute-start.16 = (bf16[2,128,512]{2,1,0:T(8,128)(2,1)}, bf16[2,128,512]{2,1,0:T(8,128)(2,1)S(1)}, u32[]{:S(2)}, u32[]{:S(2)}) collective-permute-start(bf16[2,128,512]{2,1,0:T(8,128)(2,1)} %get-tuple-element.62), channel_id=1, source_target_pairs={{0,25},{1,24},{2,27},{3,26},{4,29},{5,28},{6,31},{7,30},{8,17},{9,... | collective-permute-start | bytes 786440 | tf_op jit(solution)/shard_map/ppermute | solution.py:441
  49.5 41.5 %copy-start.20 = (bf16[2,128,512]{2,1,0:T(8,128)(2,1)}, bf16[2,128,512]{2,1,0:T(8,128)(2,1)S(1)}, u32[]{:S(2)}) copy-start(bf16[2,128,512]{2,1,0:T(8,128)(2,1)S(1)} %collective-permute-done.12.rest_12_) | copy-start | bytes 786436
  49.5 21.6 %collective-permute-start.17 = (bf16[2,128,512]{2,1,0:T(8,128)(2,1)}, bf16[2,128,512]{2,1,0:T(8,128)(2,1)S(1)}, u32[]{:S(2)}, u32[]{:S(2)}) collective-permute-start(bf16[2,128,512]{2,1,0:T(8,128)(2,1)} %get-tuple-element.63), channel_id=1, source_target_pairs={{0,8},{1,9},{2,10},{3,11},{4,12},{5,13},{6,14},{7,15},{8,0},{9,1},... | collective-permute-start | bytes 786440 | tf_op jit(solution)/shard_map/ppermute | solution.py:441
  49.5 41.5 %copy-start.22 = (bf16[2,128,512]{2,1,0:T(8,128)(2,1)}, bf16[2,128,512]{2,1,0:T(8,128)(2,1)S(1)}, u32[]{:S(2)}) copy-start(bf16[2,128,512]{2,1,0:T(8,128)(2,1)S(1)} %collective-permute-done.13.rest_13_) | copy-start | bytes 786436
  49.5 22.1 %collective-permute-start.3 = (bf16[2,128,512]{2,1,0:T(8,128)(2,1)}, bf16[2,128,512]{2,1,0:T(8,128)(2,1)S(1)}, u32[]{:S(2)}, u32[]{:S(2)}) collective-permute-start(bf16[2,128,512]{2,1,0:T(8,128)(2,1)} %get-tuple-element.49), channel_id=1, source_target_pairs={{0,1},{1,0},{2,3},{3,2},{4,5},{5,4},{6,7},{7,6},{8,9},{9,8},{10,11... | collective-permute-start | bytes 786440 | tf_op jit(solution)/shard_map/ppermute | solution.py:441
  49.6 41.4 %copy-start.23 = (bf16[2,128,512]{2,1,0:T(8,128)(2,1)}, bf16[2,128,512]{2,1,0:T(8,128)(2,1)S(1)}, u32[]{:S(2)}) copy-start(bf16[2,128,512]{2,1,0:T(8,128)(2,1)S(1)} %collective-permute-done.14.rest_14_) | copy-start | bytes 786436
  49.6 35.6 %collective-permute-start.4 = (bf16[2,128,512]{2,1,0:T(8,128)(2,1)}, bf16[2,128,512]{2,1,0:T(8,128)(2,1)S(1)}, u32[]{:S(2)}, u32[]{:S(2)}) collective-permute-start(bf16[2,128,512]{2,1,0:T(8,128)(2,1)} %get-tuple-element.50), channel_id=1, source_target_pairs={{0,19},{1,18},{2,17},{3,16},{4,23},{5,22},{6,21},{7,20},{8,27},{9,... | collective-permute-start | bytes 786440 | tf_op jit(solution)/shard_map/ppermute | solution.py:441
  59.8 25.4 %collective-permute-start.5 = (bf16[2,128,512]{2,1,0:T(8,128)(2,1)}, bf16[2,128,512]{2,1,0:T(8,128)(2,1)S(1)}, u32[]{:S(2)}, u32[]{:S(2)}) collective-permute-start(bf16[2,128,512]{2,1,0:T(8,128)(2,1)} %get-tuple-element.51), channel_id=1, source_target_pairs={{0,2},{1,3},{2,0},{3,1},{4,6},{5,7},{6,4},{7,5},{8,10},{9,11},{10,... | collective-permute-start | bytes 786440 | tf_op jit(solution)/shard_map/ppermute | solution.py:441
  61.2 62.3 %collective-permute-start = (bf16[2,128,512]{2,1,0:T(8,128)(2,1)S(1)}, bf16[2,128,512]{2,1,0:T(8,128)(2,1)S(1)}, u32[]{:S(2)}, u32[]{:S(2)}) collective-permute-start(bf16[2,128,512]{2,1,0:T(8,128)(2,1)S(1)} %copy-done.7), channel_id=1, source_target_pairs={{0,16},{1,17},{2,18},{3,19},{4,20},{5,21},{6,22},{7,23},{8,24},{9,... | collective-permute-start | bytes 786440 | tf_op jit(solution)/shard_map/ppermute | solution.py:441
  71.0 32.6 %collective-permute-start.6 = (bf16[2,128,512]{2,1,0:T(8,128)(2,1)}, bf16[2,128,512]{2,1,0:T(8,128)(2,1)S(1)}, u32[]{:S(2)}, u32[]{:S(2)}) collective-permute-start(bf16[2,128,512]{2,1,0:T(8,128)(2,1)} %get-tuple-element.52), channel_id=1, source_target_pairs={{0,20},{1,21},{2,22},{3,23},{4,16},{5,17},{6,18},{7,19},{8,28},{9,... | collective-permute-start | bytes 786440 | tf_op jit(solution)/shard_map/ppermute | solution.py:441
  71.6 32.0 %collective-permute-start.7 = (bf16[2,128,512]{2,1,0:T(8,128)(2,1)}, bf16[2,128,512]{2,1,0:T(8,128)(2,1)}, u32[]{:S(2)}, u32[]{:S(2)}) collective-permute-start(bf16[2,128,512]{2,1,0:T(8,128)(2,1)} %get-tuple-element.53), channel_id=1, source_target_pairs={{0,3},{1,2},{2,1},{3,0},{4,7},{5,6},{6,5},{7,4},{8,11},{9,10},{10,... | collective-permute-start | bytes 786440 | tf_op jit(solution)/shard_map/ppermute | solution.py:441
  85.2 33.7 %collective-permute-start.8 = (bf16[2,128,512]{2,1,0:T(8,128)(2,1)}, bf16[2,128,512]{2,1,0:T(8,128)(2,1)}, u32[]{:S(2)}, u32[]{:S(2)}) collective-permute-start(bf16[2,128,512]{2,1,0:T(8,128)(2,1)} %get-tuple-element.54), channel_id=1, source_target_pairs={{0,21},{1,20},{2,23},{3,22},{4,17},{5,16},{6,19},{7,18},{8,29},{9,... | collective-permute-start | bytes 786440 | tf_op jit(solution)/shard_map/ppermute | solution.py:441
  85.2 38.2 %collective-permute-start.9 = (bf16[2,128,512]{2,1,0:T(8,128)(2,1)}, bf16[2,128,512]{2,1,0:T(8,128)(2,1)}, u32[]{:S(2)}, u32[]{:S(2)}) collective-permute-start(bf16[2,128,512]{2,1,0:T(8,128)(2,1)} %get-tuple-element.55), channel_id=1, source_target_pairs={{0,4},{1,5},{2,6},{3,7},{4,0},{5,1},{6,2},{7,3},{8,12},{9,13},{10,... | collective-permute-start | bytes 786440 | tf_op jit(solution)/shard_map/ppermute | solution.py:441
  91.0 74.2 %copy-start.1 = (bf16[2,65,128,128]{3,2,1,0:T(8,128)(2,1)}, bf16[2,65,128,128]{3,2,1,0:T(8,128)(2,1)S(1)}, u32[]{:S(2)}) copy-start(bf16[2,65,128,128]{3,2,1,0:T(8,128)(2,1)S(1)} %concatenate.3.tiles_ref) | copy-start | bytes 12779524
  103.6 36.2 %collective-permute-start.1 = (bf16[2,128,512]{2,1,0:T(8,128)(2,1)S(1)}, bf16[2,128,512]{2,1,0:T(8,128)(2,1)S(1)}, u32[]{:S(2)}, u32[]{:S(2)}) collective-permute-start(bf16[2,128,512]{2,1,0:T(8,128)(2,1)S(1)} %copy-done.31), channel_id=1, source_target_pairs={{0,17},{1,16},{2,19},{3,18},{4,21},{5,20},{6,23},{7,22},{8,25},{9,... | collective-permute-start | bytes 786440 | tf_op jit(solution)/shard_map/ppermute | solution.py:441
  103.6 39.4 %collective-permute-start.2 = (bf16[2,128,512]{2,1,0:T(8,128)(2,1)S(1)}, bf16[2,128,512]{2,1,0:T(8,128)(2,1)S(1)}, u32[]{:S(2)}, u32[]{:S(2)}) collective-permute-start(bf16[2,128,512]{2,1,0:T(8,128)(2,1)S(1)} %copy-done.29), channel_id=1, source_target_pairs={{0,18},{1,19},{2,16},{3,17},{4,22},{5,23},{6,20},{7,21},{8,26},{9,... | collective-permute-start | bytes 786440 | tf_op jit(solution)/shard_map/ppermute | solution.py:441
  119.0 32.8 %collective-permute-start.18 = (bf16[2,128,512]{2,1,0:T(8,128)(2,1)S(1)}, bf16[2,128,512]{2,1,0:T(8,128)(2,1)S(1)}, u32[]{:S(2)}, u32[]{:S(2)}) collective-permute-start(bf16[2,128,512]{2,1,0:T(8,128)(2,1)S(1)} %copy-done.32), channel_id=1, source_target_pairs={{0,26},{1,27},{2,24},{3,25},{4,30},{5,31},{6,28},{7,29},{8,18},{9,... | collective-permute-start | bytes 786440 | tf_op jit(solution)/shard_map/ppermute | solution.py:441
  123.4 29.2 %collective-permute-start.19 = (bf16[2,128,512]{2,1,0:T(8,128)(2,1)S(1)}, bf16[2,128,512]{2,1,0:T(8,128)(2,1)S(1)}, u32[]{:S(2)}, u32[]{:S(2)}) collective-permute-start(bf16[2,128,512]{2,1,0:T(8,128)(2,1)S(1)} %copy-done.30), channel_id=1, source_target_pairs={{0,9},{1,8},{2,11},{3,10},{4,13},{5,12},{6,15},{7,14},{8,1},{9,0},... | collective-permute-start | bytes 786440 | tf_op jit(solution)/shard_map/ppermute | solution.py:441
  123.5 32.3 %collective-permute-start.20 = (bf16[2,128,512]{2,1,0:T(8,128)(2,1)S(1)}, bf16[2,128,512]{2,1,0:T(8,128)(2,1)S(1)}, u32[]{:S(2)}, u32[]{:S(2)}) collective-permute-start(bf16[2,128,512]{2,1,0:T(8,128)(2,1)S(1)} %copy-done.27), channel_id=1, source_target_pairs={{0,27},{1,26},{2,25},{3,24},{4,31},{5,30},{6,29},{7,28},{8,19},{9,... | collective-permute-start | bytes 786440 | tf_op jit(solution)/shard_map/ppermute | solution.py:441
  124.9 40.2 %copy-start.3 = (bf16[4096,512]{1,0:T(8,128)(2,1)S(1)}, bf16[4096,512]{1,0:T(8,128)(2,1)}, u32[]{:S(2)}) copy-start(bf16[4096,512]{1,0:T(8,128)(2,1)} %param.7) | copy-start | bytes 12582916
  139.9 52.6 %copy-start.42 = (bf16[2,128,512]{2,1,0:T(8,128)(2,1)}, bf16[2,128,512]{2,1,0:T(8,128)(2,1)S(1)}, u32[]{:S(2)}) copy-start(bf16[2,128,512]{2,1,0:T(8,128)(2,1)S(1)} %collective-permute-done.1.rest_1_) | copy-start | bytes 786436
  139.9 61.8 %collective-permute-start.21 = (bf16[2,128,512]{2,1,0:T(8,128)(2,1)S(1)}, bf16[2,128,512]{2,1,0:T(8,128)(2,1)S(1)}, u32[]{:S(2)}, u32[]{:S(2)}) collective-permute-start(bf16[2,128,512]{2,1,0:T(8,128)(2,1)S(1)} %copy-done.26), channel_id=1, source_target_pairs={{0,10},{1,11},{2,8},{3,9},{4,14},{5,15},{6,12},{7,13},{8,2},{9,3},... | collective-permute-start | bytes 786440 | tf_op jit(solution)/shard_map/ppermute | solution.py:441
  143.1 58.8 %collective-permute-start.22 = (bf16[2,128,512]{2,1,0:T(8,128)(2,1)S(1)}, bf16[2,128,512]{2,1,0:T(8,128)(2,1)S(1)}, u32[]{:S(2)}, u32[]{:S(2)}) collective-permute-start(bf16[2,128,512]{2,1,0:T(8,128)(2,1)S(1)} %copy-done.25), channel_id=1, source_target_pairs={{0,28},{1,29},{2,30},{3,31},{4,24},{5,25},{6,26},{7,27},{8,20},{9,... | collective-permute-start | bytes 786440 | tf_op jit(solution)/shard_map/ppermute | solution.py:441
  151.8 40.7 %copy-start.40 = (bf16[2,128,512]{2,1,0:T(8,128)(2,1)}, bf16[2,128,512]{2,1,0:T(8,128)(2,1)S(1)}, u32[]{:S(2)}) copy-start(bf16[2,128,512]{2,1,0:T(8,128)(2,1)S(1)} %collective-permute-done.18.rest_0_) | copy-start | bytes 786436
  151.8 56.5 %collective-permute-start.23 = (bf16[2,128,512]{2,1,0:T(8,128)(2,1)S(1)}, bf16[2,128,512]{2,1,0:T(8,128)(2,1)}, u32[]{:S(2)}, u32[]{:S(2)}) collective-permute-start(bf16[2,128,512]{2,1,0:T(8,128)(2,1)S(1)} %copy-done.24), channel_id=1, source_target_pairs={{0,11},{1,10},{2,9},{3,8},{4,15},{5,14},{6,13},{7,12},{8,3},{9,2},... | collective-permute-start | bytes 786440 | tf_op jit(solution)/shard_map/ppermute | solution.py:441
  152.6 58.5 %collective-permute-start.24 = (bf16[2,128,512]{2,1,0:T(8,128)(2,1)S(1)}, bf16[2,128,512]{2,1,0:T(8,128)(2,1)}, u32[]{:S(2)}, u32[]{:S(2)}) collective-permute-start(bf16[2,128,512]{2,1,0:T(8,128)(2,1)S(1)} %copy-done.21), channel_id=1, source_target_pairs={{0,29},{1,28},{2,31},{3,30},{4,25},{5,24},{6,27},{7,26},{8,21},{9,... | collective-permute-start | bytes 786440 | tf_op jit(solution)/shard_map/ppermute | solution.py:441
  155.8 57.7 %collective-permute-start.25 = (bf16[2,128,512]{2,1,0:T(8,128)(2,1)S(1)}, bf16[2,128,512]{2,1,0:T(8,128)(2,1)}, u32[]{:S(2)}, u32[]{:S(2)}) collective-permute-start(bf16[2,128,512]{2,1,0:T(8,128)(2,1)S(1)} %copy-done.17), channel_id=1, source_target_pairs={{0,12},{1,13},{2,14},{3,15},{4,8},{5,9},{6,10},{7,11},{8,4},{9,5},... | collective-permute-start | bytes 786440 | tf_op jit(solution)/shard_map/ppermute | solution.py:441
  201.7 39.5 %collective-permute-start.26 = (bf16[2,128,512]{2,1,0:T(8,128)(2,1)S(1)}, bf16[2,128,512]{2,1,0:T(8,128)(2,1)S(1)}, u32[]{:S(2)}, u32[]{:S(2)}) collective-permute-start(bf16[2,128,512]{2,1,0:T(8,128)(2,1)S(1)} %copy-done.16), channel_id=1, source_target_pairs={{0,30},{1,31},{2,28},{3,29},{4,26},{5,27},{6,24},{7,25},{8,22},{9,... | collective-permute-start | bytes 786440 | tf_op jit(solution)/shard_map/ppermute | solution.py:441
  201.8 39.4 %collective-permute-start.27 = (bf16[2,128,512]{2,1,0:T(8,128)(2,1)S(1)}, bf16[2,128,512]{2,1,0:T(8,128)(2,1)S(1)}, u32[]{:S(2)}, u32[]{:S(2)}) collective-permute-start(bf16[2,128,512]{2,1,0:T(8,128)(2,1)S(1)} %copy-done.15), channel_id=1, source_target_pairs={{0,13},{1,12},{2,15},{3,14},{4,9},{5,8},{6,11},{7,10},{8,5},{9,4},... | collective-permute-start | bytes 786440 | tf_op jit(solution)/shard_map/ppermute | solution.py:441
  208.3 33.0 %collective-permute-start.28 = (bf16[2,128,512]{2,1,0:T(8,128)(2,1)S(1)}, bf16[2,128,512]{2,1,0:T(8,128)(2,1)S(1)}, u32[]{:S(2)}, u32[]{:S(2)}) collective-permute-start(bf16[2,128,512]{2,1,0:T(8,128)(2,1)S(1)} %copy-done.14), channel_id=1, source_target_pairs={{0,31},{1,30},{2,29},{3,28},{4,27},{5,26},{6,25},{7,24},{8,23},{9,... | collective-permute-start | bytes 786440 | tf_op jit(solution)/shard_map/ppermute | solution.py:441
  211.2 30.2 %collective-permute-start.29 = (bf16[2,128,512]{2,1,0:T(8,128)(2,1)S(1)}, bf16[2,128,512]{2,1,0:T(8,128)(2,1)S(1)}, u32[]{:S(2)}, u32[]{:S(2)}) collective-permute-start(bf16[2,128,512]{2,1,0:T(8,128)(2,1)S(1)} %copy-done.13), channel_id=1, source_target_pairs={{0,14},{1,15},{2,12},{3,13},{4,10},{5,11},{6,8},{7,9},{8,6},{9,7},... | collective-permute-start | bytes 786440 | tf_op jit(solution)/shard_map/ppermute | solution.py:441
  213.5 27.8 %collective-permute-start.30 = (bf16[2,128,512]{2,1,0:T(8,128)(2,1)S(1)}, bf16[2,128,512]{2,1,0:T(8,128)(2,1)S(1)}, u32[]{:S(2)}, u32[]{:S(2)}) collective-permute-start(bf16[2,128,512]{2,1,0:T(8,128)(2,1)S(1)} %copy-done.12), channel_id=1, source_target_pairs={{0,15},{1,14},{2,13},{3,12},{4,11},{5,10},{6,9},{7,8},{8,7},{9,6},... | collective-permute-start | bytes 786440 | tf_op jit(solution)/shard_map/ppermute | solution.py:441
  248.9 3.4 %collective-permute-start.31 = (f32[4,4,16,1024]{3,2,1,0:T(8,128)S(1)}, f32[4,4,16,1024]{3,2,1,0:T(8,128)S(1)}, u32[]{:S(2)}, u32[]{:S(2)}) collective-permute-start(f32[4,4,16,1024]{3,2,1,0:T(8,128)S(1)} %get-tuple-element.78), channel_id=1, source_target_pairs={{0,1},{1,0},{2,3},{3,2},{4,5},{5,4},{6,7},{7,6},{8,9},{9,8},{10,11... | collective-permute-start | bytes 3145736 | tf_op jit(solution)/shard_map/ppermute | solution.py:441
  252.4 9.2 %collective-permute-start.32 = (bf16[4,16,1024]{2,1,0:T(8,128)(2,1)S(1)}, bf16[4,16,1024]{2,1,0:T(8,128)(2,1)S(1)}, u32[]{:S(2)}, u32[]{:S(2)}) collective-permute-start(bf16[4,16,1024]{2,1,0:T(8,128)(2,1)S(1)} %get-tuple-element.80), channel_id=1, source_target_pairs={{0,2},{1,3},{2,0},{3,1},{4,6},{5,7},{6,4},{7,5},{8,10},{9,11},{10,... | collective-permute-start | bytes 393224 | tf_op jit(solution)/shard_map/ppermute | solution.py:441
  255.9 10.3 %collective-permute-start.33 = (bf16[4,16,1024]{2,1,0:T(8,128)(2,1)S(1)}, bf16[4,16,1024]{2,1,0:T(8,128)(2,1)S(1)}, u32[]{:S(2)}, u32[]{:S(2)}) collective-permute-start(bf16[4,16,1024]{2,1,0:T(8,128)(2,1)S(1)} %get-tuple-element.81), channel_id=1, source_target_pairs={{0,4},{1,5},{2,6},{3,7},{4,0},{5,1},{6,2},{7,3},{8,12},{9,13},{10,... | collective-permute-start | bytes 393224 | tf_op jit(solution)/shard_map/ppermute | solution.py:441
  260.1 7.9 %collective-permute-start.34 = (bf16[4,16,1024]{2,1,0:T(8,128)(2,1)S(1)}, bf16[4,16,1024]{2,1,0:T(8,128)(2,1)S(1)}, u32[]{:S(2)}, u32[]{:S(2)}) collective-permute-start(bf16[4,16,1024]{2,1,0:T(8,128)(2,1)S(1)} %get-tuple-element.82), channel_id=1, source_target_pairs={{0,6},{1,7},{2,4},{3,5},{4,2},{5,3},{6,0},{7,1},{8,14},{9,15},{10,... | collective-permute-start | bytes 393224 | tf_op jit(solution)/shard_map/ppermute | solution.py:441
  268.1 5.2 %collective-permute-start.35 = (f32[16,1024]{1,0:T(8,128)S(1)}, f32[16,1024]{1,0:T(8,128)S(1)}, u32[]{:S(2)}, u32[]{:S(2)}) collective-permute-start(f32[16,1024]{1,0:T(8,128)S(1)} %get-tuple-element.84), channel_id=1, source_target_pairs={{0,8},{1,9},{2,10},{3,11},{4,12},{5,13},{6,14},{7,15},{8,0},{9,1},... | collective-permute-start | bytes 196616 | tf_op jit(solution)/shard_map/ppermute | solution.py:441
  268.6 8.7 %collective-permute-start.36 = (f32[16,1024]{1,0:T(8,128)S(1)}, f32[16,1024]{1,0:T(8,128)S(1)}, u32[]{:S(2)}, u32[]{:S(2)}) collective-permute-start(f32[16,1024]{1,0:T(8,128)S(1)} %get-tuple-element.85), channel_id=1, source_target_pairs={{0,16},{1,17},{2,18},{3,19},{4,20},{5,21},{6,22},{7,23},{8,24},{9,... | collective-permute-start | bytes 196616 | tf_op jit(solution)/shard_map/ppermute | solution.py:441
  272.5 6.2 %collective-permute-start.37 = (f32[16,1024]{1,0:T(8,128)S(1)}, f32[16,1024]{1,0:T(8,128)S(1)}, u32[]{:S(2)}, u32[]{:S(2)}) collective-permute-start(f32[16,1024]{1,0:T(8,128)S(1)} %get-tuple-element.86), channel_id=1, source_target_pairs={{0,24},{1,25},{2,26},{3,27},{4,28},{5,29},{6,30},{7,31},{8,16},{9,... | collective-permute-start | bytes 196616 | tf_op jit(solution)/shard_map/ppermute | solution.py:441
  (42 other events, 816.8 us)

commit v3 on v2

--- a/solution.py
+++ b/solution.py
@@ -48,6 +48,33 @@
 
 def whole(shape, space=VMEM):
     return pl.BlockSpec(shape, lambda *_: (0,) * len(shape), memory_space=space)
+
+
+def first_kernel(masks, rank_ref, send_ref, blocks_ref, *rest):
+    outs, sems = rest[: len(masks)], rest[len(masks)]
+    cap = send_ref.shape[0]
+    copies = []
+    for n, mask in enumerate(masks):
+        for c in range(cap):
+            block = jnp.maximum(send_ref[c, rank_ref[0] ^ mask], 0)
+            copy = pltpu.make_async_copy(blocks_ref.at[block], outs[n].at[c], sems.at[n * cap + c])
+            copy.start()
+            copies.append(copy)
+    for copy in copies:
+        copy.wait()
+
+
+def first_pack(rank, send, blocks, masks):
+    cap = send.shape[0]
+    return pl.pallas_call(
+        functools.partial(first_kernel, masks),
+        out_shape=[VMEM((cap,) + blocks.shape[1:], BF16)] * len(masks),
+        in_specs=[pl.BlockSpec(memory_space=SMEM)] * 2 + [pl.BlockSpec(memory_space=HBM)],
+        out_specs=[pl.BlockSpec(memory_space=VMEM)] * len(masks),
+        scratch_shapes=[pltpu.SemaphoreType.DMA((len(masks) * cap,))],
+        compiler_params=pltpu.CompilerParams(vmem_limit_bytes=ROOM),
+        name="first_pack",
+    )(rank, send, in_hbm(blocks))
 
 
 def pack_kernel(masks, after, rank_ref, send_ref, blocks_ref, *rest):
@@ -85,8 +112,9 @@
             pltpu.SemaphoreType.DMA((count,)),
             pltpu.SemaphoreType.DMA((count,)),
         ],
+        compiler_params=pltpu.CompilerParams(vmem_limit_bytes=ROOM + 2 * count * blocks[0].size),
         name="pack",
-    )(rank, send, blocks, *after)
+    )(rank, send, in_hbm(blocks), *after)
 
 
 def slot_lists(rank, send, source, tile, local, order, starts, spare):
@@ -200,7 +228,8 @@
     )(lists, counts, tiles, pool)
 
 
-def adjoint_kernel(phase, slots, count, lists_ref, counts_ref, tiles_ref, left_ref, out_ref, sum_ref):
+def adjoint_kernel(phase, slots, count, lists_ref, counts_ref, tiles_ref, left_ref, *rest):
+    outs, sum_ref = rest[:-1], rest[-1]
     local, rows = left_ref.shape[:2]
     for s in range(2 * count):
         sum_ref[s] = jnp.zeros_like(sum_ref[s])
@@ -223,21 +252,27 @@
         return lax.fori_loop(0, (counts_ref[phase, block] + 1) // 2, two, carry)
 
     lax.fori_loop(0, 2 * local, one_block, 0)
-    for d in range(2):
-        for s in range(count):
-            out_ref[d, :, s * rows:(s + 1) * rows] = sum_ref[d * count + s].astype(BF16).T
-
-
-def adjoint(phase, lists, counts, tiles, left, count):
+    first = 0
+    for out_ref in outs:
+        size = out_ref.shape[2] // rows
+        for d in range(2):
+            for s in range(size):
+                value = sum_ref[d * count + first + s]
+                out_ref[d, :, s * rows:(s + 1) * rows] = value.astype(BF16).T
+        first += size
+
+
+def adjoint(phase, lists, counts, tiles, left, sizes):
+    count = sum(sizes)
     slots = lists.shape[1] // counts.shape[1]
     rows, vectors = left.shape[1:]
     block = pl.BlockSpec(memory_space=VMEM)
     size = 2 * count * rows * vectors
     return pl.pallas_call(
         functools.partial(adjoint_kernel, phase, slots, count),
-        out_shape=jax.ShapeDtypeStruct((2, vectors, count * rows), BF16),
+        out_shape=[jax.ShapeDtypeStruct((2, vectors, n * rows), BF16) for n in sizes],
         in_specs=[pl.BlockSpec(memory_space=SMEM)] * 2 + [block] * 2,
-        out_specs=block,
+        out_specs=[block] * len(sizes),
         scratch_shapes=[VMEM((2 * count, rows, vectors), F32)],
         compiler_params=pltpu.CompilerParams(vmem_limit_bytes=ROOM + 6 * size + 2 * left.size),
         cost_estimate=pl.CostEstimate(flops=8 * 10**9, bytes_accessed=16 * 2**20, transcendentals=0),
@@ -246,8 +281,9 @@
 
 
 def gram_kernel(
-    phase, count, slots, fixed, more, lists_ref, counts_ref, tiles_ref, in_ref, left_ref, *rest
+    phase, count, slots, fixed, more, final, lists_ref, counts_ref, tiles_ref, in_ref, left_ref, *rest
 ):
+    whole_sum = not more and phase + 1 == final
     arrivals, (sum_ref, pool_ref, held_ref, high_ref, low_ref, in_sems, sems) = rest[:count], rest[count:]
     steps, rows, vectors = held_ref.shape
     per = steps // 2
@@ -295,7 +331,9 @@
             high = value.astype(BF16)
             spot = (pl.ds(g * rows, rows), pl.ds(d * vectors, vectors))
             high_ref[spot] = high
-            low_ref[spot] = (value - high.astype(F32)).astype(BF16)
+            low = (value - high.astype(F32)).astype(BF16)
+            open_block = counts_ref[final, block] > 0 if whole_sum else True
+            low_ref[spot] = jnp.where(open_block, low, jnp.zeros_like(low))
         sum_ref[...] += jnp.dot(left_ref[step], high_ref[...], preferred_element_type=F32)
         sum_ref[...] += jnp.dot(left_ref[step], low_ref[...], preferred_element_type=F32)
         return carry
@@ -314,7 +352,7 @@
     dma = pltpu.SemaphoreType.DMA
     room = 2 * ROOM + 4 * steps * rows * vectors + sum(2 * a.size for a in arrivals)
     return pl.pallas_call(
-        functools.partial(gram_kernel, phase, len(arrivals), slots, fixed, more),
+        functools.partial(gram_kernel, phase, len(arrivals), slots, fixed, more, counts.shape[0] - 1),
         out_shape=jax.ShapeDtypeStruct((columns, 2 * vectors), F32),
         in_specs=[pl.BlockSpec(memory_space=SMEM)] * 2
         + [block, block if more else pl.BlockSpec(memory_space=HBM), block]
@@ -360,13 +398,13 @@
         ].astype(send_ref.dtype)
 
 
-def late(rank, sums, adjoint, arrivals, devices, sent):
+def late(rank, sums, adjoint, arrivals, devices, sent, last):
     columns, both = sums.shape
     own = columns // devices
     cap, rows, vectors = arrivals[0].shape
     block = pl.BlockSpec(memory_space=VMEM)
-    if own % 8:
-        halves = [jax.ShapeDtypeStruct(sums.shape, F32)]
+    if not last or own % 8:
+        halves = [VMEM(sums.shape, F32)]
     else:
         half = (devices // 8, 4, own, both)
         halves = [VMEM(half, sent), VMEM(half, F32)]
@@ -455,8 +493,8 @@
     send = send_blocks.T
 
     early = min(EARLY, len(order))
-    packed = pack(rank, send, blocks, order[:early])
-    packed += pack(rank, send, blocks, order[early:], packed[:1])
+    packed = first_pack(rank, send, blocks, order[:early])
+    packed += pack(rank, send, blocks, order[early:])
     arrived = []
     for n, mask in enumerate(order):
         arrived.append(swap(packed[n], mask, devices))
@@ -471,12 +509,16 @@
     tiles = in_vmem(tiles)
     sums = hops(lists, counts, tiles, blocks, 4)
     start, stop = groups[-1]
+    cut = stop - (stop - start) * 2 // 5
+    cap = send.shape[0]
     met = adjoint(
-        len(groups), lists, counts, tiles, left.reshape(blocks.shape), (stop - start) * send.shape[0]
+        len(groups), lists, counts, tiles, left.reshape(blocks.shape),
+        [(cut - start) * cap, (stop - cut) * cap],
     )
     for n, (first, last) in enumerate(groups[:-1]):
         sums = gram(n + 1, lists, counts, tiles, sums, left_t, arrived[first:last], 3)
-    sums = late(rank, sums, met, arrived[start:stop], devices, F32)
+    sums, = late(rank, sums, met[0], arrived[start:cut], devices, F32, False)
+    sums = late(rank, sums, met[1], arrived[cut:stop], devices, F32, True)
     if len(sums) == 1:
         mine = lax.psum_scatter(sums[0] * scale, "rows", scatter_dimension=0, tiled=True)
         return mine.reshape(mine.shape[0], 2, vectors).transpose(1, 0, 2)

time: 280 us -> 274 us (0.979)
  starting transfers between devices: 101 us -> 80.4 us
  local copies, waits for them, and re-layouts: 19.6 us -> 28.3 us
  waiting for transfers between devices: 71.7 us -> 75.2 us
  Pallas kernels: 84.2 us -> 87.2 us
    ppermute x38, starting transfers between devices: 101 us -> 80.4 us  [swap(): return lax.ppermute(value, 'rows', [(i, i ^ mask) for i in range(devices)])]
    unnamed x105 -> x93, local copies, waits for them, and re-layouts: 8.93 us -> 17.8 us
    ppermute x38, waiting for transfers between devices: 71.7 us -> 75.2 us  [swap(): return lax.ppermute(value, 'rows', [(i, i ^ mask) for i in range(devices)])]
    pallas_call x1 -> x2, Pallas kernels: 5.9 us -> 7.09 us  [late(): pl.pallas_call(functools.partial(late_kernel, len(arrivals)), out_shape=h...]
    pallas_call x2 -> x1, Pallas kernels: 12.4 us -> 11.5 us  [pack(): pl.pallas_call(functools.partial(pack_kernel, masks, len(after)), out_sha...]
  transfers between devices with their start and end apart: 38 -> 38, of which waited for: 10 -> 13; matrix products, arithmetic and copies ran while one was open for 4% -> 4% of each run, Pallas kernels for 23% -> 26%
where the time goes in v3:
time: 274 us; the launch traced here: 273 us
  Pallas kernels  87.2 us (32%)
  starting transfers between devices  80.4 us (29%)
  waiting for transfers between devices  75.2 us (27%)
  local copies, waits for them, and re-layouts  28.3 us (10%)
    ppermute x38, starting transfers between devices, swap(): return lax.ppermute(value, 'rows', [(i, i ^ mask) for i in range(devices)])  80.4 us
    ppermute x38, waiting for transfers between devices, swap(): return lax.ppermute(value, 'rows', [(i, i ^ mask) for i in range(devices)])  75.2 us
    pallas_call x1, Pallas kernels, adjoint(): pl.pallas_call(functools.partial(adjoint_kernel, phase, slots, count), ou...  27.6 us
    pallas_call x1, Pallas kernels, gram(): pl.pallas_call(functools.partial(gram_kernel, phase, len(arrivals), slots...  22.9 us
    unnamed x93, local copies, waits for them, and re-layouts  17.8 us
    pallas_call x1, Pallas kernels, hops(): pl.pallas_call(functools.partial(hops_kernel, slots, fixed), out_shape=HB...  14.7 us
    pallas_call x1, Pallas kernels, pack(): pl.pallas_call(functools.partial(pack_kernel, masks, len(after)), out_sha...  11.5 us
    pallas_call x2, Pallas kernels, late(): pl.pallas_call(functools.partial(late_kernel, len(arrivals)), out_shape=h...  7.09 us
  transfers between devices with their start and end apart: 38, of which 13 were waited for; matrix products, arithmetic and copies ran while one was open for 4% of the time, Pallas kernels for 26%

profile of v3, /device:TPU:0, one launch (start us, length us, event | category | flops | bytes accessed | tf_op | source)
XLA Modules:
  0.0 273.2 jit_solution(7388163721403428807)
XLA Ops:
  0.8 11.5 %pack.1 = (bf16[2,128,512]{2,1,0:T(8,128)(2,1)S(1)}, bf16[2,128,512]{2,1,0:T(8,128)(2,1)S(1)}, bf16[2,128,512]{2,1,0:T(8,128)(2,1)S(1)}, bf16[2,128,512]{2,1,0:T...) custom-call(s32[1]{0:T(128)} %bitcast.rank_ref, ...), custom_call_target="tpu_custom_call" | custom-call | tf_op jit(solution)/shard_map/pack/pallas_call | solution.py:104
  19.3 5.9 %collective-permute-start.10 = (bf16[2,128,512]{2,1,0:T(8,128)(2,1)}, bf16[2,128,512]{2,1,0:T(8,128)(2,1)}, u32[]{:S(2)}, u32[]{:S(2)}) collective-permute-start(bf16[2,128,512]{2,1,0:T(8,128)(2,1)} %get-tuple-element.58), channel_id=1, source_target_pairs={{0,22},{1,23},{2,20},{3,21},{4,18},{5,19},{6,16},{7,17},{8,30},{9,... | collective-permute-start | bytes 786440 | tf_op jit(solution)/shard_map/ppermute | solution.py:479
  25.2 1.5 collective-permute-start.12
  26.7 1.4 collective-permute-start.13
  28.1 4.0 %collective-permute-start.14 = (bf16[2,128,512]{2,1,0:T(8,128)(2,1)}, bf16[2,128,512]{2,1,0:T(8,128)(2,1)}, u32[]{:S(2)}, u32[]{:S(2)}) collective-permute-start(bf16[2,128,512]{2,1,0:T(8,128)(2,1)} %get-tuple-element.62), channel_id=1, source_target_pairs={{0,24},{1,25},{2,26},{3,27},{4,28},{5,29},{6,30},{7,31},{8,16},{9,... | collective-permute-start | bytes 786440 | tf_op jit(solution)/shard_map/ppermute | solution.py:479
  34.5 15.1 %collective-permute-done.10.rest_10_ = bf16[2,128,512]{2,1,0:T(8,128)(2,1)} collective-permute-done((bf16[2,128,512]{2,1,0:T(8,128)(2,1)}, bf16[2,128,512]{2,1,0:T(8,128)(2,1)}, u32[]{:S(2)}, u32[]{:S(2)}) %collective-permute-start.10) | collective-permute-done | bytes 262176 | tf_op jit(solution)/shard_map/ppermute | solution.py:479
  50.7 4.0 %collective-permute-start.16 = (bf16[2,128,512]{2,1,0:T(8,128)(2,1)}, bf16[2,128,512]{2,1,0:T(8,128)(2,1)}, u32[]{:S(2)}, u32[]{:S(2)}) collective-permute-start(bf16[2,128,512]{2,1,0:T(8,128)(2,1)} %copy-done.19), channel_id=1, source_target_pairs={{0,25},{1,24},{2,27},{3,26},{4,29},{5,28},{6,31},{7,30},{8,17},{9,... | collective-permute-start | bytes 786440 | tf_op jit(solution)/shard_map/ppermute | solution.py:479
  55.1 13.0 %collective-permute-start.4 = (bf16[2,128,512]{2,1,0:T(8,128)(2,1)}, bf16[2,128,512]{2,1,0:T(8,128)(2,1)}, u32[]{:S(2)}, u32[]{:S(2)}) collective-permute-start(bf16[2,128,512]{2,1,0:T(8,128)(2,1)} %copy-done.16), channel_id=1, source_target_pairs={{0,19},{1,18},{2,17},{3,16},{4,23},{5,22},{6,21},{7,20},{8,27},{9,... | collective-permute-start | bytes 786440 | tf_op jit(solution)/shard_map/ppermute | solution.py:479
  68.1 1.2 collective-permute-start.5
  69.4 2.6 first_pack.1
  73.0 3.2 %concatenate.3.tiles_ref = bf16[2,65,128,128]{3,2,1,0:T(8,128)(2,1)S(1)} pad(bf16[2,64,128,128]{3,2,1,0:T(8,128)(2,1)} %param.9, bf16[]{:T(256)} %constant.66.clone.1), padding=0_0x0_1x0_0x0_0 | pad | bytes 8454146 | tf_op jit(solution)/shard_map/concatenate | solution.py:506
  76.3 3.0 %collective-permute-start.6 = (bf16[2,128,512]{2,1,0:T(8,128)(2,1)S(1)}, bf16[2,128,512]{2,1,0:T(8,128)(2,1)S(1)}, u32[]{:S(2)}, u32[]{:S(2)}) collective-permute-start(bf16[2,128,512]{2,1,0:T(8,128)(2,1)S(1)} %copy-done.14), channel_id=1, source_target_pairs={{0,20},{1,21},{2,22},{3,23},{4,16},{5,17},{6,18},{7,19},{8,28},{9,... | collective-permute-start | bytes 786440 | tf_op jit(solution)/shard_map/ppermute | solution.py:479
  79.4 1.3 collective-permute-start.8
  80.8 12.8 %collective-permute-done.4.rest_4_ = bf16[2,128,512]{2,1,0:T(8,128)(2,1)} collective-permute-done((bf16[2,128,512]{2,1,0:T(8,128)(2,1)}, bf16[2,128,512]{2,1,0:T(8,128)(2,1)}, u32[]{:S(2)}, u32[]{:S(2)}) %collective-permute-start.4) | collective-permute-done | bytes 262176 | tf_op jit(solution)/shard_map/ppermute | solution.py:479
  93.6 1.3 collective-permute-start
  94.9 14.7 %hops.1.in_ref = f32[64,128,512]{2,1,0:T(8,128)} custom-call(s32[3,1024]{1,0:T(4,128)S(1)} %add.78.lists_ref, s32[3,64]{1,0:T(4,128)S(1)} %get-tuple-element.91.counts_ref, bf16[2,65,128,128]{3,2,1,0:T(8,128)(2,1)S(1)} %concatenate.3.tiles_ref, bf16[32,128,512]{2,1,0:T(8,128)(2,1)S(1)} %bitcast.16), custom_call_target="tpu_custom_call" | custom-call | flops 8000000000 | bytes 41943040 | tf_op jit(solution)/shard_map/hops/pallas_call | solution.py:217
  109.6 1.9 collective-permute-start.1
  111.5 2.8 %collective-permute-start.2 = (bf16[2,128,512]{2,1,0:T(8,128)(2,1)}, bf16[2,128,512]{2,1,0:T(8,128)(2,1)}, u32[]{:S(2)}, u32[]{:S(2)}) collective-permute-start(bf16[2,128,512]{2,1,0:T(8,128)(2,1)} %get-tuple-element.50), channel_id=1, source_target_pairs={{0,18},{1,19},{2,16},{3,17},{4,22},{5,23},{6,20},{7,21},{8,26},{9,... | collective-permute-start | bytes 786440 | tf_op jit(solution)/shard_map/ppermute | solution.py:479
  114.3 4.3 %collective-permute-start.18 = (bf16[2,128,512]{2,1,0:T(8,128)(2,1)S(1)}, bf16[2,128,512]{2,1,0:T(8,128)(2,1)}, u32[]{:S(2)}, u32[]{:S(2)}) collective-permute-start(bf16[2,128,512]{2,1,0:T(8,128)(2,1)S(1)} %get-tuple-element.67), channel_id=1, source_target_pairs={{0,26},{1,27},{2,24},{3,25},{4,30},{5,31},{6,28},{7,29},{8,18},{9,... | collective-permute-start | bytes 786440 | tf_op jit(solution)/shard_map/ppermute | solution.py:479
  118.6 15.4 %collective-permute-done.rest_0_ = bf16[2,128,512]{2,1,0:T(8,128)(2,1)S(1)} collective-permute-done((bf16[2,128,512]{2,1,0:T(8,128)(2,1)S(1)}, bf16[2,128,512]{2,1,0:T(8,128)(2,1)S(1)}, u32[]{:S(2)}, u32[]{:S(2)}) %collective-permute-start) | collective-permute-done | bytes 262176 | tf_op jit(solution)/shard_map/ppermute | solution.py:479
  134.0 2.0 collective-permute-start.20
  136.0 27.6 %adjoint.1 = (bf16[2,512,2048]{2,1,0:T(8,128)(2,1)S(1)}, bf16[2,512,1280]{2,1,0:T(8,128)(2,1)S(1)}) custom-call(s32[3,1024]{1,0:T(4,128)S(1)} %add.78.lists_ref, s32[3,64]{1,0:T(4,128)S(1)} %get-tuple-element.91.counts_ref, bf16[2,65,128,128]{3,2,1,0:T(8,128)(2,1)S(1)} %concatenate.3.tiles_ref, bf16[32,128,512]{2,1,0:T(8,128)(2,1)S(1)} %bitcast.18), custom_call_target="tpu_custom_call" | custom-call | flops 8000000000 | bytes 16777216 | tf_op jit(solution)/shard_map/adjoint/pallas_call | solution.py:271
  163.6 2.0 copy-done.23
  165.6 1.5 copy-done.25
  167.1 6.3 %copy.20 = bf16[4,1024,512]{1,2,0:T(8,128)(2,1)} copy(bf16[4,1024,512]{2,1,0:T(8,128)(2,1)} %bitcast.17) | data formatting | bytes 8388608 | tf_op jit(solution)/shard_map/reshape | solution.py:508
  173.3 6.1 %collective-permute-start.22 = (bf16[2,128,512]{2,1,0:T(8,128)(2,1)S(1)}, bf16[2,128,512]{2,1,0:T(8,128)(2,1)S(1)}, u32[]{:S(2)}, u32[]{:S(2)}) collective-permute-start(bf16[2,128,512]{2,1,0:T(8,128)(2,1)S(1)} %get-tuple-element.71), channel_id=1, source_target_pairs={{0,28},{1,29},{2,30},{3,31},{4,24},{5,25},{6,26},{7,27},{8,20},{9,... | collective-permute-start | bytes 786440 | tf_op jit(solution)/shard_map/ppermute | solution.py:479
  179.5 3.1 %collective-permute-start.24 = (bf16[2,128,512]{2,1,0:T(8,128)(2,1)S(1)}, bf16[2,128,512]{2,1,0:T(8,128)(2,1)S(1)}, u32[]{:S(2)}, u32[]{:S(2)}) collective-permute-start(bf16[2,128,512]{2,1,0:T(8,128)(2,1)S(1)} %get-tuple-element.73), channel_id=1, source_target_pairs={{0,29},{1,28},{2,31},{3,30},{4,25},{5,24},{6,27},{7,26},{8,21},{9,... | collective-permute-start | bytes 786440 | tf_op jit(solution)/shard_map/ppermute | solution.py:479
  182.6 2.2 copy-done.2
  184.8 2.2 copy-done.4
  187.0 22.9 %gram.1.in_ref = f32[512,1024]{1,0:T(8,128)S(1)} custom-call(s32[3,1024]{1,0:T(4,128)S(1)} %add.78.lists_ref, s32[3,64]{1,0:T(4,128)S(1)} %get-tuple-element.91.counts_ref, bf16[2,65,128,128]{3,2,1,0:T(8,128)(2,1)S(1)} %copy-done.2, f32[64,128,512]{2,1,0:T(8,128)} %hops.1.in_ref, bf16[4,512,1024]{2,1,0:T(8,128)(2,1)S(1)} %bitcast.19, ...), custom_call_target="tpu_custom_call" | custom-call | flops 12000000000 | bytes 25165824 | tf_op jit(solution)/shard_map/gram/pallas_call | solution.py:354
  209.9 4.8 %collective-permute-start.26 = (bf16[2,128,512]{2,1,0:T(8,128)(2,1)S(1)}, bf16[2,128,512]{2,1,0:T(8,128)(2,1)S(1)}, u32[]{:S(2)}, u32[]{:S(2)}) collective-permute-start(bf16[2,128,512]{2,1,0:T(8,128)(2,1)S(1)} %get-tuple-element.76), channel_id=1, source_target_pairs={{0,30},{1,31},{2,28},{3,29},{4,26},{5,27},{6,24},{7,25},{8,22},{9,... | collective-permute-start | bytes 786440 | tf_op jit(solution)/shard_map/ppermute | solution.py:479
  214.7 1.2 collective-permute-start.27
  215.9 2.4 collective-permute-start.28
  218.2 5.4 %collective-permute-start.29 = (bf16[2,128,512]{2,1,0:T(8,128)(2,1)S(1)}, bf16[2,128,512]{2,1,0:T(8,128)(2,1)S(1)}, u32[]{:S(2)}, u32[]{:S(2)}) collective-permute-start(bf16[2,128,512]{2,1,0:T(8,128)(2,1)S(1)} %get-tuple-element.79), channel_id=1, source_target_pairs={{0,14},{1,15},{2,12},{3,13},{4,10},{5,11},{6,8},{7,9},{8,6},{9,7},... | collective-permute-start | bytes 786440 | tf_op jit(solution)/shard_map/ppermute | solution.py:479
  224.4 4.0 %late.2.in_ref = f32[512,1024]{1,0:T(8,128)S(1)} custom-call(s32[1]{0:T(128)} %bitcast.rank_ref, f32[512,1024]{1,0:T(8,128)S(1)} %gram.1.in_ref, bf16[2,512,2048]{2,1,0:T(8,128)(2,1)S(1)} %copy-done.24, bf16[2,128,512]{2,1,0:T(8,128)(2,1)} %collective-permute-done.18.rest_0_, bf16[2,128,512]{2,1,0:T(8,128)(2,1)} %collective-permute-done.19.rest_1_, ...), custom_call_target="tpu_custom_call" | custom-call | flops 4000000000 | bytes 12582912 | tf_op jit(solution)/shard_map/late/pallas_call | solution.py:411
  228.4 4.9 %collective-permute-done.27.rest_1_ = bf16[2,128,512]{2,1,0:T(8,128)(2,1)S(1)} collective-permute-done((bf16[2,128,512]{2,1,0:T(8,128)(2,1)S(1)}, bf16[2,128,512]{2,1,0:T(8,128)(2,1)S(1)}, u32[]{:S(2)}, u32[]{:S(2)}) %collective-permute-start.27) | collective-permute-done | bytes 262176 | tf_op jit(solution)/shard_map/ppermute | solution.py:479
  234.2 8.7 %collective-permute-done.29.rest_3_ = bf16[2,128,512]{2,1,0:T(8,128)(2,1)S(1)} collective-permute-done((bf16[2,128,512]{2,1,0:T(8,128)(2,1)S(1)}, bf16[2,128,512]{2,1,0:T(8,128)(2,1)S(1)}, u32[]{:S(2)}, u32[]{:S(2)}) %collective-permute-start.29) | collective-permute-done | bytes 262176 | tf_op jit(solution)/shard_map/ppermute | solution.py:479
  242.8 4.2 %collective-permute-done.30.rest_4_ = bf16[2,128,512]{2,1,0:T(8,128)(2,1)S(1)} collective-permute-done((bf16[2,128,512]{2,1,0:T(8,128)(2,1)S(1)}, bf16[2,128,512]{2,1,0:T(8,128)(2,1)S(1)}, u32[]{:S(2)}, u32[]{:S(2)}) %collective-permute-start.30) | collective-permute-done | bytes 262176 | tf_op jit(solution)/shard_map/ppermute | solution.py:479
  247.8 3.0 %late.3 = (f32[4,4,16,1024]{3,2,1,0:T(8,128)S(1)}, f32[4,4,16,1024]{3,2,1,0:T(8,128)S(1)}) custom-call(s32[1]{0:T(128)} %bitcast.rank_ref, f32[512,1024]{1,0:T(8,128)S(1)} %late.2.in_ref, bf16[2,512,1280]{2,1,0:T(8,128)(2,1)S(1)} %copy-done.26, bf16[2,128,512]{2,1,0:T(8,128)(2,1)} %copy-done.41, bf16[2,128,512]{2,1,0:T(8,128)(2,1)} %copy-done.42, ...), custom_call_target="tpu_custom_call" | custom-call | flops 4000000000 | bytes 12582912 | tf_op jit(solution)/shard_map/late/pallas_call | solution.py:411
  250.9 2.6 collective-permute-done.31.rest_0_
  254.6 1.5 collective-permute-start.33
  256.1 1.4 collective-permute-start.34
  257.5 2.6 collective-permute-done.32.rest_0_
  260.1 1.8 collective-permute-done.33.rest_1_
  261.9 1.8 collective-permute-done.34.rest_2_
  263.8 1.6 collective-permute-start.35
  266.1 2.2 collective-permute-start.37
  268.8 3.7 %collective-permute-done.36.rest_1_ = f32[16,1024]{1,0:T(8,128)S(1)} collective-permute-done((f32[16,1024]{1,0:T(8,128)S(1)}, f32[16,1024]{1,0:T(8,128)S(1)}, u32[]{:S(2)}, u32[]{:S(2)}) %collective-permute-start.36) | collective-permute-done | bytes 65568 | tf_op jit(solution)/shard_map/ppermute | solution.py:479
  (152 shorter events, 16.8 us)
Async XLA Ops:
  0.0 32.4 %copy-start.29 = (s32[31]{0:T(128)S(1)}, s32[31]{0:T(128)}, u32[]{:S(2)}) copy-start(s32[31]{0:T(128)} %constant.67.clone) | copy-start | bytes 376
  0.0 32.2 %copy-start.6 = (s32[32,2]{0,1:T(2,128)S(1)}, s32[32,2]{0,1:T(2,128)}, u32[]{:S(2)}) copy-start(s32[32,2]{0,1:T(2,128)} %param.12) | copy-start | bytes 772
  0.8 31.4 %copy-start.27 = (s32[2,32,16]{1,2,0:T(8,128)S(1)}, s32[2,32,16]{1,2,0:T(8,128)}, u32[]{:S(2)}) copy-start(s32[2,32,16]{1,2,0:T(8,128)} %param.11) | copy-start | bytes 12292
  0.8 31.5 %copy-start.28 = (s32[2,32,16]{1,2,0:T(8,128)S(1)}, s32[2,32,16]{1,2,0:T(8,128)}, u32[]{:S(2)}) copy-start(s32[2,32,16]{1,2,0:T(8,128)} %param.10) | copy-start | bytes 12292
  19.3 30.3 %collective-permute-start.10 = (bf16[2,128,512]{2,1,0:T(8,128)(2,1)}, bf16[2,128,512]{2,1,0:T(8,128)(2,1)}, u32[]{:S(2)}, u32[]{:S(2)}) collective-permute-start(bf16[2,128,512]{2,1,0:T(8,128)(2,1)} %get-tuple-element.58), channel_id=1, source_target_pairs={{0,22},{1,23},{2,20},{3,21},{4,18},{5,19},{6,16},{7,17},{8,30},{9,... | collective-permute-start | bytes 786440 | tf_op jit(solution)/shard_map/ppermute | solution.py:479
  25.2 25.4 %collective-permute-start.11 = (bf16[2,128,512]{2,1,0:T(8,128)(2,1)}, bf16[2,128,512]{2,1,0:T(8,128)(2,1)}, u32[]{:S(2)}, u32[]{:S(2)}) collective-permute-start(bf16[2,128,512]{2,1,0:T(8,128)(2,1)} %get-tuple-element.59), channel_id=1, source_target_pairs={{0,5},{1,4},{2,7},{3,6},{4,1},{5,0},{6,3},{7,2},{8,13},{9,12},{10,... | collective-permute-start | bytes 786440 | tf_op jit(solution)/shard_map/ppermute | solution.py:479
  25.2 29.5 %collective-permute-start.12 = (bf16[2,128,512]{2,1,0:T(8,128)(2,1)}, bf16[2,128,512]{2,1,0:T(8,128)(2,1)}, u32[]{:S(2)}, u32[]{:S(2)}) collective-permute-start(bf16[2,128,512]{2,1,0:T(8,128)(2,1)} %get-tuple-element.60), channel_id=1, source_target_pairs={{0,23},{1,22},{2,21},{3,20},{4,19},{5,18},{6,17},{7,16},{8,31},{9,... | collective-permute-start | bytes 786440 | tf_op jit(solution)/shard_map/ppermute | solution.py:479
  26.7 28.4 %collective-permute-start.13 = (bf16[2,128,512]{2,1,0:T(8,128)(2,1)}, bf16[2,128,512]{2,1,0:T(8,128)(2,1)}, u32[]{:S(2)}, u32[]{:S(2)}) collective-permute-start(bf16[2,128,512]{2,1,0:T(8,128)(2,1)} %get-tuple-element.61), channel_id=1, source_target_pairs={{0,6},{1,7},{2,4},{3,5},{4,2},{5,3},{6,0},{7,1},{8,14},{9,15},{10,... | collective-permute-start | bytes 786440 | tf_op jit(solution)/shard_map/ppermute | solution.py:479
  28.1 27.0 %collective-permute-start.14 = (bf16[2,128,512]{2,1,0:T(8,128)(2,1)}, bf16[2,128,512]{2,1,0:T(8,128)(2,1)}, u32[]{:S(2)}, u32[]{:S(2)}) collective-permute-start(bf16[2,128,512]{2,1,0:T(8,128)(2,1)} %get-tuple-element.62), channel_id=1, source_target_pairs={{0,24},{1,25},{2,26},{3,27},{4,28},{5,29},{6,30},{7,31},{8,16},{9,... | collective-permute-start | bytes 786440 | tf_op jit(solution)/shard_map/ppermute | solution.py:479
  49.5 18.6 %collective-permute-start.15 = (bf16[2,128,512]{2,1,0:T(8,128)(2,1)}, bf16[2,128,512]{2,1,0:T(8,128)(2,1)S(1)}, u32[]{:S(2)}, u32[]{:S(2)}) collective-permute-start(bf16[2,128,512]{2,1,0:T(8,128)(2,1)} %copy-done.20), channel_id=1, source_target_pairs={{0,7},{1,6},{2,5},{3,4},{4,3},{5,2},{6,1},{7,0},{8,15},{9,14},{10,... | collective-permute-start | bytes 786440 | tf_op jit(solution)/shard_map/ppermute | solution.py:479
  50.7 25.6 %collective-permute-start.16 = (bf16[2,128,512]{2,1,0:T(8,128)(2,1)}, bf16[2,128,512]{2,1,0:T(8,128)(2,1)}, u32[]{:S(2)}, u32[]{:S(2)}) collective-permute-start(bf16[2,128,512]{2,1,0:T(8,128)(2,1)} %copy-done.19), channel_id=1, source_target_pairs={{0,25},{1,24},{2,27},{3,26},{4,29},{5,28},{6,31},{7,30},{8,17},{9,... | collective-permute-start | bytes 786440 | tf_op jit(solution)/shard_map/ppermute | solution.py:479
  54.7 24.6 %collective-permute-start.17 = (bf16[2,128,512]{2,1,0:T(8,128)(2,1)}, bf16[2,128,512]{2,1,0:T(8,128)(2,1)}, u32[]{:S(2)}, u32[]{:S(2)}) collective-permute-start(bf16[2,128,512]{2,1,0:T(8,128)(2,1)} %copy-done.18), channel_id=1, source_target_pairs={{0,8},{1,9},{2,10},{3,11},{4,12},{5,13},{6,14},{7,15},{8,0},{9,1},... | collective-permute-start | bytes 786440 | tf_op jit(solution)/shard_map/ppermute | solution.py:479
  55.1 24.3 %collective-permute-start.3 = (bf16[2,128,512]{2,1,0:T(8,128)(2,1)}, bf16[2,128,512]{2,1,0:T(8,128)(2,1)}, u32[]{:S(2)}, u32[]{:S(2)}) collective-permute-start(bf16[2,128,512]{2,1,0:T(8,128)(2,1)} %copy-done.17), channel_id=1, source_target_pairs={{0,1},{1,0},{2,3},{3,2},{4,5},{5,4},{6,7},{7,6},{8,9},{9,8},{10,11... | collective-permute-start | bytes 786440 | tf_op jit(solution)/shard_map/ppermute | solution.py:479
  55.1 38.4 %collective-permute-start.4 = (bf16[2,128,512]{2,1,0:T(8,128)(2,1)}, bf16[2,128,512]{2,1,0:T(8,128)(2,1)}, u32[]{:S(2)}, u32[]{:S(2)}) collective-permute-start(bf16[2,128,512]{2,1,0:T(8,128)(2,1)} %copy-done.16), channel_id=1, source_target_pairs={{0,19},{1,18},{2,17},{3,16},{4,23},{5,22},{6,21},{7,20},{8,27},{9,... | collective-permute-start | bytes 786440 | tf_op jit(solution)/shard_map/ppermute | solution.py:479
  68.1 25.5 %collective-permute-start.5 = (bf16[2,128,512]{2,1,0:T(8,128)(2,1)}, bf16[2,128,512]{2,1,0:T(8,128)(2,1)}, u32[]{:S(2)}, u32[]{:S(2)}) collective-permute-start(bf16[2,128,512]{2,1,0:T(8,128)(2,1)} %copy-done.15), channel_id=1, source_target_pairs={{0,2},{1,3},{2,0},{3,1},{4,6},{5,7},{6,4},{7,5},{8,10},{9,11},{10,... | collective-permute-start | bytes 786440 | tf_op jit(solution)/shard_map/ppermute | solution.py:479
  76.3 59.8 %copy-start.1 = (bf16[2,65,128,128]{3,2,1,0:T(8,128)(2,1)}, bf16[2,65,128,128]{3,2,1,0:T(8,128)(2,1)S(1)}, u32[]{:S(2)}) copy-start(bf16[2,65,128,128]{3,2,1,0:T(8,128)(2,1)S(1)} %concatenate.3.tiles_ref) | copy-start | bytes 12779524
  76.3 33.3 %collective-permute-start.6 = (bf16[2,128,512]{2,1,0:T(8,128)(2,1)S(1)}, bf16[2,128,512]{2,1,0:T(8,128)(2,1)S(1)}, u32[]{:S(2)}, u32[]{:S(2)}) collective-permute-start(bf16[2,128,512]{2,1,0:T(8,128)(2,1)S(1)} %copy-done.14), channel_id=1, source_target_pairs={{0,20},{1,21},{2,22},{3,23},{4,16},{5,17},{6,18},{7,19},{8,28},{9,... | collective-permute-start | bytes 786440 | tf_op jit(solution)/shard_map/ppermute | solution.py:479
  79.3 32.2 %collective-permute-start.7 = (bf16[2,128,512]{2,1,0:T(8,128)(2,1)S(1)}, bf16[2,128,512]{2,1,0:T(8,128)(2,1)S(1)}, u32[]{:S(2)}, u32[]{:S(2)}) collective-permute-start(bf16[2,128,512]{2,1,0:T(8,128)(2,1)S(1)} %copy-done.12), channel_id=1, source_target_pairs={{0,3},{1,2},{2,1},{3,0},{4,7},{5,6},{6,5},{7,4},{8,11},{9,10},{10,... | collective-permute-start | bytes 786440 | tf_op jit(solution)/shard_map/ppermute | solution.py:479
  79.4 34.9 %collective-permute-start.8 = (bf16[2,128,512]{2,1,0:T(8,128)(2,1)S(1)}, bf16[2,128,512]{2,1,0:T(8,128)(2,1)S(1)}, u32[]{:S(2)}, u32[]{:S(2)}) collective-permute-start(bf16[2,128,512]{2,1,0:T(8,128)(2,1)S(1)} %copy-done.10), channel_id=1, source_target_pairs={{0,21},{1,20},{2,23},{3,22},{4,17},{5,16},{6,19},{7,18},{8,29},{9,... | collective-permute-start | bytes 786440 | tf_op jit(solution)/shard_map/ppermute | solution.py:479
  93.6 25.0 %collective-permute-start.9 = (bf16[2,128,512]{2,1,0:T(8,128)(2,1)S(1)}, bf16[2,128,512]{2,1,0:T(8,128)(2,1)S(1)}, u32[]{:S(2)}, u32[]{:S(2)}) collective-permute-start(bf16[2,128,512]{2,1,0:T(8,128)(2,1)S(1)} %copy-done.8), channel_id=1, source_target_pairs={{0,4},{1,5},{2,6},{3,7},{4,0},{5,1},{6,2},{7,3},{8,12},{9,13},{10,... | collective-permute-start | bytes 786440 | tf_op jit(solution)/shard_map/ppermute | solution.py:479
  93.6 40.4 %collective-permute-start = (bf16[2,128,512]{2,1,0:T(8,128)(2,1)S(1)}, bf16[2,128,512]{2,1,0:T(8,128)(2,1)S(1)}, u32[]{:S(2)}, u32[]{:S(2)}) collective-permute-start(bf16[2,128,512]{2,1,0:T(8,128)(2,1)S(1)} %copy-done.22), channel_id=1, source_target_pairs={{0,16},{1,17},{2,18},{3,19},{4,20},{5,21},{6,22},{7,23},{8,24},{9,... | collective-permute-start | bytes 786440 | tf_op jit(solution)/shard_map/ppermute | solution.py:479
  94.9 41.2 %copy-start.3 = (bf16[4096,512]{1,0:T(8,128)(2,1)S(1)}, bf16[4096,512]{1,0:T(8,128)(2,1)}, u32[]{:S(2)}) copy-start(bf16[4096,512]{1,0:T(8,128)(2,1)} %param.7) | copy-start | bytes 12582916
  109.6 26.4 %copy-start.31 = (bf16[2,128,512]{2,1,0:T(8,128)(2,1)}, bf16[2,128,512]{2,1,0:T(8,128)(2,1)S(1)}, u32[]{:S(2)}) copy-start(bf16[2,128,512]{2,1,0:T(8,128)(2,1)S(1)} %collective-permute-done.6.rest_6_) | copy-start | bytes 786436
  109.6 63.7 %collective-permute-start.1 = (bf16[2,128,512]{2,1,0:T(8,128)(2,1)}, bf16[2,128,512]{2,1,0:T(8,128)(2,1)}, u32[]{:S(2)}, u32[]{:S(2)}) collective-permute-start(bf16[2,128,512]{2,1,0:T(8,128)(2,1)} %get-tuple-element.49), channel_id=1, source_target_pairs={{0,17},{1,16},{2,19},{3,18},{4,21},{5,20},{6,23},{7,22},{8,25},{9,... | collective-permute-start | bytes 786440 | tf_op jit(solution)/shard_map/ppermute | solution.py:479
  111.5 24.5 %copy-start.32 = (bf16[2,128,512]{2,1,0:T(8,128)(2,1)}, bf16[2,128,512]{2,1,0:T(8,128)(2,1)S(1)}, u32[]{:S(2)}) copy-start(bf16[2,128,512]{2,1,0:T(8,128)(2,1)S(1)} %collective-permute-done.7.rest_7_) | copy-start | bytes 786436
  111.5 61.8 %collective-permute-start.2 = (bf16[2,128,512]{2,1,0:T(8,128)(2,1)}, bf16[2,128,512]{2,1,0:T(8,128)(2,1)}, u32[]{:S(2)}, u32[]{:S(2)}) collective-permute-start(bf16[2,128,512]{2,1,0:T(8,128)(2,1)} %get-tuple-element.50), channel_id=1, source_target_pairs={{0,18},{1,19},{2,16},{3,17},{4,22},{5,23},{6,20},{7,21},{8,26},{9,... | collective-permute-start | bytes 786440 | tf_op jit(solution)/shard_map/ppermute | solution.py:479
  114.3 65.2 %collective-permute-start.18 = (bf16[2,128,512]{2,1,0:T(8,128)(2,1)S(1)}, bf16[2,128,512]{2,1,0:T(8,128)(2,1)}, u32[]{:S(2)}, u32[]{:S(2)}) collective-permute-start(bf16[2,128,512]{2,1,0:T(8,128)(2,1)S(1)} %get-tuple-element.67), channel_id=1, source_target_pairs={{0,26},{1,27},{2,24},{3,25},{4,30},{5,31},{6,28},{7,29},{8,18},{9,... | collective-permute-start | bytes 786440 | tf_op jit(solution)/shard_map/ppermute | solution.py:479
  118.6 60.9 %collective-permute-start.19 = (bf16[2,128,512]{2,1,0:T(8,128)(2,1)S(1)}, bf16[2,128,512]{2,1,0:T(8,128)(2,1)}, u32[]{:S(2)}, u32[]{:S(2)}) collective-permute-start(bf16[2,128,512]{2,1,0:T(8,128)(2,1)S(1)} %get-tuple-element.68), channel_id=1, source_target_pairs={{0,9},{1,8},{2,11},{3,10},{4,13},{5,12},{6,15},{7,14},{8,1},{9,0},... | collective-permute-start | bytes 786440 | tf_op jit(solution)/shard_map/ppermute | solution.py:479
  134.0 48.6 %collective-permute-start.20 = (bf16[2,128,512]{2,1,0:T(8,128)(2,1)S(1)}, bf16[2,128,512]{2,1,0:T(8,128)(2,1)}, u32[]{:S(2)}, u32[]{:S(2)}) collective-permute-start(bf16[2,128,512]{2,1,0:T(8,128)(2,1)S(1)} %get-tuple-element.69), channel_id=1, source_target_pairs={{0,27},{1,26},{2,25},{3,24},{4,31},{5,30},{6,29},{7,28},{8,19},{9,... | collective-permute-start | bytes 786440 | tf_op jit(solution)/shard_map/ppermute | solution.py:479
  173.3 36.5 %collective-permute-start.21 = (bf16[2,128,512]{2,1,0:T(8,128)(2,1)S(1)}, bf16[2,128,512]{2,1,0:T(8,128)(2,1)S(1)}, u32[]{:S(2)}, u32[]{:S(2)}) collective-permute-start(bf16[2,128,512]{2,1,0:T(8,128)(2,1)S(1)} %get-tuple-element.70), channel_id=1, source_target_pairs={{0,10},{1,11},{2,8},{3,9},{4,14},{5,15},{6,12},{7,13},{8,2},{9,3},... | collective-permute-start | bytes 786440 | tf_op jit(solution)/shard_map/ppermute | solution.py:479
  173.3 41.3 %collective-permute-start.22 = (bf16[2,128,512]{2,1,0:T(8,128)(2,1)S(1)}, bf16[2,128,512]{2,1,0:T(8,128)(2,1)S(1)}, u32[]{:S(2)}, u32[]{:S(2)}) collective-permute-start(bf16[2,128,512]{2,1,0:T(8,128)(2,1)S(1)} %get-tuple-element.71), channel_id=1, source_target_pairs={{0,28},{1,29},{2,30},{3,31},{4,24},{5,25},{6,26},{7,27},{8,20},{9,... | collective-permute-start | bytes 786440 | tf_op jit(solution)/shard_map/ppermute | solution.py:479
  179.5 36.4 %collective-permute-start.23 = (bf16[2,128,512]{2,1,0:T(8,128)(2,1)S(1)}, bf16[2,128,512]{2,1,0:T(8,128)(2,1)S(1)}, u32[]{:S(2)}, u32[]{:S(2)}) collective-permute-start(bf16[2,128,512]{2,1,0:T(8,128)(2,1)S(1)} %get-tuple-element.72), channel_id=1, source_target_pairs={{0,11},{1,10},{2,9},{3,8},{4,15},{5,14},{6,13},{7,12},{8,3},{9,2},... | collective-permute-start | bytes 786440 | tf_op jit(solution)/shard_map/ppermute | solution.py:479
  179.5 38.7 %collective-permute-start.24 = (bf16[2,128,512]{2,1,0:T(8,128)(2,1)S(1)}, bf16[2,128,512]{2,1,0:T(8,128)(2,1)S(1)}, u32[]{:S(2)}, u32[]{:S(2)}) collective-permute-start(bf16[2,128,512]{2,1,0:T(8,128)(2,1)S(1)} %get-tuple-element.73), channel_id=1, source_target_pairs={{0,29},{1,28},{2,31},{3,30},{4,25},{5,24},{6,27},{7,26},{8,21},{9,... | collective-permute-start | bytes 786440 | tf_op jit(solution)/shard_map/ppermute | solution.py:479
  182.6 41.1 %collective-permute-start.25 = (bf16[2,128,512]{2,1,0:T(8,128)(2,1)S(1)}, bf16[2,128,512]{2,1,0:T(8,128)(2,1)S(1)}, u32[]{:S(2)}, u32[]{:S(2)}) collective-permute-start(bf16[2,128,512]{2,1,0:T(8,128)(2,1)S(1)} %get-tuple-element.74), channel_id=1, source_target_pairs={{0,12},{1,13},{2,14},{3,15},{4,8},{5,9},{6,10},{7,11},{8,4},{9,5},... | collective-permute-start | bytes 786440 | tf_op jit(solution)/shard_map/ppermute | solution.py:479
  187.0 37.4 %copy-start.24 = (bf16[2,512,2048]{2,1,0:T(8,128)(2,1)S(1)}, bf16[2,512,2048]{2,1,0:T(8,128)(2,1)}, u32[]{:S(2)}) copy-start(bf16[2,512,2048]{2,1,0:T(8,128)(2,1)} %copy-done.23) | copy-start | bytes 12582916
  209.9 18.5 %collective-permute-start.26 = (bf16[2,128,512]{2,1,0:T(8,128)(2,1)S(1)}, bf16[2,128,512]{2,1,0:T(8,128)(2,1)S(1)}, u32[]{:S(2)}, u32[]{:S(2)}) collective-permute-start(bf16[2,128,512]{2,1,0:T(8,128)(2,1)S(1)} %get-tuple-element.76), channel_id=1, source_target_pairs={{0,30},{1,31},{2,28},{3,29},{4,26},{5,27},{6,24},{7,25},{8,22},{9,... | collective-permute-start | bytes 786440 | tf_op jit(solution)/shard_map/ppermute | solution.py:479
  214.7 18.7 %collective-permute-start.27 = (bf16[2,128,512]{2,1,0:T(8,128)(2,1)S(1)}, bf16[2,128,512]{2,1,0:T(8,128)(2,1)S(1)}, u32[]{:S(2)}, u32[]{:S(2)}) collective-permute-start(bf16[2,128,512]{2,1,0:T(8,128)(2,1)S(1)} %get-tuple-element.77), channel_id=1, source_target_pairs={{0,13},{1,12},{2,15},{3,14},{4,9},{5,8},{6,11},{7,10},{8,5},{9,4},... | collective-permute-start | bytes 786440 | tf_op jit(solution)/shard_map/ppermute | solution.py:479
  215.9 18.3 %collective-permute-start.28 = (bf16[2,128,512]{2,1,0:T(8,128)(2,1)S(1)}, bf16[2,128,512]{2,1,0:T(8,128)(2,1)S(1)}, u32[]{:S(2)}, u32[]{:S(2)}) collective-permute-start(bf16[2,128,512]{2,1,0:T(8,128)(2,1)S(1)} %get-tuple-element.78), channel_id=1, source_target_pairs={{0,31},{1,30},{2,29},{3,28},{4,27},{5,26},{6,25},{7,24},{8,23},{9,... | collective-permute-start | bytes 786440 | tf_op jit(solution)/shard_map/ppermute | solution.py:479
  218.2 24.6 %collective-permute-start.29 = (bf16[2,128,512]{2,1,0:T(8,128)(2,1)S(1)}, bf16[2,128,512]{2,1,0:T(8,128)(2,1)S(1)}, u32[]{:S(2)}, u32[]{:S(2)}) collective-permute-start(bf16[2,128,512]{2,1,0:T(8,128)(2,1)S(1)} %get-tuple-element.79), channel_id=1, source_target_pairs={{0,14},{1,15},{2,12},{3,13},{4,10},{5,11},{6,8},{7,9},{8,6},{9,7},... | collective-permute-start | bytes 786440 | tf_op jit(solution)/shard_map/ppermute | solution.py:479
  223.7 23.4 %collective-permute-start.30 = (bf16[2,128,512]{2,1,0:T(8,128)(2,1)S(1)}, bf16[2,128,512]{2,1,0:T(8,128)(2,1)S(1)}, u32[]{:S(2)}, u32[]{:S(2)}) collective-permute-start(bf16[2,128,512]{2,1,0:T(8,128)(2,1)S(1)} %get-tuple-element.80), channel_id=1, source_target_pairs={{0,15},{1,14},{2,13},{3,12},{4,11},{5,10},{6,9},{7,8},{8,7},{9,6},... | collective-permute-start | bytes 786440 | tf_op jit(solution)/shard_map/ppermute | solution.py:479
  224.4 23.4 %copy-start.26 = (bf16[2,512,1280]{2,1,0:T(8,128)(2,1)S(1)}, bf16[2,512,1280]{2,1,0:T(8,128)(2,1)}, u32[]{:S(2)}) copy-start(bf16[2,512,1280]{2,1,0:T(8,128)(2,1)} %copy-done.25) | copy-start | bytes 7864324
  250.8 2.7 collective-permute-start.31
  253.7 6.4 %collective-permute-start.32 = (bf16[4,16,1024]{2,1,0:T(8,128)(2,1)S(1)}, bf16[4,16,1024]{2,1,0:T(8,128)(2,1)S(1)}, u32[]{:S(2)}, u32[]{:S(2)}) collective-permute-start(bf16[4,16,1024]{2,1,0:T(8,128)(2,1)S(1)} %get-tuple-element.84), channel_id=1, source_target_pairs={{0,2},{1,3},{2,0},{3,1},{4,6},{5,7},{6,4},{7,5},{8,10},{9,11},{10,... | collective-permute-start | bytes 393224 | tf_op jit(solution)/shard_map/ppermute | solution.py:479
  254.6 7.4 %collective-permute-start.33 = (bf16[4,16,1024]{2,1,0:T(8,128)(2,1)S(1)}, bf16[4,16,1024]{2,1,0:T(8,128)(2,1)S(1)}, u32[]{:S(2)}, u32[]{:S(2)}) collective-permute-start(bf16[4,16,1024]{2,1,0:T(8,128)(2,1)S(1)} %get-tuple-element.85), channel_id=1, source_target_pairs={{0,4},{1,5},{2,6},{3,7},{4,0},{5,1},{6,2},{7,3},{8,12},{9,13},{10,... | collective-permute-start | bytes 393224 | tf_op jit(solution)/shard_map/ppermute | solution.py:479
  256.1 7.7 %collective-permute-start.34 = (bf16[4,16,1024]{2,1,0:T(8,128)(2,1)S(1)}, bf16[4,16,1024]{2,1,0:T(8,128)(2,1)S(1)}, u32[]{:S(2)}, u32[]{:S(2)}) collective-permute-start(bf16[4,16,1024]{2,1,0:T(8,128)(2,1)S(1)} %get-tuple-element.86), channel_id=1, source_target_pairs={{0,6},{1,7},{2,4},{3,5},{4,2},{5,3},{6,0},{7,1},{8,14},{9,15},{10,... | collective-permute-start | bytes 393224 | tf_op jit(solution)/shard_map/ppermute | solution.py:479
  263.8 5.0 %collective-permute-start.35 = (f32[16,1024]{1,0:T(8,128)S(1)}, f32[16,1024]{1,0:T(8,128)S(1)}, u32[]{:S(2)}, u32[]{:S(2)}) collective-permute-start(f32[16,1024]{1,0:T(8,128)S(1)} %get-tuple-element.88), channel_id=1, source_target_pairs={{0,8},{1,9},{2,10},{3,11},{4,12},{5,13},{6,14},{7,15},{8,0},{9,1},... | collective-permute-start | bytes 196616 | tf_op jit(solution)/shard_map/ppermute | solution.py:479
  265.5 7.1 %collective-permute-start.36 = (f32[16,1024]{1,0:T(8,128)S(1)}, f32[16,1024]{1,0:T(8,128)S(1)}, u32[]{:S(2)}, u32[]{:S(2)}) collective-permute-start(f32[16,1024]{1,0:T(8,128)S(1)} %get-tuple-element.89), channel_id=1, source_target_pairs={{0,16},{1,17},{2,18},{3,19},{4,20},{5,21},{6,22},{7,23},{8,24},{9,... | collective-permute-start | bytes 196616 | tf_op jit(solution)/shard_map/ppermute | solution.py:479
  266.1 6.4 %collective-permute-start.37 = (f32[16,1024]{1,0:T(8,128)S(1)}, f32[16,1024]{1,0:T(8,128)S(1)}, u32[]{:S(2)}, u32[]{:S(2)}) collective-permute-start(f32[16,1024]{1,0:T(8,128)S(1)} %get-tuple-element.90), channel_id=1, source_target_pairs={{0,24},{1,25},{2,26},{3,27},{4,28},{5,29},{6,30},{7,31},{8,16},{9,... | collective-permute-start | bytes 196616 | tf_op jit(solution)/shard_map/ppermute | solution.py:479
  (36 other events, 227.3 us)

commit v4 on v3

--- a/solution.py
+++ b/solution.py
@@ -74,7 +74,7 @@
         scratch_shapes=[pltpu.SemaphoreType.DMA((len(masks) * cap,))],
         compiler_params=pltpu.CompilerParams(vmem_limit_bytes=ROOM),
         name="first_pack",
-    )(rank, send, in_hbm(blocks))
+    )(rank, in_hbm(send), in_hbm(blocks))
 
 
 def pack_kernel(masks, after, rank_ref, send_ref, blocks_ref, *rest):
@@ -526,9 +526,10 @@
     outer = devices // 8
     got = swap(send, 1, devices)
     parts = split(rank, keep, [got], 4, 1, BF16)
-    got = [swap(parts[n], n << 1, devices) for n in range(1, 4)]
+    got = [swap(parts[n], n << 1, devices) for n in (3, 1, 2)]
     parts = split(rank, parts[0], got, outer, 3, F32)
-    got = [swap(parts[n], n << 3, devices) for n in range(1, outer)]
+    far_first = sorted(range(1, outer), key=lambda n: (n < outer // 2, n))
+    got = [swap(parts[n], n << 3, devices) for n in far_first]
     return finish(rank, parts[0], got, scale)
 
 

time: 274 us -> 274 us (level)
  no operation moved by 1% of the time
where the time goes in v4:
time: 274 us
  Pallas kernels  87.3 us (32%)
  starting transfers between devices  80.7 us (29%)
  waiting for transfers between devices  75.5 us (28%)
  local copies, waits for them, and re-layouts  28.3 us (10%)
    ppermute x38, starting transfers between devices, swap(): return lax.ppermute(value, 'rows', [(i, i ^ mask) for i in range(devices)])  80.7 us
    ppermute x38, waiting for transfers between devices, swap(): return lax.ppermute(value, 'rows', [(i, i ^ mask) for i in range(devices)])  75.5 us
    pallas_call x1, Pallas kernels, adjoint(): pl.pallas_call(functools.partial(adjoint_kernel, phase, slots, count), ou...  27.6 us
    pallas_call x1, Pallas kernels, gram(): pl.pallas_call(functools.partial(gram_kernel, phase, len(arrivals), slots...  22.9 us
    unnamed x93, local copies, waits for them, and re-layouts  17.8 us
    pallas_call x1, Pallas kernels, hops(): pl.pallas_call(functools.partial(hops_kernel, slots, fixed), out_shape=HB...  14.7 us
    pallas_call x1, Pallas kernels, pack(): pl.pallas_call(functools.partial(pack_kernel, masks, len(after)), out_sha...  11.5 us
    pallas_call x2, Pallas kernels, late(): pl.pallas_call(functools.partial(late_kernel, len(arrivals)), out_shape=h...  7.09 us
  transfers between devices with their start and end apart: 38, of which 13 were waited for; matrix products, arithmetic and copies ran while one was open for 4% of the time, Pallas kernels for 26%

profile of v4, /device:TPU:0, one launch (start us, length us, event | category | flops | bytes accessed | tf_op | source)
XLA Modules:
  0.0 274.0 jit_solution(10680782598168575369)
XLA Ops:
  0.8 11.5 %pack.1 = (bf16[2,128,512]{2,1,0:T(8,128)(2,1)S(1)}, bf16[2,128,512]{2,1,0:T(8,128)(2,1)S(1)}, bf16[2,128,512]{2,1,0:T(8,128)(2,1)S(1)}, bf16[2,128,512]{2,1,0:T...) custom-call(s32[1]{0:T(128)} %bitcast.rank_ref, ...), custom_call_target="tpu_custom_call" | custom-call | tf_op jit(solution)/shard_map/pack/pallas_call | solution.py:104
  19.3 5.9 %collective-permute-start.10 = (bf16[2,128,512]{2,1,0:T(8,128)(2,1)}, bf16[2,128,512]{2,1,0:T(8,128)(2,1)}, u32[]{:S(2)}, u32[]{:S(2)}) collective-permute-start(bf16[2,128,512]{2,1,0:T(8,128)(2,1)} %get-tuple-element.58), channel_id=1, source_target_pairs={{0,22},{1,23},{2,20},{3,21},{4,18},{5,19},{6,16},{7,17},{8,30},{9,... | collective-permute-start | bytes 786440 | tf_op jit(solution)/shard_map/ppermute | solution.py:479
  25.2 1.5 collective-permute-start.12
  26.7 1.4 collective-permute-start.13
  28.1 4.0 %collective-permute-start.14 = (bf16[2,128,512]{2,1,0:T(8,128)(2,1)}, bf16[2,128,512]{2,1,0:T(8,128)(2,1)}, u32[]{:S(2)}, u32[]{:S(2)}) collective-permute-start(bf16[2,128,512]{2,1,0:T(8,128)(2,1)} %get-tuple-element.62), channel_id=1, source_target_pairs={{0,24},{1,25},{2,26},{3,27},{4,28},{5,29},{6,30},{7,31},{8,16},{9,... | collective-permute-start | bytes 786440 | tf_op jit(solution)/shard_map/ppermute | solution.py:479
  34.5 15.1 %collective-permute-done.10.rest_10_ = bf16[2,128,512]{2,1,0:T(8,128)(2,1)} collective-permute-done((bf16[2,128,512]{2,1,0:T(8,128)(2,1)}, bf16[2,128,512]{2,1,0:T(8,128)(2,1)}, u32[]{:S(2)}, u32[]{:S(2)}) %collective-permute-start.10) | collective-permute-done | bytes 262176 | tf_op jit(solution)/shard_map/ppermute | solution.py:479
  49.5 0.9 collective-permute-start.15
  50.7 4.0 %collective-permute-start.16 = (bf16[2,128,512]{2,1,0:T(8,128)(2,1)}, bf16[2,128,512]{2,1,0:T(8,128)(2,1)}, u32[]{:S(2)}, u32[]{:S(2)}) collective-permute-start(bf16[2,128,512]{2,1,0:T(8,128)(2,1)} %copy-done.19), channel_id=1, source_target_pairs={{0,25},{1,24},{2,27},{3,26},{4,29},{5,28},{6,31},{7,30},{8,17},{9,... | collective-permute-start | bytes 786440 | tf_op jit(solution)/shard_map/ppermute | solution.py:479
  55.1 13.0 %collective-permute-start.4 = (bf16[2,128,512]{2,1,0:T(8,128)(2,1)}, bf16[2,128,512]{2,1,0:T(8,128)(2,1)}, u32[]{:S(2)}, u32[]{:S(2)}) collective-permute-start(bf16[2,128,512]{2,1,0:T(8,128)(2,1)} %copy-done.16), channel_id=1, source_target_pairs={{0,19},{1,18},{2,17},{3,16},{4,23},{5,22},{6,21},{7,20},{8,27},{9,... | collective-permute-start | bytes 786440 | tf_op jit(solution)/shard_map/ppermute | solution.py:479
  68.1 1.2 collective-permute-start.5
  69.4 2.8 %first_pack.1 = (bf16[2,128,512]{2,1,0:T(8,128)(2,1)S(1)}, bf16[2,128,512]{2,1,0:T(8,128)(2,1)}, bf16[2,128,512]{2,1,0:T(8,128)(2,1)}) custom-call(s32[1]{0:T(128)} %bitcast.rank_ref, s32[2,32]{1,0:T(2,128)} %bitcast.20, bf16[32,128,512]{2,1,0:T(8,128)(2,1)} %bitcast.15), custom_call_target="tpu_custom_call" | custom-call | tf_op jit(solution)/shard_map/first_pack/pallas_call | solution.py:69
  73.2 3.2 %concatenate.3.tiles_ref = bf16[2,65,128,128]{3,2,1,0:T(8,128)(2,1)S(1)} pad(bf16[2,64,128,128]{3,2,1,0:T(8,128)(2,1)} %param.9, bf16[]{:T(256)} %constant.66.clone.1), padding=0_0x0_1x0_0x0_0 | pad | bytes 8454146 | tf_op jit(solution)/shard_map/concatenate | solution.py:506
  76.4 2.8 %collective-permute-start.6 = (bf16[2,128,512]{2,1,0:T(8,128)(2,1)S(1)}, bf16[2,128,512]{2,1,0:T(8,128)(2,1)S(1)}, u32[]{:S(2)}, u32[]{:S(2)}) collective-permute-start(bf16[2,128,512]{2,1,0:T(8,128)(2,1)S(1)} %copy-done.14), channel_id=1, source_target_pairs={{0,20},{1,21},{2,22},{3,23},{4,16},{5,17},{6,18},{7,19},{8,28},{9,... | collective-permute-start | bytes 786440 | tf_op jit(solution)/shard_map/ppermute | solution.py:479
  79.4 1.4 collective-permute-start.8
  80.9 12.7 %collective-permute-done.4.rest_4_ = bf16[2,128,512]{2,1,0:T(8,128)(2,1)} collective-permute-done((bf16[2,128,512]{2,1,0:T(8,128)(2,1)}, bf16[2,128,512]{2,1,0:T(8,128)(2,1)}, u32[]{:S(2)}, u32[]{:S(2)}) %collective-permute-start.4) | collective-permute-done | bytes 262176 | tf_op jit(solution)/shard_map/ppermute | solution.py:479
  93.6 1.3 collective-permute-start
  94.9 14.7 %hops.1.in_ref = f32[64,128,512]{2,1,0:T(8,128)} custom-call(s32[3,1024]{1,0:T(4,128)S(1)} %add.78.lists_ref, s32[3,64]{1,0:T(4,128)S(1)} %get-tuple-element.91.counts_ref, bf16[2,65,128,128]{3,2,1,0:T(8,128)(2,1)S(1)} %concatenate.3.tiles_ref, bf16[32,128,512]{2,1,0:T(8,128)(2,1)S(1)} %bitcast.16), custom_call_target="tpu_custom_call" | custom-call | flops 8000000000 | bytes 41943040 | tf_op jit(solution)/shard_map/hops/pallas_call | solution.py:217
  109.6 1.9 collective-permute-start.1
  111.5 2.8 %collective-permute-start.2 = (bf16[2,128,512]{2,1,0:T(8,128)(2,1)}, bf16[2,128,512]{2,1,0:T(8,128)(2,1)}, u32[]{:S(2)}, u32[]{:S(2)}) collective-permute-start(bf16[2,128,512]{2,1,0:T(8,128)(2,1)} %get-tuple-element.50), channel_id=1, source_target_pairs={{0,18},{1,19},{2,16},{3,17},{4,22},{5,23},{6,20},{7,21},{8,26},{9,... | collective-permute-start | bytes 786440 | tf_op jit(solution)/shard_map/ppermute | solution.py:479
  114.3 4.3 %collective-permute-start.18 = (bf16[2,128,512]{2,1,0:T(8,128)(2,1)S(1)}, bf16[2,128,512]{2,1,0:T(8,128)(2,1)}, u32[]{:S(2)}, u32[]{:S(2)}) collective-permute-start(bf16[2,128,512]{2,1,0:T(8,128)(2,1)S(1)} %get-tuple-element.67), channel_id=1, source_target_pairs={{0,26},{1,27},{2,24},{3,25},{4,30},{5,31},{6,28},{7,29},{8,18},{9,... | collective-permute-start | bytes 786440 | tf_op jit(solution)/shard_map/ppermute | solution.py:479
  118.6 15.4 %collective-permute-done.rest_0_ = bf16[2,128,512]{2,1,0:T(8,128)(2,1)S(1)} collective-permute-done((bf16[2,128,512]{2,1,0:T(8,128)(2,1)S(1)}, bf16[2,128,512]{2,1,0:T(8,128)(2,1)S(1)}, u32[]{:S(2)}, u32[]{:S(2)}) %collective-permute-start) | collective-permute-done | bytes 262176 | tf_op jit(solution)/shard_map/ppermute | solution.py:479
  134.0 2.0 collective-permute-start.20
  136.0 27.6 %adjoint.1 = (bf16[2,512,2048]{2,1,0:T(8,128)(2,1)S(1)}, bf16[2,512,1280]{2,1,0:T(8,128)(2,1)S(1)}) custom-call(s32[3,1024]{1,0:T(4,128)S(1)} %add.78.lists_ref, s32[3,64]{1,0:T(4,128)S(1)} %get-tuple-element.91.counts_ref, bf16[2,65,128,128]{3,2,1,0:T(8,128)(2,1)S(1)} %concatenate.3.tiles_ref, bf16[32,128,512]{2,1,0:T(8,128)(2,1)S(1)} %bitcast.18), custom_call_target="tpu_custom_call" | custom-call | flops 8000000000 | bytes 16777216 | tf_op jit(solution)/shard_map/adjoint/pallas_call | solution.py:271
  163.6 2.0 copy-done.23
  165.6 1.5 copy-done.25
  167.1 6.3 %copy.20 = bf16[4,1024,512]{1,2,0:T(8,128)(2,1)} copy(bf16[4,1024,512]{2,1,0:T(8,128)(2,1)} %bitcast.17) | data formatting | bytes 8388608 | tf_op jit(solution)/shard_map/reshape | solution.py:508
  173.3 6.1 %collective-permute-start.22 = (bf16[2,128,512]{2,1,0:T(8,128)(2,1)S(1)}, bf16[2,128,512]{2,1,0:T(8,128)(2,1)S(1)}, u32[]{:S(2)}, u32[]{:S(2)}) collective-permute-start(bf16[2,128,512]{2,1,0:T(8,128)(2,1)S(1)} %get-tuple-element.71), channel_id=1, source_target_pairs={{0,28},{1,29},{2,30},{3,31},{4,24},{5,25},{6,26},{7,27},{8,20},{9,... | collective-permute-start | bytes 786440 | tf_op jit(solution)/shard_map/ppermute | solution.py:479
  179.5 3.1 %collective-permute-start.24 = (bf16[2,128,512]{2,1,0:T(8,128)(2,1)S(1)}, bf16[2,128,512]{2,1,0:T(8,128)(2,1)S(1)}, u32[]{:S(2)}, u32[]{:S(2)}) collective-permute-start(bf16[2,128,512]{2,1,0:T(8,128)(2,1)S(1)} %get-tuple-element.73), channel_id=1, source_target_pairs={{0,29},{1,28},{2,31},{3,30},{4,25},{5,24},{6,27},{7,26},{8,21},{9,... | collective-permute-start | bytes 786440 | tf_op jit(solution)/shard_map/ppermute | solution.py:479
  182.6 2.2 copy-done.2
  184.8 2.2 copy-done.4
  187.0 22.9 %gram.1.in_ref = f32[512,1024]{1,0:T(8,128)S(1)} custom-call(s32[3,1024]{1,0:T(4,128)S(1)} %add.78.lists_ref, s32[3,64]{1,0:T(4,128)S(1)} %get-tuple-element.91.counts_ref, bf16[2,65,128,128]{3,2,1,0:T(8,128)(2,1)S(1)} %copy-done.2, f32[64,128,512]{2,1,0:T(8,128)} %hops.1.in_ref, bf16[4,512,1024]{2,1,0:T(8,128)(2,1)S(1)} %bitcast.19, ...), custom_call_target="tpu_custom_call" | custom-call | flops 12000000000 | bytes 25165824 | tf_op jit(solution)/shard_map/gram/pallas_call | solution.py:354
  209.9 4.8 %collective-permute-start.26 = (bf16[2,128,512]{2,1,0:T(8,128)(2,1)S(1)}, bf16[2,128,512]{2,1,0:T(8,128)(2,1)S(1)}, u32[]{:S(2)}, u32[]{:S(2)}) collective-permute-start(bf16[2,128,512]{2,1,0:T(8,128)(2,1)S(1)} %get-tuple-element.76), channel_id=1, source_target_pairs={{0,30},{1,31},{2,28},{3,29},{4,26},{5,27},{6,24},{7,25},{8,22},{9,... | collective-permute-start | bytes 786440 | tf_op jit(solution)/shard_map/ppermute | solution.py:479
  214.7 1.2 collective-permute-start.27
  215.9 2.4 collective-permute-start.28
  218.2 5.4 %collective-permute-start.29 = (bf16[2,128,512]{2,1,0:T(8,128)(2,1)S(1)}, bf16[2,128,512]{2,1,0:T(8,128)(2,1)S(1)}, u32[]{:S(2)}, u32[]{:S(2)}) collective-permute-start(bf16[2,128,512]{2,1,0:T(8,128)(2,1)S(1)} %get-tuple-element.79), channel_id=1, source_target_pairs={{0,14},{1,15},{2,12},{3,13},{4,10},{5,11},{6,8},{7,9},{8,6},{9,7},... | collective-permute-start | bytes 786440 | tf_op jit(solution)/shard_map/ppermute | solution.py:479
  224.4 4.0 %late.2.in_ref = f32[512,1024]{1,0:T(8,128)S(1)} custom-call(s32[1]{0:T(128)} %bitcast.rank_ref, f32[512,1024]{1,0:T(8,128)S(1)} %gram.1.in_ref, bf16[2,512,2048]{2,1,0:T(8,128)(2,1)S(1)} %copy-done.24, bf16[2,128,512]{2,1,0:T(8,128)(2,1)} %collective-permute-done.18.rest_0_, bf16[2,128,512]{2,1,0:T(8,128)(2,1)} %collective-permute-done.19.rest_1_, ...), custom_call_target="tpu_custom_call" | custom-call | flops 4000000000 | bytes 12582912 | tf_op jit(solution)/shard_map/late/pallas_call | solution.py:411
  228.4 4.9 %collective-permute-done.27.rest_1_ = bf16[2,128,512]{2,1,0:T(8,128)(2,1)S(1)} collective-permute-done((bf16[2,128,512]{2,1,0:T(8,128)(2,1)S(1)}, bf16[2,128,512]{2,1,0:T(8,128)(2,1)S(1)}, u32[]{:S(2)}, u32[]{:S(2)}) %collective-permute-start.27) | collective-permute-done | bytes 262176 | tf_op jit(solution)/shard_map/ppermute | solution.py:479
  234.2 8.7 %collective-permute-done.29.rest_3_ = bf16[2,128,512]{2,1,0:T(8,128)(2,1)S(1)} collective-permute-done((bf16[2,128,512]{2,1,0:T(8,128)(2,1)S(1)}, bf16[2,128,512]{2,1,0:T(8,128)(2,1)S(1)}, u32[]{:S(2)}, u32[]{:S(2)}) %collective-permute-start.29) | collective-permute-done | bytes 262176 | tf_op jit(solution)/shard_map/ppermute | solution.py:479
  242.8 4.2 %collective-permute-done.30.rest_4_ = bf16[2,128,512]{2,1,0:T(8,128)(2,1)S(1)} collective-permute-done((bf16[2,128,512]{2,1,0:T(8,128)(2,1)S(1)}, bf16[2,128,512]{2,1,0:T(8,128)(2,1)S(1)}, u32[]{:S(2)}, u32[]{:S(2)}) %collective-permute-start.30) | collective-permute-done | bytes 262176 | tf_op jit(solution)/shard_map/ppermute | solution.py:479
  247.8 3.0 %late.3 = (f32[4,4,16,1024]{3,2,1,0:T(8,128)S(1)}, f32[4,4,16,1024]{3,2,1,0:T(8,128)S(1)}) custom-call(s32[1]{0:T(128)} %bitcast.rank_ref, f32[512,1024]{1,0:T(8,128)S(1)} %late.2.in_ref, bf16[2,512,1280]{2,1,0:T(8,128)(2,1)S(1)} %copy-done.26, bf16[2,128,512]{2,1,0:T(8,128)(2,1)} %copy-done.41, bf16[2,128,512]{2,1,0:T(8,128)(2,1)} %copy-done.42, ...), custom_call_target="tpu_custom_call" | custom-call | flops 4000000000 | bytes 12582912 | tf_op jit(solution)/shard_map/late/pallas_call | solution.py:411
  250.9 2.6 collective-permute-done.31.rest_0_
  253.7 1.7 collective-permute-start.32
  255.4 2.1 collective-permute-start.33
  257.5 3.5 %collective-permute-done.32.rest_0_ = bf16[4,16,1024]{2,1,0:T(8,128)(2,1)S(1)} collective-permute-done((bf16[4,16,1024]{2,1,0:T(8,128)(2,1)S(1)}, bf16[4,16,1024]{2,1,0:T(8,128)(2,1)S(1)}, u32[]{:S(2)}, u32[]{:S(2)}) %collective-permute-start.32) | collective-permute-done | bytes 131104 | tf_op jit(solution)/shard_map/ppermute | solution.py:479
  261.0 2.8 %collective-permute-done.33.rest_1_ = bf16[4,16,1024]{2,1,0:T(8,128)(2,1)S(1)} collective-permute-done((bf16[4,16,1024]{2,1,0:T(8,128)(2,1)S(1)}, bf16[4,16,1024]{2,1,0:T(8,128)(2,1)S(1)}, u32[]{:S(2)}, u32[]{:S(2)}) %collective-permute-start.33) | collective-permute-done | bytes 131104 | tf_op jit(solution)/shard_map/ppermute | solution.py:479
  263.9 2.2 collective-permute-start.35
  266.1 2.6 collective-permute-start.36
  268.7 3.4 %collective-permute-done.35.rest_0_ = f32[16,1024]{1,0:T(8,128)S(1)} collective-permute-done((f32[16,1024]{1,0:T(8,128)S(1)}, f32[16,1024]{1,0:T(8,128)S(1)}, u32[]{:S(2)}, u32[]{:S(2)}) %collective-permute-start.35) | collective-permute-done | bytes 65568 | tf_op jit(solution)/shard_map/ppermute | solution.py:479
  (152 shorter events, 15.0 us)
Async XLA Ops:
  0.0 32.4 %copy-start.29 = (s32[31]{0:T(128)S(1)}, s32[31]{0:T(128)}, u32[]{:S(2)}) copy-start(s32[31]{0:T(128)} %constant.67.clone) | copy-start | bytes 376
  0.0 32.2 %copy-start.6 = (s32[32,2]{0,1:T(2,128)S(1)}, s32[32,2]{0,1:T(2,128)}, u32[]{:S(2)}) copy-start(s32[32,2]{0,1:T(2,128)} %param.12) | copy-start | bytes 772
  0.8 31.4 %copy-start.27 = (s32[2,32,16]{1,2,0:T(8,128)S(1)}, s32[2,32,16]{1,2,0:T(8,128)}, u32[]{:S(2)}) copy-start(s32[2,32,16]{1,2,0:T(8,128)} %param.11) | copy-start | bytes 12292
  0.8 31.5 %copy-start.28 = (s32[2,32,16]{1,2,0:T(8,128)S(1)}, s32[2,32,16]{1,2,0:T(8,128)}, u32[]{:S(2)}) copy-start(s32[2,32,16]{1,2,0:T(8,128)} %param.10) | copy-start | bytes 12292
  19.3 30.3 %collective-permute-start.10 = (bf16[2,128,512]{2,1,0:T(8,128)(2,1)}, bf16[2,128,512]{2,1,0:T(8,128)(2,1)}, u32[]{:S(2)}, u32[]{:S(2)}) collective-permute-start(bf16[2,128,512]{2,1,0:T(8,128)(2,1)} %get-tuple-element.58), channel_id=1, source_target_pairs={{0,22},{1,23},{2,20},{3,21},{4,18},{5,19},{6,16},{7,17},{8,30},{9,... | collective-permute-start | bytes 786440 | tf_op jit(solution)/shard_map/ppermute | solution.py:479
  25.2 25.4 %collective-permute-start.11 = (bf16[2,128,512]{2,1,0:T(8,128)(2,1)}, bf16[2,128,512]{2,1,0:T(8,128)(2,1)}, u32[]{:S(2)}, u32[]{:S(2)}) collective-permute-start(bf16[2,128,512]{2,1,0:T(8,128)(2,1)} %get-tuple-element.59), channel_id=1, source_target_pairs={{0,5},{1,4},{2,7},{3,6},{4,1},{5,0},{6,3},{7,2},{8,13},{9,12},{10,... | collective-permute-start | bytes 786440 | tf_op jit(solution)/shard_map/ppermute | solution.py:479
  25.2 29.5 %collective-permute-start.12 = (bf16[2,128,512]{2,1,0:T(8,128)(2,1)}, bf16[2,128,512]{2,1,0:T(8,128)(2,1)}, u32[]{:S(2)}, u32[]{:S(2)}) collective-permute-start(bf16[2,128,512]{2,1,0:T(8,128)(2,1)} %get-tuple-element.60), channel_id=1, source_target_pairs={{0,23},{1,22},{2,21},{3,20},{4,19},{5,18},{6,17},{7,16},{8,31},{9,... | collective-permute-start | bytes 786440 | tf_op jit(solution)/shard_map/ppermute | solution.py:479
  26.7 28.4 %collective-permute-start.13 = (bf16[2,128,512]{2,1,0:T(8,128)(2,1)}, bf16[2,128,512]{2,1,0:T(8,128)(2,1)}, u32[]{:S(2)}, u32[]{:S(2)}) collective-permute-start(bf16[2,128,512]{2,1,0:T(8,128)(2,1)} %get-tuple-element.61), channel_id=1, source_target_pairs={{0,6},{1,7},{2,4},{3,5},{4,2},{5,3},{6,0},{7,1},{8,14},{9,15},{10,... | collective-permute-start | bytes 786440 | tf_op jit(solution)/shard_map/ppermute | solution.py:479
  28.1 27.0 %collective-permute-start.14 = (bf16[2,128,512]{2,1,0:T(8,128)(2,1)}, bf16[2,128,512]{2,1,0:T(8,128)(2,1)}, u32[]{:S(2)}, u32[]{:S(2)}) collective-permute-start(bf16[2,128,512]{2,1,0:T(8,128)(2,1)} %get-tuple-element.62), channel_id=1, source_target_pairs={{0,24},{1,25},{2,26},{3,27},{4,28},{5,29},{6,30},{7,31},{8,16},{9,... | collective-permute-start | bytes 786440 | tf_op jit(solution)/shard_map/ppermute | solution.py:479
  49.5 18.6 %collective-permute-start.15 = (bf16[2,128,512]{2,1,0:T(8,128)(2,1)}, bf16[2,128,512]{2,1,0:T(8,128)(2,1)S(1)}, u32[]{:S(2)}, u32[]{:S(2)}) collective-permute-start(bf16[2,128,512]{2,1,0:T(8,128)(2,1)} %copy-done.20), channel_id=1, source_target_pairs={{0,7},{1,6},{2,5},{3,4},{4,3},{5,2},{6,1},{7,0},{8,15},{9,14},{10,... | collective-permute-start | bytes 786440 | tf_op jit(solution)/shard_map/ppermute | solution.py:479
  50.7 25.7 %collective-permute-start.16 = (bf16[2,128,512]{2,1,0:T(8,128)(2,1)}, bf16[2,128,512]{2,1,0:T(8,128)(2,1)}, u32[]{:S(2)}, u32[]{:S(2)}) collective-permute-start(bf16[2,128,512]{2,1,0:T(8,128)(2,1)} %copy-done.19), channel_id=1, source_target_pairs={{0,25},{1,24},{2,27},{3,26},{4,29},{5,28},{6,31},{7,30},{8,17},{9,... | collective-permute-start | bytes 786440 | tf_op jit(solution)/shard_map/ppermute | solution.py:479
  54.7 24.6 %collective-permute-start.17 = (bf16[2,128,512]{2,1,0:T(8,128)(2,1)}, bf16[2,128,512]{2,1,0:T(8,128)(2,1)}, u32[]{:S(2)}, u32[]{:S(2)}) collective-permute-start(bf16[2,128,512]{2,1,0:T(8,128)(2,1)} %copy-done.18), channel_id=1, source_target_pairs={{0,8},{1,9},{2,10},{3,11},{4,12},{5,13},{6,14},{7,15},{8,0},{9,1},... | collective-permute-start | bytes 786440 | tf_op jit(solution)/shard_map/ppermute | solution.py:479
  55.1 24.3 %collective-permute-start.3 = (bf16[2,128,512]{2,1,0:T(8,128)(2,1)}, bf16[2,128,512]{2,1,0:T(8,128)(2,1)}, u32[]{:S(2)}, u32[]{:S(2)}) collective-permute-start(bf16[2,128,512]{2,1,0:T(8,128)(2,1)} %copy-done.17), channel_id=1, source_target_pairs={{0,1},{1,0},{2,3},{3,2},{4,5},{5,4},{6,7},{7,6},{8,9},{9,8},{10,11... | collective-permute-start | bytes 786440 | tf_op jit(solution)/shard_map/ppermute | solution.py:479
  55.1 38.4 %collective-permute-start.4 = (bf16[2,128,512]{2,1,0:T(8,128)(2,1)}, bf16[2,128,512]{2,1,0:T(8,128)(2,1)}, u32[]{:S(2)}, u32[]{:S(2)}) collective-permute-start(bf16[2,128,512]{2,1,0:T(8,128)(2,1)} %copy-done.16), channel_id=1, source_target_pairs={{0,19},{1,18},{2,17},{3,16},{4,23},{5,22},{6,21},{7,20},{8,27},{9,... | collective-permute-start | bytes 786440 | tf_op jit(solution)/shard_map/ppermute | solution.py:479
  68.1 25.5 %collective-permute-start.5 = (bf16[2,128,512]{2,1,0:T(8,128)(2,1)}, bf16[2,128,512]{2,1,0:T(8,128)(2,1)}, u32[]{:S(2)}, u32[]{:S(2)}) collective-permute-start(bf16[2,128,512]{2,1,0:T(8,128)(2,1)} %copy-done.15), channel_id=1, source_target_pairs={{0,2},{1,3},{2,0},{3,1},{4,6},{5,7},{6,4},{7,5},{8,10},{9,11},{10,... | collective-permute-start | bytes 786440 | tf_op jit(solution)/shard_map/ppermute | solution.py:479
  76.4 59.6 %copy-start.1 = (bf16[2,65,128,128]{3,2,1,0:T(8,128)(2,1)}, bf16[2,65,128,128]{3,2,1,0:T(8,128)(2,1)S(1)}, u32[]{:S(2)}) copy-start(bf16[2,65,128,128]{3,2,1,0:T(8,128)(2,1)S(1)} %concatenate.3.tiles_ref) | copy-start | bytes 12779524
  76.4 33.2 %collective-permute-start.6 = (bf16[2,128,512]{2,1,0:T(8,128)(2,1)S(1)}, bf16[2,128,512]{2,1,0:T(8,128)(2,1)S(1)}, u32[]{:S(2)}, u32[]{:S(2)}) collective-permute-start(bf16[2,128,512]{2,1,0:T(8,128)(2,1)S(1)} %copy-done.14), channel_id=1, source_target_pairs={{0,20},{1,21},{2,22},{3,23},{4,16},{5,17},{6,18},{7,19},{8,28},{9,... | collective-permute-start | bytes 786440 | tf_op jit(solution)/shard_map/ppermute | solution.py:479
  79.3 32.2 %collective-permute-start.7 = (bf16[2,128,512]{2,1,0:T(8,128)(2,1)S(1)}, bf16[2,128,512]{2,1,0:T(8,128)(2,1)S(1)}, u32[]{:S(2)}, u32[]{:S(2)}) collective-permute-start(bf16[2,128,512]{2,1,0:T(8,128)(2,1)S(1)} %copy-done.12), channel_id=1, source_target_pairs={{0,3},{1,2},{2,1},{3,0},{4,7},{5,6},{6,5},{7,4},{8,11},{9,10},{10,... | collective-permute-start | bytes 786440 | tf_op jit(solution)/shard_map/ppermute | solution.py:479
  79.4 34.9 %collective-permute-start.8 = (bf16[2,128,512]{2,1,0:T(8,128)(2,1)S(1)}, bf16[2,128,512]{2,1,0:T(8,128)(2,1)S(1)}, u32[]{:S(2)}, u32[]{:S(2)}) collective-permute-start(bf16[2,128,512]{2,1,0:T(8,128)(2,1)S(1)} %copy-done.10), channel_id=1, source_target_pairs={{0,21},{1,20},{2,23},{3,22},{4,17},{5,16},{6,19},{7,18},{8,29},{9,... | collective-permute-start | bytes 786440 | tf_op jit(solution)/shard_map/ppermute | solution.py:479
  93.6 25.0 %collective-permute-start.9 = (bf16[2,128,512]{2,1,0:T(8,128)(2,1)S(1)}, bf16[2,128,512]{2,1,0:T(8,128)(2,1)S(1)}, u32[]{:S(2)}, u32[]{:S(2)}) collective-permute-start(bf16[2,128,512]{2,1,0:T(8,128)(2,1)S(1)} %copy-done.8), channel_id=1, source_target_pairs={{0,4},{1,5},{2,6},{3,7},{4,0},{5,1},{6,2},{7,3},{8,12},{9,13},{10,... | collective-permute-start | bytes 786440 | tf_op jit(solution)/shard_map/ppermute | solution.py:479
  93.6 40.4 %collective-permute-start = (bf16[2,128,512]{2,1,0:T(8,128)(2,1)S(1)}, bf16[2,128,512]{2,1,0:T(8,128)(2,1)S(1)}, u32[]{:S(2)}, u32[]{:S(2)}) collective-permute-start(bf16[2,128,512]{2,1,0:T(8,128)(2,1)S(1)} %copy-done.22), channel_id=1, source_target_pairs={{0,16},{1,17},{2,18},{3,19},{4,20},{5,21},{6,22},{7,23},{8,24},{9,... | collective-permute-start | bytes 786440 | tf_op jit(solution)/shard_map/ppermute | solution.py:479
  94.9 41.2 %copy-start.3 = (bf16[4096,512]{1,0:T(8,128)(2,1)S(1)}, bf16[4096,512]{1,0:T(8,128)(2,1)}, u32[]{:S(2)}) copy-start(bf16[4096,512]{1,0:T(8,128)(2,1)} %param.7) | copy-start | bytes 12582916
  109.6 26.4 %copy-start.31 = (bf16[2,128,512]{2,1,0:T(8,128)(2,1)}, bf16[2,128,512]{2,1,0:T(8,128)(2,1)S(1)}, u32[]{:S(2)}) copy-start(bf16[2,128,512]{2,1,0:T(8,128)(2,1)S(1)} %collective-permute-done.6.rest_6_) | copy-start | bytes 786436
  109.6 63.7 %collective-permute-start.1 = (bf16[2,128,512]{2,1,0:T(8,128)(2,1)}, bf16[2,128,512]{2,1,0:T(8,128)(2,1)}, u32[]{:S(2)}, u32[]{:S(2)}) collective-permute-start(bf16[2,128,512]{2,1,0:T(8,128)(2,1)} %get-tuple-element.49), channel_id=1, source_target_pairs={{0,17},{1,16},{2,19},{3,18},{4,21},{5,20},{6,23},{7,22},{8,25},{9,... | collective-permute-start | bytes 786440 | tf_op jit(solution)/shard_map/ppermute | solution.py:479
  111.5 24.5 %copy-start.32 = (bf16[2,128,512]{2,1,0:T(8,128)(2,1)}, bf16[2,128,512]{2,1,0:T(8,128)(2,1)S(1)}, u32[]{:S(2)}) copy-start(bf16[2,128,512]{2,1,0:T(8,128)(2,1)S(1)} %collective-permute-done.7.rest_7_) | copy-start | bytes 786436
  111.5 61.8 %collective-permute-start.2 = (bf16[2,128,512]{2,1,0:T(8,128)(2,1)}, bf16[2,128,512]{2,1,0:T(8,128)(2,1)}, u32[]{:S(2)}, u32[]{:S(2)}) collective-permute-start(bf16[2,128,512]{2,1,0:T(8,128)(2,1)} %get-tuple-element.50), channel_id=1, source_target_pairs={{0,18},{1,19},{2,16},{3,17},{4,22},{5,23},{6,20},{7,21},{8,26},{9,... | collective-permute-start | bytes 786440 | tf_op jit(solution)/shard_map/ppermute | solution.py:479
  114.3 65.2 %collective-permute-start.18 = (bf16[2,128,512]{2,1,0:T(8,128)(2,1)S(1)}, bf16[2,128,512]{2,1,0:T(8,128)(2,1)}, u32[]{:S(2)}, u32[]{:S(2)}) collective-permute-start(bf16[2,128,512]{2,1,0:T(8,128)(2,1)S(1)} %get-tuple-element.67), channel_id=1, source_target_pairs={{0,26},{1,27},{2,24},{3,25},{4,30},{5,31},{6,28},{7,29},{8,18},{9,... | collective-permute-start | bytes 786440 | tf_op jit(solution)/shard_map/ppermute | solution.py:479
  118.6 60.9 %collective-permute-start.19 = (bf16[2,128,512]{2,1,0:T(8,128)(2,1)S(1)}, bf16[2,128,512]{2,1,0:T(8,128)(2,1)}, u32[]{:S(2)}, u32[]{:S(2)}) collective-permute-start(bf16[2,128,512]{2,1,0:T(8,128)(2,1)S(1)} %get-tuple-element.68), channel_id=1, source_target_pairs={{0,9},{1,8},{2,11},{3,10},{4,13},{5,12},{6,15},{7,14},{8,1},{9,0},... | collective-permute-start | bytes 786440 | tf_op jit(solution)/shard_map/ppermute | solution.py:479
  134.0 48.6 %collective-permute-start.20 = (bf16[2,128,512]{2,1,0:T(8,128)(2,1)S(1)}, bf16[2,128,512]{2,1,0:T(8,128)(2,1)}, u32[]{:S(2)}, u32[]{:S(2)}) collective-permute-start(bf16[2,128,512]{2,1,0:T(8,128)(2,1)S(1)} %get-tuple-element.69), channel_id=1, source_target_pairs={{0,27},{1,26},{2,25},{3,24},{4,31},{5,30},{6,29},{7,28},{8,19},{9,... | collective-permute-start | bytes 786440 | tf_op jit(solution)/shard_map/ppermute | solution.py:479
  173.3 36.5 %collective-permute-start.21 = (bf16[2,128,512]{2,1,0:T(8,128)(2,1)S(1)}, bf16[2,128,512]{2,1,0:T(8,128)(2,1)S(1)}, u32[]{:S(2)}, u32[]{:S(2)}) collective-permute-start(bf16[2,128,512]{2,1,0:T(8,128)(2,1)S(1)} %get-tuple-element.70), channel_id=1, source_target_pairs={{0,10},{1,11},{2,8},{3,9},{4,14},{5,15},{6,12},{7,13},{8,2},{9,3},... | collective-permute-start | bytes 786440 | tf_op jit(solution)/shard_map/ppermute | solution.py:479
  173.3 41.3 %collective-permute-start.22 = (bf16[2,128,512]{2,1,0:T(8,128)(2,1)S(1)}, bf16[2,128,512]{2,1,0:T(8,128)(2,1)S(1)}, u32[]{:S(2)}, u32[]{:S(2)}) collective-permute-start(bf16[2,128,512]{2,1,0:T(8,128)(2,1)S(1)} %get-tuple-element.71), channel_id=1, source_target_pairs={{0,28},{1,29},{2,30},{3,31},{4,24},{5,25},{6,26},{7,27},{8,20},{9,... | collective-permute-start | bytes 786440 | tf_op jit(solution)/shard_map/ppermute | solution.py:479
  179.5 36.4 %collective-permute-start.23 = (bf16[2,128,512]{2,1,0:T(8,128)(2,1)S(1)}, bf16[2,128,512]{2,1,0:T(8,128)(2,1)S(1)}, u32[]{:S(2)}, u32[]{:S(2)}) collective-permute-start(bf16[2,128,512]{2,1,0:T(8,128)(2,1)S(1)} %get-tuple-element.72), channel_id=1, source_target_pairs={{0,11},{1,10},{2,9},{3,8},{4,15},{5,14},{6,13},{7,12},{8,3},{9,2},... | collective-permute-start | bytes 786440 | tf_op jit(solution)/shard_map/ppermute | solution.py:479
  179.5 38.7 %collective-permute-start.24 = (bf16[2,128,512]{2,1,0:T(8,128)(2,1)S(1)}, bf16[2,128,512]{2,1,0:T(8,128)(2,1)S(1)}, u32[]{:S(2)}, u32[]{:S(2)}) collective-permute-start(bf16[2,128,512]{2,1,0:T(8,128)(2,1)S(1)} %get-tuple-element.73), channel_id=1, source_target_pairs={{0,29},{1,28},{2,31},{3,30},{4,25},{5,24},{6,27},{7,26},{8,21},{9,... | collective-permute-start | bytes 786440 | tf_op jit(solution)/shard_map/ppermute | solution.py:479
  182.6 41.1 %collective-permute-start.25 = (bf16[2,128,512]{2,1,0:T(8,128)(2,1)S(1)}, bf16[2,128,512]{2,1,0:T(8,128)(2,1)S(1)}, u32[]{:S(2)}, u32[]{:S(2)}) collective-permute-start(bf16[2,128,512]{2,1,0:T(8,128)(2,1)S(1)} %get-tuple-element.74), channel_id=1, source_target_pairs={{0,12},{1,13},{2,14},{3,15},{4,8},{5,9},{6,10},{7,11},{8,4},{9,5},... | collective-permute-start | bytes 786440 | tf_op jit(solution)/shard_map/ppermute | solution.py:479
  187.0 37.4 %copy-start.24 = (bf16[2,512,2048]{2,1,0:T(8,128)(2,1)S(1)}, bf16[2,512,2048]{2,1,0:T(8,128)(2,1)}, u32[]{:S(2)}) copy-start(bf16[2,512,2048]{2,1,0:T(8,128)(2,1)} %copy-done.23) | copy-start | bytes 12582916
  209.9 18.5 %collective-permute-start.26 = (bf16[2,128,512]{2,1,0:T(8,128)(2,1)S(1)}, bf16[2,128,512]{2,1,0:T(8,128)(2,1)S(1)}, u32[]{:S(2)}, u32[]{:S(2)}) collective-permute-start(bf16[2,128,512]{2,1,0:T(8,128)(2,1)S(1)} %get-tuple-element.76), channel_id=1, source_target_pairs={{0,30},{1,31},{2,28},{3,29},{4,26},{5,27},{6,24},{7,25},{8,22},{9,... | collective-permute-start | bytes 786440 | tf_op jit(solution)/shard_map/ppermute | solution.py:479
  214.7 18.7 %collective-permute-start.27 = (bf16[2,128,512]{2,1,0:T(8,128)(2,1)S(1)}, bf16[2,128,512]{2,1,0:T(8,128)(2,1)S(1)}, u32[]{:S(2)}, u32[]{:S(2)}) collective-permute-start(bf16[2,128,512]{2,1,0:T(8,128)(2,1)S(1)} %get-tuple-element.77), channel_id=1, source_target_pairs={{0,13},{1,12},{2,15},{3,14},{4,9},{5,8},{6,11},{7,10},{8,5},{9,4},... | collective-permute-start | bytes 786440 | tf_op jit(solution)/shard_map/ppermute | solution.py:479
  215.9 18.3 %collective-permute-start.28 = (bf16[2,128,512]{2,1,0:T(8,128)(2,1)S(1)}, bf16[2,128,512]{2,1,0:T(8,128)(2,1)S(1)}, u32[]{:S(2)}, u32[]{:S(2)}) collective-permute-start(bf16[2,128,512]{2,1,0:T(8,128)(2,1)S(1)} %get-tuple-element.78), channel_id=1, source_target_pairs={{0,31},{1,30},{2,29},{3,28},{4,27},{5,26},{6,25},{7,24},{8,23},{9,... | collective-permute-start | bytes 786440 | tf_op jit(solution)/shard_map/ppermute | solution.py:479
  218.2 24.6 %collective-permute-start.29 = (bf16[2,128,512]{2,1,0:T(8,128)(2,1)S(1)}, bf16[2,128,512]{2,1,0:T(8,128)(2,1)S(1)}, u32[]{:S(2)}, u32[]{:S(2)}) collective-permute-start(bf16[2,128,512]{2,1,0:T(8,128)(2,1)S(1)} %get-tuple-element.79), channel_id=1, source_target_pairs={{0,14},{1,15},{2,12},{3,13},{4,10},{5,11},{6,8},{7,9},{8,6},{9,7},... | collective-permute-start | bytes 786440 | tf_op jit(solution)/shard_map/ppermute | solution.py:479
  223.7 23.4 %collective-permute-start.30 = (bf16[2,128,512]{2,1,0:T(8,128)(2,1)S(1)}, bf16[2,128,512]{2,1,0:T(8,128)(2,1)S(1)}, u32[]{:S(2)}, u32[]{:S(2)}) collective-permute-start(bf16[2,128,512]{2,1,0:T(8,128)(2,1)S(1)} %get-tuple-element.80), channel_id=1, source_target_pairs={{0,15},{1,14},{2,13},{3,12},{4,11},{5,10},{6,9},{7,8},{8,7},{9,6},... | collective-permute-start | bytes 786440 | tf_op jit(solution)/shard_map/ppermute | solution.py:479
  224.4 23.4 %copy-start.26 = (bf16[2,512,1280]{2,1,0:T(8,128)(2,1)S(1)}, bf16[2,512,1280]{2,1,0:T(8,128)(2,1)}, u32[]{:S(2)}) copy-start(bf16[2,512,1280]{2,1,0:T(8,128)(2,1)} %copy-done.25) | copy-start | bytes 7864324
  250.8 2.7 collective-permute-start.31
  253.7 7.3 %collective-permute-start.32 = (bf16[4,16,1024]{2,1,0:T(8,128)(2,1)S(1)}, bf16[4,16,1024]{2,1,0:T(8,128)(2,1)S(1)}, u32[]{:S(2)}, u32[]{:S(2)}) collective-permute-start(bf16[4,16,1024]{2,1,0:T(8,128)(2,1)S(1)} %get-tuple-element.84), channel_id=1, source_target_pairs={{0,6},{1,7},{2,4},{3,5},{4,2},{5,3},{6,0},{7,1},{8,14},{9,15},{10,... | collective-permute-start | bytes 393224 | tf_op jit(solution)/shard_map/ppermute | solution.py:479
  255.4 8.4 %collective-permute-start.33 = (bf16[4,16,1024]{2,1,0:T(8,128)(2,1)S(1)}, bf16[4,16,1024]{2,1,0:T(8,128)(2,1)S(1)}, u32[]{:S(2)}, u32[]{:S(2)}) collective-permute-start(bf16[4,16,1024]{2,1,0:T(8,128)(2,1)S(1)} %get-tuple-element.85), channel_id=1, source_target_pairs={{0,2},{1,3},{2,0},{3,1},{4,6},{5,7},{6,4},{7,5},{8,10},{9,11},{10,... | collective-permute-start | bytes 393224 | tf_op jit(solution)/shard_map/ppermute | solution.py:479
  257.5 6.3 %collective-permute-start.34 = (bf16[4,16,1024]{2,1,0:T(8,128)(2,1)S(1)}, bf16[4,16,1024]{2,1,0:T(8,128)(2,1)S(1)}, u32[]{:S(2)}, u32[]{:S(2)}) collective-permute-start(bf16[4,16,1024]{2,1,0:T(8,128)(2,1)S(1)} %get-tuple-element.86), channel_id=1, source_target_pairs={{0,4},{1,5},{2,6},{3,7},{4,0},{5,1},{6,2},{7,3},{8,12},{9,13},{10,... | collective-permute-start | bytes 393224 | tf_op jit(solution)/shard_map/ppermute | solution.py:479
  263.9 8.2 %collective-permute-start.35 = (f32[16,1024]{1,0:T(8,128)S(1)}, f32[16,1024]{1,0:T(8,128)S(1)}, u32[]{:S(2)}, u32[]{:S(2)}) collective-permute-start(f32[16,1024]{1,0:T(8,128)S(1)} %get-tuple-element.88), channel_id=1, source_target_pairs={{0,16},{1,17},{2,18},{3,19},{4,20},{5,21},{6,22},{7,23},{8,24},{9,... | collective-permute-start | bytes 196616 | tf_op jit(solution)/shard_map/ppermute | solution.py:479
  266.1 6.7 %collective-permute-start.36 = (f32[16,1024]{1,0:T(8,128)S(1)}, f32[16,1024]{1,0:T(8,128)S(1)}, u32[]{:S(2)}, u32[]{:S(2)}) collective-permute-start(f32[16,1024]{1,0:T(8,128)S(1)} %get-tuple-element.89), channel_id=1, source_target_pairs={{0,24},{1,25},{2,26},{3,27},{4,28},{5,29},{6,30},{7,31},{8,16},{9,... | collective-permute-start | bytes 196616 | tf_op jit(solution)/shard_map/ppermute | solution.py:479
  268.7 4.7 %collective-permute-start.37 = (f32[16,1024]{1,0:T(8,128)S(1)}, f32[16,1024]{1,0:T(8,128)S(1)}, u32[]{:S(2)}, u32[]{:S(2)}) collective-permute-start(f32[16,1024]{1,0:T(8,128)S(1)} %get-tuple-element.90), channel_id=1, source_target_pairs={{0,8},{1,9},{2,10},{3,11},{4,12},{5,13},{6,14},{7,15},{8,0},{9,1},... | collective-permute-start | bytes 196616 | tf_op jit(solution)/shard_map/ppermute | solution.py:479
  (36 other events, 226.8 us)

commit v5 on v4

--- a/solution.py
+++ b/solution.py
@@ -374,14 +374,9 @@
 
 def late_kernel(count, rank_ref, in_ref, adjoint_ref, *rest):
     arrivals, rest = rest[:count], rest[count:]
-    outs, (sum_ref, pool_ref, sems) = rest[:-3], rest[-3:]
-    blocks, rows, vectors = pool_ref.shape
-    loads = pool_loads(arrivals, pool_ref, sems)
-    for copy in loads:
-        copy.start()
-    for copy in loads:
-        copy.wait()
-    pool = pool_ref[...].reshape(blocks * rows, vectors)
+    outs, sum_ref = rest[:-1], rest[-1]
+    vectors = arrivals[0].shape[2]
+    pool = jnp.concatenate([ref[...].reshape(-1, vectors) for ref in arrivals], axis=0)
     for d in range(2):
         side = (slice(None), slice(d * vectors, (d + 1) * vectors))
         sum_ref[side] = in_ref[side] + jnp.dot(adjoint_ref[d], pool, preferred_element_type=F32)
@@ -401,7 +396,6 @@
 def late(rank, sums, adjoint, arrivals, devices, sent, last):
     columns, both = sums.shape
     own = columns // devices
-    cap, rows, vectors = arrivals[0].shape
     block = pl.BlockSpec(memory_space=VMEM)
     if not last or own % 8:
         halves = [VMEM(sums.shape, F32)]
@@ -411,20 +405,13 @@
     return pl.pallas_call(
         functools.partial(late_kernel, len(arrivals)),
         out_shape=halves,
-        in_specs=[pl.BlockSpec(memory_space=SMEM), block, block]
-        + [pl.BlockSpec(memory_space=HBM)] * len(arrivals),
+        in_specs=[pl.BlockSpec(memory_space=SMEM)] + [block] * (2 + len(arrivals)),
         out_specs=[block] * len(halves),
-        scratch_shapes=[
-            VMEM(sums.shape, F32),
-            VMEM((len(arrivals) * cap, rows, vectors), BF16),
-            pltpu.SemaphoreType.DMA((len(arrivals),)),
-        ],
-        compiler_params=pltpu.CompilerParams(
-            vmem_limit_bytes=2 * ROOM + sum(2 * a.size for a in arrivals)
-        ),
+        scratch_shapes=[VMEM(sums.shape, F32)],
+        compiler_params=pltpu.CompilerParams(vmem_limit_bytes=2 * ROOM),
         cost_estimate=pl.CostEstimate(flops=4 * 10**9, bytes_accessed=12 * 2**20, transcendentals=0),
         name="late",
-    )(rank, in_vmem(sums), in_vmem(adjoint), *map(in_hbm, arrivals))
+    )(rank, *map(in_vmem, (sums, adjoint, *arrivals)))
 
 
 def split_kernel(width, shift, count, final, scale, rank_ref, keep_ref, *rest):

time: 274 us -> 272 us (level)
    unnamed x93 -> x73, local copies, waits for them, and re-layouts: 17.8 us -> 16.4 us
where the time goes in v5:
time: 272 us
  Pallas kernels  85.5 us (31%)
  starting transfers between devices  80.7 us (30%)
  waiting for transfers between devices  76.6 us (28%)
  local copies, waits for them, and re-layouts  27 us (10%)
    ppermute x38, starting transfers between devices, swap(): return lax.ppermute(value, 'rows', [(i, i ^ mask) for i in range(devices)])  80.7 us
    ppermute x38, waiting for transfers between devices, swap(): return lax.ppermute(value, 'rows', [(i, i ^ mask) for i in range(devices)])  76.6 us
    pallas_call x1, Pallas kernels, adjoint(): pl.pallas_call(functools.partial(adjoint_kernel, phase, slots, count), ou...  27.6 us
    pallas_call x1, Pallas kernels, gram(): pl.pallas_call(functools.partial(gram_kernel, phase, len(arrivals), slots...  22.9 us
    unnamed x73, local copies, waits for them, and re-layouts  16.4 us
    pallas_call x1, Pallas kernels, hops(): pl.pallas_call(functools.partial(hops_kernel, slots, fixed), out_shape=HB...  14.7 us
    pallas_call x1, Pallas kernels, pack(): pl.pallas_call(functools.partial(pack_kernel, masks, len(after)), out_sha...  11.5 us
    reshape x1, local copies, waits for them, and re-layouts, body(): left_t = left.reshape(-1, bunch, vectors).transpose(0, 2, 1)  6.26 us
  transfers between devices with their start and end apart: 38, of which 13 were waited for; matrix products, arithmetic and copies ran while one was open for 4% of the time, Pallas kernels for 26%

profile of v5, /device:TPU:0, one launch (start us, length us, event | category | flops | bytes accessed | tf_op | source)
XLA Modules:
  0.0 272.0 jit_solution(12153119182546094604)
XLA Ops:
  0.8 11.5 %pack.1 = (bf16[2,128,512]{2,1,0:T(8,128)(2,1)S(1)}, bf16[2,128,512]{2,1,0:T(8,128)(2,1)S(1)}, bf16[2,128,512]{2,1,0:T(8,128)(2,1)S(1)}, bf16[2,128,512]{2,1,0:T...) custom-call(s32[1]{0:T(128)} %bitcast.rank_ref, ...), custom_call_target="tpu_custom_call" | custom-call | tf_op jit(solution)/shard_map/pack/pallas_call | solution.py:104
  19.3 5.9 %collective-permute-start.10 = (bf16[2,128,512]{2,1,0:T(8,128)(2,1)}, bf16[2,128,512]{2,1,0:T(8,128)(2,1)}, u32[]{:S(2)}, u32[]{:S(2)}) collective-permute-start(bf16[2,128,512]{2,1,0:T(8,128)(2,1)} %get-tuple-element.58), channel_id=1, source_target_pairs={{0,22},{1,23},{2,20},{3,21},{4,18},{5,19},{6,16},{7,17},{8,30},{9,... | collective-permute-start | bytes 786440 | tf_op jit(solution)/shard_map/ppermute | solution.py:466
  25.3 1.5 collective-permute-start.12
  26.7 1.4 collective-permute-start.13
  28.2 4.0 %collective-permute-start.14 = (bf16[2,128,512]{2,1,0:T(8,128)(2,1)}, bf16[2,128,512]{2,1,0:T(8,128)(2,1)}, u32[]{:S(2)}, u32[]{:S(2)}) collective-permute-start(bf16[2,128,512]{2,1,0:T(8,128)(2,1)} %get-tuple-element.62), channel_id=1, source_target_pairs={{0,24},{1,25},{2,26},{3,27},{4,28},{5,29},{6,30},{7,31},{8,16},{9,... | collective-permute-start | bytes 786440 | tf_op jit(solution)/shard_map/ppermute | solution.py:466
  34.7 14.9 %collective-permute-done.10.rest_10_ = bf16[2,128,512]{2,1,0:T(8,128)(2,1)} collective-permute-done((bf16[2,128,512]{2,1,0:T(8,128)(2,1)}, bf16[2,128,512]{2,1,0:T(8,128)(2,1)}, u32[]{:S(2)}, u32[]{:S(2)}) %collective-permute-start.10) | collective-permute-done | bytes 262176 | tf_op jit(solution)/shard_map/ppermute | solution.py:466
  49.6 0.9 collective-permute-start.15
  50.7 4.0 %collective-permute-start.16 = (bf16[2,128,512]{2,1,0:T(8,128)(2,1)}, bf16[2,128,512]{2,1,0:T(8,128)(2,1)}, u32[]{:S(2)}, u32[]{:S(2)}) collective-permute-start(bf16[2,128,512]{2,1,0:T(8,128)(2,1)} %copy-done.19), channel_id=1, source_target_pairs={{0,25},{1,24},{2,27},{3,26},{4,29},{5,28},{6,31},{7,30},{8,17},{9,... | collective-permute-start | bytes 786440 | tf_op jit(solution)/shard_map/ppermute | solution.py:466
  55.2 13.0 %collective-permute-start.4 = (bf16[2,128,512]{2,1,0:T(8,128)(2,1)}, bf16[2,128,512]{2,1,0:T(8,128)(2,1)}, u32[]{:S(2)}, u32[]{:S(2)}) collective-permute-start(bf16[2,128,512]{2,1,0:T(8,128)(2,1)} %copy-done.16), channel_id=1, source_target_pairs={{0,19},{1,18},{2,17},{3,16},{4,23},{5,22},{6,21},{7,20},{8,27},{9,... | collective-permute-start | bytes 786440 | tf_op jit(solution)/shard_map/ppermute | solution.py:466
  68.1 1.2 collective-permute-start.5
  69.4 2.8 %first_pack.1 = (bf16[2,128,512]{2,1,0:T(8,128)(2,1)S(1)}, bf16[2,128,512]{2,1,0:T(8,128)(2,1)}, bf16[2,128,512]{2,1,0:T(8,128)(2,1)}) custom-call(s32[1]{0:T(128)} %bitcast.rank_ref, s32[2,32]{1,0:T(2,128)} %bitcast.20, bf16[32,128,512]{2,1,0:T(8,128)(2,1)} %bitcast.15), custom_call_target="tpu_custom_call" | custom-call | tf_op jit(solution)/shard_map/first_pack/pallas_call | solution.py:69
  73.2 3.2 %concatenate.3.tiles_ref = bf16[2,65,128,128]{3,2,1,0:T(8,128)(2,1)S(1)} pad(bf16[2,64,128,128]{3,2,1,0:T(8,128)(2,1)} %param.9, bf16[]{:T(256)} %constant.66.clone.1), padding=0_0x0_1x0_0x0_0 | pad | bytes 8454146 | tf_op jit(solution)/shard_map/concatenate | solution.py:493
  76.4 2.9 %collective-permute-start.6 = (bf16[2,128,512]{2,1,0:T(8,128)(2,1)S(1)}, bf16[2,128,512]{2,1,0:T(8,128)(2,1)S(1)}, u32[]{:S(2)}, u32[]{:S(2)}) collective-permute-start(bf16[2,128,512]{2,1,0:T(8,128)(2,1)S(1)} %copy-done.14), channel_id=1, source_target_pairs={{0,20},{1,21},{2,22},{3,23},{4,16},{5,17},{6,18},{7,19},{8,28},{9,... | collective-permute-start | bytes 786440 | tf_op jit(solution)/shard_map/ppermute | solution.py:466
  79.5 1.4 collective-permute-start.8
  80.9 12.7 %collective-permute-done.4.rest_4_ = bf16[2,128,512]{2,1,0:T(8,128)(2,1)} collective-permute-done((bf16[2,128,512]{2,1,0:T(8,128)(2,1)}, bf16[2,128,512]{2,1,0:T(8,128)(2,1)}, u32[]{:S(2)}, u32[]{:S(2)}) %collective-permute-start.4) | collective-permute-done | bytes 262176 | tf_op jit(solution)/shard_map/ppermute | solution.py:466
  93.6 1.3 collective-permute-start
  94.9 14.7 %hops.1.in_ref = f32[64,128,512]{2,1,0:T(8,128)} custom-call(s32[3,1024]{1,0:T(4,128)S(1)} %add.78.lists_ref, s32[3,64]{1,0:T(4,128)S(1)} %get-tuple-element.91.counts_ref, bf16[2,65,128,128]{3,2,1,0:T(8,128)(2,1)S(1)} %concatenate.3.tiles_ref, bf16[32,128,512]{2,1,0:T(8,128)(2,1)S(1)} %bitcast.16), custom_call_target="tpu_custom_call" | custom-call | flops 8000000000 | bytes 41943040 | tf_op jit(solution)/shard_map/hops/pallas_call | solution.py:217
  109.6 1.9 collective-permute-start.1
  111.5 2.8 %collective-permute-start.2 = (bf16[2,128,512]{2,1,0:T(8,128)(2,1)}, bf16[2,128,512]{2,1,0:T(8,128)(2,1)}, u32[]{:S(2)}, u32[]{:S(2)}) collective-permute-start(bf16[2,128,512]{2,1,0:T(8,128)(2,1)} %get-tuple-element.50), channel_id=1, source_target_pairs={{0,18},{1,19},{2,16},{3,17},{4,22},{5,23},{6,20},{7,21},{8,26},{9,... | collective-permute-start | bytes 786440 | tf_op jit(solution)/shard_map/ppermute | solution.py:466
  114.3 4.3 %collective-permute-start.18 = (bf16[2,128,512]{2,1,0:T(8,128)(2,1)S(1)}, bf16[2,128,512]{2,1,0:T(8,128)(2,1)}, u32[]{:S(2)}, u32[]{:S(2)}) collective-permute-start(bf16[2,128,512]{2,1,0:T(8,128)(2,1)S(1)} %get-tuple-element.67), channel_id=1, source_target_pairs={{0,26},{1,27},{2,24},{3,25},{4,30},{5,31},{6,28},{7,29},{8,18},{9,... | collective-permute-start | bytes 786440 | tf_op jit(solution)/shard_map/ppermute | solution.py:466
  118.6 15.4 %collective-permute-done.rest_0_ = bf16[2,128,512]{2,1,0:T(8,128)(2,1)S(1)} collective-permute-done((bf16[2,128,512]{2,1,0:T(8,128)(2,1)S(1)}, bf16[2,128,512]{2,1,0:T(8,128)(2,1)S(1)}, u32[]{:S(2)}, u32[]{:S(2)}) %collective-permute-start) | collective-permute-done | bytes 262176 | tf_op jit(solution)/shard_map/ppermute | solution.py:466
  134.0 2.0 collective-permute-start.20
  136.1 27.6 %adjoint.1 = (bf16[2,512,2048]{2,1,0:T(8,128)(2,1)S(1)}, bf16[2,512,1280]{2,1,0:T(8,128)(2,1)S(1)}) custom-call(s32[3,1024]{1,0:T(4,128)S(1)} %add.78.lists_ref, s32[3,64]{1,0:T(4,128)S(1)} %get-tuple-element.91.counts_ref, bf16[2,65,128,128]{3,2,1,0:T(8,128)(2,1)S(1)} %concatenate.3.tiles_ref, bf16[32,128,512]{2,1,0:T(8,128)(2,1)S(1)} %bitcast.18), custom_call_target="tpu_custom_call" | custom-call | flops 8000000000 | bytes 16777216 | tf_op jit(solution)/shard_map/adjoint/pallas_call | solution.py:271
  163.7 2.0 copy-done.23
  165.7 1.5 copy-done.25
  167.2 6.3 %copy.20 = bf16[4,1024,512]{1,2,0:T(8,128)(2,1)} copy(bf16[4,1024,512]{2,1,0:T(8,128)(2,1)} %bitcast.17) | data formatting | bytes 8388608 | tf_op jit(solution)/shard_map/reshape | solution.py:495
  173.4 6.1 %collective-permute-start.22 = (bf16[2,128,512]{2,1,0:T(8,128)(2,1)S(1)}, bf16[2,128,512]{2,1,0:T(8,128)(2,1)S(1)}, u32[]{:S(2)}, u32[]{:S(2)}) collective-permute-start(bf16[2,128,512]{2,1,0:T(8,128)(2,1)S(1)} %get-tuple-element.71), channel_id=1, source_target_pairs={{0,28},{1,29},{2,30},{3,31},{4,24},{5,25},{6,26},{7,27},{8,20},{9,... | collective-permute-start | bytes 786440 | tf_op jit(solution)/shard_map/ppermute | solution.py:466
  179.6 3.0 %collective-permute-start.24 = (bf16[2,128,512]{2,1,0:T(8,128)(2,1)S(1)}, bf16[2,128,512]{2,1,0:T(8,128)(2,1)S(1)}, u32[]{:S(2)}, u32[]{:S(2)}) collective-permute-start(bf16[2,128,512]{2,1,0:T(8,128)(2,1)S(1)} %get-tuple-element.73), channel_id=1, source_target_pairs={{0,29},{1,28},{2,31},{3,30},{4,25},{5,24},{6,27},{7,26},{8,21},{9,... | collective-permute-start | bytes 786440 | tf_op jit(solution)/shard_map/ppermute | solution.py:466
  182.6 2.2 copy-done.2
  184.8 2.2 copy-done.4
  187.0 22.9 %gram.1.in_ref = f32[512,1024]{1,0:T(8,128)S(1)} custom-call(s32[3,1024]{1,0:T(4,128)S(1)} %add.78.lists_ref, s32[3,64]{1,0:T(4,128)S(1)} %get-tuple-element.91.counts_ref, bf16[2,65,128,128]{3,2,1,0:T(8,128)(2,1)S(1)} %copy-done.2, f32[64,128,512]{2,1,0:T(8,128)} %hops.1.in_ref, bf16[4,512,1024]{2,1,0:T(8,128)(2,1)S(1)} %bitcast.19, ...), custom_call_target="tpu_custom_call" | custom-call | flops 12000000000 | bytes 25165824 | tf_op jit(solution)/shard_map/gram/pallas_call | solution.py:354
  209.9 4.8 %collective-permute-start.26 = (bf16[2,128,512]{2,1,0:T(8,128)(2,1)S(1)}, bf16[2,128,512]{2,1,0:T(8,128)(2,1)S(1)}, u32[]{:S(2)}, u32[]{:S(2)}) collective-permute-start(bf16[2,128,512]{2,1,0:T(8,128)(2,1)S(1)} %get-tuple-element.76), channel_id=1, source_target_pairs={{0,30},{1,31},{2,28},{3,29},{4,26},{5,27},{6,24},{7,25},{8,22},{9,... | collective-permute-start | bytes 786440 | tf_op jit(solution)/shard_map/ppermute | solution.py:466
  214.7 1.1 collective-permute-start.27
  215.9 2.4 collective-permute-start.28
  218.3 5.4 %collective-permute-start.29 = (bf16[2,128,512]{2,1,0:T(8,128)(2,1)S(1)}, bf16[2,128,512]{2,1,0:T(8,128)(2,1)S(1)}, u32[]{:S(2)}, u32[]{:S(2)}) collective-permute-start(bf16[2,128,512]{2,1,0:T(8,128)(2,1)S(1)} %get-tuple-element.79), channel_id=1, source_target_pairs={{0,14},{1,15},{2,12},{3,13},{4,10},{5,11},{6,8},{7,9},{8,6},{9,7},... | collective-permute-start | bytes 786440 | tf_op jit(solution)/shard_map/ppermute | solution.py:466
  223.7 3.6 %late.2.in_ref = f32[512,1024]{1,0:T(8,128)S(1)} custom-call(s32[1]{0:T(128)} %bitcast.rank_ref, f32[512,1024]{1,0:T(8,128)S(1)} %gram.1.in_ref, bf16[2,512,2048]{2,1,0:T(8,128)(2,1)S(1)} %copy-done.24, bf16[2,128,512]{2,1,0:T(8,128)(2,1)} %collective-permute-done.18.rest_0_, bf16[2,128,512]{2,1,0:T(8,128)(2,1)} %collective-permute-done.19.rest_1_, ...), custom_call_target="tpu_custom_call" | custom-call | flops 4000000000 | bytes 12582912 | tf_op jit(solution)/shard_map/late/pallas_call | solution.py:405
  227.3 6.1 %collective-permute-done.27.rest_1_ = bf16[2,128,512]{2,1,0:T(8,128)(2,1)S(1)} collective-permute-done((bf16[2,128,512]{2,1,0:T(8,128)(2,1)S(1)}, bf16[2,128,512]{2,1,0:T(8,128)(2,1)S(1)}, u32[]{:S(2)}, u32[]{:S(2)}) %collective-permute-start.27) | collective-permute-done | bytes 262176 | tf_op jit(solution)/shard_map/ppermute | solution.py:466
  234.3 8.7 %collective-permute-done.29.rest_3_ = bf16[2,128,512]{2,1,0:T(8,128)(2,1)S(1)} collective-permute-done((bf16[2,128,512]{2,1,0:T(8,128)(2,1)S(1)}, bf16[2,128,512]{2,1,0:T(8,128)(2,1)S(1)}, u32[]{:S(2)}, u32[]{:S(2)}) %collective-permute-start.29) | collective-permute-done | bytes 262176 | tf_op jit(solution)/shard_map/ppermute | solution.py:466
  243.0 4.3 %collective-permute-done.30.rest_4_ = bf16[2,128,512]{2,1,0:T(8,128)(2,1)S(1)} collective-permute-done((bf16[2,128,512]{2,1,0:T(8,128)(2,1)S(1)}, bf16[2,128,512]{2,1,0:T(8,128)(2,1)S(1)}, u32[]{:S(2)}, u32[]{:S(2)}) %collective-permute-start.30) | collective-permute-done | bytes 262176 | tf_op jit(solution)/shard_map/ppermute | solution.py:466
  247.2 1.7 late.3
  249.0 2.6 collective-permute-done.31.rest_0_
  251.8 1.6 collective-permute-start.32
  253.4 2.1 collective-permute-start.33
  255.5 3.6 %collective-permute-done.32.rest_0_ = bf16[4,16,1024]{2,1,0:T(8,128)(2,1)S(1)} collective-permute-done((bf16[4,16,1024]{2,1,0:T(8,128)(2,1)S(1)}, bf16[4,16,1024]{2,1,0:T(8,128)(2,1)S(1)}, u32[]{:S(2)}, u32[]{:S(2)}) %collective-permute-start.32) | collective-permute-done | bytes 131104 | tf_op jit(solution)/shard_map/ppermute | solution.py:466
  259.1 2.7 collective-permute-done.33.rest_1_
  261.9 2.2 collective-permute-start.35
  264.0 2.6 collective-permute-start.36
  266.7 3.4 %collective-permute-done.35.rest_0_ = f32[16,1024]{1,0:T(8,128)S(1)} collective-permute-done((f32[16,1024]{1,0:T(8,128)S(1)}, f32[16,1024]{1,0:T(8,128)S(1)}, u32[]{:S(2)}, u32[]{:S(2)}) %collective-permute-start.35) | collective-permute-done | bytes 65568 | tf_op jit(solution)/shard_map/ppermute | solution.py:466
  (132 shorter events, 13.9 us)
Async XLA Ops:
  0.0 32.4 %copy-start.29 = (s32[31]{0:T(128)S(1)}, s32[31]{0:T(128)}, u32[]{:S(2)}) copy-start(s32[31]{0:T(128)} %constant.67.clone) | copy-start | bytes 376
  0.0 32.2 %copy-start.6 = (s32[32,2]{0,1:T(2,128)S(1)}, s32[32,2]{0,1:T(2,128)}, u32[]{:S(2)}) copy-start(s32[32,2]{0,1:T(2,128)} %param.12) | copy-start | bytes 772
  0.8 31.5 %copy-start.27 = (s32[2,32,16]{1,2,0:T(8,128)S(1)}, s32[2,32,16]{1,2,0:T(8,128)}, u32[]{:S(2)}) copy-start(s32[2,32,16]{1,2,0:T(8,128)} %param.11) | copy-start | bytes 12292
  0.8 31.6 %copy-start.28 = (s32[2,32,16]{1,2,0:T(8,128)S(1)}, s32[2,32,16]{1,2,0:T(8,128)}, u32[]{:S(2)}) copy-start(s32[2,32,16]{1,2,0:T(8,128)} %param.10) | copy-start | bytes 12292
  19.3 30.3 %collective-permute-start.10 = (bf16[2,128,512]{2,1,0:T(8,128)(2,1)}, bf16[2,128,512]{2,1,0:T(8,128)(2,1)}, u32[]{:S(2)}, u32[]{:S(2)}) collective-permute-start(bf16[2,128,512]{2,1,0:T(8,128)(2,1)} %get-tuple-element.58), channel_id=1, source_target_pairs={{0,22},{1,23},{2,20},{3,21},{4,18},{5,19},{6,16},{7,17},{8,30},{9,... | collective-permute-start | bytes 786440 | tf_op jit(solution)/shard_map/ppermute | solution.py:466
  25.3 25.4 %collective-permute-start.11 = (bf16[2,128,512]{2,1,0:T(8,128)(2,1)}, bf16[2,128,512]{2,1,0:T(8,128)(2,1)}, u32[]{:S(2)}, u32[]{:S(2)}) collective-permute-start(bf16[2,128,512]{2,1,0:T(8,128)(2,1)} %get-tuple-element.59), channel_id=1, source_target_pairs={{0,5},{1,4},{2,7},{3,6},{4,1},{5,0},{6,3},{7,2},{8,13},{9,12},{10,... | collective-permute-start | bytes 786440 | tf_op jit(solution)/shard_map/ppermute | solution.py:466
  25.3 29.5 %collective-permute-start.12 = (bf16[2,128,512]{2,1,0:T(8,128)(2,1)}, bf16[2,128,512]{2,1,0:T(8,128)(2,1)}, u32[]{:S(2)}, u32[]{:S(2)}) collective-permute-start(bf16[2,128,512]{2,1,0:T(8,128)(2,1)} %get-tuple-element.60), channel_id=1, source_target_pairs={{0,23},{1,22},{2,21},{3,20},{4,19},{5,18},{6,17},{7,16},{8,31},{9,... | collective-permute-start | bytes 786440 | tf_op jit(solution)/shard_map/ppermute | solution.py:466
  26.7 28.4 %collective-permute-start.13 = (bf16[2,128,512]{2,1,0:T(8,128)(2,1)}, bf16[2,128,512]{2,1,0:T(8,128)(2,1)}, u32[]{:S(2)}, u32[]{:S(2)}) collective-permute-start(bf16[2,128,512]{2,1,0:T(8,128)(2,1)} %get-tuple-element.61), channel_id=1, source_target_pairs={{0,6},{1,7},{2,4},{3,5},{4,2},{5,3},{6,0},{7,1},{8,14},{9,15},{10,... | collective-permute-start | bytes 786440 | tf_op jit(solution)/shard_map/ppermute | solution.py:466
  28.2 27.0 %collective-permute-start.14 = (bf16[2,128,512]{2,1,0:T(8,128)(2,1)}, bf16[2,128,512]{2,1,0:T(8,128)(2,1)}, u32[]{:S(2)}, u32[]{:S(2)}) collective-permute-start(bf16[2,128,512]{2,1,0:T(8,128)(2,1)} %get-tuple-element.62), channel_id=1, source_target_pairs={{0,24},{1,25},{2,26},{3,27},{4,28},{5,29},{6,30},{7,31},{8,16},{9,... | collective-permute-start | bytes 786440 | tf_op jit(solution)/shard_map/ppermute | solution.py:466
  49.6 18.6 %collective-permute-start.15 = (bf16[2,128,512]{2,1,0:T(8,128)(2,1)}, bf16[2,128,512]{2,1,0:T(8,128)(2,1)S(1)}, u32[]{:S(2)}, u32[]{:S(2)}) collective-permute-start(bf16[2,128,512]{2,1,0:T(8,128)(2,1)} %copy-done.20), channel_id=1, source_target_pairs={{0,7},{1,6},{2,5},{3,4},{4,3},{5,2},{6,1},{7,0},{8,15},{9,14},{10,... | collective-permute-start | bytes 786440 | tf_op jit(solution)/shard_map/ppermute | solution.py:466
  50.7 25.7 %collective-permute-start.16 = (bf16[2,128,512]{2,1,0:T(8,128)(2,1)}, bf16[2,128,512]{2,1,0:T(8,128)(2,1)}, u32[]{:S(2)}, u32[]{:S(2)}) collective-permute-start(bf16[2,128,512]{2,1,0:T(8,128)(2,1)} %copy-done.19), channel_id=1, source_target_pairs={{0,25},{1,24},{2,27},{3,26},{4,29},{5,28},{6,31},{7,30},{8,17},{9,... | collective-permute-start | bytes 786440 | tf_op jit(solution)/shard_map/ppermute | solution.py:466
  54.7 24.6 %collective-permute-start.17 = (bf16[2,128,512]{2,1,0:T(8,128)(2,1)}, bf16[2,128,512]{2,1,0:T(8,128)(2,1)}, u32[]{:S(2)}, u32[]{:S(2)}) collective-permute-start(bf16[2,128,512]{2,1,0:T(8,128)(2,1)} %copy-done.18), channel_id=1, source_target_pairs={{0,8},{1,9},{2,10},{3,11},{4,12},{5,13},{6,14},{7,15},{8,0},{9,1},... | collective-permute-start | bytes 786440 | tf_op jit(solution)/shard_map/ppermute | solution.py:466
  55.2 24.3 %collective-permute-start.3 = (bf16[2,128,512]{2,1,0:T(8,128)(2,1)}, bf16[2,128,512]{2,1,0:T(8,128)(2,1)}, u32[]{:S(2)}, u32[]{:S(2)}) collective-permute-start(bf16[2,128,512]{2,1,0:T(8,128)(2,1)} %copy-done.17), channel_id=1, source_target_pairs={{0,1},{1,0},{2,3},{3,2},{4,5},{5,4},{6,7},{7,6},{8,9},{9,8},{10,11... | collective-permute-start | bytes 786440 | tf_op jit(solution)/shard_map/ppermute | solution.py:466
  55.2 38.4 %collective-permute-start.4 = (bf16[2,128,512]{2,1,0:T(8,128)(2,1)}, bf16[2,128,512]{2,1,0:T(8,128)(2,1)}, u32[]{:S(2)}, u32[]{:S(2)}) collective-permute-start(bf16[2,128,512]{2,1,0:T(8,128)(2,1)} %copy-done.16), channel_id=1, source_target_pairs={{0,19},{1,18},{2,17},{3,16},{4,23},{5,22},{6,21},{7,20},{8,27},{9,... | collective-permute-start | bytes 786440 | tf_op jit(solution)/shard_map/ppermute | solution.py:466
  68.1 25.5 %collective-permute-start.5 = (bf16[2,128,512]{2,1,0:T(8,128)(2,1)}, bf16[2,128,512]{2,1,0:T(8,128)(2,1)}, u32[]{:S(2)}, u32[]{:S(2)}) collective-permute-start(bf16[2,128,512]{2,1,0:T(8,128)(2,1)} %copy-done.15), channel_id=1, source_target_pairs={{0,2},{1,3},{2,0},{3,1},{4,6},{5,7},{6,4},{7,5},{8,10},{9,11},{10,... | collective-permute-start | bytes 786440 | tf_op jit(solution)/shard_map/ppermute | solution.py:466
  76.4 59.7 %copy-start.1 = (bf16[2,65,128,128]{3,2,1,0:T(8,128)(2,1)}, bf16[2,65,128,128]{3,2,1,0:T(8,128)(2,1)S(1)}, u32[]{:S(2)}) copy-start(bf16[2,65,128,128]{3,2,1,0:T(8,128)(2,1)S(1)} %concatenate.3.tiles_ref) | copy-start | bytes 12779524
  76.4 33.2 %collective-permute-start.6 = (bf16[2,128,512]{2,1,0:T(8,128)(2,1)S(1)}, bf16[2,128,512]{2,1,0:T(8,128)(2,1)S(1)}, u32[]{:S(2)}, u32[]{:S(2)}) collective-permute-start(bf16[2,128,512]{2,1,0:T(8,128)(2,1)S(1)} %copy-done.14), channel_id=1, source_target_pairs={{0,20},{1,21},{2,22},{3,23},{4,16},{5,17},{6,18},{7,19},{8,28},{9,... | collective-permute-start | bytes 786440 | tf_op jit(solution)/shard_map/ppermute | solution.py:466
  79.3 32.2 %collective-permute-start.7 = (bf16[2,128,512]{2,1,0:T(8,128)(2,1)S(1)}, bf16[2,128,512]{2,1,0:T(8,128)(2,1)S(1)}, u32[]{:S(2)}, u32[]{:S(2)}) collective-permute-start(bf16[2,128,512]{2,1,0:T(8,128)(2,1)S(1)} %copy-done.12), channel_id=1, source_target_pairs={{0,3},{1,2},{2,1},{3,0},{4,7},{5,6},{6,5},{7,4},{8,11},{9,10},{10,... | collective-permute-start | bytes 786440 | tf_op jit(solution)/shard_map/ppermute | solution.py:466
  79.5 34.8 %collective-permute-start.8 = (bf16[2,128,512]{2,1,0:T(8,128)(2,1)S(1)}, bf16[2,128,512]{2,1,0:T(8,128)(2,1)S(1)}, u32[]{:S(2)}, u32[]{:S(2)}) collective-permute-start(bf16[2,128,512]{2,1,0:T(8,128)(2,1)S(1)} %copy-done.10), channel_id=1, source_target_pairs={{0,21},{1,20},{2,23},{3,22},{4,17},{5,16},{6,19},{7,18},{8,29},{9,... | collective-permute-start | bytes 786440 | tf_op jit(solution)/shard_map/ppermute | solution.py:466
  93.6 25.0 %collective-permute-start.9 = (bf16[2,128,512]{2,1,0:T(8,128)(2,1)S(1)}, bf16[2,128,512]{2,1,0:T(8,128)(2,1)S(1)}, u32[]{:S(2)}, u32[]{:S(2)}) collective-permute-start(bf16[2,128,512]{2,1,0:T(8,128)(2,1)S(1)} %copy-done.8), channel_id=1, source_target_pairs={{0,4},{1,5},{2,6},{3,7},{4,0},{5,1},{6,2},{7,3},{8,12},{9,13},{10,... | collective-permute-start | bytes 786440 | tf_op jit(solution)/shard_map/ppermute | solution.py:466
  93.6 40.4 %collective-permute-start = (bf16[2,128,512]{2,1,0:T(8,128)(2,1)S(1)}, bf16[2,128,512]{2,1,0:T(8,128)(2,1)S(1)}, u32[]{:S(2)}, u32[]{:S(2)}) collective-permute-start(bf16[2,128,512]{2,1,0:T(8,128)(2,1)S(1)} %copy-done.22), channel_id=1, source_target_pairs={{0,16},{1,17},{2,18},{3,19},{4,20},{5,21},{6,22},{7,23},{8,24},{9,... | collective-permute-start | bytes 786440 | tf_op jit(solution)/shard_map/ppermute | solution.py:466
  94.9 41.2 %copy-start.3 = (bf16[4096,512]{1,0:T(8,128)(2,1)S(1)}, bf16[4096,512]{1,0:T(8,128)(2,1)}, u32[]{:S(2)}) copy-start(bf16[4096,512]{1,0:T(8,128)(2,1)} %param.7) | copy-start | bytes 12582916
  109.6 26.5 %copy-start.31 = (bf16[2,128,512]{2,1,0:T(8,128)(2,1)}, bf16[2,128,512]{2,1,0:T(8,128)(2,1)S(1)}, u32[]{:S(2)}) copy-start(bf16[2,128,512]{2,1,0:T(8,128)(2,1)S(1)} %collective-permute-done.6.rest_6_) | copy-start | bytes 786436
  109.6 63.8 %collective-permute-start.1 = (bf16[2,128,512]{2,1,0:T(8,128)(2,1)}, bf16[2,128,512]{2,1,0:T(8,128)(2,1)}, u32[]{:S(2)}, u32[]{:S(2)}) collective-permute-start(bf16[2,128,512]{2,1,0:T(8,128)(2,1)} %get-tuple-element.49), channel_id=1, source_target_pairs={{0,17},{1,16},{2,19},{3,18},{4,21},{5,20},{6,23},{7,22},{8,25},{9,... | collective-permute-start | bytes 786440 | tf_op jit(solution)/shard_map/ppermute | solution.py:466
  111.5 24.5 %copy-start.32 = (bf16[2,128,512]{2,1,0:T(8,128)(2,1)}, bf16[2,128,512]{2,1,0:T(8,128)(2,1)S(1)}, u32[]{:S(2)}) copy-start(bf16[2,128,512]{2,1,0:T(8,128)(2,1)S(1)} %collective-permute-done.7.rest_7_) | copy-start | bytes 786436
  111.5 61.9 %collective-permute-start.2 = (bf16[2,128,512]{2,1,0:T(8,128)(2,1)}, bf16[2,128,512]{2,1,0:T(8,128)(2,1)}, u32[]{:S(2)}, u32[]{:S(2)}) collective-permute-start(bf16[2,128,512]{2,1,0:T(8,128)(2,1)} %get-tuple-element.50), channel_id=1, source_target_pairs={{0,18},{1,19},{2,16},{3,17},{4,22},{5,23},{6,20},{7,21},{8,26},{9,... | collective-permute-start | bytes 786440 | tf_op jit(solution)/shard_map/ppermute | solution.py:466
  114.3 65.3 %collective-permute-start.18 = (bf16[2,128,512]{2,1,0:T(8,128)(2,1)S(1)}, bf16[2,128,512]{2,1,0:T(8,128)(2,1)}, u32[]{:S(2)}, u32[]{:S(2)}) collective-permute-start(bf16[2,128,512]{2,1,0:T(8,128)(2,1)S(1)} %get-tuple-element.67), channel_id=1, source_target_pairs={{0,26},{1,27},{2,24},{3,25},{4,30},{5,31},{6,28},{7,29},{8,18},{9,... | collective-permute-start | bytes 786440 | tf_op jit(solution)/shard_map/ppermute | solution.py:466
  118.6 60.9 %collective-permute-start.19 = (bf16[2,128,512]{2,1,0:T(8,128)(2,1)S(1)}, bf16[2,128,512]{2,1,0:T(8,128)(2,1)}, u32[]{:S(2)}, u32[]{:S(2)}) collective-permute-start(bf16[2,128,512]{2,1,0:T(8,128)(2,1)S(1)} %get-tuple-element.68), channel_id=1, source_target_pairs={{0,9},{1,8},{2,11},{3,10},{4,13},{5,12},{6,15},{7,14},{8,1},{9,0},... | collective-permute-start | bytes 786440 | tf_op jit(solution)/shard_map/ppermute | solution.py:466
  134.0 48.6 %collective-permute-start.20 = (bf16[2,128,512]{2,1,0:T(8,128)(2,1)S(1)}, bf16[2,128,512]{2,1,0:T(8,128)(2,1)}, u32[]{:S(2)}, u32[]{:S(2)}) collective-permute-start(bf16[2,128,512]{2,1,0:T(8,128)(2,1)S(1)} %get-tuple-element.69), channel_id=1, source_target_pairs={{0,27},{1,26},{2,25},{3,24},{4,31},{5,30},{6,29},{7,28},{8,19},{9,... | collective-permute-start | bytes 786440 | tf_op jit(solution)/shard_map/ppermute | solution.py:466
  173.4 36.5 %collective-permute-start.21 = (bf16[2,128,512]{2,1,0:T(8,128)(2,1)S(1)}, bf16[2,128,512]{2,1,0:T(8,128)(2,1)S(1)}, u32[]{:S(2)}, u32[]{:S(2)}) collective-permute-start(bf16[2,128,512]{2,1,0:T(8,128)(2,1)S(1)} %get-tuple-element.70), channel_id=1, source_target_pairs={{0,10},{1,11},{2,8},{3,9},{4,14},{5,15},{6,12},{7,13},{8,2},{9,3},... | collective-permute-start | bytes 786440 | tf_op jit(solution)/shard_map/ppermute | solution.py:466
  173.4 41.3 %collective-permute-start.22 = (bf16[2,128,512]{2,1,0:T(8,128)(2,1)S(1)}, bf16[2,128,512]{2,1,0:T(8,128)(2,1)S(1)}, u32[]{:S(2)}, u32[]{:S(2)}) collective-permute-start(bf16[2,128,512]{2,1,0:T(8,128)(2,1)S(1)} %get-tuple-element.71), channel_id=1, source_target_pairs={{0,28},{1,29},{2,30},{3,31},{4,24},{5,25},{6,26},{7,27},{8,20},{9,... | collective-permute-start | bytes 786440 | tf_op jit(solution)/shard_map/ppermute | solution.py:466
  179.6 36.3 %collective-permute-start.23 = (bf16[2,128,512]{2,1,0:T(8,128)(2,1)S(1)}, bf16[2,128,512]{2,1,0:T(8,128)(2,1)S(1)}, u32[]{:S(2)}, u32[]{:S(2)}) collective-permute-start(bf16[2,128,512]{2,1,0:T(8,128)(2,1)S(1)} %get-tuple-element.72), channel_id=1, source_target_pairs={{0,11},{1,10},{2,9},{3,8},{4,15},{5,14},{6,13},{7,12},{8,3},{9,2},... | collective-permute-start | bytes 786440 | tf_op jit(solution)/shard_map/ppermute | solution.py:466
  179.6 38.7 %collective-permute-start.24 = (bf16[2,128,512]{2,1,0:T(8,128)(2,1)S(1)}, bf16[2,128,512]{2,1,0:T(8,128)(2,1)S(1)}, u32[]{:S(2)}, u32[]{:S(2)}) collective-permute-start(bf16[2,128,512]{2,1,0:T(8,128)(2,1)S(1)} %get-tuple-element.73), channel_id=1, source_target_pairs={{0,29},{1,28},{2,31},{3,30},{4,25},{5,24},{6,27},{7,26},{8,21},{9,... | collective-permute-start | bytes 786440 | tf_op jit(solution)/shard_map/ppermute | solution.py:466
  182.6 41.1 %collective-permute-start.25 = (bf16[2,128,512]{2,1,0:T(8,128)(2,1)S(1)}, bf16[2,128,512]{2,1,0:T(8,128)(2,1)S(1)}, u32[]{:S(2)}, u32[]{:S(2)}) collective-permute-start(bf16[2,128,512]{2,1,0:T(8,128)(2,1)S(1)} %get-tuple-element.74), channel_id=1, source_target_pairs={{0,12},{1,13},{2,14},{3,15},{4,8},{5,9},{6,10},{7,11},{8,4},{9,5},... | collective-permute-start | bytes 786440 | tf_op jit(solution)/shard_map/ppermute | solution.py:466
  187.0 36.7 %copy-start.24 = (bf16[2,512,2048]{2,1,0:T(8,128)(2,1)S(1)}, bf16[2,512,2048]{2,1,0:T(8,128)(2,1)}, u32[]{:S(2)}) copy-start(bf16[2,512,2048]{2,1,0:T(8,128)(2,1)} %copy-done.23) | copy-start | bytes 12582916
  209.9 17.4 %collective-permute-start.26 = (bf16[2,128,512]{2,1,0:T(8,128)(2,1)S(1)}, bf16[2,128,512]{2,1,0:T(8,128)(2,1)S(1)}, u32[]{:S(2)}, u32[]{:S(2)}) collective-permute-start(bf16[2,128,512]{2,1,0:T(8,128)(2,1)S(1)} %get-tuple-element.76), channel_id=1, source_target_pairs={{0,30},{1,31},{2,28},{3,29},{4,26},{5,27},{6,24},{7,25},{8,22},{9,... | collective-permute-start | bytes 786440 | tf_op jit(solution)/shard_map/ppermute | solution.py:466
  214.7 18.7 %collective-permute-start.27 = (bf16[2,128,512]{2,1,0:T(8,128)(2,1)S(1)}, bf16[2,128,512]{2,1,0:T(8,128)(2,1)S(1)}, u32[]{:S(2)}, u32[]{:S(2)}) collective-permute-start(bf16[2,128,512]{2,1,0:T(8,128)(2,1)S(1)} %get-tuple-element.77), channel_id=1, source_target_pairs={{0,13},{1,12},{2,15},{3,14},{4,9},{5,8},{6,11},{7,10},{8,5},{9,4},... | collective-permute-start | bytes 786440 | tf_op jit(solution)/shard_map/ppermute | solution.py:466
  215.9 18.4 %collective-permute-start.28 = (bf16[2,128,512]{2,1,0:T(8,128)(2,1)S(1)}, bf16[2,128,512]{2,1,0:T(8,128)(2,1)S(1)}, u32[]{:S(2)}, u32[]{:S(2)}) collective-permute-start(bf16[2,128,512]{2,1,0:T(8,128)(2,1)S(1)} %get-tuple-element.78), channel_id=1, source_target_pairs={{0,31},{1,30},{2,29},{3,28},{4,27},{5,26},{6,25},{7,24},{8,23},{9,... | collective-permute-start | bytes 786440 | tf_op jit(solution)/shard_map/ppermute | solution.py:466
  218.3 24.7 %collective-permute-start.29 = (bf16[2,128,512]{2,1,0:T(8,128)(2,1)S(1)}, bf16[2,128,512]{2,1,0:T(8,128)(2,1)S(1)}, u32[]{:S(2)}, u32[]{:S(2)}) collective-permute-start(bf16[2,128,512]{2,1,0:T(8,128)(2,1)S(1)} %get-tuple-element.79), channel_id=1, source_target_pairs={{0,14},{1,15},{2,12},{3,13},{4,10},{5,11},{6,8},{7,9},{8,6},{9,7},... | collective-permute-start | bytes 786440 | tf_op jit(solution)/shard_map/ppermute | solution.py:466
  223.7 23.5 %collective-permute-start.30 = (bf16[2,128,512]{2,1,0:T(8,128)(2,1)S(1)}, bf16[2,128,512]{2,1,0:T(8,128)(2,1)S(1)}, u32[]{:S(2)}, u32[]{:S(2)}) collective-permute-start(bf16[2,128,512]{2,1,0:T(8,128)(2,1)S(1)} %get-tuple-element.80), channel_id=1, source_target_pairs={{0,15},{1,14},{2,13},{3,12},{4,11},{5,10},{6,9},{7,8},{8,7},{9,6},... | collective-permute-start | bytes 786440 | tf_op jit(solution)/shard_map/ppermute | solution.py:466
  223.7 23.5 %copy-start.26 = (bf16[2,512,1280]{2,1,0:T(8,128)(2,1)S(1)}, bf16[2,512,1280]{2,1,0:T(8,128)(2,1)}, u32[]{:S(2)}) copy-start(bf16[2,512,1280]{2,1,0:T(8,128)(2,1)} %copy-done.25) | copy-start | bytes 7864324
  248.9 2.7 %collective-permute-start.31 = (f32[4,4,16,1024]{3,2,1,0:T(8,128)S(1)}, f32[4,4,16,1024]{3,2,1,0:T(8,128)S(1)}, u32[]{:S(2)}, u32[]{:S(2)}) collective-permute-start(f32[4,4,16,1024]{3,2,1,0:T(8,128)S(1)} %get-tuple-element.82), channel_id=1, source_target_pairs={{0,1},{1,0},{2,3},{3,2},{4,5},{5,4},{6,7},{7,6},{8,9},{9,8},{10,11... | collective-permute-start | bytes 3145736 | tf_op jit(solution)/shard_map/ppermute | solution.py:466
  251.8 7.3 %collective-permute-start.32 = (bf16[4,16,1024]{2,1,0:T(8,128)(2,1)S(1)}, bf16[4,16,1024]{2,1,0:T(8,128)(2,1)S(1)}, u32[]{:S(2)}, u32[]{:S(2)}) collective-permute-start(bf16[4,16,1024]{2,1,0:T(8,128)(2,1)S(1)} %get-tuple-element.84), channel_id=1, source_target_pairs={{0,6},{1,7},{2,4},{3,5},{4,2},{5,3},{6,0},{7,1},{8,14},{9,15},{10,... | collective-permute-start | bytes 393224 | tf_op jit(solution)/shard_map/ppermute | solution.py:466
  253.4 8.4 %collective-permute-start.33 = (bf16[4,16,1024]{2,1,0:T(8,128)(2,1)S(1)}, bf16[4,16,1024]{2,1,0:T(8,128)(2,1)S(1)}, u32[]{:S(2)}, u32[]{:S(2)}) collective-permute-start(bf16[4,16,1024]{2,1,0:T(8,128)(2,1)S(1)} %get-tuple-element.85), channel_id=1, source_target_pairs={{0,2},{1,3},{2,0},{3,1},{4,6},{5,7},{6,4},{7,5},{8,10},{9,11},{10,... | collective-permute-start | bytes 393224 | tf_op jit(solution)/shard_map/ppermute | solution.py:466
  255.5 6.3 %collective-permute-start.34 = (bf16[4,16,1024]{2,1,0:T(8,128)(2,1)S(1)}, bf16[4,16,1024]{2,1,0:T(8,128)(2,1)S(1)}, u32[]{:S(2)}, u32[]{:S(2)}) collective-permute-start(bf16[4,16,1024]{2,1,0:T(8,128)(2,1)S(1)} %get-tuple-element.86), channel_id=1, source_target_pairs={{0,4},{1,5},{2,6},{3,7},{4,0},{5,1},{6,2},{7,3},{8,12},{9,13},{10,... | collective-permute-start | bytes 393224 | tf_op jit(solution)/shard_map/ppermute | solution.py:466
  261.9 8.2 %collective-permute-start.35 = (f32[16,1024]{1,0:T(8,128)S(1)}, f32[16,1024]{1,0:T(8,128)S(1)}, u32[]{:S(2)}, u32[]{:S(2)}) collective-permute-start(f32[16,1024]{1,0:T(8,128)S(1)} %get-tuple-element.88), channel_id=1, source_target_pairs={{0,16},{1,17},{2,18},{3,19},{4,20},{5,21},{6,22},{7,23},{8,24},{9,... | collective-permute-start | bytes 196616 | tf_op jit(solution)/shard_map/ppermute | solution.py:466
  264.0 6.8 %collective-permute-start.36 = (f32[16,1024]{1,0:T(8,128)S(1)}, f32[16,1024]{1,0:T(8,128)S(1)}, u32[]{:S(2)}, u32[]{:S(2)}) collective-permute-start(f32[16,1024]{1,0:T(8,128)S(1)} %get-tuple-element.89), channel_id=1, source_target_pairs={{0,24},{1,25},{2,26},{3,27},{4,28},{5,29},{6,30},{7,31},{8,16},{9,... | collective-permute-start | bytes 196616 | tf_op jit(solution)/shard_map/ppermute | solution.py:466
  266.7 4.7 %collective-permute-start.37 = (f32[16,1024]{1,0:T(8,128)S(1)}, f32[16,1024]{1,0:T(8,128)S(1)}, u32[]{:S(2)}, u32[]{:S(2)}) collective-permute-start(f32[16,1024]{1,0:T(8,128)S(1)} %get-tuple-element.90), channel_id=1, source_target_pairs={{0,8},{1,9},{2,10},{3,11},{4,12},{5,13},{6,14},{7,15},{8,0},{9,1},... | collective-permute-start | bytes 196616 | tf_op jit(solution)/shard_map/ppermute | solution.py:466
  (26 other events, 140.0 us)

commit v6 on v5

--- a/solution.py
+++ b/solution.py
@@ -228,7 +228,7 @@
     )(lists, counts, tiles, pool)
 
 
-def adjoint_kernel(phase, slots, count, lists_ref, counts_ref, tiles_ref, left_ref, *rest):
+def adjoint_kernel(phase, slots, count, own, lists_ref, counts_ref, tiles_ref, left_ref, *rest):
     outs, sum_ref = rest[:-1], rest[-1]
     local, rows = left_ref.shape[:2]
     for s in range(2 * count):
@@ -258,18 +258,26 @@
         for d in range(2):
             for s in range(size):
                 value = sum_ref[d * count + first + s]
-                out_ref[d, :, s * rows:(s + 1) * rows] = value.astype(BF16).T
+                turned = value.astype(BF16).T
+                if not own:
+                    out_ref[d, :, s * rows:(s + 1) * rows] = turned
+                    continue
+                half = turned.shape[0] // 2
+                for n in range(half // own):
+                    for core in range(2):
+                        row, place = (2 * n + core) * own, core * half + n * own
+                        out_ref[d, place:place + own, s * rows:(s + 1) * rows] = turned[row:row + own]
         first += size
 
 
-def adjoint(phase, lists, counts, tiles, left, sizes):
+def adjoint(phase, lists, counts, tiles, left, sizes, own):
     count = sum(sizes)
     slots = lists.shape[1] // counts.shape[1]
     rows, vectors = left.shape[1:]
     block = pl.BlockSpec(memory_space=VMEM)
     size = 2 * count * rows * vectors
     return pl.pallas_call(
-        functools.partial(adjoint_kernel, phase, slots, count),
+        functools.partial(adjoint_kernel, phase, slots, count, own),
         out_shape=[jax.ShapeDtypeStruct((2, vectors, n * rows), BF16) for n in sizes],
         in_specs=[pl.BlockSpec(memory_space=SMEM)] * 2 + [block] * 2,
         out_specs=[block] * len(sizes),
@@ -372,44 +380,30 @@
     )(lists, counts, tiles, current if more else in_hbm(current), in_vmem(left_t), *map(in_hbm, arrivals))
 
 
-def late_kernel(count, rank_ref, in_ref, adjoint_ref, *rest):
-    arrivals, rest = rest[:count], rest[count:]
-    outs, sum_ref = rest[:-1], rest[-1]
+def late_kernel(other, rank_ref, in_ref, adjoint_ref, *rest):
+    arrivals, out_ref = rest[:-1], rest[-1]
     vectors = arrivals[0].shape[2]
     pool = jnp.concatenate([ref[...].reshape(-1, vectors) for ref in arrivals], axis=0)
+    if other is None:
+        rows = slice(None)
+    else:
+        half = in_ref.shape[0] // 2
+        rows = pl.ds(pl.multiple_of(((rank_ref[0] + other) % 2) * half, half), half)
     for d in range(2):
-        side = (slice(None), slice(d * vectors, (d + 1) * vectors))
-        sum_ref[side] = in_ref[side] + jnp.dot(adjoint_ref[d], pool, preferred_element_type=F32)
-    if len(outs) == 1:
-        outs[0][...] = sum_ref[...]
-        return
-    send_ref, keep_ref = outs
-    core = rank_ref[0] % 2
-    outer, inner, own = send_ref.shape[:3]
-    for n in range(outer * inner):
-        keep_ref[n // inner, n % inner] = sum_ref[pl.ds(pl.multiple_of((2 * n + core) * own, own), own), :]
-        send_ref[n // inner, n % inner] = sum_ref[
-            pl.ds(pl.multiple_of((2 * n + 1 - core) * own, own), own), :
-        ].astype(send_ref.dtype)
-
-
-def late(rank, sums, adjoint, arrivals, devices, sent, last):
-    columns, both = sums.shape
-    own = columns // devices
+        side = slice(d * vectors, (d + 1) * vectors)
+        value = in_ref[rows, side] + jnp.dot(adjoint_ref[d, rows], pool, preferred_element_type=F32)
+        out_ref[..., side] = value.reshape(out_ref.shape[:-1] + (vectors,))
+
+
+def late(rank, sums, adjoint, arrivals, shape, other=None):
     block = pl.BlockSpec(memory_space=VMEM)
-    if not last or own % 8:
-        halves = [VMEM(sums.shape, F32)]
-    else:
-        half = (devices // 8, 4, own, both)
-        halves = [VMEM(half, sent), VMEM(half, F32)]
-    return pl.pallas_call(
-        functools.partial(late_kernel, len(arrivals)),
-        out_shape=halves,
+    return pl.pallas_call(
+        functools.partial(late_kernel, other),
+        out_shape=VMEM(shape, F32),
         in_specs=[pl.BlockSpec(memory_space=SMEM)] + [block] * (2 + len(arrivals)),
-        out_specs=[block] * len(halves),
-        scratch_shapes=[VMEM(sums.shape, F32)],
+        out_specs=block,
         compiler_params=pltpu.CompilerParams(vmem_limit_bytes=2 * ROOM),
-        cost_estimate=pl.CostEstimate(flops=4 * 10**9, bytes_accessed=12 * 2**20, transcendentals=0),
+        cost_estimate=pl.CostEstimate(flops=2 * 10**9, bytes_accessed=12 * 2**20, transcendentals=0),
         name="late",
     )(rank, *map(in_vmem, (sums, adjoint, *arrivals)))
 
@@ -493,6 +487,9 @@
     tiles = jnp.concatenate([tiles, jnp.zeros((2, 1) + tiles.shape[2:], tiles.dtype)], axis=1)
     bunch = math.gcd(local, 8) * block_rows
     left_t = left.reshape(-1, bunch, vectors).transpose(0, 2, 1)
+    own = 0 if vectors % (8 * devices) else vectors // devices
+    if own:
+        left_t = left_t.reshape(-1, devices // 2, 2, own, bunch).swapaxes(1, 2).reshape(left_t.shape)
     tiles = in_vmem(tiles)
     sums = hops(lists, counts, tiles, blocks, 4)
     start, stop = groups[-1]
@@ -500,18 +497,20 @@
     cap = send.shape[0]
     met = adjoint(
         len(groups), lists, counts, tiles, left.reshape(blocks.shape),
-        [(cut - start) * cap, (stop - cut) * cap],
+        [(cut - start) * cap, (stop - cut) * cap], own,
     )
     for n, (first, last) in enumerate(groups[:-1]):
         sums = gram(n + 1, lists, counts, tiles, sums, left_t, arrived[first:last], 3)
-    sums, = late(rank, sums, met[0], arrived[start:cut], devices, F32, False)
-    sums = late(rank, sums, met[1], arrived[cut:stop], devices, F32, True)
-    if len(sums) == 1:
-        mine = lax.psum_scatter(sums[0] * scale, "rows", scatter_dimension=0, tiled=True)
+    sums = late(rank, sums, met[0], arrived[start:cut], sums.shape)
+    if not own:
+        sums = late(rank, sums, met[1], arrived[cut:stop], sums.shape)
+        mine = lax.psum_scatter(sums * scale, "rows", scatter_dimension=0, tiled=True)
         return mine.reshape(mine.shape[0], 2, vectors).transpose(1, 0, 2)
-    send, keep = sums
     outer = devices // 8
+    half = (outer, 4, own, 2 * vectors)
+    send = late(rank, sums, met[1], arrived[cut:stop], half, 1)
     got = swap(send, 1, devices)
+    keep = late(rank, sums, met[1], arrived[cut:stop], half, 0)
     parts = split(rank, keep, [got], 4, 1, BF16)
     got = [swap(parts[n], n << 1, devices) for n in (3, 1, 2)]
     parts = split(rank, parts[0], got, outer, 3, F32)

time: 272 us -> 260 us (0.956)
  waiting for transfers between devices: 76.6 us -> 59.4 us
  starting transfers between devices: 80.7 us -> 88.8 us
    ppermute x38, waiting for transfers between devices: 76.6 us -> 59.4 us  [swap(): return lax.ppermute(value, 'rows', [(i, i ^ mask) for i in range(devices)])]
    transpose x0 -> x2, local copies, waits for them, and re-layouts: none -> 9.47 us  [the longest x1 6.3 us: body(): left_t = left.reshape(-1, bunch, vectors).transpose(0, 2, 1)]
    ppermute x38, starting transfers between devices: 80.7 us -> 88.8 us  [swap(): return lax.ppermute(value, 'rows', [(i, i ^ mask) for i in range(devices)])]
    unnamed x73 -> x57, local copies, waits for them, and re-layouts: 16.4 us -> 9.77 us
    reshape x1 -> x0, local copies, waits for them, and re-layouts: 6.26 us -> none  [body(): left_t = left.reshape(-1, bunch, vectors).transpose(0, 2, 1)]
    pallas_call x3 -> x4, Pallas kernels: 32.9 us -> 31.6 us  [the longest x1 27.6 us: adjoint(): pl.pallas_call(functools.partial(adjoint_kernel, phase, slots, count, own...]
  transfers between devices with their start and end apart: 38 -> 38, of which waited for: 13 -> 13; matrix products, arithmetic and copies ran while one was open for 4% -> 6% of each run, Pallas kernels for 26% -> 31%
where the time goes in v6:
time: 260 us; the launch traced here: 259 us
  starting transfers between devices  88.8 us (34%)
  Pallas kernels  83.9 us (32%)
  waiting for transfers between devices  59.4 us (23%)
  local copies, waits for them, and re-layouts  25.1 us (10%)
    ppermute x38, starting transfers between devices, swap(): return lax.ppermute(value, 'rows', [(i, i ^ mask) for i in range(devices)])  88.8 us
    ppermute x38, waiting for transfers between devices, swap(): return lax.ppermute(value, 'rows', [(i, i ^ mask) for i in range(devices)])  59.4 us
    pallas_call x1, Pallas kernels, adjoint(): pl.pallas_call(functools.partial(adjoint_kernel, phase, slots, count, own...  27.6 us
    pallas_call x1, Pallas kernels, gram(): pl.pallas_call(functools.partial(gram_kernel, phase, len(arrivals), slots...  22.9 us
    pallas_call x1, Pallas kernels, hops(): pl.pallas_call(functools.partial(hops_kernel, slots, fixed), out_shape=HB...  14.7 us
    pallas_call x1, Pallas kernels, pack(): pl.pallas_call(functools.partial(pack_kernel, masks, len(after)), out_sha...  10.9 us
    unnamed x57, local copies, waits for them, and re-layouts  9.77 us
    transpose x1, local copies, waits for them, and re-layouts, body(): left_t = left.reshape(-1, bunch, vectors).transpose(0, 2, 1)  6.3 us
  transfers between devices with their start and end apart: 38, of which 13 were waited for; matrix products, arithmetic and copies ran while one was open for 6% of the time, Pallas kernels for 31%

profile of v6, /device:TPU:0, one launch (start us, length us, event | category | flops | bytes accessed | tf_op | source)
XLA Modules:
  0.0 259.4 jit_solution(739375696598805005)
XLA Ops:
  0.0 3.0 %first_pack.1 = (bf16[2,128,512]{2,1,0:T(8,128)(2,1)}, bf16[2,128,512]{2,1,0:T(8,128)(2,1)}, bf16[2,128,512]{2,1,0:T(8,128)(2,1)}) custom-call(s32[1]{0:T(128)} %bitcast.rank_ref, s32[2,32]{1,0:T(2,128)} %bitcast.27, bf16[32,128,512]{2,1,0:T(8,128)(2,1)} %bitcast.19), custom_call_target="tpu_custom_call" | custom-call | tf_op jit(solution)/shard_map/first_pack/pallas_call | solution.py:69
  3.0 4.1 %collective-permute-start = (bf16[2,128,512]{2,1,0:T(8,128)(2,1)}, bf16[2,128,512]{2,1,0:T(8,128)(2,1)}, u32[]{:S(2)}, u32[]{:S(2)}) collective-permute-start(bf16[2,128,512]{2,1,0:T(8,128)(2,1)} %get-tuple-element.46), channel_id=1, source_target_pairs={{0,16},{1,17},{2,18},{3,19},{4,20},{5,21},{6,22},{7,23},{8,24},{9,... | collective-permute-start | bytes 786440 | tf_op jit(solution)/shard_map/ppermute | solution.py:460
  7.1 3.0 %collective-permute-start.2 = (bf16[2,128,512]{2,1,0:T(8,128)(2,1)}, bf16[2,128,512]{2,1,0:T(8,128)(2,1)}, u32[]{:S(2)}, u32[]{:S(2)}) collective-permute-start(bf16[2,128,512]{2,1,0:T(8,128)(2,1)} %get-tuple-element.48), channel_id=1, source_target_pairs={{0,18},{1,19},{2,16},{3,17},{4,22},{5,23},{6,20},{7,21},{8,26},{9,... | collective-permute-start | bytes 786440 | tf_op jit(solution)/shard_map/ppermute | solution.py:460
  10.1 10.9 %pack.1 = (bf16[2,128,512]{2,1,0:T(8,128)(2,1)}, bf16[2,128,512]{2,1,0:T(8,128)(2,1)}, bf16[2,128,512]{2,1,0:T(8,128)(2,1)S(1)}, bf16[2,128,512]{2,1,0:T(8,128)(...) custom-call(s32[1]{0:T(128)} %bitcast.rank_ref, ...), custom_call_target="tpu_custom_call" | custom-call | tf_op jit(solution)/shard_map/pack/pallas_call | solution.py:104
  24.6 0.7 copy-done.12
  26.8 0.8 collective-permute-start.3
  28.1 3.4 %collective-permute-done.rest_0_ = bf16[2,128,512]{2,1,0:T(8,128)(2,1)} collective-permute-done((bf16[2,128,512]{2,1,0:T(8,128)(2,1)}, bf16[2,128,512]{2,1,0:T(8,128)(2,1)}, u32[]{:S(2)}, u32[]{:S(2)}) %collective-permute-start) | collective-permute-done | bytes 262176 | tf_op jit(solution)/shard_map/ppermute | solution.py:460
  31.4 1.8 collective-permute-start.5
  35.3 5.7 %collective-permute-done.1.rest_1_ = bf16[2,128,512]{2,1,0:T(8,128)(2,1)} collective-permute-done((bf16[2,128,512]{2,1,0:T(8,128)(2,1)}, bf16[2,128,512]{2,1,0:T(8,128)(2,1)}, u32[]{:S(2)}, u32[]{:S(2)}) %collective-permute-start.1) | collective-permute-done | bytes 262176 | tf_op jit(solution)/shard_map/ppermute | solution.py:460
  41.0 2.5 collective-permute-start.6
  43.5 11.7 %collective-permute-done.2.rest_2_ = bf16[2,128,512]{2,1,0:T(8,128)(2,1)} collective-permute-done((bf16[2,128,512]{2,1,0:T(8,128)(2,1)}, bf16[2,128,512]{2,1,0:T(8,128)(2,1)}, u32[]{:S(2)}, u32[]{:S(2)}) %collective-permute-start.2) | collective-permute-done | bytes 262176 | tf_op jit(solution)/shard_map/ppermute | solution.py:460
  55.2 0.8 collective-permute-start.8
  55.9 2.7 %collective-permute-done.4.rest_4_ = bf16[2,128,512]{2,1,0:T(8,128)(2,1)} collective-permute-done((bf16[2,128,512]{2,1,0:T(8,128)(2,1)}, bf16[2,128,512]{2,1,0:T(8,128)(2,1)}, u32[]{:S(2)}, u32[]{:S(2)}) %collective-permute-start.4) | collective-permute-done | bytes 262176 | tf_op jit(solution)/shard_map/ppermute | solution.py:460
  58.6 1.5 collective-permute-start.9
  60.2 1.5 collective-permute-start.10
  61.9 10.1 %collective-permute-done.6.rest_6_ = bf16[2,128,512]{2,1,0:T(8,128)(2,1)S(1)} collective-permute-done((bf16[2,128,512]{2,1,0:T(8,128)(2,1)}, bf16[2,128,512]{2,1,0:T(8,128)(2,1)S(1)}, u32[]{:S(2)}, u32[]{:S(2)}) %collective-permute-start.6) | collective-permute-done | bytes 262176 | tf_op jit(solution)/shard_map/ppermute | solution.py:460
  72.7 2.7 %collective-permute-done.8.rest_8_ = bf16[2,128,512]{2,1,0:T(8,128)(2,1)S(1)} collective-permute-done((bf16[2,128,512]{2,1,0:T(8,128)(2,1)}, bf16[2,128,512]{2,1,0:T(8,128)(2,1)S(1)}, u32[]{:S(2)}, u32[]{:S(2)}) %collective-permute-start.8) | collective-permute-done | bytes 262176 | tf_op jit(solution)/shard_map/ppermute | solution.py:460
  75.4 7.1 %collective-permute-start.13 = (bf16[2,128,512]{2,1,0:T(8,128)(2,1)S(1)}, bf16[2,128,512]{2,1,0:T(8,128)(2,1)}, u32[]{:S(2)}, u32[]{:S(2)}) collective-permute-start(bf16[2,128,512]{2,1,0:T(8,128)(2,1)S(1)} %get-tuple-element.59), channel_id=1, source_target_pairs={{0,6},{1,7},{2,4},{3,5},{4,2},{5,3},{6,0},{7,1},{8,14},{9,15},{10,... | collective-permute-start | bytes 786440 | tf_op jit(solution)/shard_map/ppermute | solution.py:460
  82.5 10.1 %collective-permute-start.14 = (bf16[2,128,512]{2,1,0:T(8,128)(2,1)S(1)}, bf16[2,128,512]{2,1,0:T(8,128)(2,1)}, u32[]{:S(2)}, u32[]{:S(2)}) collective-permute-start(bf16[2,128,512]{2,1,0:T(8,128)(2,1)S(1)} %get-tuple-element.60), channel_id=1, source_target_pairs={{0,24},{1,25},{2,26},{3,27},{4,28},{5,29},{6,30},{7,31},{8,16},{9,... | collective-permute-start | bytes 786440 | tf_op jit(solution)/shard_map/ppermute | solution.py:460
  92.6 8.4 %collective-permute-done.10.rest_10_ = bf16[2,128,512]{2,1,0:T(8,128)(2,1)S(1)} collective-permute-done((bf16[2,128,512]{2,1,0:T(8,128)(2,1)}, bf16[2,128,512]{2,1,0:T(8,128)(2,1)S(1)}, u32[]{:S(2)}, u32[]{:S(2)}) %collective-permute-start.10) | collective-permute-done | bytes 262176 | tf_op jit(solution)/shard_map/ppermute | solution.py:460
  101.7 0.8 copy.28
  102.4 1.0 add.78.lists_ref
  103.5 3.2 %concatenate.3.tiles_ref = bf16[2,65,128,128]{3,2,1,0:T(8,128)(2,1)S(1)} pad(bf16[2,64,128,128]{3,2,1,0:T(8,128)(2,1)} %param.9, bf16[]{:T(256)} %constant.66.clone.1), padding=0_0x0_1x0_0x0_0 | pad | bytes 8454146 | tf_op jit(solution)/shard_map/concatenate | solution.py:487
  106.7 12.4 %collective-permute-start.16 = (bf16[2,128,512]{2,1,0:T(8,128)(2,1)S(1)}, bf16[2,128,512]{2,1,0:T(8,128)(2,1)S(1)}, u32[]{:S(2)}, u32[]{:S(2)}) collective-permute-start(bf16[2,128,512]{2,1,0:T(8,128)(2,1)S(1)} %get-tuple-element.62), channel_id=1, source_target_pairs={{0,25},{1,24},{2,27},{3,26},{4,29},{5,28},{6,31},{7,30},{8,17},{9,... | collective-permute-start | bytes 786440 | tf_op jit(solution)/shard_map/ppermute | solution.py:460
  119.1 1.3 collective-permute-start.18
  120.9 3.8 %collective-permute-start.20 = (bf16[2,128,512]{2,1,0:T(8,128)(2,1)S(1)}, bf16[2,128,512]{2,1,0:T(8,128)(2,1)S(1)}, u32[]{:S(2)}, u32[]{:S(2)}) collective-permute-start(bf16[2,128,512]{2,1,0:T(8,128)(2,1)S(1)} %get-tuple-element.67), channel_id=1, source_target_pairs={{0,27},{1,26},{2,25},{3,24},{4,31},{5,30},{6,29},{7,28},{8,19},{9,... | collective-permute-start | bytes 786440 | tf_op jit(solution)/shard_map/ppermute | solution.py:460
  124.7 14.7 %hops.1.in_ref = f32[64,128,512]{2,1,0:T(8,128)} custom-call(s32[3,1024]{1,0:T(4,128)S(1)} %add.78.lists_ref, s32[3,64]{1,0:T(4,128)S(1)} %get-tuple-element.87.counts_ref, bf16[2,65,128,128]{3,2,1,0:T(8,128)(2,1)S(1)} %concatenate.3.tiles_ref, bf16[32,128,512]{2,1,0:T(8,128)(2,1)S(1)} %bitcast.21), custom_call_target="tpu_custom_call" | custom-call | flops 8000000000 | bytes 41943040 | tf_op jit(solution)/shard_map/hops/pallas_call | solution.py:217
  140.1 7.8 %collective-permute-start.22 = (bf16[2,128,512]{2,1,0:T(8,128)(2,1)}, bf16[2,128,512]{2,1,0:T(8,128)(2,1)S(1)}, u32[]{:S(2)}, u32[]{:S(2)}) collective-permute-start(bf16[2,128,512]{2,1,0:T(8,128)(2,1)} %get-tuple-element.69), channel_id=1, source_target_pairs={{0,28},{1,29},{2,30},{3,31},{4,24},{5,25},{6,26},{7,27},{8,20},{9,... | collective-permute-start | bytes 786440 | tf_op jit(solution)/shard_map/ppermute | solution.py:460
  148.0 1.0 collective-permute-done.20.rest_2_
  149.0 27.6 %adjoint.1 = (bf16[2,512,2048]{2,1,0:T(8,128)(2,1)S(1)}, bf16[2,512,1280]{2,1,0:T(8,128)(2,1)S(1)}) custom-call(s32[3,1024]{1,0:T(4,128)S(1)} %add.78.lists_ref, s32[3,64]{1,0:T(4,128)S(1)} %get-tuple-element.87.counts_ref, bf16[2,65,128,128]{3,2,1,0:T(8,128)(2,1)S(1)} %concatenate.3.tiles_ref, bf16[32,128,512]{2,1,0:T(8,128)(2,1)S(1)} %bitcast.25), custom_call_target="tpu_custom_call" | custom-call | flops 8000000000 | bytes 16777216 | tf_op jit(solution)/shard_map/adjoint/pallas_call | solution.py:279
  176.6 2.0 copy-done.3
  178.6 1.5 copy-done.14
  180.0 6.3 %copy.29 = bf16[4,512,1024]{2,1,0:T(8,128)(2,1)} copy(bf16[4,512,1024]{1,2,0:T(8,128)(2,1)} %bitcast.24) | data formatting | bytes 8388608 | tf_op jit(solution)/shard_map/transpose | solution.py:489
  186.3 3.2 %copy.30 = bf16[4,2,16,16,1024]{4,3,2,1,0:T(8,128)(2,1)S(1)} copy(bf16[4,2,16,16,1024]{4,3,1,2,0:T(8,128)(2,1)} %bitcast.29) | data formatting | bytes 8388608 | tf_op jit(solution)/shard_map/transpose | solution.py:492
  189.6 7.8 %collective-permute-start.27 = (bf16[2,128,512]{2,1,0:T(8,128)(2,1)S(1)}, bf16[2,128,512]{2,1,0:T(8,128)(2,1)S(1)}, u32[]{:S(2)}, u32[]{:S(2)}) collective-permute-start(bf16[2,128,512]{2,1,0:T(8,128)(2,1)S(1)} %get-tuple-element.75), channel_id=1, source_target_pairs={{0,13},{1,12},{2,15},{3,14},{4,9},{5,8},{6,11},{7,10},{8,5},{9,4},... | collective-permute-start | bytes 786440 | tf_op jit(solution)/shard_map/ppermute | solution.py:460
  197.4 4.3 %collective-permute-start.28 = (bf16[2,128,512]{2,1,0:T(8,128)(2,1)S(1)}, bf16[2,128,512]{2,1,0:T(8,128)(2,1)S(1)}, u32[]{:S(2)}, u32[]{:S(2)}) collective-permute-start(bf16[2,128,512]{2,1,0:T(8,128)(2,1)S(1)} %get-tuple-element.76), channel_id=1, source_target_pairs={{0,31},{1,30},{2,29},{3,28},{4,27},{5,26},{6,25},{7,24},{8,23},{9,... | collective-permute-start | bytes 786440 | tf_op jit(solution)/shard_map/ppermute | solution.py:460
  201.7 4.2 %collective-permute-start.29 = (bf16[2,128,512]{2,1,0:T(8,128)(2,1)S(1)}, bf16[2,128,512]{2,1,0:T(8,128)(2,1)S(1)}, u32[]{:S(2)}, u32[]{:S(2)}) collective-permute-start(bf16[2,128,512]{2,1,0:T(8,128)(2,1)S(1)} %get-tuple-element.77), channel_id=1, source_target_pairs={{0,14},{1,15},{2,12},{3,13},{4,10},{5,11},{6,8},{7,9},{8,6},{9,7},... | collective-permute-start | bytes 786440 | tf_op jit(solution)/shard_map/ppermute | solution.py:460
  205.9 22.9 %gram.1.in_ref = f32[512,1024]{1,0:T(8,128)S(1)} custom-call(s32[3,1024]{1,0:T(4,128)S(1)} %add.78.lists_ref, s32[3,64]{1,0:T(4,128)S(1)} %get-tuple-element.87.counts_ref, bf16[2,65,128,128]{3,2,1,0:T(8,128)(2,1)S(1)} %bitcast.23, f32[64,128,512]{2,1,0:T(8,128)} %hops.1.in_ref, bf16[4,512,1024]{2,1,0:T(8,128)(2,1)S(1)} %bitcast.26, ...), custom_call_target="tpu_custom_call" | custom-call | flops 12000000000 | bytes 25165824 | tf_op jit(solution)/shard_map/gram/pallas_call | solution.py:362
  228.8 2.4 late.3.in_ref
  231.2 0.8 late.5
  232.2 0.8 late.4.keep_ref
  233.0 1.8 collective-permute-done.31.rest_0_
  234.9 4.1 %collective-permute-start.32 = (bf16[4,16,1024]{2,1,0:T(8,128)(2,1)S(1)}, bf16[4,16,1024]{2,1,0:T(8,128)(2,1)S(1)}, u32[]{:S(2)}, u32[]{:S(2)}) collective-permute-start(bf16[4,16,1024]{2,1,0:T(8,128)(2,1)S(1)} %get-tuple-element.80), channel_id=1, source_target_pairs={{0,6},{1,7},{2,4},{3,5},{4,2},{5,3},{6,0},{7,1},{8,14},{9,15},{10,... | collective-permute-start | bytes 393224 | tf_op jit(solution)/shard_map/ppermute | solution.py:460
  239.0 3.4 %collective-permute-start.33 = (bf16[4,16,1024]{2,1,0:T(8,128)(2,1)S(1)}, bf16[4,16,1024]{2,1,0:T(8,128)(2,1)S(1)}, u32[]{:S(2)}, u32[]{:S(2)}) collective-permute-start(bf16[4,16,1024]{2,1,0:T(8,128)(2,1)S(1)} %get-tuple-element.81), channel_id=1, source_target_pairs={{0,2},{1,3},{2,0},{3,1},{4,6},{5,7},{6,4},{7,5},{8,10},{9,11},{10,... | collective-permute-start | bytes 393224 | tf_op jit(solution)/shard_map/ppermute | solution.py:460
  242.8 6.2 %collective-permute-done.33.rest_1_ = bf16[4,16,1024]{2,1,0:T(8,128)(2,1)S(1)} collective-permute-done((bf16[4,16,1024]{2,1,0:T(8,128)(2,1)S(1)}, bf16[4,16,1024]{2,1,0:T(8,128)(2,1)S(1)}, u32[]{:S(2)}, u32[]{:S(2)}) %collective-permute-start.33) | collective-permute-done | bytes 131104 | tf_op jit(solution)/shard_map/ppermute | solution.py:460
  249.0 3.6 %collective-permute-start.35 = (f32[16,1024]{1,0:T(8,128)S(1)}, f32[16,1024]{1,0:T(8,128)S(1)}, u32[]{:S(2)}, u32[]{:S(2)}) collective-permute-start(f32[16,1024]{1,0:T(8,128)S(1)} %get-tuple-element.84), channel_id=1, source_target_pairs={{0,16},{1,17},{2,18},{3,19},{4,20},{5,21},{6,22},{7,23},{8,24},{9,... | collective-permute-start | bytes 196616 | tf_op jit(solution)/shard_map/ppermute | solution.py:460
  253.3 2.4 collective-permute-done.35.rest_0_
  255.7 3.1 %collective-permute-done.36.rest_1_ = f32[16,1024]{1,0:T(8,128)S(1)} collective-permute-done((f32[16,1024]{1,0:T(8,128)S(1)}, f32[16,1024]{1,0:T(8,128)S(1)}, u32[]{:S(2)}, u32[]{:S(2)}) %collective-permute-start.36) | collective-permute-done | bytes 65568 | tf_op jit(solution)/shard_map/ppermute | solution.py:460
  (119 shorter events, 11.2 us)
Async XLA Ops:
  0.0 27.7 %copy-start.17 = (s32[2,32,16]{1,2,0:T(8,128)S(1)}, s32[2,32,16]{1,2,0:T(8,128)}, u32[]{:S(2)}) copy-start(s32[2,32,16]{1,2,0:T(8,128)} %param.10) | copy-start | bytes 12292
  0.0 27.8 %copy-start.16 = (s32[2,32,16]{1,2,0:T(8,128)S(1)}, s32[2,32,16]{1,2,0:T(8,128)}, u32[]{:S(2)}) copy-start(s32[2,32,16]{1,2,0:T(8,128)} %param.11) | copy-start | bytes 12292
  0.0 27.9 %copy-start.18 = (s32[31]{0:T(128)S(1)}, s32[31]{0:T(128)}, u32[]{:S(2)}) copy-start(s32[31]{0:T(128)} %constant.67.clone) | copy-start | bytes 376
  3.0 28.5 %collective-permute-start = (bf16[2,128,512]{2,1,0:T(8,128)(2,1)}, bf16[2,128,512]{2,1,0:T(8,128)(2,1)}, u32[]{:S(2)}, u32[]{:S(2)}) collective-permute-start(bf16[2,128,512]{2,1,0:T(8,128)(2,1)} %get-tuple-element.46), channel_id=1, source_target_pairs={{0,16},{1,17},{2,18},{3,19},{4,20},{5,21},{6,22},{7,23},{8,24},{9,... | collective-permute-start | bytes 786440 | tf_op jit(solution)/shard_map/ppermute | solution.py:460
  7.1 33.9 %collective-permute-start.1 = (bf16[2,128,512]{2,1,0:T(8,128)(2,1)}, bf16[2,128,512]{2,1,0:T(8,128)(2,1)}, u32[]{:S(2)}, u32[]{:S(2)}) collective-permute-start(bf16[2,128,512]{2,1,0:T(8,128)(2,1)} %get-tuple-element.47), channel_id=1, source_target_pairs={{0,17},{1,16},{2,19},{3,18},{4,21},{5,20},{6,23},{7,22},{8,25},{9,... | collective-permute-start | bytes 786440 | tf_op jit(solution)/shard_map/ppermute | solution.py:460
  7.1 48.0 %collective-permute-start.2 = (bf16[2,128,512]{2,1,0:T(8,128)(2,1)}, bf16[2,128,512]{2,1,0:T(8,128)(2,1)}, u32[]{:S(2)}, u32[]{:S(2)}) collective-permute-start(bf16[2,128,512]{2,1,0:T(8,128)(2,1)} %get-tuple-element.48), channel_id=1, source_target_pairs={{0,18},{1,19},{2,16},{3,17},{4,22},{5,23},{6,20},{7,21},{8,26},{9,... | collective-permute-start | bytes 786440 | tf_op jit(solution)/shard_map/ppermute | solution.py:460
  26.8 28.4 %collective-permute-start.3 = (bf16[2,128,512]{2,1,0:T(8,128)(2,1)}, bf16[2,128,512]{2,1,0:T(8,128)(2,1)}, u32[]{:S(2)}, u32[]{:S(2)}) collective-permute-start(bf16[2,128,512]{2,1,0:T(8,128)(2,1)} %get-tuple-element.49), channel_id=1, source_target_pairs={{0,1},{1,0},{2,3},{3,2},{4,5},{5,4},{6,7},{7,6},{8,9},{9,8},{10,11... | collective-permute-start | bytes 786440 | tf_op jit(solution)/shard_map/ppermute | solution.py:460
  27.6 31.1 %collective-permute-start.4 = (bf16[2,128,512]{2,1,0:T(8,128)(2,1)}, bf16[2,128,512]{2,1,0:T(8,128)(2,1)}, u32[]{:S(2)}, u32[]{:S(2)}) collective-permute-start(bf16[2,128,512]{2,1,0:T(8,128)(2,1)} %get-tuple-element.50), channel_id=1, source_target_pairs={{0,19},{1,18},{2,17},{3,16},{4,23},{5,22},{6,21},{7,20},{8,27},{9,... | collective-permute-start | bytes 786440 | tf_op jit(solution)/shard_map/ppermute | solution.py:460
  31.4 28.7 %collective-permute-start.5 = (bf16[2,128,512]{2,1,0:T(8,128)(2,1)}, bf16[2,128,512]{2,1,0:T(8,128)(2,1)}, u32[]{:S(2)}, u32[]{:S(2)}) collective-permute-start(bf16[2,128,512]{2,1,0:T(8,128)(2,1)} %copy-done.13), channel_id=1, source_target_pairs={{0,2},{1,3},{2,0},{3,1},{4,6},{5,7},{6,4},{7,5},{8,10},{9,11},{10,... | collective-permute-start | bytes 786440 | tf_op jit(solution)/shard_map/ppermute | solution.py:460
  41.0 31.1 %collective-permute-start.6 = (bf16[2,128,512]{2,1,0:T(8,128)(2,1)}, bf16[2,128,512]{2,1,0:T(8,128)(2,1)S(1)}, u32[]{:S(2)}, u32[]{:S(2)}) collective-permute-start(bf16[2,128,512]{2,1,0:T(8,128)(2,1)} %copy-done.12), channel_id=1, source_target_pairs={{0,20},{1,21},{2,22},{3,23},{4,16},{5,17},{6,18},{7,19},{8,28},{9,... | collective-permute-start | bytes 786440 | tf_op jit(solution)/shard_map/ppermute | solution.py:460
  55.2 16.9 %collective-permute-start.7 = (bf16[2,128,512]{2,1,0:T(8,128)(2,1)}, bf16[2,128,512]{2,1,0:T(8,128)(2,1)S(1)}, u32[]{:S(2)}, u32[]{:S(2)}) collective-permute-start(bf16[2,128,512]{2,1,0:T(8,128)(2,1)} %copy-done.11), channel_id=1, source_target_pairs={{0,3},{1,2},{2,1},{3,0},{4,7},{5,6},{6,5},{7,4},{8,11},{9,10},{10,... | collective-permute-start | bytes 786440 | tf_op jit(solution)/shard_map/ppermute | solution.py:460
  55.2 20.3 %collective-permute-start.8 = (bf16[2,128,512]{2,1,0:T(8,128)(2,1)}, bf16[2,128,512]{2,1,0:T(8,128)(2,1)S(1)}, u32[]{:S(2)}, u32[]{:S(2)}) collective-permute-start(bf16[2,128,512]{2,1,0:T(8,128)(2,1)} %copy-done.10), channel_id=1, source_target_pairs={{0,21},{1,20},{2,23},{3,22},{4,17},{5,16},{6,19},{7,18},{8,29},{9,... | collective-permute-start | bytes 786440 | tf_op jit(solution)/shard_map/ppermute | solution.py:460
  58.6 23.8 %collective-permute-start.9 = (bf16[2,128,512]{2,1,0:T(8,128)(2,1)}, bf16[2,128,512]{2,1,0:T(8,128)(2,1)S(1)}, u32[]{:S(2)}, u32[]{:S(2)}) collective-permute-start(bf16[2,128,512]{2,1,0:T(8,128)(2,1)} %copy-done.9), channel_id=1, source_target_pairs={{0,4},{1,5},{2,6},{3,7},{4,0},{5,1},{6,2},{7,3},{8,12},{9,13},{10,... | collective-permute-start | bytes 786440 | tf_op jit(solution)/shard_map/ppermute | solution.py:460
  60.2 40.8 %collective-permute-start.10 = (bf16[2,128,512]{2,1,0:T(8,128)(2,1)}, bf16[2,128,512]{2,1,0:T(8,128)(2,1)S(1)}, u32[]{:S(2)}, u32[]{:S(2)}) collective-permute-start(bf16[2,128,512]{2,1,0:T(8,128)(2,1)} %copy-done.8), channel_id=1, source_target_pairs={{0,22},{1,23},{2,20},{3,21},{4,18},{5,19},{6,16},{7,17},{8,30},{9,... | collective-permute-start | bytes 786440 | tf_op jit(solution)/shard_map/ppermute | solution.py:460
  72.0 29.1 %copy-start.19 = (bf16[2,128,512]{2,1,0:T(8,128)(2,1)}, bf16[2,128,512]{2,1,0:T(8,128)(2,1)S(1)}, u32[]{:S(2)}) copy-start(bf16[2,128,512]{2,1,0:T(8,128)(2,1)S(1)} %collective-permute-done.6.rest_6_) | copy-start | bytes 786436
  72.0 34.6 %collective-permute-start.11 = (bf16[2,128,512]{2,1,0:T(8,128)(2,1)}, bf16[2,128,512]{2,1,0:T(8,128)(2,1)}, u32[]{:S(2)}, u32[]{:S(2)}) collective-permute-start(bf16[2,128,512]{2,1,0:T(8,128)(2,1)} %copy-done.7), channel_id=1, source_target_pairs={{0,5},{1,4},{2,7},{3,6},{4,1},{5,0},{6,3},{7,2},{8,13},{9,12},{10,... | collective-permute-start | bytes 786440 | tf_op jit(solution)/shard_map/ppermute | solution.py:460
  72.0 29.1 %copy-start.20 = (bf16[2,128,512]{2,1,0:T(8,128)(2,1)}, bf16[2,128,512]{2,1,0:T(8,128)(2,1)S(1)}, u32[]{:S(2)}) copy-start(bf16[2,128,512]{2,1,0:T(8,128)(2,1)S(1)} %collective-permute-done.7.rest_7_) | copy-start | bytes 786436
  72.0 47.0 %collective-permute-start.12 = (bf16[2,128,512]{2,1,0:T(8,128)(2,1)}, bf16[2,128,512]{2,1,0:T(8,128)(2,1)}, u32[]{:S(2)}, u32[]{:S(2)}) collective-permute-start(bf16[2,128,512]{2,1,0:T(8,128)(2,1)} %copy-done.6), channel_id=1, source_target_pairs={{0,23},{1,22},{2,21},{3,20},{4,19},{5,18},{6,17},{7,16},{8,31},{9,... | collective-permute-start | bytes 786440 | tf_op jit(solution)/shard_map/ppermute | solution.py:460
  75.4 25.7 %copy-start.21 = (bf16[2,128,512]{2,1,0:T(8,128)(2,1)}, bf16[2,128,512]{2,1,0:T(8,128)(2,1)S(1)}, u32[]{:S(2)}) copy-start(bf16[2,128,512]{2,1,0:T(8,128)(2,1)S(1)} %collective-permute-done.8.rest_8_) | copy-start | bytes 786436
  75.4 43.7 %collective-permute-start.13 = (bf16[2,128,512]{2,1,0:T(8,128)(2,1)S(1)}, bf16[2,128,512]{2,1,0:T(8,128)(2,1)}, u32[]{:S(2)}, u32[]{:S(2)}) collective-permute-start(bf16[2,128,512]{2,1,0:T(8,128)(2,1)S(1)} %get-tuple-element.59), channel_id=1, source_target_pairs={{0,6},{1,7},{2,4},{3,5},{4,2},{5,3},{6,0},{7,1},{8,14},{9,15},{10,... | collective-permute-start | bytes 786440 | tf_op jit(solution)/shard_map/ppermute | solution.py:460
  82.5 37.9 %collective-permute-start.14 = (bf16[2,128,512]{2,1,0:T(8,128)(2,1)S(1)}, bf16[2,128,512]{2,1,0:T(8,128)(2,1)}, u32[]{:S(2)}, u32[]{:S(2)}) collective-permute-start(bf16[2,128,512]{2,1,0:T(8,128)(2,1)S(1)} %get-tuple-element.60), channel_id=1, source_target_pairs={{0,24},{1,25},{2,26},{3,27},{4,28},{5,29},{6,30},{7,31},{8,16},{9,... | collective-permute-start | bytes 786440 | tf_op jit(solution)/shard_map/ppermute | solution.py:460
  101.0 19.9 %collective-permute-start.15 = (bf16[2,128,512]{2,1,0:T(8,128)(2,1)S(1)}, bf16[2,128,512]{2,1,0:T(8,128)(2,1)}, u32[]{:S(2)}, u32[]{:S(2)}) collective-permute-start(bf16[2,128,512]{2,1,0:T(8,128)(2,1)S(1)} %get-tuple-element.61), channel_id=1, source_target_pairs={{0,7},{1,6},{2,5},{3,4},{4,3},{5,2},{6,1},{7,0},{8,15},{9,14},{10,... | collective-permute-start | bytes 786440 | tf_op jit(solution)/shard_map/ppermute | solution.py:460
  106.6 42.3 %copy-start.1 = (bf16[2,65,128,128]{3,2,1,0:T(8,128)(2,1)}, bf16[2,65,128,128]{3,2,1,0:T(8,128)(2,1)S(1)}, u32[]{:S(2)}) copy-start(bf16[2,65,128,128]{3,2,1,0:T(8,128)(2,1)S(1)} %concatenate.3.tiles_ref) | copy-start | bytes 12779524
  106.7 32.7 %collective-permute-start.16 = (bf16[2,128,512]{2,1,0:T(8,128)(2,1)S(1)}, bf16[2,128,512]{2,1,0:T(8,128)(2,1)S(1)}, u32[]{:S(2)}, u32[]{:S(2)}) collective-permute-start(bf16[2,128,512]{2,1,0:T(8,128)(2,1)S(1)} %get-tuple-element.62), channel_id=1, source_target_pairs={{0,25},{1,24},{2,27},{3,26},{4,29},{5,28},{6,31},{7,30},{8,17},{9,... | collective-permute-start | bytes 786440 | tf_op jit(solution)/shard_map/ppermute | solution.py:460
  119.1 21.0 %collective-permute-start.17 = (bf16[2,128,512]{2,1,0:T(8,128)(2,1)S(1)}, bf16[2,128,512]{2,1,0:T(8,128)(2,1)S(1)}, u32[]{:S(2)}, u32[]{:S(2)}) collective-permute-start(bf16[2,128,512]{2,1,0:T(8,128)(2,1)S(1)} %get-tuple-element.63), channel_id=1, source_target_pairs={{0,8},{1,9},{2,10},{3,11},{4,12},{5,13},{6,14},{7,15},{8,0},{9,1},... | collective-permute-start | bytes 786440 | tf_op jit(solution)/shard_map/ppermute | solution.py:460
  119.1 28.8 %collective-permute-start.18 = (bf16[2,128,512]{2,1,0:T(8,128)(2,1)S(1)}, bf16[2,128,512]{2,1,0:T(8,128)(2,1)S(1)}, u32[]{:S(2)}, u32[]{:S(2)}) collective-permute-start(bf16[2,128,512]{2,1,0:T(8,128)(2,1)S(1)} %get-tuple-element.65), channel_id=1, source_target_pairs={{0,26},{1,27},{2,24},{3,25},{4,30},{5,31},{6,28},{7,29},{8,18},{9,... | collective-permute-start | bytes 786440 | tf_op jit(solution)/shard_map/ppermute | solution.py:460
  120.4 27.5 %collective-permute-start.19 = (bf16[2,128,512]{2,1,0:T(8,128)(2,1)S(1)}, bf16[2,128,512]{2,1,0:T(8,128)(2,1)S(1)}, u32[]{:S(2)}, u32[]{:S(2)}) collective-permute-start(bf16[2,128,512]{2,1,0:T(8,128)(2,1)S(1)} %get-tuple-element.66), channel_id=1, source_target_pairs={{0,9},{1,8},{2,11},{3,10},{4,13},{5,12},{6,15},{7,14},{8,1},{9,0},... | collective-permute-start | bytes 786440 | tf_op jit(solution)/shard_map/ppermute | solution.py:460
  120.9 28.0 %collective-permute-start.20 = (bf16[2,128,512]{2,1,0:T(8,128)(2,1)S(1)}, bf16[2,128,512]{2,1,0:T(8,128)(2,1)S(1)}, u32[]{:S(2)}, u32[]{:S(2)}) collective-permute-start(bf16[2,128,512]{2,1,0:T(8,128)(2,1)S(1)} %get-tuple-element.67), channel_id=1, source_target_pairs={{0,27},{1,26},{2,25},{3,24},{4,31},{5,30},{6,29},{7,28},{8,19},{9,... | collective-permute-start | bytes 786440 | tf_op jit(solution)/shard_map/ppermute | solution.py:460
  124.7 24.3 %copy-start.2 = (bf16[4096,512]{1,0:T(8,128)(2,1)S(1)}, bf16[4096,512]{1,0:T(8,128)(2,1)}, u32[]{:S(2)}) copy-start(bf16[4096,512]{1,0:T(8,128)(2,1)} %param.7) | copy-start | bytes 12582916
  139.4 50.1 %collective-permute-start.21 = (bf16[2,128,512]{2,1,0:T(8,128)(2,1)}, bf16[2,128,512]{2,1,0:T(8,128)(2,1)S(1)}, u32[]{:S(2)}, u32[]{:S(2)}) collective-permute-start(bf16[2,128,512]{2,1,0:T(8,128)(2,1)} %get-tuple-element.68), channel_id=1, source_target_pairs={{0,10},{1,11},{2,8},{3,9},{4,14},{5,15},{6,12},{7,13},{8,2},{9,3},... | collective-permute-start | bytes 786440 | tf_op jit(solution)/shard_map/ppermute | solution.py:460
  140.1 49.5 %collective-permute-start.22 = (bf16[2,128,512]{2,1,0:T(8,128)(2,1)}, bf16[2,128,512]{2,1,0:T(8,128)(2,1)S(1)}, u32[]{:S(2)}, u32[]{:S(2)}) collective-permute-start(bf16[2,128,512]{2,1,0:T(8,128)(2,1)} %get-tuple-element.69), channel_id=1, source_target_pairs={{0,28},{1,29},{2,30},{3,31},{4,24},{5,25},{6,26},{7,27},{8,20},{9,... | collective-permute-start | bytes 786440 | tf_op jit(solution)/shard_map/ppermute | solution.py:460
  147.9 49.5 %collective-permute-start.23 = (bf16[2,128,512]{2,1,0:T(8,128)(2,1)}, bf16[2,128,512]{2,1,0:T(8,128)(2,1)S(1)}, u32[]{:S(2)}, u32[]{:S(2)}) collective-permute-start(bf16[2,128,512]{2,1,0:T(8,128)(2,1)} %get-tuple-element.70), channel_id=1, source_target_pairs={{0,11},{1,10},{2,9},{3,8},{4,15},{5,14},{6,13},{7,12},{8,3},{9,2},... | collective-permute-start | bytes 786440 | tf_op jit(solution)/shard_map/ppermute | solution.py:460
  147.9 53.8 %collective-permute-start.24 = (bf16[2,128,512]{2,1,0:T(8,128)(2,1)}, bf16[2,128,512]{2,1,0:T(8,128)(2,1)S(1)}, u32[]{:S(2)}, u32[]{:S(2)}) collective-permute-start(bf16[2,128,512]{2,1,0:T(8,128)(2,1)} %get-tuple-element.71), channel_id=1, source_target_pairs={{0,29},{1,28},{2,31},{3,30},{4,25},{5,24},{6,27},{7,26},{8,21},{9,... | collective-permute-start | bytes 786440 | tf_op jit(solution)/shard_map/ppermute | solution.py:460
  148.9 56.9 %collective-permute-start.25 = (bf16[2,128,512]{2,1,0:T(8,128)(2,1)}, bf16[2,128,512]{2,1,0:T(8,128)(2,1)S(1)}, u32[]{:S(2)}, u32[]{:S(2)}) collective-permute-start(bf16[2,128,512]{2,1,0:T(8,128)(2,1)} %get-tuple-element.72), channel_id=1, source_target_pairs={{0,12},{1,13},{2,14},{3,15},{4,8},{5,9},{6,10},{7,11},{8,4},{9,5},... | collective-permute-start | bytes 786440 | tf_op jit(solution)/shard_map/ppermute | solution.py:460
  180.0 25.8 %slice-start = ((s8[4259840]{0:T(1024)(128)(4,1)}), s8[65536]{0:T(1024)(128)(4,1)S(1)}, s32[]{:S(2)}) async-start(s8[4259840]{0:T(1024)(128)(4,1)} %bitcast.22), calls=%async_computation | async-start | bytes 131072
  189.5 41.6 %collective-permute-start.26 = (bf16[2,128,512]{2,1,0:T(8,128)(2,1)S(1)}, bf16[2,128,512]{2,1,0:T(8,128)(2,1)S(1)}, u32[]{:S(2)}, u32[]{:S(2)}) collective-permute-start(bf16[2,128,512]{2,1,0:T(8,128)(2,1)S(1)} %get-tuple-element.74), channel_id=1, source_target_pairs={{0,30},{1,31},{2,28},{3,29},{4,26},{5,27},{6,24},{7,25},{8,22},{9,... | collective-permute-start | bytes 786440 | tf_op jit(solution)/shard_map/ppermute | solution.py:460
  189.6 41.6 %collective-permute-start.27 = (bf16[2,128,512]{2,1,0:T(8,128)(2,1)S(1)}, bf16[2,128,512]{2,1,0:T(8,128)(2,1)S(1)}, u32[]{:S(2)}, u32[]{:S(2)}) collective-permute-start(bf16[2,128,512]{2,1,0:T(8,128)(2,1)S(1)} %get-tuple-element.75), channel_id=1, source_target_pairs={{0,13},{1,12},{2,15},{3,14},{4,9},{5,8},{6,11},{7,10},{8,5},{9,4},... | collective-permute-start | bytes 786440 | tf_op jit(solution)/shard_map/ppermute | solution.py:460
  197.4 33.8 %collective-permute-start.28 = (bf16[2,128,512]{2,1,0:T(8,128)(2,1)S(1)}, bf16[2,128,512]{2,1,0:T(8,128)(2,1)S(1)}, u32[]{:S(2)}, u32[]{:S(2)}) collective-permute-start(bf16[2,128,512]{2,1,0:T(8,128)(2,1)S(1)} %get-tuple-element.76), channel_id=1, source_target_pairs={{0,31},{1,30},{2,29},{3,28},{4,27},{5,26},{6,25},{7,24},{8,23},{9,... | collective-permute-start | bytes 786440 | tf_op jit(solution)/shard_map/ppermute | solution.py:460
  201.7 29.5 %collective-permute-start.29 = (bf16[2,128,512]{2,1,0:T(8,128)(2,1)S(1)}, bf16[2,128,512]{2,1,0:T(8,128)(2,1)S(1)}, u32[]{:S(2)}, u32[]{:S(2)}) collective-permute-start(bf16[2,128,512]{2,1,0:T(8,128)(2,1)S(1)} %get-tuple-element.77), channel_id=1, source_target_pairs={{0,14},{1,15},{2,12},{3,13},{4,10},{5,11},{6,8},{7,9},{8,6},{9,7},... | collective-permute-start | bytes 786440 | tf_op jit(solution)/shard_map/ppermute | solution.py:460
  205.8 25.4 %collective-permute-start.30 = (bf16[2,128,512]{2,1,0:T(8,128)(2,1)S(1)}, bf16[2,128,512]{2,1,0:T(8,128)(2,1)S(1)}, u32[]{:S(2)}, u32[]{:S(2)}) collective-permute-start(bf16[2,128,512]{2,1,0:T(8,128)(2,1)S(1)} %get-tuple-element.78), channel_id=1, source_target_pairs={{0,15},{1,14},{2,13},{3,12},{4,11},{5,10},{6,9},{7,8},{8,7},{9,6},... | collective-permute-start | bytes 786440 | tf_op jit(solution)/shard_map/ppermute | solution.py:460
  205.9 22.9 %copy-start.4 = (bf16[2,512,2048]{2,1,0:T(8,128)(2,1)S(1)}, bf16[2,512,2048]{2,1,0:T(8,128)(2,1)}, u32[]{:S(2)}) copy-start(bf16[2,512,2048]{2,1,0:T(8,128)(2,1)} %copy-done.3) | copy-start | bytes 12582916
  232.1 2.7 %collective-permute-start.31 = (f32[4,4,16,1024]{3,2,1,0:T(8,128)S(1)}, f32[4,4,16,1024]{3,2,1,0:T(8,128)S(1)}, u32[]{:S(2)}, u32[]{:S(2)}) collective-permute-start(f32[4,4,16,1024]{3,2,1,0:T(8,128)S(1)} %late.5), channel_id=1, source_target_pairs={{0,1},{1,0},{2,3},{3,2},{4,5},{5,4},{6,7},{7,6},{8,9},{9,8},{10,11... | collective-permute-start | bytes 3145736 | tf_op jit(solution)/shard_map/ppermute | solution.py:460
  234.9 7.9 %collective-permute-start.32 = (bf16[4,16,1024]{2,1,0:T(8,128)(2,1)S(1)}, bf16[4,16,1024]{2,1,0:T(8,128)(2,1)S(1)}, u32[]{:S(2)}, u32[]{:S(2)}) collective-permute-start(bf16[4,16,1024]{2,1,0:T(8,128)(2,1)S(1)} %get-tuple-element.80), channel_id=1, source_target_pairs={{0,6},{1,7},{2,4},{3,5},{4,2},{5,3},{6,0},{7,1},{8,14},{9,15},{10,... | collective-permute-start | bytes 393224 | tf_op jit(solution)/shard_map/ppermute | solution.py:460
  239.0 10.0 %collective-permute-start.33 = (bf16[4,16,1024]{2,1,0:T(8,128)(2,1)S(1)}, bf16[4,16,1024]{2,1,0:T(8,128)(2,1)S(1)}, u32[]{:S(2)}, u32[]{:S(2)}) collective-permute-start(bf16[4,16,1024]{2,1,0:T(8,128)(2,1)S(1)} %get-tuple-element.81), channel_id=1, source_target_pairs={{0,2},{1,3},{2,0},{3,1},{4,6},{5,7},{6,4},{7,5},{8,10},{9,11},{10,... | collective-permute-start | bytes 393224 | tf_op jit(solution)/shard_map/ppermute | solution.py:460
  242.4 6.6 %collective-permute-start.34 = (bf16[4,16,1024]{2,1,0:T(8,128)(2,1)S(1)}, bf16[4,16,1024]{2,1,0:T(8,128)(2,1)S(1)}, u32[]{:S(2)}, u32[]{:S(2)}) collective-permute-start(bf16[4,16,1024]{2,1,0:T(8,128)(2,1)S(1)} %get-tuple-element.82), channel_id=1, source_target_pairs={{0,4},{1,5},{2,6},{3,7},{4,0},{5,1},{6,2},{7,3},{8,12},{9,13},{10,... | collective-permute-start | bytes 393224 | tf_op jit(solution)/shard_map/ppermute | solution.py:460
  249.0 6.7 %collective-permute-start.35 = (f32[16,1024]{1,0:T(8,128)S(1)}, f32[16,1024]{1,0:T(8,128)S(1)}, u32[]{:S(2)}, u32[]{:S(2)}) collective-permute-start(f32[16,1024]{1,0:T(8,128)S(1)} %get-tuple-element.84), channel_id=1, source_target_pairs={{0,16},{1,17},{2,18},{3,19},{4,20},{5,21},{6,22},{7,23},{8,24},{9,... | collective-permute-start | bytes 196616 | tf_op jit(solution)/shard_map/ppermute | solution.py:460
  252.7 6.1 %collective-permute-start.36 = (f32[16,1024]{1,0:T(8,128)S(1)}, f32[16,1024]{1,0:T(8,128)S(1)}, u32[]{:S(2)}, u32[]{:S(2)}) collective-permute-start(f32[16,1024]{1,0:T(8,128)S(1)} %get-tuple-element.85), channel_id=1, source_target_pairs={{0,24},{1,25},{2,26},{3,27},{4,28},{5,29},{6,30},{7,31},{8,16},{9,... | collective-permute-start | bytes 196616 | tf_op jit(solution)/shard_map/ppermute | solution.py:460
  252.7 6.1 %collective-permute-start.37 = (f32[16,1024]{1,0:T(8,128)S(1)}, f32[16,1024]{1,0:T(8,128)S(1)}, u32[]{:S(2)}, u32[]{:S(2)}) collective-permute-start(f32[16,1024]{1,0:T(8,128)S(1)} %get-tuple-element.86), channel_id=1, source_target_pairs={{0,8},{1,9},{2,10},{3,11},{4,12},{5,13},{6,14},{7,15},{8,0},{9,1},... | collective-permute-start | bytes 196616 | tf_op jit(solution)/shard_map/ppermute | solution.py:460
  (18 other events, 100.3 us)

commit v7 on v6

--- a/solution.py
+++ b/solution.py
@@ -493,24 +493,27 @@
     tiles = in_vmem(tiles)
     sums = hops(lists, counts, tiles, blocks, 4)
     start, stop = groups[-1]
-    cut = stop - (stop - start) * 2 // 5
+    size = stop - start
+    cuts = [start, stop - size * 2 // 5, stop - size // 4, stop]
+    spans = [slice(a, b) for a, b in zip(cuts, cuts[1:]) if a < b]
     cap = send.shape[0]
     met = adjoint(
         len(groups), lists, counts, tiles, left.reshape(blocks.shape),
-        [(cut - start) * cap, (stop - cut) * cap], own,
+        [(span.stop - span.start) * cap for span in spans], own,
     )
     for n, (first, last) in enumerate(groups[:-1]):
         sums = gram(n + 1, lists, counts, tiles, sums, left_t, arrived[first:last], 3)
-    sums = late(rank, sums, met[0], arrived[start:cut], sums.shape)
+    for part, span in zip(met[:-1], spans):
+        sums = late(rank, sums, part, arrived[span], sums.shape)
     if not own:
-        sums = late(rank, sums, met[1], arrived[cut:stop], sums.shape)
+        sums = late(rank, sums, met[-1], arrived[spans[-1]], sums.shape)
         mine = lax.psum_scatter(sums * scale, "rows", scatter_dimension=0, tiled=True)
         return mine.reshape(mine.shape[0], 2, vectors).transpose(1, 0, 2)
     outer = devices // 8
     half = (outer, 4, own, 2 * vectors)
-    send = late(rank, sums, met[1], arrived[cut:stop], half, 1)
+    send = late(rank, sums, met[-1], arrived[spans[-1]], half, 1)
     got = swap(send, 1, devices)
-    keep = late(rank, sums, met[1], arrived[cut:stop], half, 0)
+    keep = late(rank, sums, met[-1], arrived[spans[-1]], half, 0)
     parts = split(rank, keep, [got], 4, 1, BF16)
     got = [swap(parts[n], n << 1, devices) for n in (3, 1, 2)]
     parts = split(rank, parts[0], got, outer, 3, F32)

time: 260 us -> 274 us (1.054)
  waiting for transfers between devices: 59.4 us -> 66.4 us
  starting transfers between devices: 88.8 us -> 94.6 us
    ppermute x38, waiting for transfers between devices: 59.4 us -> 66.4 us  [swap(): return lax.ppermute(value, 'rows', [(i, i ^ mask) for i in range(devices)])]
    ppermute x38, starting transfers between devices: 88.8 us -> 94.6 us  [swap(): return lax.ppermute(value, 'rows', [(i, i ^ mask) for i in range(devices)])]
    unnamed x57 -> x69, local copies, waits for them, and re-layouts: 9.77 us -> 10.6 us
  transfers between devices with their start and end apart: 38 -> 38, of which waited for: 13 -> 15; matrix products, arithmetic and copies ran while one was open for 6% -> 6% of each run, Pallas kernels for 31% -> 29%
where the time goes in v7:
time: 274 us
  starting transfers between devices  94.6 us (35%)
  Pallas kernels  84.5 us (31%)
  waiting for transfers between devices  66.4 us (24%)
  local copies, waits for them, and re-layouts  25.9 us (9%)
    ppermute x38, starting transfers between devices, swap(): return lax.ppermute(value, 'rows', [(i, i ^ mask) for i in range(devices)])  94.6 us
    ppermute x38, waiting for transfers between devices, swap(): return lax.ppermute(value, 'rows', [(i, i ^ mask) for i in range(devices)])  66.4 us
    pallas_call x1, Pallas kernels, adjoint(): pl.pallas_call(functools.partial(adjoint_kernel, phase, slots, count, own...  27.5 us
    pallas_call x1, Pallas kernels, gram(): pl.pallas_call(functools.partial(gram_kernel, phase, len(arrivals), slots...  22.9 us
    pallas_call x1, Pallas kernels, hops(): pl.pallas_call(functools.partial(hops_kernel, slots, fixed), out_shape=HB...  14.7 us
    pallas_call x1, Pallas kernels, pack(): pl.pallas_call(functools.partial(pack_kernel, masks, len(after)), out_sha...  11.3 us
    unnamed x69, local copies, waits for them, and re-layouts  10.6 us
    transpose x1, local copies, waits for them, and re-layouts, body(): left_t = left.reshape(-1, bunch, vectors).transpose(0, 2, 1)  6.31 us
  transfers between devices with their start and end apart: 38, of which 15 were waited for; matrix products, arithmetic and copies ran while one was open for 6% of the time, Pallas kernels for 29%

profile of v7, /device:TPU:0, one launch (start us, length us, event | category | flops | bytes accessed | tf_op | source)
XLA Modules:
  0.0 273.7 jit_solution(13316081596259934911)
XLA Ops:
  0.0 3.0 %first_pack.1 = (bf16[2,128,512]{2,1,0:T(8,128)(2,1)}, bf16[2,128,512]{2,1,0:T(8,128)(2,1)}, bf16[2,128,512]{2,1,0:T(8,128)(2,1)}) custom-call(s32[1]{0:T(128)} %bitcast.rank_ref, s32[2,32]{1,0:T(2,128)} %bitcast.27, bf16[32,128,512]{2,1,0:T(8,128)(2,1)} %bitcast.19), custom_call_target="tpu_custom_call" | custom-call | tf_op jit(solution)/shard_map/first_pack/pallas_call | solution.py:69
  3.0 4.1 %collective-permute-start = (bf16[2,128,512]{2,1,0:T(8,128)(2,1)}, bf16[2,128,512]{2,1,0:T(8,128)(2,1)}, u32[]{:S(2)}, u32[]{:S(2)}) collective-permute-start(bf16[2,128,512]{2,1,0:T(8,128)(2,1)} %get-tuple-element.47), channel_id=1, source_target_pairs={{0,16},{1,17},{2,18},{3,19},{4,20},{5,21},{6,22},{7,23},{8,24},{9,... | collective-permute-start | bytes 786440 | tf_op jit(solution)/shard_map/ppermute | solution.py:460
  7.1 3.0 %collective-permute-start.2 = (bf16[2,128,512]{2,1,0:T(8,128)(2,1)}, bf16[2,128,512]{2,1,0:T(8,128)(2,1)}, u32[]{:S(2)}, u32[]{:S(2)}) collective-permute-start(bf16[2,128,512]{2,1,0:T(8,128)(2,1)} %get-tuple-element.49), channel_id=1, source_target_pairs={{0,18},{1,19},{2,16},{3,17},{4,22},{5,23},{6,20},{7,21},{8,26},{9,... | collective-permute-start | bytes 786440 | tf_op jit(solution)/shard_map/ppermute | solution.py:460
  10.1 11.3 %pack.1 = (bf16[2,128,512]{2,1,0:T(8,128)(2,1)}, bf16[2,128,512]{2,1,0:T(8,128)(2,1)}, bf16[2,128,512]{2,1,0:T(8,128)(2,1)S(1)}, bf16[2,128,512]{2,1,0:T(8,128)(...) custom-call(s32[1]{0:T(128)} %bitcast.rank_ref, ...), custom_call_target="tpu_custom_call" | custom-call | tf_op jit(solution)/shard_map/pack/pallas_call | solution.py:104
  30.6 0.9 collective-permute-done.rest_0_
  31.5 1.8 collective-permute-start.5
  33.3 7.7 %collective-permute-done.1.rest_1_ = bf16[2,128,512]{2,1,0:T(8,128)(2,1)} collective-permute-done((bf16[2,128,512]{2,1,0:T(8,128)(2,1)}, bf16[2,128,512]{2,1,0:T(8,128)(2,1)}, u32[]{:S(2)}, u32[]{:S(2)}) %collective-permute-start.1) | collective-permute-done | bytes 262176 | tf_op jit(solution)/shard_map/ppermute | solution.py:460
  41.0 2.5 collective-permute-start.6
  43.5 11.7 %collective-permute-done.2.rest_2_ = bf16[2,128,512]{2,1,0:T(8,128)(2,1)} collective-permute-done((bf16[2,128,512]{2,1,0:T(8,128)(2,1)}, bf16[2,128,512]{2,1,0:T(8,128)(2,1)}, u32[]{:S(2)}, u32[]{:S(2)}) %collective-permute-start.2) | collective-permute-done | bytes 262176 | tf_op jit(solution)/shard_map/ppermute | solution.py:460
  56.2 2.4 collective-permute-done.4.rest_4_
  58.7 1.5 collective-permute-start.9
  60.2 1.8 collective-permute-start.10
  62.0 10.1 %collective-permute-done.6.rest_6_ = bf16[2,128,512]{2,1,0:T(8,128)(2,1)S(1)} collective-permute-done((bf16[2,128,512]{2,1,0:T(8,128)(2,1)}, bf16[2,128,512]{2,1,0:T(8,128)(2,1)S(1)}, u32[]{:S(2)}, u32[]{:S(2)}) %collective-permute-start.6) | collective-permute-done | bytes 262176 | tf_op jit(solution)/shard_map/ppermute | solution.py:460
  73.7 1.0 add.78.lists_ref
  74.7 3.2 %concatenate.3.tiles_ref = bf16[2,65,128,128]{3,2,1,0:T(8,128)(2,1)S(1)} pad(bf16[2,64,128,128]{3,2,1,0:T(8,128)(2,1)} %param.9, bf16[]{:T(256)} %constant.66.clone.1), padding=0_0x0_1x0_0x0_0 | pad | bytes 8454146 | tf_op jit(solution)/shard_map/concatenate | solution.py:487
  77.9 4.7 %collective-permute-start.13 = (bf16[2,128,512]{2,1,0:T(8,128)(2,1)S(1)}, bf16[2,128,512]{2,1,0:T(8,128)(2,1)S(1)}, u32[]{:S(2)}, u32[]{:S(2)}) collective-permute-start(bf16[2,128,512]{2,1,0:T(8,128)(2,1)S(1)} %copy-done.8), channel_id=1, source_target_pairs={{0,6},{1,7},{2,4},{3,5},{4,2},{5,3},{6,0},{7,1},{8,14},{9,15},{10,... | collective-permute-start | bytes 786440 | tf_op jit(solution)/shard_map/ppermute | solution.py:460
  82.6 11.3 %collective-permute-start.14 = (bf16[2,128,512]{2,1,0:T(8,128)(2,1)S(1)}, bf16[2,128,512]{2,1,0:T(8,128)(2,1)S(1)}, u32[]{:S(2)}, u32[]{:S(2)}) collective-permute-start(bf16[2,128,512]{2,1,0:T(8,128)(2,1)S(1)} %get-tuple-element.61), channel_id=1, source_target_pairs={{0,24},{1,25},{2,26},{3,27},{4,28},{5,29},{6,30},{7,31},{8,16},{9,... | collective-permute-start | bytes 786440 | tf_op jit(solution)/shard_map/ppermute | solution.py:460
  93.9 7.3 %collective-permute-done.10.rest_10_ = bf16[2,128,512]{2,1,0:T(8,128)(2,1)} collective-permute-done((bf16[2,128,512]{2,1,0:T(8,128)(2,1)}, bf16[2,128,512]{2,1,0:T(8,128)(2,1)}, u32[]{:S(2)}, u32[]{:S(2)}) %collective-permute-start.10) | collective-permute-done | bytes 262176 | tf_op jit(solution)/shard_map/ppermute | solution.py:460
  101.2 17.9 %collective-permute-start.16 = (bf16[2,128,512]{2,1,0:T(8,128)(2,1)S(1)}, bf16[2,128,512]{2,1,0:T(8,128)(2,1)S(1)}, u32[]{:S(2)}, u32[]{:S(2)}) collective-permute-start(bf16[2,128,512]{2,1,0:T(8,128)(2,1)S(1)} %get-tuple-element.63), channel_id=1, source_target_pairs={{0,25},{1,24},{2,27},{3,26},{4,29},{5,28},{6,31},{7,30},{8,17},{9,... | collective-permute-start | bytes 786440 | tf_op jit(solution)/shard_map/ppermute | solution.py:460
  119.1 14.7 %hops.1.in_ref = f32[64,128,512]{2,1,0:T(8,128)} custom-call(s32[3,1024]{1,0:T(4,128)S(1)} %add.78.lists_ref, s32[3,64]{1,0:T(4,128)S(1)} %get-tuple-element.89.counts_ref, bf16[2,65,128,128]{3,2,1,0:T(8,128)(2,1)S(1)} %concatenate.3.tiles_ref, bf16[32,128,512]{2,1,0:T(8,128)(2,1)S(1)} %bitcast.21), custom_call_target="tpu_custom_call" | custom-call | flops 8000000000 | bytes 41943040 | tf_op jit(solution)/shard_map/hops/pallas_call | solution.py:217
  133.8 1.7 collective-permute-start.18
  135.5 1.4 collective-permute-start.19
  136.9 2.1 collective-permute-start.20
  139.1 6.6 %collective-permute-start.21 = (bf16[2,128,512]{2,1,0:T(8,128)(2,1)}, bf16[2,128,512]{2,1,0:T(8,128)(2,1)S(1)}, u32[]{:S(2)}, u32[]{:S(2)}) collective-permute-start(bf16[2,128,512]{2,1,0:T(8,128)(2,1)} %get-tuple-element.69), channel_id=1, source_target_pairs={{0,10},{1,11},{2,8},{3,9},{4,14},{5,15},{6,12},{7,13},{8,2},{9,3},... | collective-permute-start | bytes 786440 | tf_op jit(solution)/shard_map/ppermute | solution.py:460
  146.4 27.5 %adjoint.1 = (bf16[2,512,2048]{2,1,0:T(8,128)(2,1)S(1)}, bf16[2,512,512]{2,1,0:T(8,128)(2,1)S(1)}, bf16[2,512,768]{2,1,0:T(8,128)(2,1)S(1)}) custom-call(s32[3,1024]{1,0:T(4,128)S(1)} %add.78.lists_ref, s32[3,64]{1,0:T(4,128)S(1)} %get-tuple-element.89.counts_ref, bf16[2,65,128,128]{3,2,1,0:T(8,128)(2,1)S(1)} %concatenate.3.tiles_ref, ...), custom_call_target="tpu_custom_call" | custom-call | flops 8000000000 | bytes 16777216 | tf_op jit(solution)/shard_map/adjoint/pallas_call | solution.py:279
  173.9 2.0 copy-done.3
  175.9 1.1 copy-done.17
  177.1 1.0 copy-done.19
  178.1 6.3 %copy.29 = bf16[4,512,1024]{2,1,0:T(8,128)(2,1)} copy(bf16[4,512,1024]{1,2,0:T(8,128)(2,1)} %bitcast.24) | data formatting | bytes 8388608 | tf_op jit(solution)/shard_map/transpose | solution.py:489
  184.4 3.2 %copy.30 = bf16[4,2,16,16,1024]{4,3,2,1,0:T(8,128)(2,1)S(1)} copy(bf16[4,2,16,16,1024]{4,3,1,2,0:T(8,128)(2,1)} %bitcast.29) | data formatting | bytes 8388608 | tf_op jit(solution)/shard_map/transpose | solution.py:492
  187.6 5.9 %collective-permute-start.23 = (bf16[2,128,512]{2,1,0:T(8,128)(2,1)S(1)}, bf16[2,128,512]{2,1,0:T(8,128)(2,1)S(1)}, u32[]{:S(2)}, u32[]{:S(2)}) collective-permute-start(bf16[2,128,512]{2,1,0:T(8,128)(2,1)S(1)} %get-tuple-element.71), channel_id=1, source_target_pairs={{0,11},{1,10},{2,9},{3,8},{4,15},{5,14},{6,13},{7,12},{8,3},{9,2},... | collective-permute-start | bytes 786440 | tf_op jit(solution)/shard_map/ppermute | solution.py:460
  193.4 7.2 %collective-permute-start.24 = (bf16[2,128,512]{2,1,0:T(8,128)(2,1)S(1)}, bf16[2,128,512]{2,1,0:T(8,128)(2,1)S(1)}, u32[]{:S(2)}, u32[]{:S(2)}) collective-permute-start(bf16[2,128,512]{2,1,0:T(8,128)(2,1)S(1)} %get-tuple-element.72), channel_id=1, source_target_pairs={{0,29},{1,28},{2,31},{3,30},{4,25},{5,24},{6,27},{7,26},{8,21},{9,... | collective-permute-start | bytes 786440 | tf_op jit(solution)/shard_map/ppermute | solution.py:460
  200.9 22.9 %gram.1.in_ref = f32[512,1024]{1,0:T(8,128)S(1)} custom-call(s32[3,1024]{1,0:T(4,128)S(1)} %add.78.lists_ref, s32[3,64]{1,0:T(4,128)S(1)} %get-tuple-element.89.counts_ref, bf16[2,65,128,128]{3,2,1,0:T(8,128)(2,1)S(1)} %bitcast.23, f32[64,128,512]{2,1,0:T(8,128)} %hops.1.in_ref, bf16[4,512,1024]{2,1,0:T(8,128)(2,1)S(1)} %bitcast.26, ...), custom_call_target="tpu_custom_call" | custom-call | flops 12000000000 | bytes 25165824 | tf_op jit(solution)/shard_map/gram/pallas_call | solution.py:362
  223.8 7.0 %collective-permute-start.28 = (bf16[2,128,512]{2,1,0:T(8,128)(2,1)S(1)}, bf16[2,128,512]{2,1,0:T(8,128)(2,1)S(1)}, u32[]{:S(2)}, u32[]{:S(2)}) collective-permute-start(bf16[2,128,512]{2,1,0:T(8,128)(2,1)S(1)} %get-tuple-element.78), channel_id=1, source_target_pairs={{0,31},{1,30},{2,29},{3,28},{4,27},{5,26},{6,25},{7,24},{8,23},{9,... | collective-permute-start | bytes 786440 | tf_op jit(solution)/shard_map/ppermute | solution.py:460
  230.8 1.6 collective-permute-start.30
  232.4 2.4 late.4.in_ref
  235.6 1.9 collective-permute-done.28.rest_0_
  237.5 8.7 %collective-permute-done.29.rest_1_ = bf16[2,128,512]{2,1,0:T(8,128)(2,1)S(1)} collective-permute-done((bf16[2,128,512]{2,1,0:T(8,128)(2,1)S(1)}, bf16[2,128,512]{2,1,0:T(8,128)(2,1)S(1)}, u32[]{:S(2)}, u32[]{:S(2)}) %collective-permute-start.29) | collective-permute-done | bytes 262176 | tf_op jit(solution)/shard_map/ppermute | solution.py:460
  246.3 3.4 %collective-permute-done.30.rest_2_ = bf16[2,128,512]{2,1,0:T(8,128)(2,1)S(1)} collective-permute-done((bf16[2,128,512]{2,1,0:T(8,128)(2,1)S(1)}, bf16[2,128,512]{2,1,0:T(8,128)(2,1)S(1)}, u32[]{:S(2)}, u32[]{:S(2)}) %collective-permute-start.30) | collective-permute-done | bytes 262176 | tf_op jit(solution)/shard_map/ppermute | solution.py:460
  250.9 2.1 collective-permute-done.31.rest_0_
  253.2 1.5 collective-permute-start.33
  254.8 1.9 collective-permute-start.34
  256.7 3.8 %collective-permute-done.32.rest_0_ = bf16[4,16,1024]{2,1,0:T(8,128)(2,1)S(1)} collective-permute-done((bf16[4,16,1024]{2,1,0:T(8,128)(2,1)S(1)}, bf16[4,16,1024]{2,1,0:T(8,128)(2,1)S(1)}, u32[]{:S(2)}, u32[]{:S(2)}) %collective-permute-start.32) | collective-permute-done | bytes 131104 | tf_op jit(solution)/shard_map/ppermute | solution.py:460
  260.5 1.1 collective-permute-done.33.rest_1_
  261.6 0.9 collective-permute-done.34.rest_2_
  262.5 2.9 %collective-permute-start.35 = (f32[16,1024]{1,0:T(8,128)S(1)}, f32[16,1024]{1,0:T(8,128)S(1)}, u32[]{:S(2)}, u32[]{:S(2)}) collective-permute-start(f32[16,1024]{1,0:T(8,128)S(1)} %get-tuple-element.86), channel_id=1, source_target_pairs={{0,16},{1,17},{2,18},{3,19},{4,20},{5,21},{6,22},{7,23},{8,24},{9,... | collective-permute-start | bytes 196616 | tf_op jit(solution)/shard_map/ppermute | solution.py:460
  265.5 3.3 %collective-permute-start.36 = (f32[16,1024]{1,0:T(8,128)S(1)}, f32[16,1024]{1,0:T(8,128)S(1)}, u32[]{:S(2)}, u32[]{:S(2)}) collective-permute-start(f32[16,1024]{1,0:T(8,128)S(1)} %get-tuple-element.87), channel_id=1, source_target_pairs={{0,24},{1,25},{2,26},{3,27},{4,28},{5,29},{6,30},{7,31},{8,16},{9,... | collective-permute-start | bytes 196616 | tf_op jit(solution)/shard_map/ppermute | solution.py:460
  268.7 3.6 %collective-permute-done.36.rest_1_ = f32[16,1024]{1,0:T(8,128)S(1)} collective-permute-done((f32[16,1024]{1,0:T(8,128)S(1)}, f32[16,1024]{1,0:T(8,128)S(1)}, u32[]{:S(2)}, u32[]{:S(2)}) %collective-permute-start.36) | collective-permute-done | bytes 65568 | tf_op jit(solution)/shard_map/ppermute | solution.py:460
  (132 shorter events, 15.0 us)
Async XLA Ops:
  0.0 28.2 %copy-start.21 = (s32[2,32,16]{1,2,0:T(8,128)S(1)}, s32[2,32,16]{1,2,0:T(8,128)}, u32[]{:S(2)}) copy-start(s32[2,32,16]{1,2,0:T(8,128)} %param.11) | copy-start | bytes 12292
  0.0 28.2 %copy-start.22 = (s32[2,32,16]{1,2,0:T(8,128)S(1)}, s32[2,32,16]{1,2,0:T(8,128)}, u32[]{:S(2)}) copy-start(s32[2,32,16]{1,2,0:T(8,128)} %param.10) | copy-start | bytes 12292
  0.0 28.4 %copy-start.23 = (s32[31]{0:T(128)S(1)}, s32[31]{0:T(128)}, u32[]{:S(2)}) copy-start(s32[31]{0:T(128)} %constant.67.clone) | copy-start | bytes 376
  3.0 28.5 %collective-permute-start = (bf16[2,128,512]{2,1,0:T(8,128)(2,1)}, bf16[2,128,512]{2,1,0:T(8,128)(2,1)}, u32[]{:S(2)}, u32[]{:S(2)}) collective-permute-start(bf16[2,128,512]{2,1,0:T(8,128)(2,1)} %get-tuple-element.47), channel_id=1, source_target_pairs={{0,16},{1,17},{2,18},{3,19},{4,20},{5,21},{6,22},{7,23},{8,24},{9,... | collective-permute-start | bytes 786440 | tf_op jit(solution)/shard_map/ppermute | solution.py:460
  7.1 33.9 %collective-permute-start.1 = (bf16[2,128,512]{2,1,0:T(8,128)(2,1)}, bf16[2,128,512]{2,1,0:T(8,128)(2,1)}, u32[]{:S(2)}, u32[]{:S(2)}) collective-permute-start(bf16[2,128,512]{2,1,0:T(8,128)(2,1)} %get-tuple-element.48), channel_id=1, source_target_pairs={{0,17},{1,16},{2,19},{3,18},{4,21},{5,20},{6,23},{7,22},{8,25},{9,... | collective-permute-start | bytes 786440 | tf_op jit(solution)/shard_map/ppermute | solution.py:460
  7.1 48.0 %collective-permute-start.2 = (bf16[2,128,512]{2,1,0:T(8,128)(2,1)}, bf16[2,128,512]{2,1,0:T(8,128)(2,1)}, u32[]{:S(2)}, u32[]{:S(2)}) collective-permute-start(bf16[2,128,512]{2,1,0:T(8,128)(2,1)} %get-tuple-element.49), channel_id=1, source_target_pairs={{0,18},{1,19},{2,16},{3,17},{4,22},{5,23},{6,20},{7,21},{8,26},{9,... | collective-permute-start | bytes 786440 | tf_op jit(solution)/shard_map/ppermute | solution.py:460
  26.5 107.3 %copy-start.6 = (bf16[2,128,512]{2,1,0:T(8,128)(2,1)}, bf16[2,128,512]{2,1,0:T(8,128)(2,1)S(1)}, u32[]{:S(2)}) copy-start(bf16[2,128,512]{2,1,0:T(8,128)(2,1)S(1)} %get-tuple-element.70) | copy-start | bytes 786436
  27.2 28.2 %collective-permute-start.3 = (bf16[2,128,512]{2,1,0:T(8,128)(2,1)}, bf16[2,128,512]{2,1,0:T(8,128)(2,1)}, u32[]{:S(2)}, u32[]{:S(2)}) collective-permute-start(bf16[2,128,512]{2,1,0:T(8,128)(2,1)} %get-tuple-element.50), channel_id=1, source_target_pairs={{0,1},{1,0},{2,3},{3,2},{4,5},{5,4},{6,7},{7,6},{8,9},{9,8},{10,11... | collective-permute-start | bytes 786440 | tf_op jit(solution)/shard_map/ppermute | solution.py:460
  28.0 30.6 %collective-permute-start.4 = (bf16[2,128,512]{2,1,0:T(8,128)(2,1)}, bf16[2,128,512]{2,1,0:T(8,128)(2,1)}, u32[]{:S(2)}, u32[]{:S(2)}) collective-permute-start(bf16[2,128,512]{2,1,0:T(8,128)(2,1)} %get-tuple-element.51), channel_id=1, source_target_pairs={{0,19},{1,18},{2,17},{3,16},{4,23},{5,22},{6,21},{7,20},{8,27},{9,... | collective-permute-start | bytes 786440 | tf_op jit(solution)/shard_map/ppermute | solution.py:460
  31.5 28.7 %collective-permute-start.5 = (bf16[2,128,512]{2,1,0:T(8,128)(2,1)}, bf16[2,128,512]{2,1,0:T(8,128)(2,1)S(1)}, u32[]{:S(2)}, u32[]{:S(2)}) collective-permute-start(bf16[2,128,512]{2,1,0:T(8,128)(2,1)} %copy-done.16), channel_id=1, source_target_pairs={{0,2},{1,3},{2,0},{3,1},{4,6},{5,7},{6,4},{7,5},{8,10},{9,11},{10,... | collective-permute-start | bytes 786440 | tf_op jit(solution)/shard_map/ppermute | solution.py:460
  41.0 31.1 %collective-permute-start.6 = (bf16[2,128,512]{2,1,0:T(8,128)(2,1)}, bf16[2,128,512]{2,1,0:T(8,128)(2,1)S(1)}, u32[]{:S(2)}, u32[]{:S(2)}) collective-permute-start(bf16[2,128,512]{2,1,0:T(8,128)(2,1)} %copy-done.15), channel_id=1, source_target_pairs={{0,20},{1,21},{2,22},{3,23},{4,16},{5,17},{6,18},{7,19},{8,28},{9,... | collective-permute-start | bytes 786440 | tf_op jit(solution)/shard_map/ppermute | solution.py:460
  55.2 16.9 %collective-permute-start.7 = (bf16[2,128,512]{2,1,0:T(8,128)(2,1)}, bf16[2,128,512]{2,1,0:T(8,128)(2,1)S(1)}, u32[]{:S(2)}, u32[]{:S(2)}) collective-permute-start(bf16[2,128,512]{2,1,0:T(8,128)(2,1)} %copy-done.14), channel_id=1, source_target_pairs={{0,3},{1,2},{2,1},{3,0},{4,7},{5,6},{6,5},{7,4},{8,11},{9,10},{10,... | collective-permute-start | bytes 786440 | tf_op jit(solution)/shard_map/ppermute | solution.py:460
  55.4 22.5 %collective-permute-start.8 = (bf16[2,128,512]{2,1,0:T(8,128)(2,1)}, bf16[2,128,512]{2,1,0:T(8,128)(2,1)}, u32[]{:S(2)}, u32[]{:S(2)}) collective-permute-start(bf16[2,128,512]{2,1,0:T(8,128)(2,1)} %copy-done.13), channel_id=1, source_target_pairs={{0,21},{1,20},{2,23},{3,22},{4,17},{5,16},{6,19},{7,18},{8,29},{9,... | collective-permute-start | bytes 786440 | tf_op jit(solution)/shard_map/ppermute | solution.py:460
  58.7 23.9 %collective-permute-start.9 = (bf16[2,128,512]{2,1,0:T(8,128)(2,1)}, bf16[2,128,512]{2,1,0:T(8,128)(2,1)}, u32[]{:S(2)}, u32[]{:S(2)}) collective-permute-start(bf16[2,128,512]{2,1,0:T(8,128)(2,1)} %copy-done.12), channel_id=1, source_target_pairs={{0,4},{1,5},{2,6},{3,7},{4,0},{5,1},{6,2},{7,3},{8,12},{9,13},{10,... | collective-permute-start | bytes 786440 | tf_op jit(solution)/shard_map/ppermute | solution.py:460
  60.2 41.0 %collective-permute-start.10 = (bf16[2,128,512]{2,1,0:T(8,128)(2,1)}, bf16[2,128,512]{2,1,0:T(8,128)(2,1)}, u32[]{:S(2)}, u32[]{:S(2)}) collective-permute-start(bf16[2,128,512]{2,1,0:T(8,128)(2,1)} %copy-done.11), channel_id=1, source_target_pairs={{0,22},{1,23},{2,20},{3,21},{4,18},{5,19},{6,16},{7,17},{8,30},{9,... | collective-permute-start | bytes 786440 | tf_op jit(solution)/shard_map/ppermute | solution.py:460
  72.0 29.2 %collective-permute-start.11 = (bf16[2,128,512]{2,1,0:T(8,128)(2,1)}, bf16[2,128,512]{2,1,0:T(8,128)(2,1)}, u32[]{:S(2)}, u32[]{:S(2)}) collective-permute-start(bf16[2,128,512]{2,1,0:T(8,128)(2,1)} %copy-done.10), channel_id=1, source_target_pairs={{0,5},{1,4},{2,7},{3,6},{4,1},{5,0},{6,3},{7,2},{8,13},{9,12},{10,... | collective-permute-start | bytes 786440 | tf_op jit(solution)/shard_map/ppermute | solution.py:460
  72.1 47.0 %collective-permute-start.12 = (bf16[2,128,512]{2,1,0:T(8,128)(2,1)}, bf16[2,128,512]{2,1,0:T(8,128)(2,1)}, u32[]{:S(2)}, u32[]{:S(2)}) collective-permute-start(bf16[2,128,512]{2,1,0:T(8,128)(2,1)} %copy-done.9), channel_id=1, source_target_pairs={{0,23},{1,22},{2,21},{3,20},{4,19},{5,18},{6,17},{7,16},{8,31},{9,... | collective-permute-start | bytes 786440 | tf_op jit(solution)/shard_map/ppermute | solution.py:460
  74.7 44.4 %copy-start = (bf16[4096,512]{1,0:T(8,128)(2,1)S(1)}, bf16[4096,512]{1,0:T(8,128)(2,1)}, u32[]{:S(2)}) copy-start(bf16[4096,512]{1,0:T(8,128)(2,1)} %param.8) | copy-start | bytes 12582916
  77.9 68.5 %copy-start.1 = (bf16[2,65,128,128]{3,2,1,0:T(8,128)(2,1)}, bf16[2,65,128,128]{3,2,1,0:T(8,128)(2,1)S(1)}, u32[]{:S(2)}) copy-start(bf16[2,65,128,128]{3,2,1,0:T(8,128)(2,1)S(1)} %concatenate.3.tiles_ref) | copy-start | bytes 12779524
  77.9 55.9 %collective-permute-start.13 = (bf16[2,128,512]{2,1,0:T(8,128)(2,1)S(1)}, bf16[2,128,512]{2,1,0:T(8,128)(2,1)S(1)}, u32[]{:S(2)}, u32[]{:S(2)}) collective-permute-start(bf16[2,128,512]{2,1,0:T(8,128)(2,1)S(1)} %copy-done.8), channel_id=1, source_target_pairs={{0,6},{1,7},{2,4},{3,5},{4,2},{5,3},{6,0},{7,1},{8,14},{9,15},{10,... | collective-permute-start | bytes 786440 | tf_op jit(solution)/shard_map/ppermute | solution.py:460
  82.6 52.9 %collective-permute-start.14 = (bf16[2,128,512]{2,1,0:T(8,128)(2,1)S(1)}, bf16[2,128,512]{2,1,0:T(8,128)(2,1)S(1)}, u32[]{:S(2)}, u32[]{:S(2)}) collective-permute-start(bf16[2,128,512]{2,1,0:T(8,128)(2,1)S(1)} %get-tuple-element.61), channel_id=1, source_target_pairs={{0,24},{1,25},{2,26},{3,27},{4,28},{5,29},{6,30},{7,31},{8,16},{9,... | collective-permute-start | bytes 786440 | tf_op jit(solution)/shard_map/ppermute | solution.py:460
  101.2 35.7 %collective-permute-start.15 = (bf16[2,128,512]{2,1,0:T(8,128)(2,1)S(1)}, bf16[2,128,512]{2,1,0:T(8,128)(2,1)S(1)}, u32[]{:S(2)}, u32[]{:S(2)}) collective-permute-start(bf16[2,128,512]{2,1,0:T(8,128)(2,1)S(1)} %get-tuple-element.62), channel_id=1, source_target_pairs={{0,7},{1,6},{2,5},{3,4},{4,3},{5,2},{6,1},{7,0},{8,15},{9,14},{10,... | collective-permute-start | bytes 786440 | tf_op jit(solution)/shard_map/ppermute | solution.py:460
  101.2 37.9 %collective-permute-start.16 = (bf16[2,128,512]{2,1,0:T(8,128)(2,1)S(1)}, bf16[2,128,512]{2,1,0:T(8,128)(2,1)S(1)}, u32[]{:S(2)}, u32[]{:S(2)}) collective-permute-start(bf16[2,128,512]{2,1,0:T(8,128)(2,1)S(1)} %get-tuple-element.63), channel_id=1, source_target_pairs={{0,25},{1,24},{2,27},{3,26},{4,29},{5,28},{6,31},{7,30},{8,17},{9,... | collective-permute-start | bytes 786440 | tf_op jit(solution)/shard_map/ppermute | solution.py:460
  119.1 26.6 %collective-permute-start.17 = (bf16[2,128,512]{2,1,0:T(8,128)(2,1)S(1)}, bf16[2,128,512]{2,1,0:T(8,128)(2,1)S(1)}, u32[]{:S(2)}, u32[]{:S(2)}) collective-permute-start(bf16[2,128,512]{2,1,0:T(8,128)(2,1)S(1)} %get-tuple-element.64), channel_id=1, source_target_pairs={{0,8},{1,9},{2,10},{3,11},{4,12},{5,13},{6,14},{7,15},{8,0},{9,1},... | collective-permute-start | bytes 786440 | tf_op jit(solution)/shard_map/ppermute | solution.py:460
  119.1 27.3 %copy-start.2 = (bf16[4096,512]{1,0:T(8,128)(2,1)S(1)}, bf16[4096,512]{1,0:T(8,128)(2,1)}, u32[]{:S(2)}) copy-start(bf16[4096,512]{1,0:T(8,128)(2,1)} %param.7) | copy-start | bytes 12582916
  133.8 53.7 %collective-permute-start.18 = (bf16[2,128,512]{2,1,0:T(8,128)(2,1)}, bf16[2,128,512]{2,1,0:T(8,128)(2,1)S(1)}, u32[]{:S(2)}, u32[]{:S(2)}) collective-permute-start(bf16[2,128,512]{2,1,0:T(8,128)(2,1)} %get-tuple-element.66), channel_id=1, source_target_pairs={{0,26},{1,27},{2,24},{3,25},{4,30},{5,31},{6,28},{7,29},{8,18},{9,... | collective-permute-start | bytes 786440 | tf_op jit(solution)/shard_map/ppermute | solution.py:460
  135.5 57.9 %collective-permute-start.19 = (bf16[2,128,512]{2,1,0:T(8,128)(2,1)}, bf16[2,128,512]{2,1,0:T(8,128)(2,1)S(1)}, u32[]{:S(2)}, u32[]{:S(2)}) collective-permute-start(bf16[2,128,512]{2,1,0:T(8,128)(2,1)} %get-tuple-element.67), channel_id=1, source_target_pairs={{0,9},{1,8},{2,11},{3,10},{4,13},{5,12},{6,15},{7,14},{8,1},{9,0},... | collective-permute-start | bytes 786440 | tf_op jit(solution)/shard_map/ppermute | solution.py:460
  136.9 63.7 %collective-permute-start.20 = (bf16[2,128,512]{2,1,0:T(8,128)(2,1)}, bf16[2,128,512]{2,1,0:T(8,128)(2,1)S(1)}, u32[]{:S(2)}, u32[]{:S(2)}) collective-permute-start(bf16[2,128,512]{2,1,0:T(8,128)(2,1)} %get-tuple-element.68), channel_id=1, source_target_pairs={{0,27},{1,26},{2,25},{3,24},{4,31},{5,30},{6,29},{7,28},{8,19},{9,... | collective-permute-start | bytes 786440 | tf_op jit(solution)/shard_map/ppermute | solution.py:460
  139.1 61.6 %collective-permute-start.21 = (bf16[2,128,512]{2,1,0:T(8,128)(2,1)}, bf16[2,128,512]{2,1,0:T(8,128)(2,1)S(1)}, u32[]{:S(2)}, u32[]{:S(2)}) collective-permute-start(bf16[2,128,512]{2,1,0:T(8,128)(2,1)} %get-tuple-element.69), channel_id=1, source_target_pairs={{0,10},{1,11},{2,8},{3,9},{4,14},{5,15},{6,12},{7,13},{8,2},{9,3},... | collective-permute-start | bytes 786440 | tf_op jit(solution)/shard_map/ppermute | solution.py:460
  145.7 55.1 %collective-permute-start.22 = (bf16[2,128,512]{2,1,0:T(8,128)(2,1)}, bf16[2,128,512]{2,1,0:T(8,128)(2,1)S(1)}, u32[]{:S(2)}, u32[]{:S(2)}) collective-permute-start(bf16[2,128,512]{2,1,0:T(8,128)(2,1)} %copy-done.6), channel_id=1, source_target_pairs={{0,28},{1,29},{2,30},{3,31},{4,24},{5,25},{6,26},{7,27},{8,20},{9,... | collective-permute-start | bytes 786440 | tf_op jit(solution)/shard_map/ppermute | solution.py:460
  178.1 22.8 %slice-start = ((s8[4259840]{0:T(1024)(128)(4,1)}), s8[65536]{0:T(1024)(128)(4,1)S(1)}, s32[]{:S(2)}) async-start(s8[4259840]{0:T(1024)(128)(4,1)} %bitcast.22), calls=%async_computation | async-start | bytes 131072
  184.4 16.5 %slice-start.1 = ((s8[4259840]{0:T(1024)(128)(4,1)}), s8[4194304]{0:T(1024)(128)(4,1)S(1)}, s32[]{:S(2)}) async-start(s8[4259840]{0:T(1024)(128)(4,1)} %bitcast.22), calls=%async_computation.1 | async-start | bytes 8388608
  187.6 36.2 %collective-permute-start.23 = (bf16[2,128,512]{2,1,0:T(8,128)(2,1)S(1)}, bf16[2,128,512]{2,1,0:T(8,128)(2,1)S(1)}, u32[]{:S(2)}, u32[]{:S(2)}) collective-permute-start(bf16[2,128,512]{2,1,0:T(8,128)(2,1)S(1)} %get-tuple-element.71), channel_id=1, source_target_pairs={{0,11},{1,10},{2,9},{3,8},{4,15},{5,14},{6,13},{7,12},{8,3},{9,2},... | collective-permute-start | bytes 786440 | tf_op jit(solution)/shard_map/ppermute | solution.py:460
  193.4 37.4 %collective-permute-start.24 = (bf16[2,128,512]{2,1,0:T(8,128)(2,1)S(1)}, bf16[2,128,512]{2,1,0:T(8,128)(2,1)S(1)}, u32[]{:S(2)}, u32[]{:S(2)}) collective-permute-start(bf16[2,128,512]{2,1,0:T(8,128)(2,1)S(1)} %get-tuple-element.72), channel_id=1, source_target_pairs={{0,29},{1,28},{2,31},{3,30},{4,25},{5,24},{6,27},{7,26},{8,21},{9,... | collective-permute-start | bytes 786440 | tf_op jit(solution)/shard_map/ppermute | solution.py:460
  200.7 30.2 %collective-permute-start.25 = (bf16[2,128,512]{2,1,0:T(8,128)(2,1)S(1)}, bf16[2,128,512]{2,1,0:T(8,128)(2,1)S(1)}, u32[]{:S(2)}, u32[]{:S(2)}) collective-permute-start(bf16[2,128,512]{2,1,0:T(8,128)(2,1)S(1)} %get-tuple-element.73), channel_id=1, source_target_pairs={{0,12},{1,13},{2,14},{3,15},{4,8},{5,9},{6,10},{7,11},{8,4},{9,5},... | collective-permute-start | bytes 786440 | tf_op jit(solution)/shard_map/ppermute | solution.py:460
  200.7 34.2 %collective-permute-start.26 = (bf16[2,128,512]{2,1,0:T(8,128)(2,1)S(1)}, bf16[2,128,512]{2,1,0:T(8,128)(2,1)S(1)}, u32[]{:S(2)}, u32[]{:S(2)}) collective-permute-start(bf16[2,128,512]{2,1,0:T(8,128)(2,1)S(1)} %get-tuple-element.75), channel_id=1, source_target_pairs={{0,30},{1,31},{2,28},{3,29},{4,26},{5,27},{6,24},{7,25},{8,22},{9,... | collective-permute-start | bytes 786440 | tf_op jit(solution)/shard_map/ppermute | solution.py:460
  200.8 34.1 %collective-permute-start.27 = (bf16[2,128,512]{2,1,0:T(8,128)(2,1)S(1)}, bf16[2,128,512]{2,1,0:T(8,128)(2,1)S(1)}, u32[]{:S(2)}, u32[]{:S(2)}) collective-permute-start(bf16[2,128,512]{2,1,0:T(8,128)(2,1)S(1)} %get-tuple-element.76), channel_id=1, source_target_pairs={{0,13},{1,12},{2,15},{3,14},{4,9},{5,8},{6,11},{7,10},{8,5},{9,4},... | collective-permute-start | bytes 786440 | tf_op jit(solution)/shard_map/ppermute | solution.py:460
  200.9 31.5 %copy-start.4 = (bf16[2,512,2048]{2,1,0:T(8,128)(2,1)S(1)}, bf16[2,512,2048]{2,1,0:T(8,128)(2,1)}, u32[]{:S(2)}) copy-start(bf16[2,512,2048]{2,1,0:T(8,128)(2,1)} %copy-done.3) | copy-start | bytes 12582916
  223.8 13.7 %collective-permute-start.28 = (bf16[2,128,512]{2,1,0:T(8,128)(2,1)S(1)}, bf16[2,128,512]{2,1,0:T(8,128)(2,1)S(1)}, u32[]{:S(2)}, u32[]{:S(2)}) collective-permute-start(bf16[2,128,512]{2,1,0:T(8,128)(2,1)S(1)} %get-tuple-element.78), channel_id=1, source_target_pairs={{0,31},{1,30},{2,29},{3,28},{4,27},{5,26},{6,25},{7,24},{8,23},{9,... | collective-permute-start | bytes 786440 | tf_op jit(solution)/shard_map/ppermute | solution.py:460
  230.8 15.4 %collective-permute-start.29 = (bf16[2,128,512]{2,1,0:T(8,128)(2,1)S(1)}, bf16[2,128,512]{2,1,0:T(8,128)(2,1)S(1)}, u32[]{:S(2)}, u32[]{:S(2)}) collective-permute-start(bf16[2,128,512]{2,1,0:T(8,128)(2,1)S(1)} %get-tuple-element.79), channel_id=1, source_target_pairs={{0,14},{1,15},{2,12},{3,13},{4,10},{5,11},{6,8},{7,9},{8,6},{9,7},... | collective-permute-start | bytes 786440 | tf_op jit(solution)/shard_map/ppermute | solution.py:460
  230.8 18.9 %collective-permute-start.30 = (bf16[2,128,512]{2,1,0:T(8,128)(2,1)S(1)}, bf16[2,128,512]{2,1,0:T(8,128)(2,1)S(1)}, u32[]{:S(2)}, u32[]{:S(2)}) collective-permute-start(bf16[2,128,512]{2,1,0:T(8,128)(2,1)S(1)} %get-tuple-element.80), channel_id=1, source_target_pairs={{0,15},{1,14},{2,13},{3,12},{4,11},{5,10},{6,9},{7,8},{8,7},{9,6},... | collective-permute-start | bytes 786440 | tf_op jit(solution)/shard_map/ppermute | solution.py:460
  250.3 2.7 collective-permute-start.31
  253.2 7.3 %collective-permute-start.32 = (bf16[4,16,1024]{2,1,0:T(8,128)(2,1)S(1)}, bf16[4,16,1024]{2,1,0:T(8,128)(2,1)S(1)}, u32[]{:S(2)}, u32[]{:S(2)}) collective-permute-start(bf16[4,16,1024]{2,1,0:T(8,128)(2,1)S(1)} %get-tuple-element.82), channel_id=1, source_target_pairs={{0,6},{1,7},{2,4},{3,5},{4,2},{5,3},{6,0},{7,1},{8,14},{9,15},{10,... | collective-permute-start | bytes 393224 | tf_op jit(solution)/shard_map/ppermute | solution.py:460
  253.2 8.3 %collective-permute-start.33 = (bf16[4,16,1024]{2,1,0:T(8,128)(2,1)S(1)}, bf16[4,16,1024]{2,1,0:T(8,128)(2,1)S(1)}, u32[]{:S(2)}, u32[]{:S(2)}) collective-permute-start(bf16[4,16,1024]{2,1,0:T(8,128)(2,1)S(1)} %get-tuple-element.83), channel_id=1, source_target_pairs={{0,2},{1,3},{2,0},{3,1},{4,6},{5,7},{6,4},{7,5},{8,10},{9,11},{10,... | collective-permute-start | bytes 393224 | tf_op jit(solution)/shard_map/ppermute | solution.py:460
  254.8 7.7 %collective-permute-start.34 = (bf16[4,16,1024]{2,1,0:T(8,128)(2,1)S(1)}, bf16[4,16,1024]{2,1,0:T(8,128)(2,1)S(1)}, u32[]{:S(2)}, u32[]{:S(2)}) collective-permute-start(bf16[4,16,1024]{2,1,0:T(8,128)(2,1)S(1)} %get-tuple-element.84), channel_id=1, source_target_pairs={{0,4},{1,5},{2,6},{3,7},{4,0},{5,1},{6,2},{7,3},{8,12},{9,13},{10,... | collective-permute-start | bytes 393224 | tf_op jit(solution)/shard_map/ppermute | solution.py:460
  262.5 6.2 %collective-permute-start.35 = (f32[16,1024]{1,0:T(8,128)S(1)}, f32[16,1024]{1,0:T(8,128)S(1)}, u32[]{:S(2)}, u32[]{:S(2)}) collective-permute-start(f32[16,1024]{1,0:T(8,128)S(1)} %get-tuple-element.86), channel_id=1, source_target_pairs={{0,16},{1,17},{2,18},{3,19},{4,20},{5,21},{6,22},{7,23},{8,24},{9,... | collective-permute-start | bytes 196616 | tf_op jit(solution)/shard_map/ppermute | solution.py:460
  265.5 6.9 %collective-permute-start.36 = (f32[16,1024]{1,0:T(8,128)S(1)}, f32[16,1024]{1,0:T(8,128)S(1)}, u32[]{:S(2)}, u32[]{:S(2)}) collective-permute-start(f32[16,1024]{1,0:T(8,128)S(1)} %get-tuple-element.87), channel_id=1, source_target_pairs={{0,24},{1,25},{2,26},{3,27},{4,28},{5,29},{6,30},{7,31},{8,16},{9,... | collective-permute-start | bytes 196616 | tf_op jit(solution)/shard_map/ppermute | solution.py:460
  268.7 4.3 %collective-permute-start.37 = (f32[16,1024]{1,0:T(8,128)S(1)}, f32[16,1024]{1,0:T(8,128)S(1)}, u32[]{:S(2)}, u32[]{:S(2)}) collective-permute-start(f32[16,1024]{1,0:T(8,128)S(1)} %get-tuple-element.88), channel_id=1, source_target_pairs={{0,8},{1,9},{2,10},{3,11},{4,12},{5,13},{6,14},{7,15},{8,0},{9,1},... | collective-permute-start | bytes 196616 | tf_op jit(solution)/shard_map/ppermute | solution.py:460
  (24 other events, 94.7 us)
